TPU v7x, 32 devices: a whole 2x2x4 slice. The times are simulated.
32 devices in a mesh: aux: 8 (over y, x, core), pair: 4 (over z).
Axes of the slice: x: 2, y: 2, z: 4, core: 2. Of those that a mesh axis runs over, the one named last changes fastest.
Arguments:
- integrals: bfloat16 [3072, 32768], P('aux', 'pair'), may hold values from -0.15625 to 0.15625
- densities: bfloat16 [16, 32768], P(None, 'pair'), may hold values from -2.390625 to 2.390625
- screen: int32 [24, 256], P('aux', 'pair'), may hold values 0 or 1
- factor: float32 [3072, 3072], P('aux', 'pair'), may hold values from -0.109375 to 0.109375
- diag_inv: float32 [3072, 768], P('aux'), may hold values from -2 to 2, as said below
Outputs:
- coulomb: float32 [16, 32768], P(None, ('pair', 'aux'))
Inputs may be any that keep to these rules, and one draw needn't show every extreme that they name: `diag_inv`: each block of 768 rows is an upper triangular matrix with a positive diagonal.
All inputs are finite; a program needn't handle non-finite values. No bound on the sum of `screen` on one device may be relied on, other than what follows from the above.
Results may differ from a plain program's by a relative error of at most 0.0041.
Values may be sent and summed in bfloat16 or wider, within the bound.
No kernel may reach another device: no remote copies, remote signals or barrier semaphores. Data moves between devices by JAX's collectives and lax.ppermute only.
A program may use at most 128 MiB of HBM per device.

v0:
```python
import jax
import jax.numpy as jnp
from jax import lax
from jax.sharding import PartitionSpec as P

TILE = 128
SOLVE_BLOCKS = 4


def shards(integrals, densities, screen, factor, diag_inv):
    height = integrals.shape[0]
    breadth = factor.shape[1]
    block_size = diag_inv.shape[1]
    rows_aux = lax.axis_size("aux")
    total = height * rows_aux
    members = rows_aux // SOLVE_BLOCKS
    my_row = lax.axis_index("aux")
    my_column = lax.axis_index("pair")
    my_block = my_row // members
    count = densities.shape[0]
    highest = lax.Precision.HIGHEST
    expanded = jnp.repeat(jnp.repeat(screen, TILE, axis=0), TILE, axis=1).astype(jnp.bfloat16)
    masked = integrals * expanded
    partial_fit = lax.dot_general(
        densities, masked, (((1,), (1,)), ((), ())), preferred_element_type=jnp.float32
    )
    column_block = (my_column * breadth + jnp.arange(breadth, dtype=jnp.int32)) // block_size
    factor_low = jnp.where((column_block < my_block)[None, :], factor, 0.0)

    def apply_inverse(values):
        return jnp.dot(values, diag_inv, precision=highest, preferred_element_type=jnp.float32)

    def own_columns(whole):
        return lax.dynamic_slice_in_dim(whole, my_column * breadth, breadth, 1)

    def times_factor(known):
        return lax.dot_general(
            known,
            factor_low,
            (((1,), (1,)), ((), ())),
            precision=highest,
            preferred_element_type=jnp.float32,
        )

    zero_block = jnp.zeros((count, block_size), jnp.float32)
    solved = jnp.zeros((count, total), jnp.float32)
    for k in range(SOLVE_BLOCKS):

        def on_group(current):
            return apply_inverse(partial_fit - times_factor(own_columns(current)))

        def off_group(current):
            return zero_block

        summand = lax.cond(my_block == k, on_group, off_group, solved)
        arrived = lax.psum(summand, ("aux", "pair"))
        solved = lax.dynamic_update_slice_in_dim(solved, arrived, k * block_size, 1)
    own_coef = jnp.zeros((count, height), jnp.float32)
    contrib = jnp.zeros((count, total), jnp.float32)
    for target in reversed(range(SOLVE_BLOCKS)):
        if target < SOLVE_BLOCKS - 1:
            portion = contrib[:, target * block_size : (target + 1) * block_size]
            behind = lax.psum(portion, ("aux", "pair"))
            settled = solved[:, target * block_size : (target + 1) * block_size] - behind
        else:
            settled = solved[:, target * block_size : (target + 1) * block_size]

        def on_group(state):
            coef = lax.dot_general(
                settled,
                diag_inv,
                (((1,), (1,)), ((), ())),
                precision=highest,
                preferred_element_type=jnp.float32,
            )
            if target > 0:
                spread_out = jnp.dot(
                    coef, factor_low, precision=highest, preferred_element_type=jnp.float32
                )
                fresh = lax.dynamic_update_slice_in_dim(
                    jnp.zeros((count, total), jnp.float32), spread_out, my_column * breadth, 1
                )
            else:
                fresh = state[1]
            return (coef, fresh)

        def keep_state(state):
            return state

        own_coef, contrib = lax.cond(my_block == target, on_group, keep_state, (own_coef, contrib))
    rounded = own_coef.astype(jnp.bfloat16)
    summand = jnp.dot(rounded, masked, preferred_element_type=jnp.float32)
    result = lax.psum_scatter(summand, "aux", scatter_dimension=1, tiled=True)
    return result


def solution(mesh):
    in_specs = (
        P("aux", "pair"),
        P(None, "pair"),
        P("aux", "pair"),
        P("aux", "pair"),
        P("aux", None),
    )
    out_specs = P(None, ("pair", "aux"))
    return jax.shard_map(shards, mesh=mesh, in_specs=in_specs, out_specs=out_specs, check_vma=False)
```

profile of v0, /device:TPU:0, one launch (start us, length us, event | category | flops | bytes accessed | tf_op | source)
XLA Modules:
  0.0 370.9 jit_solution(1663735948647780986)
XLA Ops:
  6.5 0.0 reduce-scatter.2.cloned.1.call-start
  6.6 0.7 convert_element_type.40
  7.3 1.3 broadcast_select_fusion
  8.7 0.0 copy-start.3
  8.7 3.8 %broadcast_in_dim.25 = bf16[384,64,128]{2,1,0:T(8,128)(2,1)S(1)} broadcast(bf16[384,64]{1,0:T(8,128)(2,1)S(1)} %bitcast.36), dimensions={0,1} | broadcast | bytes 6340608 | tf_op jit(solution)/shard_map/broadcast_in_dim | solution.py:22
  12.5 0.0 copy-start.2
  12.5 0.0 copy-done
  12.5 0.0 copy-start.1
  12.6 4.0 %fusion.18 = f32[16,384]{1,0:T(8,128)S(1)} fusion(bf16[16,8192]{1,0:T(8,128)(2,1)S(1)} %copy-done, bf16[384,8192]{1,0:T(8,128)(2,1)S(1)} %copy-done.3, bf16[48,8,64,128]{3,2,1,0:T(8,128)(2,1)S(1)} %bitcast.34), kind=kOutput, calls=%fused_computation.26 | convolution fusion | flops 103809024 | bytes 12869632 | tf_op jit(solution)/shard_map/dot_general | solution.py:24
  16.5 0.0 copy-done.1
  16.5 1.8 conditional.8
  16.6 1.1 convolution_subtract_fusion
  17.6 0.7 fusion.22
  18.3 41.4 %psum.49 = f32[16,768]{1,0:T(8,128)S(1)} all-reduce(f32[16,768]{1,0:T(8,128)S(1)} %get-tuple-element.168), channel_id=1, replica_groups=mesh['aux'=8,'pair'=4] {'aux','pair'}, use_global_device_ids=true, to_apply=%region_2.3 | all-reduce | flops 12288 | bytes 98304 | tf_op jit(solution)/shard_map/psum | solution.py:56
  59.8 41.6 %psum.50 = f32[16,768]{1,0:T(8,128)S(1)} all-reduce(f32[16,768]{1,0:T(8,128)S(1)} %get-tuple-element.169), channel_id=1, replica_groups=mesh['aux'=8,'pair'=4] {'aux','pair'}, use_global_device_ids=true, to_apply=%region_5.6 | all-reduce | flops 12288 | bytes 98304 | tf_op jit(solution)/shard_map/psum | solution.py:56
  101.5 40.8 %psum.51 = f32[16,768]{1,0:T(8,128)S(1)} all-reduce(f32[16,768]{1,0:T(8,128)S(1)} %get-tuple-element.170), channel_id=1, replica_groups=mesh['aux'=8,'pair'=4] {'aux','pair'}, use_global_device_ids=true, to_apply=%region_8.9 | all-reduce | flops 12288 | bytes 98304 | tf_op jit(solution)/shard_map/psum | solution.py:56
  142.3 0.2 conditional.11
  142.5 43.4 %psum.52 = f32[16,768]{1,0:T(8,128)S(1)} all-reduce(f32[16,768]{1,0:T(8,128)S(1)} %get-tuple-element.171), channel_id=1, replica_groups=mesh['aux'=8,'pair'=4] {'aux','pair'}, use_global_device_ids=true, to_apply=%region_11.12 | all-reduce | flops 12288 | bytes 98304 | tf_op jit(solution)/shard_map/psum | solution.py:56
  185.9 1.3 conditional.12
  185.9 0.6 broadcast_in_dim.17
  186.5 0.7 broadcast.57
  187.2 0.8 slice.19
  188.0 42.1 %psum.53 = f32[16,768]{1,0:T(8,128)S(1)} all-reduce(f32[16,768]{1,0:T(8,128)S(1)} %slice.19), channel_id=1, replica_groups=mesh['aux'=8,'pair'=4] {'aux','pair'}, use_global_device_ids=true, to_apply=%region_14.15 | all-reduce | flops 12288 | bytes 98304 | tf_op jit(solution)/shard_map/psum | solution.py:63
  230.1 0.8 slice.20
  230.9 44.2 %psum.54 = f32[16,768]{1,0:T(8,128)S(1)} all-reduce(f32[16,768]{1,0:T(8,128)S(1)} %slice.20), channel_id=1, replica_groups=mesh['aux'=8,'pair'=4] {'aux','pair'}, use_global_device_ids=true, to_apply=%region_17.18 | all-reduce | flops 12288 | bytes 98304 | tf_op jit(solution)/shard_map/psum | solution.py:63
  275.1 0.8 slice.21
  276.0 43.3 %psum.55 = f32[16,768]{1,0:T(8,128)S(1)} all-reduce(f32[16,768]{1,0:T(8,128)S(1)} %slice.21), channel_id=1, replica_groups=mesh['aux'=8,'pair'=4] {'aux','pair'}, use_global_device_ids=true, to_apply=%region_20.21 | all-reduce | flops 12288 | bytes 98304 | tf_op jit(solution)/shard_map/psum | solution.py:63
  319.3 1.7 conditional.15
  319.3 1.7 fusion.13
  321.0 9.1 %fusion.16 = f32[16,8192]{1,0:T(8,128)} fusion(bf16[384,8192]{1,0:T(8,128)(2,1)} %param.21, bf16[48,8,64,128]{3,2,1,0:T(8,128)(2,1)} %bitcast.35, f32[16,384]{1,0:T(8,128)} %get-tuple-element.174), kind=kOutput, calls=%fused_computation.24 | convolution fusion | flops 103815168 | bytes 13131776 | tf_op jit(solution)/shard_map/dot_general | solution.py:92
  330.1 0.0 reduce-scatter.2.cloned.1.call-update
  330.1 33.9 %reduce-scatter.2.cloned.1.call-done = f32[16,1024]{1,0:T(8,128)} async-done(((f32[16,8192]{1,0:T(8,128)}), f32[16,1024]{1,0:T(8,128)}) %reduce-scatter.2.cloned.1.call-update) | async-done | bytes 65552 | tf_op jit(solution)/shard_map/reduce_scatter | solution.py:93
  (15 shorter events, 0.2 us)
Async XLA Ops:
  6.5 6.0 %copy-start = (bf16[16,8192]{1,0:T(8,128)(2,1)S(1)}, bf16[16,8192]{1,0:T(8,128)(2,1)}, u32[]{:S(2)}) copy-start(bf16[16,8192]{1,0:T(8,128)(2,1)} %param.22) | copy-start | bytes 786436
  6.5 357.5 %reduce-scatter.2.cloned.1.call-start = ((), (), s32[]{:S(2)}) async-start(), calls=%async_computation.1 | async-start | bytes 589824 | tf_op jit(solution)/shard_map/reduce_scatter | solution.py:93
  8.7 3.9 %copy-start.3 = (bf16[384,8192]{1,0:T(8,128)(2,1)S(1)}, bf16[384,8192]{1,0:T(8,128)(2,1)}, u32[]{:S(2)}) copy-start(bf16[384,8192]{1,0:T(8,128)(2,1)} %param.21) | copy-start | bytes 18874372
  12.5 4.0 %copy-start.2 = (bf16[384,64,128]{2,1,0:T(8,128)(2,1)}, bf16[384,64,128]{2,1,0:T(8,128)(2,1)S(1)}, u32[]{:S(2)}) copy-start(bf16[384,64,128]{2,1,0:T(8,128)(2,1)S(1)} %broadcast_in_dim.25) | copy-start | bytes 18874372
  12.5 4.0 %copy-start.1 = (f32[384,768]{1,0:T(8,128)S(1)}, f32[384,768]{1,0:T(8,128)}, u32[]{:S(2)}) copy-start(f32[384,768]{1,0:T(8,128)} %param.25) | copy-start | bytes 3538948
Sparse Core Ops, SparseCore 0:
  330.2 33.7 reduce-scatter.1
where the time goes:
time: 372 us; the launch traced here: 371 us
  blocking collectives  297 us (80%)
  waiting for transfers between devices  34 us (9%)
  matrix products  16.6 us (4%)
  between operations  13.6 us (4%)
  local copies, waits for them, and re-layouts  7.62 us (2%)
    psum x4, blocking collectives, shards(): arrived = lax.psum(summand, ('aux', 'pair'))  167 us
    psum x3, blocking collectives, shards(): behind = lax.psum(portion, ('aux', 'pair'))  130 us
    reduce_scatter x1, waiting for transfers between devices, shards(): result = lax.psum_scatter(summand, 'aux', scatter_dimension=1, tiled=True)  33.9 us
    dot_general x1, matrix products, shards(): summand = jnp.dot(rounded, masked, preferred_element_type=jnp.float32)  9.1 us
  transfers between devices with their start and end apart: 1, of which 1 were waited for; matrix products, arithmetic and copies ran while one was open for 0% of the time, Pallas kernels for 0%

commit v1 on v0

v1 whole, which is shorter than its diff:
```python
import jax
import jax.numpy as jnp
from jax import lax
from jax.sharding import PartitionSpec as P

TILE = 128
SOLVE_BLOCKS = 4
AXES = ("aux", "pair")
HIGHEST = lax.Precision.HIGHEST


def mm(a, b):
    return jnp.dot(a, b, precision=HIGHEST, preferred_element_type=jnp.float32)


def mm_t(a, b):
    return lax.dot_general(
        a, b, (((1,), (1,)), ((), ())), precision=HIGHEST, preferred_element_type=jnp.float32
    )


def masked_integrals(integrals, screen):
    expanded = jnp.repeat(jnp.repeat(screen, TILE, axis=0), TILE, axis=1).astype(jnp.bfloat16)
    return integrals * expanded


def fit_partial(densities, masked):
    return lax.dot_general(
        densities, masked, (((1,), (1,)), ((), ())), preferred_element_type=jnp.float32
    )


def scatter_sum(summand):
    members = lax.axis_size("aux")
    count, width = summand.shape
    pieces = summand.astype(jnp.bfloat16).reshape(count, members, width // members)
    arrived = lax.all_to_all(pieces.transpose(1, 0, 2), "aux", 0, 0, tiled=True)
    return jnp.sum(arrived.astype(jnp.float32), axis=0)


def chip_solve(partial_fit, factor, diag_inv):
    count, height = partial_fit.shape
    half = count // 2
    planes = lax.axis_size("pair")
    row = lax.axis_index("aux")
    z = lax.axis_index("pair")
    block = row // 2
    side = row % 2

    def send(value, moves):
        pairs = []
        for (k_from, z_from), (k_to, z_to) in moves:
            for c in range(2):
                pairs.append(
                    ((2 * k_from + c) * planes + z_from, (2 * k_to + c) * planes + z_to)
                )
        return lax.ppermute(value, AXES, pairs)

    def swap(value):
        return lax.ppermute(value, "aux", [(i, i ^ 1) for i in range(2 * SOLVE_BLOCKS)])

    def join(own, other, axis):
        low = jnp.where(side == 0, own, other)
        high = jnp.where(side == 0, other, own)
        return jnp.concatenate([low, high], axis)

    factor = join(factor, swap(factor), 0)
    inverse = join(diag_inv, swap(diag_inv), 0)
    kept = lax.dynamic_slice_in_dim(partial_fit, side * half, half, 0)
    given = lax.dynamic_slice_in_dim(partial_fit, (1 - side) * half, half, 0)
    fit = join(kept, swap(given), 1)

    home = [max(k - 1, 0) for k in range(SOLVE_BLOCKS)]
    parts = fit
    for step in range(1, planes):
        fit = fit + send(
            parts, [((k, (home[k] + step) % planes), (k, home[k])) for k in range(SOLVE_BLOCKS)]
        )
    s_zero = mm(fit, inverse)
    at = lambda k, plane: (block == k) & (z == plane)
    got = send(s_zero, [((0, 0), (1, 0))])
    got = got + send(s_zero, [((0, 0), (2, 0))])
    got = got + send(s_zero, [((0, 0), (3, 0))])
    zero_copy = jnp.where(at(0, 0), s_zero, 0.0)
    for plane in range(1, planes):
        zero_copy = zero_copy + send(s_zero, [((0, 0), (0, plane))])
    term = mm_t(got, factor)
    s_one = mm(fit - term, inverse)
    out = jnp.where(block == 1, s_one, term)
    first = send(out, [((1, 0), (2, 1)), ((3, 0), (3, 1))])
    second = send(out, [((1, 0), (3, 1)), ((2, 0), (2, 1))])
    known = jnp.where(block == 3, second, first)
    behind = jnp.where(block == 3, first, second)
    term = behind + mm_t(known, factor)
    s_two = mm(fit - term, inverse)
    known = send(s_two, [((2, 1), (3, 2))])
    behind = send(term, [((3, 1), (3, 2))])
    s_three = mm(fit - behind - mm_t(known, factor), inverse)
    c_three = mm_t(s_three, inverse)
    back = mm(c_three, factor)
    into_two = send(back, [((3, 2), (2, 1))])
    three = send(c_three, [((3, 2), (3, 1))])
    three = three + send(c_three, [((3, 2), (3, 0))])
    c_two = mm_t(s_two - into_two, inverse)
    back = mm(jnp.where(block == 3, three, c_two), factor)
    into_one = send(back, [((2, 1), (1, 0)), ((3, 0), (2, 0))])
    other = send(jnp.where(block == 3, back, c_two), [((3, 1), (1, 0)), ((2, 1), (2, 0))])
    c_one = mm_t(s_one - into_one - other, inverse)
    back = mm(jnp.where(block == 2, other, c_one), factor) + jnp.where(block == 2, into_one, 0.0)
    into_zero = jnp.zeros_like(back)
    for plane in range(planes):
        into_zero = into_zero + send(
            back, [((1, 0), (0, plane)), ((2, 0), (0, (plane + 1) % planes))]
        )
    c_zero = mm_t(zero_copy - into_zero, inverse)
    have_two = at(2, 1)
    coef = jnp.where(at(1, 0), c_one, jnp.where(have_two, c_two, jnp.where(at(3, 2), c_three, 0.0)))
    spread = coef
    for step in range(1, planes):
        moves = [((1, 0), (1, step))]
        if 1 + step < planes:
            moves.append(((2, 1), (2, 1 + step)))
        if 2 + step < planes:
            moves.append(((3, 2), (3, 2 + step)))
        spread = spread + send(coef, moves)
    spread = spread + jnp.where(at(3, 0) | at(3, 1), three, 0.0) + jnp.where(at(2, 0), other, 0.0)
    final = jnp.where(block == 0, c_zero, spread).astype(jnp.bfloat16)
    own = lax.dynamic_slice_in_dim(final, side * height, height, 1)
    mate = lax.dynamic_slice_in_dim(final, (1 - side) * height, height, 1)
    return join(own, swap(mate), 0)


def chain_solve(partial_fit, factor, diag_inv):
    count, height = partial_fit.shape
    breadth = factor.shape[1]
    block_size = diag_inv.shape[1]
    rows_aux = lax.axis_size("aux")
    total = height * rows_aux
    members = rows_aux // SOLVE_BLOCKS
    my_row = lax.axis_index("aux")
    my_column = lax.axis_index("pair")
    my_block = my_row // members
    column_block = (my_column * breadth + jnp.arange(breadth, dtype=jnp.int32)) // block_size
    factor_low = jnp.where((column_block < my_block)[None, :], factor, 0.0)

    def own_columns(whole):
        return lax.dynamic_slice_in_dim(whole, my_column * breadth, breadth, 1)

    zero_block = jnp.zeros((count, block_size), jnp.float32)
    solved = jnp.zeros((count, total), jnp.float32)
    for k in range(SOLVE_BLOCKS):

        def on_group(current):
            return mm(partial_fit - mm_t(own_columns(current), factor_low), diag_inv)

        def off_group(current):
            return zero_block

        summand = lax.cond(my_block == k, on_group, off_group, solved)
        arrived = lax.psum(summand, AXES)
        solved = lax.dynamic_update_slice_in_dim(solved, arrived, k * block_size, 1)
    own_coef = jnp.zeros((count, height), jnp.float32)
    contrib = jnp.zeros((count, total), jnp.float32)
    for target in reversed(range(SOLVE_BLOCKS)):
        settled = solved[:, target * block_size : (target + 1) * block_size]
        if target < SOLVE_BLOCKS - 1:
            portion = contrib[:, target * block_size : (target + 1) * block_size]
            settled = settled - lax.psum(portion, AXES)

        def on_group(state):
            coef = mm_t(settled, diag_inv)
            if target > 0:
                fresh = lax.dynamic_update_slice_in_dim(
                    jnp.zeros((count, total), jnp.float32),
                    mm(coef, factor_low),
                    my_column * breadth,
                    1,
                )
            else:
                fresh = state[1]
            return (coef, fresh)

        def keep_state(state):
            return state

        own_coef, contrib = lax.cond(my_block == target, on_group, keep_state, (own_coef, contrib))
    return own_coef.astype(jnp.bfloat16)


def shards(integrals, densities, screen, factor, diag_inv):
    block_size = diag_inv.shape[1]
    chip_blocks = (
        lax.axis_size("aux") == 2 * SOLVE_BLOCKS
        and factor.shape[1] == block_size
        and lax.axis_size("pair") == SOLVE_BLOCKS
    )
    solve = chip_solve if chip_blocks else chain_solve
    masked = masked_integrals(integrals, screen)
    rounded = solve(fit_partial(densities, masked), factor, diag_inv)
    summand = jnp.dot(rounded, masked, preferred_element_type=jnp.float32)
    return scatter_sum(summand)


def solution(mesh):
    in_specs = (
        P("aux", "pair"),
        P(None, "pair"),
        P("aux", "pair"),
        P("aux", "pair"),
        P("aux", None),
    )
    out_specs = P(None, ("pair", "aux"))
    return jax.shard_map(shards, mesh=mesh, in_specs=in_specs, out_specs=out_specs, check_vma=False)
```

time: 372 us -> 107 us (0.29)
  blocking collectives: 297 us -> 11.6 us
  starting transfers between devices: 0.01 us -> 27.2 us
  matrix products: 16.6 us -> 36.6 us
  between operations: 13.6 us -> 0.61 us
  waiting for transfers between devices: 34 us -> 21.5 us
    psum x7 -> x0, blocking collectives: 297 us -> none  [the longest x4 167 us: shards(): arrived = lax.psum(summand, ('aux', 'pair'))]
    reduce_scatter x1 -> x0, waiting for transfers between devices: 33.9 us -> none  [shards(): result = lax.psum_scatter(summand, 'aux', scatter_dimension=1, tiled=True)]
    ppermute x0 -> x29, starting transfers between devices: none -> 27.2 us  [the longest x25 26.1 us: send(): return lax.ppermute(value, AXES, pairs)]
    ppermute x0 -> x29, waiting for transfers between devices: none -> 21.5 us  [the longest x25 19.5 us: send(): return lax.ppermute(value, AXES, pairs)]
    dot_general x4 -> x15, matrix products: 7.46 us -> 28.3 us  [the longest x7 15.8 us: mm_t(): lax.dot_general(a, b, (((1,), (1,)), ((), ())), precision=HIGHEST, prefer...]
    all_to_all x0 -> x1, blocking collectives: none -> 11.6 us  [scatter_sum(): arrived = lax.all_to_all(pieces.transpose(1, 0, 2), 'aux', 0, 0, tiled=True)]
  transfers between devices with their start and end apart: 1 -> 29, of which waited for: 1 -> 6; matrix products, arithmetic and copies ran while one was open for 0% -> 19% of each run, Pallas kernels for 0% -> 0%
where the time goes in v1:
time: 107 us; the launch traced here: 106 us
  matrix products  36.6 us (34%)
  starting transfers between devices  27.2 us (25%)
  waiting for transfers between devices  21.5 us (20%)
  blocking collectives  11.6 us (11%)
  other arithmetic  4.59 us (4%)
  local copies, waits for them, and re-layouts  3.94 us (4%)
    ppermute x25, starting transfers between devices, send(): return lax.ppermute(value, AXES, pairs)  26.1 us
    ppermute x25, waiting for transfers between devices, send(): return lax.ppermute(value, AXES, pairs)  19.5 us
    dot_general x7, matrix products, mm_t(): lax.dot_general(a, b, (((1,), (1,)), ((), ())), precision=HIGHEST, prefer...  15.8 us
    all_to_all x1, blocking collectives, scatter_sum(): arrived = lax.all_to_all(pieces.transpose(1, 0, 2), 'aux', 0, 0, tiled=True)  11.6 us
    dot_general x7, matrix products, mm(): return jnp.dot(a, b, precision=HIGHEST, preferred_element_type=jnp.float32)  8.55 us
    dot_general x1, matrix products, shards(): summand = jnp.dot(rounded, masked, preferred_element_type=jnp.float32)  8.29 us
    dot_general x1, matrix products, fit_partial(): lax.dot_general(densities, masked, (((1,), (1,)), ((), ())), preferred_el...  3.97 us
    broadcast_in_dim x1, local copies, waits for them, and re-layouts, masked_integrals(): jnp.repeat(jnp.repeat(screen, TILE, axis=0), TILE, axis=1)  3.83 us
  transfers between devices with their start and end apart: 29, of which 6 were waited for; matrix products, arithmetic and copies ran while one was open for 19% of the time, Pallas kernels for 0%

profile of v1, /device:TPU:0, one launch (start us, length us, event | category | flops | bytes accessed | tf_op | source)
XLA Modules:
  0.0 106.1 jit_solution(16904020311115000485)
XLA Ops:
  1.3 3.8 %broadcast_in_dim.15 = bf16[384,64,128]{2,1,0:T(8,128)(2,1)S(1)} broadcast(bf16[384,64]{1,0:T(8,128)(2,1)S(1)} %bitcast.27), dimensions={0,1} | broadcast | bytes 6340608 | tf_op jit(solution)/shard_map/broadcast_in_dim | solution.py:23
  5.2 4.0 %fusion = f32[384,16]{0,1:T(8,128)S(1)} fusion(bf16[16,8192]{1,0:T(8,128)(2,1)S(1)} %copy-done, bf16[384,8192]{1,0:T(8,128)(2,1)S(1)} %copy-done.8, bf16[48,8,64,128]{3,2,1,0:T(8,128)(2,1)S(1)} %bitcast.23), kind=kOutput, calls=%fused_computation.4 | convolution fusion | flops 103809024 | bytes 12869632 | tf_op jit(solution)/shard_map/dot_general | solution.py:28
  10.5 1.3 %collective-permute-start.2 = (f32[8,768]{1,0:T(8,128)S(1)}, f32[8,768]{1,0:T(8,128)S(1)}, u32[]{:S(2)}, u32[]{:S(2)}) collective-permute-start(f32[8,768]{1,0:T(8,128)S(1)} %pad_maximum_fusion.8), channel_id=1, source_target_pairs={{2,0},{6,4},{10,8},{14,12},{19,17},{23,21},{24,26},{28,30}} | collective-permute-start | bytes 73736 | tf_op jit(solution)/shard_map/ppermute | solution.py:57
  11.8 1.3 %collective-permute-start.3 = (f32[8,768]{1,0:T(8,128)S(1)}, f32[8,768]{1,0:T(8,128)S(1)}, u32[]{:S(2)}, u32[]{:S(2)}) collective-permute-start(f32[8,768]{1,0:T(8,128)S(1)} %pad_maximum_fusion.8), channel_id=1, source_target_pairs={{3,0},{7,4},{11,8},{15,12},{16,17},{20,21},{25,26},{29,30}} | collective-permute-start | bytes 73736 | tf_op jit(solution)/shard_map/ppermute | solution.py:57
  13.1 1.3 %collective-permute-start.1 = (f32[8,768]{1,0:T(8,128)S(1)}, f32[8,768]{1,0:T(8,128)S(1)}, u32[]{:S(2)}, u32[]{:S(2)}) collective-permute-start(f32[8,768]{1,0:T(8,128)S(1)} %pad_maximum_fusion.8), channel_id=1, source_target_pairs={{1,0},{5,4},{9,8},{13,12},{18,17},{22,21},{27,26},{31,30}} | collective-permute-start | bytes 73736 | tf_op jit(solution)/shard_map/ppermute | solution.py:57
  14.4 3.1 %collective-permute-done.2 = f32[8,768]{1,0:T(8,128)S(1)} collective-permute-done((f32[8,768]{1,0:T(8,128)S(1)}, f32[8,768]{1,0:T(8,128)S(1)}, u32[]{:S(2)}, u32[]{:S(2)}) %collective-permute-start.2) | collective-permute-done | bytes 24608 | tf_op jit(solution)/shard_map/ppermute | solution.py:57
  17.5 1.8 %collective-permute-done.3 = f32[8,768]{1,0:T(8,128)S(1)} collective-permute-done((f32[8,768]{1,0:T(8,128)S(1)}, f32[8,768]{1,0:T(8,128)S(1)}, u32[]{:S(2)}, u32[]{:S(2)}) %collective-permute-start.3) | collective-permute-done | bytes 24608 | tf_op jit(solution)/shard_map/ppermute | solution.py:57
  19.3 1.8 %broadcast_select_fusion.3 = (f32[384,768]{1,0:T(8,128)S(1)}, f32[384,768]{1,0:T(8,128)S(1)}) fusion(f32[384,768]{1,0:T(8,128)} %param.9, f32[384,768]{1,0:T(8,128)} %collective-permute-done.4, pred[]{:T(512)S(6)} %eq.18), kind=kLoop, calls=%fused_computation.11 | loop fusion | flops 589824 | bytes 4718593 | tf_op jit(solution)/shard_map/jit(_where)/select_n | solution.py:63
  22.3 2.9 %collective-permute-start.10 = (f32[8,768]{1,0:T(8,128)S(1)}, f32[8,768]{1,0:T(8,128)S(1)}, u32[]{:S(2)}, u32[]{:S(2)}) collective-permute-start(f32[8,768]{1,0:T(8,128)S(1)} %fusion.52), channel_id=1, source_target_pairs={{0,24},{4,28}} | collective-permute-start | bytes 73736 | tf_op jit(solution)/shard_map/ppermute | solution.py:57
  25.2 1.3 %collective-permute-start.9 = (f32[8,768]{1,0:T(8,128)S(1)}, f32[8,768]{1,0:T(8,128)S(1)}, u32[]{:S(2)}, u32[]{:S(2)}) collective-permute-start(f32[8,768]{1,0:T(8,128)S(1)} %fusion.52), channel_id=1, source_target_pairs={{0,16},{4,20}} | collective-permute-start | bytes 73736 | tf_op jit(solution)/shard_map/ppermute | solution.py:57
  26.5 1.9 %collective-permute-start.8 = (f32[8,768]{1,0:T(8,128)S(1)}, f32[8,768]{1,0:T(8,128)S(1)}, u32[]{:S(2)}, u32[]{:S(2)}) collective-permute-start(f32[8,768]{1,0:T(8,128)S(1)} %fusion.52), channel_id=1, source_target_pairs={{0,8},{4,12}} | collective-permute-start | bytes 73736 | tf_op jit(solution)/shard_map/ppermute | solution.py:57
  28.4 1.4 %broadcast_select_fusion.1 = (f32[384,768]{1,0:T(8,128)S(1)}, f32[384,768]{1,0:T(8,128)S(1)}) fusion(f32[384,768]{1,0:T(8,128)S(1)} %copy-done.9, f32[384,768]{1,0:T(8,128)} %collective-permute-done.11, pred[]{:T(512)S(6)} %eq.18), kind=kLoop, calls=%fused_computation.9 | loop fusion | flops 589824 | bytes 4718593 | tf_op jit(solution)/shard_map/jit(_where)/select_n | solution.py:63
  29.9 2.0 %fusion.6 = f32[8,768]{1,0:T(8,128)S(1)} fusion(f32[384,768]{1,0:T(8,128)S(1)} %get-tuple-element.8, f32[384,768]{1,0:T(8,128)S(1)} %get-tuple-element.7, f32[8,768]{1,0:T(8,128)S(1)} %collective-permute-done.10, f32[8,768]{1,0:T(8,128)S(1)} %collective-permute-done.8, f32[8,768]{1,0:T(8,128)S(1)} %collective-permute-done.9), kind=kOutput, calls=%fused_computation.17 | convolution fusion | flops 57225216 | bytes 2457600 | tf_op jit(solution)/shard_map/dot_general | solution.py:17
  31.9 1.2 %broadcast_select_fusion.4 = (f32[8,768]{1,0:T(8,128)S(1)}, f32[8,768]{1,0:T(8,128)S(1)}) fusion(f32[8,768]{1,0:T(8,128)S(1)} %fusion.6, pred[]{:T(512)S(6)} %eq.23, f32[384,768]{1,0:T(8,128)S(1)} %get-tuple-element.6, f32[384,768]{1,0:T(8,128)S(1)} %get-tuple-element.5, f32[8,768]{1,0:T(8,128)S(1)} %add_add_fusion), kind=kOutput, calls=%fused_computation.55 | convolution fusion | flops 57225216 | bytes 2457601 | tf_op jit(solution)/shard_map/dot_general | solution.py:13
  34.7 3.8 %select_add_fusion = f32[8,768]{1,0:T(8,128)S(1)} fusion(f32[8,768]{1,0:T(8,128)S(1)} %collective-permute-done.12, f32[8,768]{1,0:T(8,128)S(1)} %collective-permute-done.13, pred[]{:T(512)S(6)} %eq.22, f32[384,768]{1,0:T(8,128)} %copy-done.4, f32[384,768]{1,0:T(8,128)} %copy-done.1), kind=kOutput, calls=%fused_computation.38 | convolution fusion | flops 57231360 | bytes 2433025 | tf_op jit(solution)/shard_map/dot_general | solution.py:17
  38.5 1.2 %fusion.20 = f32[8,768]{1,0:T(8,128)S(1)} fusion(f32[8,768]{1,0:T(8,128)S(1)} %add_add_fusion, f32[8,768]{1,0:T(8,128)S(1)} %select_add_fusion, f32[384,768]{1,0:T(8,128)S(1)} %get-tuple-element.6, f32[384,768]{1,0:T(8,128)S(1)} %get-tuple-element.5), kind=kOutput, calls=%fused_computation.34 | convolution fusion | flops 57219072 | bytes 2433024 | tf_op jit(solution)/shard_map/dot_general | solution.py:13
  41.1 2.0 %fusion.4 = f32[8,768]{1,0:T(8,128)S(1)} fusion(f32[8,768]{1,0:T(8,128)S(1)} %collective-permute-done.15, f32[384,768]{1,0:T(8,128)S(1)} %copy-done.5, f32[384,768]{1,0:T(8,128)S(1)} %copy-done.2), kind=kOutput, calls=%fused_computation.15 | convolution fusion | flops 57212928 | bytes 2408448 | tf_op jit(solution)/shard_map/dot_general | solution.py:17
  43.1 1.2 %fusion.18 = f32[8,768]{1,0:T(8,128)S(1)} fusion(f32[8,768]{1,0:T(8,128)S(1)} %fusion.4, f32[8,768]{1,0:T(8,128)S(1)} %add_add_fusion, f32[8,768]{1,0:T(8,128)S(1)} %collective-permute-done.14, f32[384,768]{1,0:T(8,128)S(1)} %get-tuple-element.6, f32[384,768]{1,0:T(8,128)S(1)} %get-tuple-element.5), kind=kOutput, calls=%fused_computation.32 | convolution fusion | flops 57225216 | bytes 2457600 | tf_op jit(solution)/shard_map/dot_general | solution.py:13
  44.3 2.0 %fusion.51 = f32[8,768]{1,0:T(8,128)S(1)} fusion(f32[8,768]{1,0:T(8,128)S(1)} %fusion.18, f32[384,768]{1,0:T(8,128)S(1)} %get-tuple-element.6, f32[384,768]{1,0:T(8,128)S(1)} %get-tuple-element.5), kind=kOutput, calls=%fused_computation.73 | convolution fusion | flops 57212928 | bytes 2408448 | tf_op jit(solution)/shard_map/dot_general | solution.py:17
  46.3 1.2 %fusion.3 = f32[8,768]{1,0:T(8,128)S(1)} fusion(f32[8,768]{1,0:T(8,128)S(1)} %fusion.51, f32[384,768]{1,0:T(8,128)S(1)} %copy-done.5, f32[384,768]{1,0:T(8,128)S(1)} %copy-done.2), kind=kOutput, calls=%fused_computation.14 | convolution fusion | flops 57212928 | bytes 2408448 | tf_op jit(solution)/shard_map/dot_general | solution.py:13
  49.6 2.0 %fusion.16 = f32[8,768]{1,0:T(8,128)S(1)} fusion(f32[8,768]{1,0:T(8,128)S(1)} %fusion.20, f32[8,768]{1,0:T(8,128)S(1)} %collective-permute-done.18, f32[384,768]{1,0:T(8,128)S(1)} %get-tuple-element.6, f32[384,768]{1,0:T(8,128)S(1)} %get-tuple-element.5), kind=kOutput, calls=%fused_computation.30 | convolution fusion | flops 57219072 | bytes 2433024 | tf_op jit(solution)/shard_map/dot_general | solution.py:17
  54.2 1.4 %collective-permute-start.7 = (f32[8,768]{1,0:T(8,128)S(1)}, f32[8,768]{1,0:T(8,128)S(1)}, u32[]{:S(2)}, u32[]{:S(2)}) collective-permute-start(f32[8,768]{1,0:T(8,128)S(1)} %fusion.52), channel_id=1, source_target_pairs={{0,3},{4,7}} | collective-permute-start | bytes 73736 | tf_op jit(solution)/shard_map/ppermute | solution.py:57
  55.6 1.3 %collective-permute-start.6 = (f32[8,768]{1,0:T(8,128)S(1)}, f32[8,768]{1,0:T(8,128)S(1)}, u32[]{:S(2)}, u32[]{:S(2)}) collective-permute-start(f32[8,768]{1,0:T(8,128)S(1)} %fusion.52), channel_id=1, source_target_pairs={{0,2},{4,6}} | collective-permute-start | bytes 73736 | tf_op jit(solution)/shard_map/ppermute | solution.py:57
  56.9 1.5 %collective-permute-start.5 = (f32[8,768]{1,0:T(8,128)S(1)}, f32[8,768]{1,0:T(8,128)S(1)}, u32[]{:S(2)}, u32[]{:S(2)}) collective-permute-start(f32[8,768]{1,0:T(8,128)S(1)} %fusion.52), channel_id=1, source_target_pairs={{0,1},{4,5}} | collective-permute-start | bytes 73736 | tf_op jit(solution)/shard_map/ppermute | solution.py:57
  58.5 2.0 %select_select_fusion = (f32[8,768]{1,0:T(8,128)S(1)}, f32[8,768]{1,0:T(8,128)S(1)}) fusion(f32[8,768]{1,0:T(8,128)S(1)} %fusion.16, f32[8,768]{1,0:T(8,128)S(1)} %fusion.51, pred[]{:T(512)S(6)} %and.38, pred[]{:T(512)S(6)} %and.37, pred[]{:T(512)S(6)} %and.36, f32[384,768]{1,0:T(8,128)S(1)} %get-tuple-element.6, f32[384,768]{1,0:T(8,128)S(1)} %get-tuple-element.5, ...), kind=kOutput, calls=%fused_computation.20 | convolution fusion | flops 57243648 | bytes 2531331 | tf_op jit(solution)/shard_map/dot_general | solution.py:17
  61.7 1.3 %collective-permute-start.24 = (f32[8,768]{1,0:T(8,128)S(1)}, f32[8,768]{1,0:T(8,128)S(1)}, u32[]{:S(2)}, u32[]{:S(2)}) collective-permute-start(f32[8,768]{1,0:T(8,128)S(1)} %convolution_add_fusion), channel_id=1, source_target_pairs={{8,3},{12,7},{16,0},{20,4}} | collective-permute-start | bytes 73736 | tf_op jit(solution)/shard_map/ppermute | solution.py:57
  64.4 1.3 %collective-permute-start.21 = (f32[8,768]{1,0:T(8,128)S(1)}, f32[8,768]{1,0:T(8,128)S(1)}, u32[]{:S(2)}, u32[]{:S(2)}) collective-permute-start(f32[8,768]{1,0:T(8,128)S(1)} %convolution_add_fusion), channel_id=1, source_target_pairs={{8,0},{12,4},{16,1},{20,5}} | collective-permute-start | bytes 73736 | tf_op jit(solution)/shard_map/ppermute | solution.py:57
  66.3 9.8 %collective-permute-done.24 = f32[8,768]{1,0:T(8,128)S(1)} collective-permute-done((f32[8,768]{1,0:T(8,128)S(1)}, f32[8,768]{1,0:T(8,128)S(1)}, u32[]{:S(2)}, u32[]{:S(2)}) %collective-permute-start.24) | collective-permute-done | bytes 24608 | tf_op jit(solution)/shard_map/ppermute | solution.py:57
  77.5 4.7 %collective-permute-done.21 = f32[8,768]{1,0:T(8,128)S(1)} collective-permute-done((f32[8,768]{1,0:T(8,128)S(1)}, f32[8,768]{1,0:T(8,128)S(1)}, u32[]{:S(2)}, u32[]{:S(2)}) %collective-permute-start.21) | collective-permute-done | bytes 24608 | tf_op jit(solution)/shard_map/ppermute | solution.py:57
  82.2 2.0 %fusion.1 = bf16[8,768]{1,0:T(8,128)(2,1)S(1)} fusion(f32[8,768]{1,0:T(8,128)S(1)} %collective-permute-done.19, f32[8,768]{1,0:T(8,128)S(1)} %collective-permute-done.27, f32[8,768]{1,0:T(8,128)S(1)} %collective-permute-done.26, f32[8,768]{1,0:T(8,128)S(1)} %get-tuple-element.17, f32[8,768]{1,0:T(8,128)S(1)} %collective-permute-done.25, ...), kind=kOutput, calls=%fused_computation.7 | convolution fusion | flops 57323520 | bytes 2740228 | tf_op jit(solution)/shard_map/dot_general | solution.py:17
  85.5 8.3 %convolution_convert_fusion = bf16[16,8192]{1,0:T(8,128)(2,1)S(1)} fusion(bf16[384,8192]{1,0:T(8,128)(2,1)} %param.5, bf16[48,8,64,128]{3,2,1,0:T(8,128)(2,1)} %bitcast.24, bf16[8,384]{1,0:T(8,128)(2,1)S(1)} %get-tuple-element.12, bf16[8,384]{1,0:T(8,128)(2,1)S(1)} %get-tuple-element.11), kind=kOutput, calls=%fused_computation | convolution fusion | flops 103964672 | bytes 12857344 | tf_op jit(solution)/shard_map/dot_general | solution.py:200
  93.8 11.6 %all_to_all.5 = bf16[8,16,1024]{2,1,0:T(8,128)(2,1)S(1)} all-to-all(bf16[8,16,1024]{2,1,0:T(8,128)(2,1)S(1)} %bitcast.26), channel_id=1, replica_groups=mesh['aux'=8,'pair'=4] {'aux'}, dimensions={0} | all-to-all | bytes 524288 | tf_op jit(solution)/shard_map/all_to_all | solution.py:37
  (76 shorter events, 17.7 us)
Async XLA Ops:
  0.0 28.4 %collective-permute-start.11 = (f32[384,768]{1,0:T(8,128)}, f32[384,768]{1,0:T(8,128)}, u32[]{:S(2)}, u32[]{:S(2)}) collective-permute-start(f32[384,768]{1,0:T(8,128)} %param.8), channel_id=1, source_target_pairs={{0,4},{4,0},{8,12},{12,8},{16,20},{20,16},{24,28},{28,24},{1,5},{5... | collective-permute-start | bytes 3538952 | tf_op jit(solution)/shard_map/ppermute | solution.py:60
  0.5 18.8 %collective-permute-start.4 = (f32[384,768]{1,0:T(8,128)}, f32[384,768]{1,0:T(8,128)}, u32[]{:S(2)}, u32[]{:S(2)}) collective-permute-start(f32[384,768]{1,0:T(8,128)} %param.9), channel_id=1, source_target_pairs={{0,4},{4,0},{8,12},{12,8},{16,20},{20,16},{24,28},{28,24},{1,5},{5... | collective-permute-start | bytes 3538952 | tf_op jit(solution)/shard_map/ppermute | solution.py:60
  9.1 1.3 %collective-permute-start = (f32[8,384]{1,0:T(8,128)S(1)}, f32[8,384]{1,0:T(8,128)S(1)}, u32[]{:S(2)}, u32[]{:S(2)}) collective-permute-start(f32[8,384]{1,0:T(8,128)S(1)} %dynamic-slice_bitcast_fusion), channel_id=1, source_target_pairs={{0,4},{4,0},{8,12},{12,8},{16,20},{20,16},{24,28},{28,24},{1,5},{5... | collective-permute-start | bytes 36872 | tf_op jit(solution)/shard_map/ppermute | solution.py:60
  10.5 7.0 %collective-permute-start.2 = (f32[8,768]{1,0:T(8,128)S(1)}, f32[8,768]{1,0:T(8,128)S(1)}, u32[]{:S(2)}, u32[]{:S(2)}) collective-permute-start(f32[8,768]{1,0:T(8,128)S(1)} %pad_maximum_fusion.8), channel_id=1, source_target_pairs={{2,0},{6,4},{10,8},{14,12},{19,17},{23,21},{24,26},{28,30}} | collective-permute-start | bytes 73736 | tf_op jit(solution)/shard_map/ppermute | solution.py:57
  11.8 7.5 %collective-permute-start.3 = (f32[8,768]{1,0:T(8,128)S(1)}, f32[8,768]{1,0:T(8,128)S(1)}, u32[]{:S(2)}, u32[]{:S(2)}) collective-permute-start(f32[8,768]{1,0:T(8,128)S(1)} %pad_maximum_fusion.8), channel_id=1, source_target_pairs={{3,0},{7,4},{11,8},{15,12},{16,17},{20,21},{25,26},{29,30}} | collective-permute-start | bytes 73736 | tf_op jit(solution)/shard_map/ppermute | solution.py:57
  13.1 6.2 %collective-permute-start.1 = (f32[8,768]{1,0:T(8,128)S(1)}, f32[8,768]{1,0:T(8,128)S(1)}, u32[]{:S(2)}, u32[]{:S(2)}) collective-permute-start(f32[8,768]{1,0:T(8,128)S(1)} %pad_maximum_fusion.8), channel_id=1, source_target_pairs={{1,0},{5,4},{9,8},{13,12},{18,17},{22,21},{27,26},{31,30}} | collective-permute-start | bytes 73736 | tf_op jit(solution)/shard_map/ppermute | solution.py:57
  21.1 7.3 %copy-start.9 = (f32[384,768]{1,0:T(8,128)S(1)}, f32[384,768]{1,0:T(8,128)}, u32[]{:S(2)}) copy-start(f32[384,768]{1,0:T(8,128)} %param.8) | copy-start | bytes 3538948
  22.3 7.5 %collective-permute-start.10 = (f32[8,768]{1,0:T(8,128)S(1)}, f32[8,768]{1,0:T(8,128)S(1)}, u32[]{:S(2)}, u32[]{:S(2)}) collective-permute-start(f32[8,768]{1,0:T(8,128)S(1)} %fusion.52), channel_id=1, source_target_pairs={{0,24},{4,28}} | collective-permute-start | bytes 73736 | tf_op jit(solution)/shard_map/ppermute | solution.py:57
  25.2 4.7 %collective-permute-start.9 = (f32[8,768]{1,0:T(8,128)S(1)}, f32[8,768]{1,0:T(8,128)S(1)}, u32[]{:S(2)}, u32[]{:S(2)}) collective-permute-start(f32[8,768]{1,0:T(8,128)S(1)} %fusion.52), channel_id=1, source_target_pairs={{0,16},{4,20}} | collective-permute-start | bytes 73736 | tf_op jit(solution)/shard_map/ppermute | solution.py:57
  26.5 3.4 %collective-permute-start.8 = (f32[8,768]{1,0:T(8,128)S(1)}, f32[8,768]{1,0:T(8,128)S(1)}, u32[]{:S(2)}, u32[]{:S(2)}) collective-permute-start(f32[8,768]{1,0:T(8,128)S(1)} %fusion.52), channel_id=1, source_target_pairs={{0,8},{4,12}} | collective-permute-start | bytes 73736 | tf_op jit(solution)/shard_map/ppermute | solution.py:57
  33.2 1.5 %collective-permute-start.13 = (f32[8,768]{1,0:T(8,128)S(1)}, f32[8,768]{1,0:T(8,128)S(1)}, u32[]{:S(2)}, u32[]{:S(2)}) collective-permute-start(f32[8,768]{1,0:T(8,128)S(1)} %get-tuple-element.13), channel_id=1, source_target_pairs={{8,25},{12,29},{16,17},{20,21}} | collective-permute-start | bytes 73736 | tf_op jit(solution)/shard_map/ppermute | solution.py:57
  33.8 0.9 collective-permute-start.12
  34.7 6.4 %copy-start.2 = (f32[384,768]{1,0:T(8,128)S(1)}, f32[384,768]{1,0:T(8,128)}, u32[]{:S(2)}) copy-start(f32[384,768]{1,0:T(8,128)} %copy-done.1) | copy-start | bytes 3538948
  34.7 6.4 %copy-start.5 = (f32[384,768]{1,0:T(8,128)S(1)}, f32[384,768]{1,0:T(8,128)}, u32[]{:S(2)}) copy-start(f32[384,768]{1,0:T(8,128)} %copy-done.4) | copy-start | bytes 3538948
  39.7 1.3 %collective-permute-start.15 = (f32[8,768]{1,0:T(8,128)S(1)}, f32[8,768]{1,0:T(8,128)S(1)}, u32[]{:S(2)}, u32[]{:S(2)}) collective-permute-start(f32[8,768]{1,0:T(8,128)S(1)} %fusion.20), channel_id=1, source_target_pairs={{17,26},{21,30}} | collective-permute-start | bytes 73736 | tf_op jit(solution)/shard_map/ppermute | solution.py:57
  40.4 2.7 %collective-permute-start.14 = (f32[8,768]{1,0:T(8,128)S(1)}, f32[8,768]{1,0:T(8,128)S(1)}, u32[]{:S(2)}, u32[]{:S(2)}) collective-permute-start(f32[8,768]{1,0:T(8,128)S(1)} %select_add_fusion), channel_id=1, source_target_pairs={{25,26},{29,30}} | collective-permute-start | bytes 73736 | tf_op jit(solution)/shard_map/ppermute | solution.py:57
  47.6 2.0 %collective-permute-start.18 = (f32[8,768]{1,0:T(8,128)S(1)}, f32[8,768]{1,0:T(8,128)S(1)}, u32[]{:S(2)}, u32[]{:S(2)}) collective-permute-start(f32[8,768]{1,0:T(8,128)S(1)} %fusion.3), channel_id=1, source_target_pairs={{26,17},{30,21}} | collective-permute-start | bytes 73736 | tf_op jit(solution)/shard_map/ppermute | solution.py:57
  48.2 3.4 %collective-permute-start.17 = (f32[8,768]{1,0:T(8,128)S(1)}, f32[8,768]{1,0:T(8,128)S(1)}, u32[]{:S(2)}, u32[]{:S(2)}) collective-permute-start(f32[8,768]{1,0:T(8,128)S(1)} %fusion.51), channel_id=1, source_target_pairs={{26,24},{30,28}} | collective-permute-start | bytes 73736 | tf_op jit(solution)/shard_map/ppermute | solution.py:57
  48.9 2.7 %collective-permute-start.16 = (f32[8,768]{1,0:T(8,128)S(1)}, f32[8,768]{1,0:T(8,128)S(1)}, u32[]{:S(2)}, u32[]{:S(2)}) collective-permute-start(f32[8,768]{1,0:T(8,128)S(1)} %fusion.51), channel_id=1, source_target_pairs={{26,25},{30,29}} | collective-permute-start | bytes 73736 | tf_op jit(solution)/shard_map/ppermute | solution.py:57
  52.8 5.6 %collective-permute-start.19 = (f32[8,768]{1,0:T(8,128)S(1)}, f32[8,768]{1,0:T(8,128)S(1)}, u32[]{:S(2)}, u32[]{:S(2)}) collective-permute-start(f32[8,768]{1,0:T(8,128)S(1)} %get-tuple-element.15), channel_id=1, source_target_pairs={{25,8},{29,12},{17,16},{21,20}} | collective-permute-start | bytes 73736 | tf_op jit(solution)/shard_map/ppermute | solution.py:57
  53.5 5.0 %collective-permute-start.20 = (f32[8,768]{1,0:T(8,128)S(1)}, f32[8,768]{1,0:T(8,128)S(1)}, u32[]{:S(2)}, u32[]{:S(2)}) collective-permute-start(f32[8,768]{1,0:T(8,128)S(1)} %get-tuple-element.16), channel_id=1, source_target_pairs={{17,8},{21,12},{24,16},{28,20}} | collective-permute-start | bytes 73736 | tf_op jit(solution)/shard_map/ppermute | solution.py:57
  54.2 9.5 %collective-permute-start.7 = (f32[8,768]{1,0:T(8,128)S(1)}, f32[8,768]{1,0:T(8,128)S(1)}, u32[]{:S(2)}, u32[]{:S(2)}) collective-permute-start(f32[8,768]{1,0:T(8,128)S(1)} %fusion.52), channel_id=1, source_target_pairs={{0,3},{4,7}} | collective-permute-start | bytes 73736 | tf_op jit(solution)/shard_map/ppermute | solution.py:57
  55.6 8.7 %collective-permute-start.6 = (f32[8,768]{1,0:T(8,128)S(1)}, f32[8,768]{1,0:T(8,128)S(1)}, u32[]{:S(2)}, u32[]{:S(2)}) collective-permute-start(f32[8,768]{1,0:T(8,128)S(1)} %fusion.52), channel_id=1, source_target_pairs={{0,2},{4,6}} | collective-permute-start | bytes 73736 | tf_op jit(solution)/shard_map/ppermute | solution.py:57
  56.9 8.7 %collective-permute-start.5 = (f32[8,768]{1,0:T(8,128)S(1)}, f32[8,768]{1,0:T(8,128)S(1)}, u32[]{:S(2)}, u32[]{:S(2)}) collective-permute-start(f32[8,768]{1,0:T(8,128)S(1)} %fusion.52), channel_id=1, source_target_pairs={{0,1},{4,5}} | collective-permute-start | bytes 73736 | tf_op jit(solution)/shard_map/ppermute | solution.py:57
  61.7 14.4 %collective-permute-start.24 = (f32[8,768]{1,0:T(8,128)S(1)}, f32[8,768]{1,0:T(8,128)S(1)}, u32[]{:S(2)}, u32[]{:S(2)}) collective-permute-start(f32[8,768]{1,0:T(8,128)S(1)} %convolution_add_fusion), channel_id=1, source_target_pairs={{8,3},{12,7},{16,0},{20,4}} | collective-permute-start | bytes 73736 | tf_op jit(solution)/shard_map/ppermute | solution.py:57
  63.0 13.8 %collective-permute-start.23 = (f32[8,768]{1,0:T(8,128)S(1)}, f32[8,768]{1,0:T(8,128)S(1)}, u32[]{:S(2)}, u32[]{:S(2)}) collective-permute-start(f32[8,768]{1,0:T(8,128)S(1)} %convolution_add_fusion), channel_id=1, source_target_pairs={{8,2},{12,6},{16,3},{20,7}} | collective-permute-start | bytes 73736 | tf_op jit(solution)/shard_map/ppermute | solution.py:57
  63.7 13.8 %collective-permute-start.22 = (f32[8,768]{1,0:T(8,128)S(1)}, f32[8,768]{1,0:T(8,128)S(1)}, u32[]{:S(2)}, u32[]{:S(2)}) collective-permute-start(f32[8,768]{1,0:T(8,128)S(1)} %convolution_add_fusion), channel_id=1, source_target_pairs={{8,1},{12,5},{16,2},{20,6}} | collective-permute-start | bytes 73736 | tf_op jit(solution)/shard_map/ppermute | solution.py:57
  64.4 17.9 %collective-permute-start.21 = (f32[8,768]{1,0:T(8,128)S(1)}, f32[8,768]{1,0:T(8,128)S(1)}, u32[]{:S(2)}, u32[]{:S(2)}) collective-permute-start(f32[8,768]{1,0:T(8,128)S(1)} %convolution_add_fusion), channel_id=1, source_target_pairs={{8,0},{12,4},{16,1},{20,5}} | collective-permute-start | bytes 73736 | tf_op jit(solution)/shard_map/ppermute | solution.py:57
  65.7 16.6 %collective-permute-start.27 = (f32[8,768]{1,0:T(8,128)S(1)}, f32[8,768]{1,0:T(8,128)S(1)}, u32[]{:S(2)}, u32[]{:S(2)}) collective-permute-start(f32[8,768]{1,0:T(8,128)S(1)} %get-tuple-element.17), channel_id=1, source_target_pairs={{8,11},{12,15}} | collective-permute-start | bytes 73736 | tf_op jit(solution)/shard_map/ppermute | solution.py:57
  76.1 6.1 %collective-permute-start.26 = (f32[8,768]{1,0:T(8,128)S(1)}, f32[8,768]{1,0:T(8,128)S(1)}, u32[]{:S(2)}, u32[]{:S(2)}) collective-permute-start(f32[8,768]{1,0:T(8,128)S(1)} %get-tuple-element.17), channel_id=1, source_target_pairs={{8,10},{12,14},{17,19},{21,23}} | collective-permute-start | bytes 73736 | tf_op jit(solution)/shard_map/ppermute | solution.py:57
  76.8 5.5 %collective-permute-start.25 = (f32[8,768]{1,0:T(8,128)S(1)}, f32[8,768]{1,0:T(8,128)S(1)}, u32[]{:S(2)}, u32[]{:S(2)}) collective-permute-start(f32[8,768]{1,0:T(8,128)S(1)} %get-tuple-element.17), channel_id=1, source_target_pairs={{8,9},{12,13},{17,18},{21,22},{26,27},{30,31}} | collective-permute-start | bytes 73736 | tf_op jit(solution)/shard_map/ppermute | solution.py:57
  84.3 1.2 %collective-permute-start.28 = (bf16[8,384]{1,0:T(8,128)(2,1)S(1)}, bf16[8,384]{1,0:T(8,128)(2,1)S(1)}, u32[]{:S(2)}, u32[]{:S(2)}) collective-permute-start(bf16[8,384]{1,0:T(8,128)(2,1)S(1)} %constant_dynamic-slice_fusion), channel_id=1, source_target_pairs={{0,4},{4,0},{8,12},{12,8},{16,20},{20,16},{24,28},{28,24},{1,5},{5... | collective-permute-start | bytes 18440 | tf_op jit(solution)/shard_map/ppermute | solution.py:60
  (7 other events, 32.2 us)

commit v2 on v1

v2 whole, which is shorter than its diff:
```python
import functools

import jax
import jax.numpy as jnp
from jax import lax
from jax.experimental import pallas as pl
from jax.experimental.pallas import tpu as pltpu
from jax.sharding import PartitionSpec as P

TILE = 128
SOLVE_BLOCKS = 4
AXES = ("aux", "pair")
HIGHEST = lax.Precision.HIGHEST
F32 = jnp.float32
BF16 = jnp.bfloat16
VMEM = pl.BlockSpec(memory_space=pltpu.VMEM)
SMEM = pl.BlockSpec(memory_space=pltpu.SMEM)
MIB = 1024 * 1024
NN = (((1,), (0,)), ((), ()))
NT = (((1,), (1,)), ((), ()))
TN = (((0,), (0,)), ((), ()))


def chunk_of(width):
    return 1024 if width % 1024 == 0 else width


def fit_kernel(screen, densities, integrals, out):
    step = pl.program_id(0)
    strips = integrals.shape[0] // TILE
    tiles = integrals.shape[1] // TILE

    @pl.when(step == 0)
    def _():
        out[...] = jnp.zeros_like(out)

    for i in range(strips):
        masked = jnp.concatenate(
            [
                jnp.where(
                    screen[i, step * tiles + j] != 0,
                    densities[:, j * TILE : (j + 1) * TILE],
                    jnp.zeros((), BF16),
                )
                for j in range(tiles)
            ],
            axis=1,
        )
        out[:, i * TILE : (i + 1) * TILE] += lax.dot_general(
            masked, integrals[i * TILE : (i + 1) * TILE, :], NT, preferred_element_type=F32
        )


def fit_partial(densities, integrals, screen):
    count = densities.shape[0]
    height, width = integrals.shape
    chunk = chunk_of(width)
    return pl.pallas_call(
        fit_kernel,
        grid=(width // chunk,),
        in_specs=[
            SMEM,
            pl.BlockSpec((count, chunk), lambda j: (0, j)),
            pl.BlockSpec((height, chunk), lambda j: (0, j)),
        ],
        out_specs=pl.BlockSpec((count, height), lambda j: (0, 0)),
        out_shape=jax.ShapeDtypeStruct((count, height), F32),
        compiler_params=pltpu.CompilerParams(vmem_limit_bytes=12 * MIB),
        name="fit",
    )(screen, densities, integrals)


def coulomb_kernel(screen, rounded, integrals, out):
    step = pl.program_id(0)
    strips = integrals.shape[0] // TILE
    tiles = integrals.shape[1] // TILE
    for j in range(tiles):
        masked = jnp.concatenate(
            [
                jnp.where(
                    screen[i, step * tiles + j] != 0,
                    rounded[:, i * TILE : (i + 1) * TILE],
                    jnp.zeros((), BF16),
                )
                for i in range(strips)
            ],
            axis=1,
        )
        part = jnp.dot(
            masked, integrals[:, j * TILE : (j + 1) * TILE], preferred_element_type=F32
        )
        out[:, j * TILE : (j + 1) * TILE] = part.astype(out.dtype)


def coulomb_partial(rounded, integrals, screen):
    count, height = rounded.shape
    width = integrals.shape[1]
    members = lax.axis_size("aux")
    chunk = width // members
    return pl.pallas_call(
        coulomb_kernel,
        grid=(members,),
        in_specs=[
            SMEM,
            pl.BlockSpec((count, height), lambda j: (0, 0)),
            pl.BlockSpec((height, chunk), lambda j: (0, j)),
        ],
        out_specs=pl.BlockSpec((None, count, chunk), lambda j: (j, 0, 0)),
        out_shape=jax.ShapeDtypeStruct((members, count, chunk), BF16),
        compiler_params=pltpu.CompilerParams(vmem_limit_bytes=12 * MIB),
        name="coulomb",
    )(screen, rounded, integrals)


def scatter_sum(slabs):
    arrived = lax.all_to_all(slabs, "aux", 0, 0, tiled=True)
    return jnp.sum(arrived.astype(F32), axis=0)


def high_low(value):
    high = value.astype(BF16)
    return high, (value - high.astype(F32)).astype(BF16)


def times(value, high, low, dims):
    rows = value.shape[0]
    coarse = value.astype(BF16).astype(F32)
    pair = jnp.concatenate([coarse, value - coarse], axis=0).astype(BF16)
    both = lax.dot_general(pair, high, dims, preferred_element_type=F32)
    both += lax.dot_general(pair, low, dims, preferred_element_type=F32)
    return both[:rows] + both[rows:]


def my_block():
    return lax.axis_index("aux") // 2


def call(kernel, outs, *operands, limit=12):
    return pl.pallas_call(
        kernel,
        out_shape=outs,
        in_specs=[VMEM] * len(operands),
        out_specs=jax.tree.map(lambda _: VMEM, outs),
        compiler_params=pltpu.CompilerParams(vmem_limit_bytes=limit * MIB),
        name=kernel.__name__,
    )(*operands)


def prepare(own_inv, mate_inv, own_fac, mate_fac, inv_high, inv_low, k_high, k_low):
    side = lax.axis_index("aux") % 2
    height = own_inv.shape[0]
    here = pl.ds(pl.multiple_of(side * height, height), height)
    there = pl.ds(pl.multiple_of((1 - side) * height, height), height)
    for ref, rows in ((own_inv, here), (mate_inv, there)):
        high, low = high_low(ref[...])
        inv_high[rows, :] = high
        inv_low[rows, :] = low

    @pl.when(my_block() > 0)
    def _():
        total = jnp.zeros(k_high.shape, F32)
        for inv, fac in ((own_inv, own_fac), (mate_inv, mate_fac)):
            ih, il = high_low(inv[...])
            fh, fl = high_low(fac[...])
            total += lax.dot_general(ih, fh, TN, preferred_element_type=F32)
            total += lax.dot_general(ih, fl, TN, preferred_element_type=F32)
            total += lax.dot_general(il, fh, TN, preferred_element_type=F32)
        high, low = high_low(total)
        k_high[...] = high
        k_low[...] = low


def start_solve(f0, f1, f2, f3, high, low, out):
    out[...] = times(f0[...] + f1[...] + f2[...] + f3[...], high[...], low[...], NN)


def after_zero(known, e, high, low, out):
    term = times(known[...], high[...], low[...], NT)
    out[...] = jnp.where(my_block() == 1, e[...] - term, term)


def after_one(first, second, e, high, low, out):
    last = my_block() == 3
    known = jnp.where(last, second[...], first[...])
    behind = jnp.where(last, first[...], second[...])
    total = behind + times(known, high[...], low[...], NT)
    out[...] = jnp.where(last, total, e[...] - total)


def turn(known, behind, e, high, low, settled, back):
    value = e[...] - behind[...] - times(known[...], high[...], low[...], NT)
    settled[...] = value
    back[...] = times(value, high[...], low[...], NN)


def back_two(into, near, far, s, high, low, settled, back):
    value = jnp.where(my_block() == 3, near[...] + far[...], s[...] - into[...])
    settled[...] = value
    back[...] = times(value, high[...], low[...], NN)


def back_one(into, other, s, high, low, settled, back):
    two = my_block() == 2
    value = jnp.where(two, other[...], s[...] - into[...] - other[...])
    settled[...] = value
    back[...] = times(value, high[...], low[...], NN) + jnp.where(two, into[...], 0.0)


def finish(own, mate, high, low, out):
    side = lax.axis_index("aux") % 2
    height = out.shape[1]
    here = pl.ds(pl.multiple_of(side * height, height), height)
    even = side == 0
    value = jnp.concatenate(
        [jnp.where(even, own[...], mate[...]), jnp.where(even, mate[...], own[...])], axis=0
    )
    out[...] = times(value, high[here, :], low[here, :], NT).astype(out.dtype)


def mm(a, b):
    return jnp.dot(a, b, precision=HIGHEST, preferred_element_type=F32)


def mm_t(a, b):
    return lax.dot_general(a, b, NT, precision=HIGHEST, preferred_element_type=F32)


def chip_solve(partial_fit, factor, diag_inv):
    count, height = partial_fit.shape
    half = count // 2
    size = 2 * height
    planes = lax.axis_size("pair")
    row = lax.axis_index("aux")
    z = lax.axis_index("pair")
    block = row // 2
    side = row % 2

    def send(value, moves, fill=()):
        pairs = []
        for (k_from, z_from), (k_to, z_to) in tuple(moves) + tuple(fill):
            for c in range(2):
                pairs.append(
                    ((2 * k_from + c) * planes + z_from, (2 * k_to + c) * planes + z_to)
                )
        return lax.ppermute(value, AXES, pairs)

    def swap(value):
        return lax.ppermute(value, "aux", [(i, i ^ 1) for i in range(2 * SOLVE_BLOCKS)])

    panel = jax.ShapeDtypeStruct((half, size), F32)
    square = jax.ShapeDtypeStruct((size, size), BF16)
    inv_high, inv_low, k_high, k_low = call(
        prepare, [square] * 4, diag_inv, swap(diag_inv), factor, swap(factor), limit=32
    )
    kept = lax.dynamic_slice_in_dim(partial_fit, side * half, half, 0)
    given = lax.dynamic_slice_in_dim(partial_fit, (1 - side) * half, half, 0)
    mate = swap(given)
    fit = jnp.concatenate(
        [jnp.where(side == 0, kept, mate), jnp.where(side == 0, mate, kept)], axis=1
    )
    everyone = [(k, plane) for k in range(SOLVE_BLOCKS) for plane in range(planes)]
    shifted = [
        send(fit, [((k, plane), (k, (plane + step) % planes)) for k, plane in everyone])
        for step in range(1, planes)
    ]
    e = call(start_solve, panel, fit, *shifted, inv_high, inv_low)

    def at(k, plane):
        return (block == k) & (z == plane)

    got = send(
        e,
        [((0, 0), (1, 0)), ((0, 1), (2, 0)), ((0, 2), (3, 0))],
        [((1, 3), (0, 0)), ((2, 3), (0, 1)), ((3, 3), (0, 2))],
    )
    one = call(after_zero, panel, got, e, k_high, k_low)
    first = send(one, [((1, 0), (2, 1)), ((3, 0), (3, 1))], [((1, 3), (1, 0))])
    second = send(one, [((1, 0), (3, 1)), ((2, 0), (2, 1))], [((1, 3), (1, 0))])
    two = call(after_one, panel, first, second, e, k_high, k_low)
    known = send(two, [((2, 1), (3, 2))], [((2, 3), (2, 1))])
    behind = send(two, [((3, 1), (3, 2))], [((3, 3), (3, 1))])
    t_three, back = call(turn, [panel] * 2, known, behind, e, k_high, k_low)
    into_two = send(back, [((3, 2), (2, 1))], [((3, 3), (3, 2))])
    near = send(t_three, [((3, 2), (3, 1))], [((3, 3), (3, 2))])
    far = send(t_three, [((3, 2), (3, 0))], [((3, 3), (3, 2))])
    near = jnp.where(at(3, 1), near, 0.0)
    far = jnp.where(at(3, 0), far, 0.0)
    t_two, back = call(back_two, [panel] * 2, into_two, near, far, two, k_high, k_low)
    into_one = send(back, [((2, 1), (1, 0)), ((3, 0), (2, 0))], [((2, 3), (2, 1))])
    other = send(
        jnp.where(block == 3, back, t_two),
        [((3, 1), (1, 0)), ((2, 1), (2, 0))],
        [((2, 3), (2, 1))],
    )
    t_one, back = call(back_one, [panel] * 2, into_one, other, one, k_high, k_low)
    into_zero = [
        send(
            back,
            [((1, 0), (0, plane)), ((2, 0), (0, (plane + 1) % planes))],
            [((1, 3), (1, 0))],
        )
        for plane in range(planes)
    ]
    t_zero = e - sum(into_zero)
    t = jnp.where(at(1, 0), t_one, jnp.where(at(2, 1), t_two, jnp.where(at(3, 2), t_three, 0.0)))
    spread = t
    for step in range(1, planes):
        moves = [((1, 0), (1, step))]
        if 1 + step < planes:
            moves.append(((2, 1), (2, 1 + step)))
        if 2 + step < planes:
            moves.append(((3, 2), (3, 2 + step)))
        spread = spread + send(t, moves)
    spread = spread + near + far + jnp.where(at(2, 0), other, 0.0)
    t = jnp.where(block == 0, t_zero, spread)
    return call(
        finish, jax.ShapeDtypeStruct((count, height), BF16), t, swap(t), inv_high, inv_low
    )


def chain_solve(partial_fit, factor, diag_inv):
    count, height = partial_fit.shape
    breadth = factor.shape[1]
    block_size = diag_inv.shape[1]
    rows_aux = lax.axis_size("aux")
    total = height * rows_aux
    members = rows_aux // SOLVE_BLOCKS
    my_row = lax.axis_index("aux")
    my_column = lax.axis_index("pair")
    my_block = my_row // members
    column_block = (my_column * breadth + jnp.arange(breadth, dtype=jnp.int32)) // block_size
    factor_low = jnp.where((column_block < my_block)[None, :], factor, 0.0)

    def own_columns(whole):
        return lax.dynamic_slice_in_dim(whole, my_column * breadth, breadth, 1)

    zero_block = jnp.zeros((count, block_size), jnp.float32)
    solved = jnp.zeros((count, total), jnp.float32)
    for k in range(SOLVE_BLOCKS):

        def on_group(current):
            return mm(partial_fit - mm_t(own_columns(current), factor_low), diag_inv)

        def off_group(current):
            return zero_block

        summand = lax.cond(my_block == k, on_group, off_group, solved)
        arrived = lax.psum(summand, AXES)
        solved = lax.dynamic_update_slice_in_dim(solved, arrived, k * block_size, 1)
    own_coef = jnp.zeros((count, height), jnp.float32)
    contrib = jnp.zeros((count, total), jnp.float32)
    for target in reversed(range(SOLVE_BLOCKS)):
        settled = solved[:, target * block_size : (target + 1) * block_size]
        if target < SOLVE_BLOCKS - 1:
            portion = contrib[:, target * block_size : (target + 1) * block_size]
            settled = settled - lax.psum(portion, AXES)

        def on_group(state):
            coef = mm_t(settled, diag_inv)
            if target > 0:
                fresh = lax.dynamic_update_slice_in_dim(
                    jnp.zeros((count, total), jnp.float32),
                    mm(coef, factor_low),
                    my_column * breadth,
                    1,
                )
            else:
                fresh = state[1]
            return (coef, fresh)

        def keep_state(state):
            return state

        own_coef, contrib = lax.cond(my_block == target, on_group, keep_state, (own_coef, contrib))
    return own_coef.astype(jnp.bfloat16)


def shards(integrals, densities, screen, factor, diag_inv):
    block_size = diag_inv.shape[1]
    chip_blocks = (
        lax.axis_size("aux") == 2 * SOLVE_BLOCKS
        and factor.shape[1] == block_size
        and lax.axis_size("pair") == SOLVE_BLOCKS
    )
    solve = chip_solve if chip_blocks else chain_solve
    rounded = solve(fit_partial(densities, integrals, screen), factor, diag_inv)
    return scatter_sum(coulomb_partial(rounded, integrals, screen))


def solution(mesh):
    in_specs = (
        P("aux", "pair"),
        P(None, "pair"),
        P("aux", "pair"),
        P("aux", "pair"),
        P("aux", None),
    )
    out_specs = P(None, ("pair", "aux"))
    return jax.shard_map(shards, mesh=mesh, in_specs=in_specs, out_specs=out_specs, check_vma=False)
```

time: 107 us -> 114 us (1.065)
  matrix products: 36.6 us -> 0 us
  local copies, waits for them, and re-layouts: 3.94 us -> 20.8 us
  Pallas kernels: 0 us -> 14.2 us
  waiting for transfers between devices: 21.5 us -> 29.3 us
  blocking collectives: 11.6 us -> 17.6 us
  other arithmetic: 4.59 us -> 2.1 us
  starting transfers between devices: 27.2 us -> 29 us
    dot_general x16 -> x0, matrix products: 36.6 us -> none  [the longest x7 15.8 us: mm_t(): lax.dot_general(a, b, (((1,), (1,)), ((), ())), precision=HIGHEST, prefer...]
    unnamed x20 -> x44, local copies, waits for them, and re-layouts: 0.06 us -> 20.8 us
    pallas_call x0 -> x10, Pallas kernels: none -> 14.2 us  [the longest x8 7.53 us: call(): pl.pallas_call(kernel, out_shape=outs, in_specs=[VMEM] * len(operands), o...]
    ppermute x25 -> x20, waiting for transfers between devices: 19.5 us -> 27.3 us  [send(): return lax.ppermute(value, AXES, pairs)]
    all_to_all x1, blocking collectives: 11.6 us -> 17.6 us  [scatter_sum(): arrived = lax.all_to_all(slabs, 'aux', 0, 0, tiled=True)]
    broadcast_in_dim x2 -> x0, local copies, waits for them, and re-layouts: 3.85 us -> none  [the longest x1 3.83 us: masked_integrals(): jnp.repeat(jnp.repeat(screen, TILE, axis=0), TILE, axis=1)]
    select_n x4 -> x6, other arithmetic: 3.22 us -> 1.43 us  [the longest x1 0.78 us: chip_solve(): t = jnp.where(block == 0, t_zero, spread)]
    ppermute x25 -> x20, starting transfers between devices: 26.1 us -> 27.8 us  [send(): return lax.ppermute(value, AXES, pairs)]
  transfers between devices with their start and end apart: 29 -> 24, of which waited for: 6 -> 4; matrix products, arithmetic and copies ran while one was open for 19% -> 0% of each run, Pallas kernels for 0% -> 3%
where the time goes in v2:
time: 114 us; the launch traced here: 113 us
  waiting for transfers between devices  29.3 us (26%)
  starting transfers between devices  29 us (25%)
  local copies, waits for them, and re-layouts  20.8 us (18%)
  blocking collectives  17.6 us (15%)
  Pallas kernels  14.2 us (12%)
  other arithmetic  2.1 us (2%)
    ppermute x20, starting transfers between devices, send(): return lax.ppermute(value, AXES, pairs)  27.8 us
    ppermute x20, waiting for transfers between devices, send(): return lax.ppermute(value, AXES, pairs)  27.3 us
    unnamed x44, local copies, waits for them, and re-layouts  20.8 us
    all_to_all x1, blocking collectives, scatter_sum(): arrived = lax.all_to_all(slabs, 'aux', 0, 0, tiled=True)  17.6 us
    pallas_call x8, Pallas kernels, call(): pl.pallas_call(kernel, out_shape=outs, in_specs=[VMEM] * len(operands), o...  7.53 us
    pallas_call x1, Pallas kernels, fit_partial(): pl.pallas_call(fit_kernel, grid=(width // chunk,), in_specs=[SMEM, pl.Blo...  3.6 us
    pallas_call x1, Pallas kernels, coulomb_partial(): pl.pallas_call(coulomb_kernel, grid=(members,), in_specs=[SMEM, pl.BlockS...  3.1 us
  transfers between devices with their start and end apart: 24, of which 4 were waited for; matrix products, arithmetic and copies ran while one was open for 0% of the time, Pallas kernels for 3%

profile of v2, /device:TPU:0, one launch (start us, length us, event | category | flops | bytes accessed | tf_op | source)
XLA Modules:
  0.0 113.3 jit_solution(14911864088679747384)
XLA Ops:
  0.5 2.8 %copy-done = bf16[384,8192]{1,0:T(8,128)(2,1)S(1)} copy-done((bf16[384,8192]{1,0:T(8,128)(2,1)S(1)}, bf16[384,8192]{1,0:T(8,128)(2,1)}, u32[]{:S(2)}) %copy-start) | copy-done | bytes 6291480
  3.3 0.9 copy-done.11
  4.9 3.6 %fit.1 = f32[16,384]{1,0:T(8,128)S(1)} custom-call(s32[3,64]{1,0:T(4,128)S(1)} %copy-done.18, bf16[16,8192]{1,0:T(8,128)(2,1)S(1)} %copy-done.11, bf16[384,8192]{1,0:T(8,128)(2,1)S(1)} %copy-done), custom_call_target="tpu_custom_call" | custom-call | tf_op jit(solution)/shard_map/fit/pallas_call | solution.py:58
  9.1 0.8 collective-permute-done
  9.9 3.0 %collective-permute-start.1 = (f32[8,768]{1,0:T(8,128)S(1)}, f32[8,768]{1,0:T(8,128)S(1)}, u32[]{:S(2)}, u32[]{:S(2)}) collective-permute-start(f32[8,768]{1,0:T(8,128)S(1)} %pad_maximum_fusion.f0), channel_id=1, source_target_pairs={{0,1},{4,5},{1,2},{5,6},{2,3},{6,7},{3,0},{7,4},{8,9},{12,13},{9,1... | collective-permute-start | bytes 73736 | tf_op jit(solution)/shard_map/ppermute | solution.py:245
  12.9 2.6 %collective-permute-start.2 = (f32[8,768]{1,0:T(8,128)S(1)}, f32[8,768]{1,0:T(8,128)S(1)}, u32[]{:S(2)}, u32[]{:S(2)}) collective-permute-start(f32[8,768]{1,0:T(8,128)S(1)} %pad_maximum_fusion.f0), channel_id=1, source_target_pairs={{0,2},{4,6},{1,3},{5,7},{2,0},{6,4},{3,1},{7,5},{8,10},{12,14},{9,... | collective-permute-start | bytes 73736 | tf_op jit(solution)/shard_map/ppermute | solution.py:245
  15.5 1.3 %collective-permute-start.3 = (f32[8,768]{1,0:T(8,128)S(1)}, f32[8,768]{1,0:T(8,128)S(1)}, u32[]{:S(2)}, u32[]{:S(2)}) collective-permute-start(f32[8,768]{1,0:T(8,128)S(1)} %pad_maximum_fusion.f0), channel_id=1, source_target_pairs={{0,3},{4,7},{1,0},{5,4},{2,1},{6,5},{3,2},{7,6},{8,11},{12,15},{9,... | collective-permute-start | bytes 73736 | tf_op jit(solution)/shard_map/ppermute | solution.py:245
  16.8 1.0 copy-done.6
  17.9 1.0 copy-done.8
  18.9 1.3 %copy-done.4 = f32[384,768]{1,0:T(8,128)S(1)} copy-done((f32[384,768]{1,0:T(8,128)S(1)}, f32[384,768]{1,0:T(8,128)}, u32[]{:S(2)}) %copy-start.4) | copy-done | bytes 1179672
  20.2 1.3 %copy-done.5 = f32[384,768]{1,0:T(8,128)S(1)} copy-done((f32[384,768]{1,0:T(8,128)S(1)}, f32[384,768]{1,0:T(8,128)}, u32[]{:S(2)}) %copy-start.5) | copy-done | bytes 1179672
  21.4 1.3 %copy-done.7 = f32[384,768]{1,0:T(8,128)S(1)} copy-done((f32[384,768]{1,0:T(8,128)S(1)}, f32[384,768]{1,0:T(8,128)}, u32[]{:S(2)}) %copy-start.7) | copy-done | bytes 1179672
  22.7 1.3 %copy-done.9 = f32[384,768]{1,0:T(8,128)S(1)} copy-done((f32[384,768]{1,0:T(8,128)S(1)}, f32[384,768]{1,0:T(8,128)}, u32[]{:S(2)}) %copy-start.9) | copy-done | bytes 1179672
  25.4 7.3 %collective-permute-start.6 = (f32[8,768]{1,0:T(8,128)S(1)}, f32[8,768]{1,0:T(8,128)S(1)}, u32[]{:S(2)}, u32[]{:S(2)}) collective-permute-start(f32[8,768]{1,0:T(8,128)S(1)} %start_solve.1.e), channel_id=1, source_target_pairs={{0,8},{4,12},{1,16},{5,20},{2,24},{6,28},{11,0},{15,4},{19,1},{23,... | collective-permute-start | bytes 73736 | tf_op jit(solution)/shard_map/ppermute | solution.py:245
  32.7 1.5 %collective-permute-done.6.known = f32[8,768]{1,0:T(8,128)S(1)} collective-permute-done((f32[8,768]{1,0:T(8,128)S(1)}, f32[8,768]{1,0:T(8,128)S(1)}, u32[]{:S(2)}, u32[]{:S(2)}) %collective-permute-start.6) | collective-permute-done | bytes 24608 | tf_op jit(solution)/shard_map/ppermute | solution.py:245
  39.5 2.1 %turn.1 = (f32[8,768]{1,0:T(8,128)}, f32[8,768]{1,0:T(8,128)S(1)}) custom-call(f32[8,768]{1,0:T(8,128)S(1)} %collective-permute-done.9.known, f32[8,768]{1,0:T(8,128)S(1)} %collective-permute-done.10.behind, f32[8,768]{1,0:T(8,128)S(1)} %start_solve.1.e, bf16[768,768]{1,0:T(8,128)(2,1)S(1)} %get-tuple-element.17.high, bf16[768,768]{1,0:T(8,128)(2,1)S(1)} %get-tuple-element.18.low), custom_call_target="tpu_custom_call" | custom-call | tf_op jit(solution)/shard_map/turn/pallas_call | solution.py:139
  42.2 1.3 %collective-permute-start.13 = (f32[8,768]{1,0:T(8,128)}, f32[8,768]{1,0:T(8,128)}, u32[]{:S(2)}, u32[]{:S(2)}) collective-permute-start(f32[8,768]{1,0:T(8,128)} %get-tuple-element.20), channel_id=1, source_target_pairs={{26,24},{30,28},{27,26},{31,30}} | collective-permute-start | bytes 73736 | tf_op jit(solution)/shard_map/ppermute | solution.py:245
  45.5 0.7 copy-done.15
  46.2 1.0 back_two.1
  48.5 1.3 %collective-permute-start.15 = (f32[8,768]{1,0:T(8,128)}, f32[8,768]{1,0:T(8,128)}, u32[]{:S(2)}, u32[]{:S(2)}) collective-permute-start(f32[8,768]{1,0:T(8,128)} %broadcast_select_fusion.2), channel_id=1, source_target_pairs={{25,8},{29,12},{17,16},{21,20},{19,17},{23,21}} | collective-permute-start | bytes 73736 | tf_op jit(solution)/shard_map/ppermute | solution.py:245
  49.7 1.2 %collective-permute-start.14 = (f32[8,768]{1,0:T(8,128)}, f32[8,768]{1,0:T(8,128)}, u32[]{:S(2)}, u32[]{:S(2)}) collective-permute-start(f32[8,768]{1,0:T(8,128)} %get-tuple-element.21), channel_id=1, source_target_pairs={{17,8},{21,12},{24,16},{28,20},{19,17},{23,21}} | collective-permute-start | bytes 73736 | tf_op jit(solution)/shard_map/ppermute | solution.py:245
  51.0 0.7 copy-done.13
  51.7 1.8 %back_one.1 = (f32[8,768]{1,0:T(8,128)S(1)}, f32[8,768]{1,0:T(8,128)}) custom-call(f32[8,768]{1,0:T(8,128)} %collective-permute-done.14.into, f32[8,768]{1,0:T(8,128)} %collective-permute-done.15.other, f32[8,768]{1,0:T(8,128)S(1)} %copy-done.13, bf16[768,768]{1,0:T(8,128)(2,1)S(1)} %get-tuple-element.17.high, bf16[768,768]{1,0:T(8,128)(2,1)S(1)} %get-tuple-element.18.low), custom_call_target="tpu_custom_call" | custom-call | tf_op jit(solution)/shard_map/back_one/pallas_call | solution.py:139
  55.6 1.3 %collective-permute-start.16 = (f32[8,768]{1,0:T(8,128)}, f32[8,768]{1,0:T(8,128)S(1)}, u32[]{:S(2)}, u32[]{:S(2)}) collective-permute-start(f32[8,768]{1,0:T(8,128)} %get-tuple-element.23), channel_id=1, source_target_pairs={{8,0},{12,4},{16,1},{20,5},{11,8},{15,12}} | collective-permute-start | bytes 73736 | tf_op jit(solution)/shard_map/ppermute | solution.py:245
  58.2 1.3 %collective-permute-start.19 = (f32[8,768]{1,0:T(8,128)}, f32[8,768]{1,0:T(8,128)S(1)}, u32[]{:S(2)}, u32[]{:S(2)}) collective-permute-start(f32[8,768]{1,0:T(8,128)} %get-tuple-element.23), channel_id=1, source_target_pairs={{8,3},{12,7},{16,0},{20,4},{11,8},{15,12}} | collective-permute-start | bytes 73736 | tf_op jit(solution)/shard_map/ppermute | solution.py:245
  59.5 25.8 %collective-permute-done.16 = f32[8,768]{1,0:T(8,128)S(1)} collective-permute-done((f32[8,768]{1,0:T(8,128)}, f32[8,768]{1,0:T(8,128)S(1)}, u32[]{:S(2)}, u32[]{:S(2)}) %collective-permute-start.16) | collective-permute-done | bytes 24608 | tf_op jit(solution)/shard_map/ppermute | solution.py:245
  85.3 0.8 add_select_fusion.own
  86.2 1.2 %collective-permute-done.23.mate = f32[8,768]{1,0:T(8,128)S(1)} collective-permute-done((f32[8,768]{1,0:T(8,128)S(1)}, f32[8,768]{1,0:T(8,128)S(1)}, u32[]{:S(2)}, u32[]{:S(2)}) %collective-permute-start.23) | collective-permute-done | bytes 24608 | tf_op jit(solution)/shard_map/ppermute | solution.py:248
  87.4 1.3 %copy-done.3 = bf16[768,768]{1,0:T(8,128)(2,1)S(1)} copy-done((bf16[768,768]{1,0:T(8,128)(2,1)S(1)}, bf16[768,768]{1,0:T(8,128)(2,1)}, u32[]{:S(2)}) %copy-start.3) | copy-done | bytes 1179672
  89.1 2.8 %copy-done.1 = bf16[384,8192]{1,0:T(8,128)(2,1)S(1)} copy-done((bf16[384,8192]{1,0:T(8,128)(2,1)S(1)}, bf16[384,8192]{1,0:T(8,128)(2,1)}, u32[]{:S(2)}) %copy-start.1) | copy-done | bytes 6291480
  91.9 3.1 %coulomb.1 = bf16[8,16,1024]{2,1,0:T(8,128)(2,1)S(1)} custom-call(s32[3,64]{1,0:T(4,128)S(1)} %copy-done.19, bf16[16,384]{1,0:T(8,128)(2,1)S(1)} %finish.1.rounded, bf16[384,8192]{1,0:T(8,128)(2,1)S(1)} %copy-done.1), custom_call_target="tpu_custom_call" | custom-call | tf_op jit(solution)/shard_map/coulomb/pallas_call | solution.py:100
  95.0 17.6 %all_to_all.5 = bf16[8,16,1024]{2,1,0:T(8,128)(2,1)S(1)} all-to-all(bf16[8,16,1024]{2,1,0:T(8,128)(2,1)S(1)} %coulomb.1), channel_id=1, replica_groups=mesh['aux'=8,'pair'=4] {'aux'}, dimensions={0} | all-to-all | bytes 524288 | tf_op jit(solution)/shard_map/all_to_all | solution.py:116
  (80 shorter events, 16.7 us)
Async XLA Ops:
  0.0 16.8 %collective-permute-start.4 = (f32[384,768]{1,0:T(8,128)}, f32[384,768]{1,0:T(8,128)S(1)}, u32[]{:S(2)}, u32[]{:S(2)}) collective-permute-start(f32[384,768]{1,0:T(8,128)} %own_inv.1), channel_id=1, source_target_pairs={{0,4},{4,0},{8,12},{12,8},{16,20},{20,16},{24,28},{28,24},{1,5},{5... | collective-permute-start | bytes 3538952 | tf_op jit(solution)/shard_map/ppermute | solution.py:248
  0.5 17.4 %collective-permute-start.5 = (f32[384,768]{1,0:T(8,128)}, f32[384,768]{1,0:T(8,128)S(1)}, u32[]{:S(2)}, u32[]{:S(2)}) collective-permute-start(f32[384,768]{1,0:T(8,128)} %own_fac.1), channel_id=1, source_target_pairs={{0,4},{4,0},{8,12},{12,8},{16,20},{20,16},{24,28},{28,24},{1,5},{5... | collective-permute-start | bytes 3538952 | tf_op jit(solution)/shard_map/ppermute | solution.py:248
  0.5 2.8 %copy-start = (bf16[384,8192]{1,0:T(8,128)(2,1)S(1)}, bf16[384,8192]{1,0:T(8,128)(2,1)}, u32[]{:S(2)}) copy-start(bf16[384,8192]{1,0:T(8,128)(2,1)} %integrals.3) | copy-start | bytes 18874372
  8.5 1.4 %collective-permute-start = (f32[8,384]{1,0:T(8,128)S(1)}, f32[8,384]{1,0:T(8,128)S(1)}, u32[]{:S(2)}, u32[]{:S(2)}) collective-permute-start(f32[8,384]{1,0:T(8,128)S(1)} %constant_dynamic-slice_fusion), channel_id=1, source_target_pairs={{0,4},{4,0},{8,12},{12,8},{16,20},{20,16},{24,28},{28,24},{1,5},{5... | collective-permute-start | bytes 36872 | tf_op jit(solution)/shard_map/ppermute | solution.py:248
  9.9 14.4 %collective-permute-start.1 = (f32[8,768]{1,0:T(8,128)S(1)}, f32[8,768]{1,0:T(8,128)S(1)}, u32[]{:S(2)}, u32[]{:S(2)}) collective-permute-start(f32[8,768]{1,0:T(8,128)S(1)} %pad_maximum_fusion.f0), channel_id=1, source_target_pairs={{0,1},{4,5},{1,2},{5,6},{2,3},{6,7},{3,0},{7,4},{8,9},{12,13},{9,1... | collective-permute-start | bytes 73736 | tf_op jit(solution)/shard_map/ppermute | solution.py:245
  12.9 11.5 %collective-permute-start.2 = (f32[8,768]{1,0:T(8,128)S(1)}, f32[8,768]{1,0:T(8,128)S(1)}, u32[]{:S(2)}, u32[]{:S(2)}) collective-permute-start(f32[8,768]{1,0:T(8,128)S(1)} %pad_maximum_fusion.f0), channel_id=1, source_target_pairs={{0,2},{4,6},{1,3},{5,7},{2,0},{6,4},{3,1},{7,5},{8,10},{12,14},{9,... | collective-permute-start | bytes 73736 | tf_op jit(solution)/shard_map/ppermute | solution.py:245
  15.5 8.9 %collective-permute-start.3 = (f32[8,768]{1,0:T(8,128)S(1)}, f32[8,768]{1,0:T(8,128)S(1)}, u32[]{:S(2)}, u32[]{:S(2)}) collective-permute-start(f32[8,768]{1,0:T(8,128)S(1)} %pad_maximum_fusion.f0), channel_id=1, source_target_pairs={{0,3},{4,7},{1,0},{5,4},{2,1},{6,5},{3,2},{7,6},{8,11},{12,15},{9,... | collective-permute-start | bytes 73736 | tf_op jit(solution)/shard_map/ppermute | solution.py:245
  18.9 1.3 %copy-start.4 = (f32[384,768]{1,0:T(8,128)S(1)}, f32[384,768]{1,0:T(8,128)}, u32[]{:S(2)}) copy-start(f32[384,768]{1,0:T(8,128)} %own_inv.1) | copy-start | bytes 3538948
  20.2 1.3 %copy-start.5 = (f32[384,768]{1,0:T(8,128)S(1)}, f32[384,768]{1,0:T(8,128)}, u32[]{:S(2)}) copy-start(f32[384,768]{1,0:T(8,128)} %own_fac.1) | copy-start | bytes 3538948
  25.4 14.2 %copy-start.10 = (f32[8,768]{1,0:T(8,128)}, f32[8,768]{1,0:T(8,128)S(1)}, u32[]{:S(2)}) copy-start(f32[8,768]{1,0:T(8,128)S(1)} %start_solve.1.e) | copy-start | bytes 73732
  25.4 8.8 %collective-permute-start.6 = (f32[8,768]{1,0:T(8,128)S(1)}, f32[8,768]{1,0:T(8,128)S(1)}, u32[]{:S(2)}, u32[]{:S(2)}) collective-permute-start(f32[8,768]{1,0:T(8,128)S(1)} %start_solve.1.e), channel_id=1, source_target_pairs={{0,8},{4,12},{1,16},{5,20},{2,24},{6,28},{11,0},{15,4},{19,1},{23,... | collective-permute-start | bytes 73736 | tf_op jit(solution)/shard_map/ppermute | solution.py:245
  34.9 2.0 %collective-permute-start.7 = (f32[8,768]{1,0:T(8,128)S(1)}, f32[8,768]{1,0:T(8,128)S(1)}, u32[]{:S(2)}, u32[]{:S(2)}) collective-permute-start(f32[8,768]{1,0:T(8,128)S(1)} %after_zero.1.s), channel_id=1, source_target_pairs={{8,17},{12,21},{24,25},{28,29},{11,8},{15,12}} | collective-permute-start | bytes 73736 | tf_op jit(solution)/shard_map/ppermute | solution.py:245
  35.6 1.3 %collective-permute-start.8 = (f32[8,768]{1,0:T(8,128)S(1)}, f32[8,768]{1,0:T(8,128)S(1)}, u32[]{:S(2)}, u32[]{:S(2)}) collective-permute-start(f32[8,768]{1,0:T(8,128)S(1)} %after_zero.1.s), channel_id=1, source_target_pairs={{8,25},{12,29},{16,17},{20,21},{11,8},{15,12}} | collective-permute-start | bytes 73736 | tf_op jit(solution)/shard_map/ppermute | solution.py:245
  37.6 2.0 %collective-permute-start.10 = (f32[8,768]{1,0:T(8,128)S(1)}, f32[8,768]{1,0:T(8,128)S(1)}, u32[]{:S(2)}, u32[]{:S(2)}) collective-permute-start(f32[8,768]{1,0:T(8,128)S(1)} %after_one.1.s), channel_id=1, source_target_pairs={{25,26},{29,30},{27,25},{31,29}} | collective-permute-start | bytes 73736 | tf_op jit(solution)/shard_map/ppermute | solution.py:245
  38.2 1.3 %collective-permute-start.9 = (f32[8,768]{1,0:T(8,128)S(1)}, f32[8,768]{1,0:T(8,128)S(1)}, u32[]{:S(2)}, u32[]{:S(2)}) collective-permute-start(f32[8,768]{1,0:T(8,128)S(1)} %after_one.1.s), channel_id=1, source_target_pairs={{17,26},{21,30},{19,17},{23,21}} | collective-permute-start | bytes 73736 | tf_op jit(solution)/shard_map/ppermute | solution.py:245
  42.2 2.6 %collective-permute-start.13 = (f32[8,768]{1,0:T(8,128)}, f32[8,768]{1,0:T(8,128)}, u32[]{:S(2)}, u32[]{:S(2)}) collective-permute-start(f32[8,768]{1,0:T(8,128)} %get-tuple-element.20), channel_id=1, source_target_pairs={{26,24},{30,28},{27,26},{31,30}} | collective-permute-start | bytes 73736 | tf_op jit(solution)/shard_map/ppermute | solution.py:245
  43.5 1.4 %collective-permute-start.12 = (f32[8,768]{1,0:T(8,128)}, f32[8,768]{1,0:T(8,128)S(1)}, u32[]{:S(2)}, u32[]{:S(2)}) collective-permute-start(f32[8,768]{1,0:T(8,128)} %get-tuple-element.20), channel_id=1, source_target_pairs={{26,25},{30,29},{27,26},{31,30}} | collective-permute-start | bytes 73736 | tf_op jit(solution)/shard_map/ppermute | solution.py:245
  44.2 1.3 %collective-permute-start.11 = (f32[8,768]{1,0:T(8,128)}, f32[8,768]{1,0:T(8,128)S(1)}, u32[]{:S(2)}, u32[]{:S(2)}) collective-permute-start(f32[8,768]{1,0:T(8,128)} %copy-done.20), channel_id=1, source_target_pairs={{26,17},{30,21},{27,26},{31,30}} | collective-permute-start | bytes 73736 | tf_op jit(solution)/shard_map/ppermute | solution.py:245
  48.5 2.5 %collective-permute-start.15 = (f32[8,768]{1,0:T(8,128)}, f32[8,768]{1,0:T(8,128)}, u32[]{:S(2)}, u32[]{:S(2)}) collective-permute-start(f32[8,768]{1,0:T(8,128)} %broadcast_select_fusion.2), channel_id=1, source_target_pairs={{25,8},{29,12},{17,16},{21,20},{19,17},{23,21}} | collective-permute-start | bytes 73736 | tf_op jit(solution)/shard_map/ppermute | solution.py:245
  49.7 1.3 %collective-permute-start.14 = (f32[8,768]{1,0:T(8,128)}, f32[8,768]{1,0:T(8,128)}, u32[]{:S(2)}, u32[]{:S(2)}) collective-permute-start(f32[8,768]{1,0:T(8,128)} %get-tuple-element.21), channel_id=1, source_target_pairs={{17,8},{21,12},{24,16},{28,20},{19,17},{23,21}} | collective-permute-start | bytes 73736 | tf_op jit(solution)/shard_map/ppermute | solution.py:245
  51.7 1.8 %copy-start.17 = (f32[8,768]{1,0:T(8,128)S(1)}, f32[8,768]{1,0:T(8,128)}, u32[]{:S(2)}) copy-start(f32[8,768]{1,0:T(8,128)} %copy-done.16) | copy-start | bytes 73732
  53.6 4.0 %collective-permute-start.20 = (f32[8,768]{1,0:T(8,128)S(1)}, f32[8,768]{1,0:T(8,128)S(1)}, u32[]{:S(2)}, u32[]{:S(2)}) collective-permute-start(f32[8,768]{1,0:T(8,128)S(1)} %select_select_fusion), channel_id=1, source_target_pairs={{8,9},{12,13},{17,18},{21,22},{26,27},{30,31}} | collective-permute-start | bytes 73736 | tf_op jit(solution)/shard_map/ppermute | solution.py:245
  54.2 4.0 %collective-permute-start.21 = (f32[8,768]{1,0:T(8,128)S(1)}, f32[8,768]{1,0:T(8,128)S(1)}, u32[]{:S(2)}, u32[]{:S(2)}) collective-permute-start(f32[8,768]{1,0:T(8,128)S(1)} %select_select_fusion), channel_id=1, source_target_pairs={{8,10},{12,14},{17,19},{21,23}} | collective-permute-start | bytes 73736 | tf_op jit(solution)/shard_map/ppermute | solution.py:245
  54.9 4.6 %collective-permute-start.22 = (f32[8,768]{1,0:T(8,128)S(1)}, f32[8,768]{1,0:T(8,128)S(1)}, u32[]{:S(2)}, u32[]{:S(2)}) collective-permute-start(f32[8,768]{1,0:T(8,128)S(1)} %select_select_fusion), channel_id=1, source_target_pairs={{8,11},{12,15}} | collective-permute-start | bytes 73736 | tf_op jit(solution)/shard_map/ppermute | solution.py:245
  55.6 29.7 %collective-permute-start.16 = (f32[8,768]{1,0:T(8,128)}, f32[8,768]{1,0:T(8,128)S(1)}, u32[]{:S(2)}, u32[]{:S(2)}) collective-permute-start(f32[8,768]{1,0:T(8,128)} %get-tuple-element.23), channel_id=1, source_target_pairs={{8,0},{12,4},{16,1},{20,5},{11,8},{15,12}} | collective-permute-start | bytes 73736 | tf_op jit(solution)/shard_map/ppermute | solution.py:245
  56.9 28.4 %collective-permute-start.17 = (f32[8,768]{1,0:T(8,128)}, f32[8,768]{1,0:T(8,128)S(1)}, u32[]{:S(2)}, u32[]{:S(2)}) collective-permute-start(f32[8,768]{1,0:T(8,128)} %get-tuple-element.23), channel_id=1, source_target_pairs={{8,1},{12,5},{16,2},{20,6},{11,8},{15,12}} | collective-permute-start | bytes 73736 | tf_op jit(solution)/shard_map/ppermute | solution.py:245
  57.5 27.8 %collective-permute-start.18 = (f32[8,768]{1,0:T(8,128)}, f32[8,768]{1,0:T(8,128)S(1)}, u32[]{:S(2)}, u32[]{:S(2)}) collective-permute-start(f32[8,768]{1,0:T(8,128)} %get-tuple-element.23), channel_id=1, source_target_pairs={{8,2},{12,6},{16,3},{20,7},{11,8},{15,12}} | collective-permute-start | bytes 73736 | tf_op jit(solution)/shard_map/ppermute | solution.py:245
  58.2 27.1 %collective-permute-start.19 = (f32[8,768]{1,0:T(8,128)}, f32[8,768]{1,0:T(8,128)S(1)}, u32[]{:S(2)}, u32[]{:S(2)}) collective-permute-start(f32[8,768]{1,0:T(8,128)} %get-tuple-element.23), channel_id=1, source_target_pairs={{8,3},{12,7},{16,0},{20,4},{11,8},{15,12}} | collective-permute-start | bytes 73736 | tf_op jit(solution)/shard_map/ppermute | solution.py:245
  85.3 3.8 %copy-start.19 = (s32[3,64]{1,0:T(4,128)S(1)}, s32[3,64]{1,0:T(4,128)}, u32[]{:S(2)}) copy-start(s32[3,64]{1,0:T(4,128)} %screen.3) | copy-start | bytes 2308
  86.1 1.3 %collective-permute-start.23 = (f32[8,768]{1,0:T(8,128)S(1)}, f32[8,768]{1,0:T(8,128)S(1)}, u32[]{:S(2)}, u32[]{:S(2)}) collective-permute-start(f32[8,768]{1,0:T(8,128)S(1)} %add_select_fusion.own), channel_id=1, source_target_pairs={{0,4},{4,0},{8,12},{12,8},{16,20},{20,16},{24,28},{28,24},{1,5},{5... | collective-permute-start | bytes 73736 | tf_op jit(solution)/shard_map/ppermute | solution.py:248
  87.4 1.3 %copy-start.3 = (bf16[768,768]{1,0:T(8,128)(2,1)S(1)}, bf16[768,768]{1,0:T(8,128)(2,1)}, u32[]{:S(2)}) copy-start(bf16[768,768]{1,0:T(8,128)(2,1)} %copy-done.2) | copy-start | bytes 3538948
  89.1 2.8 %copy-start.1 = (bf16[384,8192]{1,0:T(8,128)(2,1)S(1)}, bf16[384,8192]{1,0:T(8,128)(2,1)}, u32[]{:S(2)}) copy-start(bf16[384,8192]{1,0:T(8,128)(2,1)} %integrals.3) | copy-start | bytes 18874372
  (14 other events, 11.8 us)

commit v3 on v0

v3 whole, which is shorter than its diff:
```python
import jax
import jax.numpy as jnp
from jax import lax
from jax.experimental import pallas as pl
from jax.experimental.pallas import tpu as pltpu
from jax.sharding import PartitionSpec as P

TILE = 128
SOLVE_BLOCKS = 4
AXES = ("aux", "pair")
HIGHEST = lax.Precision.HIGHEST
F32 = jnp.float32
BF16 = jnp.bfloat16
VMEM = pl.BlockSpec(memory_space=pltpu.VMEM)
SMEM = pl.BlockSpec(memory_space=pltpu.SMEM)
HBM = pl.BlockSpec(memory_space=pltpu.HBM)
MIB = 1024 * 1024
NN = (((1,), (0,)), ((), ()))
NT = (((1,), (1,)), ((), ()))
TN = (((0,), (0,)), ((), ()))


def struct(shape, dtype=F32):
    return jax.ShapeDtypeStruct(shape, dtype)


def call(kernel, outs, *operands, limit=12, specs=None, scratch=()):
    return pl.pallas_call(
        kernel,
        out_shape=outs,
        in_specs=specs or [VMEM] * len(operands),
        out_specs=jax.tree.map(lambda _: VMEM, outs),
        scratch_shapes=scratch,
        compiler_params=pltpu.CompilerParams(vmem_limit_bytes=limit * MIB),
        name=kernel.__name__,
    )(*operands)


def side_of():
    return lax.rem(lax.axis_index("aux"), 2)


def block_of():
    return lax.div(lax.axis_index("aux"), 2)


def fit(screen_in, densities_in, integrals, held, kept, given, screen, densities, total, arrived):
    height, width = integrals.shape
    pieces = arrived.shape[0] - 2
    chunk = width // pieces
    half = kept.shape[0]
    small = [
        pltpu.make_async_copy(screen_in, screen, arrived.at[pieces]),
        pltpu.make_async_copy(densities_in, densities, arrived.at[pieces + 1]),
    ]
    copies = [
        pltpu.make_async_copy(
            integrals.at[:, j * chunk : (j + 1) * chunk],
            held.at[:, j * chunk : (j + 1) * chunk],
            arrived.at[j],
        )
        for j in range(pieces)
    ]
    for copy in small + copies:
        copy.start()
    total[...] = jnp.zeros_like(total)
    for copy in small:
        copy.wait()
    for j in range(pieces):
        copies[j].wait()
        columns = slice(j * chunk, (j + 1) * chunk)
        for i in range(height // TILE):
            rows = slice(i * TILE, (i + 1) * TILE)
            masked = jnp.concatenate(
                [
                    jnp.where(
                        screen[i, t] != 0,
                        densities[:, t * TILE : (t + 1) * TILE],
                        jnp.zeros((), BF16),
                    )
                    for t in range(j * chunk // TILE, (j + 1) * chunk // TILE)
                ],
                axis=1,
            )
            total[rows, :] += lax.dot_general(
                held[rows, columns], masked, NT, preferred_element_type=F32
            )
    done = total[...].T
    even = side_of() == 0
    kept[...] = jnp.where(even, done[:half], done[half:])
    given[...] = jnp.where(even, done[half:], done[:half])


def fit_partial(densities, integrals, screen):
    count = densities.shape[0]
    height, width = integrals.shape
    pieces = 8 if width % (8 * TILE) == 0 else width // TILE
    half = struct((count // 2, height))
    return call(
        fit,
        [struct(integrals.shape, BF16), half, half],
        screen,
        densities,
        integrals,
        specs=[HBM] * 3,
        scratch=[
            pltpu.SMEM(screen.shape, jnp.int32),
            pltpu.VMEM(densities.shape, BF16),
            pltpu.VMEM((height, count), F32),
            pltpu.SemaphoreType.DMA((pieces + 2,)),
        ],
    )


def coulomb(screen, rounded, held, out):
    members, _, chunk = out.shape
    height = held.shape[0]
    for m in range(members):
        for t in range(m * chunk // TILE, (m + 1) * chunk // TILE):
            masked = jnp.concatenate(
                [
                    jnp.where(
                        screen[i, t] != 0,
                        rounded[:, i * TILE : (i + 1) * TILE],
                        jnp.zeros((), BF16),
                    )
                    for i in range(height // TILE)
                ],
                axis=1,
            )
            part = jnp.dot(
                masked, held[:, t * TILE : (t + 1) * TILE], preferred_element_type=F32
            )
            first = t * TILE - m * chunk
            out[m, :, first : first + TILE] = part.astype(out.dtype)


def coulomb_partial(rounded, held, screen):
    members = lax.axis_size("aux")
    out = struct((members, rounded.shape[0], held.shape[1] // members), BF16)
    return call(coulomb, out, screen, rounded, held, specs=[SMEM, VMEM, VMEM])


def scatter_sum(slabs):
    arrived = lax.all_to_all(slabs, "aux", 0, 0, tiled=True)
    return jnp.sum(arrived.astype(F32), axis=0)


def high_low(value):
    high = value.astype(BF16)
    return high, (value - high.astype(F32)).astype(BF16)


def times(value, high, low, dims=NN):
    rows = value.shape[0]
    coarse = value.astype(BF16).astype(F32)
    pair = jnp.concatenate([coarse, value - coarse], axis=0).astype(BF16)
    both = lax.dot_general(pair, high, dims, preferred_element_type=F32)
    both += lax.dot_general(pair, low, dims, preferred_element_type=F32)
    return both[:rows] + both[rows:]


def prepare(own_inv, mate_inv, own_fac, mate_fac, inv_high, inv_low, k_high, k_low, kt_high, kt_low):
    height = own_inv.shape[0]
    side = side_of()
    here = pl.ds(pl.multiple_of(side * height, height), height)
    there = pl.ds(pl.multiple_of((1 - side) * height, height), height)
    for ref, rows in ((own_inv, here), (mate_inv, there)):
        high, low = high_low(ref[...])
        inv_high[rows, :] = high
        inv_low[rows, :] = low

    @pl.when(block_of() > 0)
    def _():
        total = jnp.zeros(k_high.shape, F32)
        for inv, fac in ((own_inv, own_fac), (mate_inv, mate_fac)):
            ih, il = high_low(inv[...])
            fh, fl = high_low(fac[...])
            total += lax.dot_general(ih, fh, TN, preferred_element_type=F32)
            total += lax.dot_general(ih, fl, TN, preferred_element_type=F32)
            total += lax.dot_general(il, fh, TN, preferred_element_type=F32)
        high, low = high_low(total)
        k_high[...] = high
        k_low[...] = low
        high, low = high_low(total.T)
        kt_high[...] = high
        kt_low[...] = low


def merge(kept, mate, out):
    even = side_of() == 0
    height = kept.shape[1]
    out[:, :height] = jnp.where(even, kept[...], mate[...])
    out[:, height:] = jnp.where(even, mate[...], kept[...])


def begin(f0, f1, f2, f3, high, low, out):
    out[...] = times(f0[...] + f1[...] + f2[...] + f3[...], high[...], low[...])


def after_zero(one, two, three, e, high, low, out):
    block = block_of()
    known = jnp.where(block == 1, one[...], jnp.where(block == 2, two[...], three[...]))
    term = times(known, high[...], low[...])
    out[...] = jnp.where(block == 0, e[...], jnp.where(block == 1, e[...] - term, term))


def after_one(first, second, e, high, low, out):
    block = block_of()
    known = jnp.where(block == 3, second[...], first[...])
    behind = jnp.where(block == 3, first[...], second[...])
    total = behind + times(known, high[...], low[...])
    out[...] = jnp.where(block == 0, e[...], jnp.where(block == 3, total, e[...] - total))


def turn(known, behind, e, kt_high, kt_low, high, low, settled, back):
    value = e[...] - behind[...] - times(known[...], kt_high[...], kt_low[...])
    settled[...] = value
    back[...] = times(value, high[...], low[...])


def back_two(into, near, far, t, s, high, low, settled, back, mixed):
    plane = lax.axis_index("pair")
    last = block_of() == 3
    passed = jnp.where(plane == 0, far[...], jnp.where(plane == 1, near[...], t[...]))
    value = jnp.where(last, passed, s[...] - into[...])
    product = times(value, high[...], low[...])
    settled[...] = value
    back[...] = product
    mixed[...] = jnp.where(last, product, value)


def back_one(into, other, t, s, high, low, settled, back):
    plane = lax.axis_index("pair")
    block = block_of()
    passed = jnp.where(plane == 0, other[...], t[...])
    value = jnp.where(
        block == 1,
        s[...] - into[...] - other[...],
        jnp.where(block == 2, passed, t[...]),
    )
    settled[...] = value
    product = times(value, high[...], low[...])
    back[...] = jnp.where(block == 2, product + into[...], product)


def collect(e, z1, z2, z3, i0, i1, i2, i3, t, p1, p2, p3, out):
    plane = lax.axis_index("pair")
    block = block_of()

    def by_plane(a, b, c, d):
        return jnp.where(
            plane == 0, a[...], jnp.where(plane == 1, b[...], jnp.where(plane == 2, c[...], d[...]))
        )

    start = by_plane(e, z1, z2, z3)
    zero = start - by_plane(i0, i1, i2, i3) - by_plane(i3, i0, i1, i2)
    one = by_plane(t, p1, p2, p3)
    two = by_plane(t, t, p1, p2)
    three = by_plane(t, t, t, p1)
    out[...] = jnp.where(
        block == 0, zero, jnp.where(block == 1, one, jnp.where(block == 2, two, three))
    )


def finish(own, mate, inv, out):
    even = side_of() == 0
    value = jnp.concatenate(
        [jnp.where(even, own[...], mate[...]), jnp.where(even, mate[...], own[...])], axis=0
    )
    high, low = high_low(inv[...])
    out[...] = times(value, high, low, NT).astype(out.dtype)


def mm(a, b):
    return jnp.dot(a, b, precision=HIGHEST, preferred_element_type=F32)


def mm_t(a, b):
    return lax.dot_general(a, b, NT, precision=HIGHEST, preferred_element_type=F32)


def complete(moves, idle):
    chips = [(k, plane) for k in range(SOLVE_BLOCKS) for plane in range(SOLVE_BLOCKS)]
    used = {chip for move in moves for chip in move}
    spare = [chip for chip in idle if chip not in used] + [
        chip for chip in reversed(chips) if chip not in used and chip not in idle
    ]
    to = {}
    for (source, target), via in zip(moves, spare):
        to.update({source: target, target: via, via: source})
    return [(chip, to.get(chip, chip)) for chip in chips]


IDLE = [(1, 3), (2, 3), (3, 3), (0, 3), (1, 2), (2, 2), (0, 2), (1, 1), (0, 1)]


def chip_solve(kept, given, factor, diag_inv):
    half, height = kept.shape
    size = 2 * height
    planes = lax.axis_size("pair")

    def pairs_of(routes):
        pairs = []
        for (k_from, z_from), (k_to, z_to) in routes:
            for c in range(2):
                d = 1 - c if (k_from, z_from) == (k_to, z_to) else c
                pairs.append(
                    ((2 * k_from + c) * planes + z_from, (2 * k_to + d) * planes + z_to)
                )
        return pairs

    def send(value, *moves):
        return lax.ppermute(value, AXES, pairs_of(complete(moves, IDLE)))

    def swap(value):
        return lax.ppermute(value, "aux", [(i, i ^ 1) for i in range(2 * SOLVE_BLOCKS)])

    panel = struct((half, size))
    square = struct((size, size), BF16)
    inv_high, inv_low, k_high, k_low, kt_high, kt_low = call(
        prepare, [square] * 6, diag_inv, swap(diag_inv), factor, swap(factor), limit=32
    )
    part = call(merge, panel, kept, swap(given))
    home = [max(k - 1, 0) for k in range(SOLVE_BLOCKS)]
    gathered = []
    for step in range(1, planes):
        routes = []
        for k in range(SOLVE_BLOCKS):
            far = (home[k] + step) % planes
            for plane in range(planes):
                to = {home[k]: far, far: home[k]}.get(plane, plane)
                routes.append(((k, plane), (k, to)))
        gathered.append(lax.ppermute(part, AXES, pairs_of(routes)))
    e = call(begin, panel, part, *gathered, inv_high, inv_low)
    reach = [send(e, ((0, 0), (k, 0))) for k in range(1, SOLVE_BLOCKS)]
    one = call(after_zero, panel, *reach, e, kt_high, kt_low)
    first = send(one, ((1, 0), (2, 1)), ((3, 0), (3, 1)), ((0, 0), (0, 1)))
    second = send(one, ((1, 0), (3, 1)), ((2, 0), (2, 1)), ((0, 0), (0, 2)))
    two = call(after_one, panel, first, second, e, kt_high, kt_low)
    behind = send(two, ((3, 1), (3, 2)), ((0, 0), (0, 3)))
    known = send(two, ((2, 1), (3, 2)))
    t, back = call(turn, [panel] * 2, known, behind, e, kt_high, kt_low, k_high, k_low)
    into = send(back, ((3, 2), (2, 1)))
    near = send(t, ((3, 2), (3, 1)))
    far = send(t, ((3, 2), (3, 0)))
    t, back, mixed = call(back_two, [panel] * 3, into, near, far, t, two, k_high, k_low)
    into = send(back, ((2, 1), (1, 0)), ((3, 0), (2, 0)))
    other = send(mixed, ((3, 1), (1, 0)), ((2, 1), (2, 0)))
    t, back = call(back_one, [panel] * 2, into, other, t, one, k_high, k_low)
    into = [
        send(back, ((1, 0), (0, plane)), ((2, 0), (0, (plane + 1) % planes)))
        for plane in range(planes)
    ]
    spread = []
    for step in range(1, planes):
        moves = [((1, 0), (1, step))]
        if 1 + step < planes:
            moves.append(((2, 1), (2, 1 + step)))
        if 2 + step < planes:
            moves.append(((3, 2), (3, 2 + step)))
        spread.append(send(t, *moves))
    t = call(collect, panel, e, first, second, behind, *into, t, *spread)
    return call(finish, struct((2 * half, height), BF16), t, swap(t), diag_inv)


def chain_solve(kept, given, factor, diag_inv):
    even = lax.rem(lax.axis_index("aux"), 2) == 0
    partial_fit = jnp.concatenate(
        [jnp.where(even, kept, given), jnp.where(even, given, kept)], axis=0
    )
    count, height = partial_fit.shape
    breadth = factor.shape[1]
    block_size = diag_inv.shape[1]
    rows_aux = lax.axis_size("aux")
    total = height * rows_aux
    members = rows_aux // SOLVE_BLOCKS
    my_row = lax.axis_index("aux")
    my_column = lax.axis_index("pair")
    my_block = my_row // members
    column_block = (my_column * breadth + jnp.arange(breadth, dtype=jnp.int32)) // block_size
    factor_low = jnp.where((column_block < my_block)[None, :], factor, 0.0)

    def own_columns(whole):
        return lax.dynamic_slice_in_dim(whole, my_column * breadth, breadth, 1)

    zero_block = jnp.zeros((count, block_size), jnp.float32)
    solved = jnp.zeros((count, total), jnp.float32)
    for k in range(SOLVE_BLOCKS):

        def on_group(current):
            return mm(partial_fit - mm_t(own_columns(current), factor_low), diag_inv)

        def off_group(current):
            return zero_block

        summand = lax.cond(my_block == k, on_group, off_group, solved)
        arrived = lax.psum(summand, AXES)
        solved = lax.dynamic_update_slice_in_dim(solved, arrived, k * block_size, 1)
    own_coef = jnp.zeros((count, height), jnp.float32)
    contrib = jnp.zeros((count, total), jnp.float32)
    for target in reversed(range(SOLVE_BLOCKS)):
        settled = solved[:, target * block_size : (target + 1) * block_size]
        if target < SOLVE_BLOCKS - 1:
            portion = contrib[:, target * block_size : (target + 1) * block_size]
            settled = settled - lax.psum(portion, AXES)

        def on_group(state):
            coef = mm_t(settled, diag_inv)
            if target > 0:
                fresh = lax.dynamic_update_slice_in_dim(
                    jnp.zeros((count, total), jnp.float32),
                    mm(coef, factor_low),
                    my_column * breadth,
                    1,
                )
            else:
                fresh = state[1]
            return (coef, fresh)

        def keep_state(state):
            return state

        own_coef, contrib = lax.cond(my_block == target, on_group, keep_state, (own_coef, contrib))
    return own_coef.astype(jnp.bfloat16)


def shards(integrals, densities, screen, factor, diag_inv):
    block_size = diag_inv.shape[1]
    chip_blocks = (
        lax.axis_size("aux") == 2 * SOLVE_BLOCKS
        and factor.shape[1] == block_size
        and lax.axis_size("pair") == SOLVE_BLOCKS
    )
    solve = chip_solve if chip_blocks else chain_solve
    held, kept, given = fit_partial(densities, integrals, screen)
    rounded = solve(kept, given, factor, diag_inv)
    return scatter_sum(coulomb_partial(rounded, held, screen))


def solution(mesh):
    in_specs = (
        P("aux", "pair"),
        P(None, "pair"),
        P("aux", "pair"),
        P("aux", "pair"),
        P("aux", None),
    )
    out_specs = P(None, ("pair", "aux"))
    return jax.shard_map(shards, mesh=mesh, in_specs=in_specs, out_specs=out_specs, check_vma=False)
```

time: 372 us -> 85.3 us (0.23)
  blocking collectives: 297 us -> 15.5 us
  starting transfers between devices: 0.01 us -> 24.8 us
  matrix products: 16.6 us -> 0 us
  between operations: 13.6 us -> 0.11 us
  Pallas kernels: 0 us -> 9.33 us
  waiting for transfers between devices: 34 us -> 30.2 us
    psum x7 -> x0, blocking collectives: 297 us -> none  [the longest x4 167 us: shards(): arrived = lax.psum(summand, ('aux', 'pair'))]
    reduce_scatter x1 -> x0, waiting for transfers between devices: 33.9 us -> none  [shards(): result = lax.psum_scatter(summand, 'aux', scatter_dimension=1, tiled=True)]
    ppermute x0 -> x26, waiting for transfers between devices: none -> 30.2 us  [the longest x19 24 us: send(): return lax.ppermute(value, AXES, pairs_of(complete(moves, IDLE)))]
    ppermute x0 -> x26, starting transfers between devices: none -> 24.8 us  [the longest x19 18.6 us: send(): return lax.ppermute(value, AXES, pairs_of(complete(moves, IDLE)))]
    dot_general x5 -> x0, matrix products: 16.6 us -> none  [the longest x1 9.1 us: shards(): summand = jnp.dot(rounded, masked, preferred_element_type=jnp.float32)]
    all_to_all x0 -> x1, blocking collectives: none -> 15.5 us  [scatter_sum(): arrived = lax.all_to_all(slabs, 'aux', 0, 0, tiled=True)]
    pallas_call x0 -> x12, Pallas kernels: none -> 9.33 us  [call(): pl.pallas_call(kernel, out_shape=outs, in_specs=specs or [VMEM] * len(ope...]
    broadcast_in_dim x3 -> x0, local copies, waits for them, and re-layouts: 4.46 us -> none  [the longest x1 3.83 us: shards(): jnp.repeat(jnp.repeat(screen, TILE, axis=0), TILE, axis=1)]
  transfers between devices with their start and end apart: 1 -> 26, of which waited for: 1 -> 18; matrix products, arithmetic and copies ran while one was open for 0% -> 0% of each run, Pallas kernels for 0% -> 5%
where the time goes in v3:
time: 85.3 us; the launch traced here: 85.1 us
  waiting for transfers between devices  30.2 us (35%)
  starting transfers between devices  24.8 us (29%)
  blocking collectives  15.5 us (18%)
  Pallas kernels  9.33 us (11%)
  local copies, waits for them, and re-layouts  4.43 us (5%)
    ppermute x19, waiting for transfers between devices, send(): return lax.ppermute(value, AXES, pairs_of(complete(moves, IDLE)))  24 us
    ppermute x19, starting transfers between devices, send(): return lax.ppermute(value, AXES, pairs_of(complete(moves, IDLE)))  18.6 us
    all_to_all x1, blocking collectives, scatter_sum(): arrived = lax.all_to_all(slabs, 'aux', 0, 0, tiled=True)  15.5 us
    pallas_call x12, Pallas kernels, call(): pl.pallas_call(kernel, out_shape=outs, in_specs=specs or [VMEM] * len(ope...  9.33 us
    ppermute x3, starting transfers between devices, chip_solve(): gathered.append(lax.ppermute(part, AXES, pairs_of(routes)))  4.94 us
    unnamed x12, local copies, waits for them, and re-layouts  4.43 us
    ppermute x3, waiting for transfers between devices, chip_solve(): gathered.append(lax.ppermute(part, AXES, pairs_of(routes)))  4.34 us
    ppermute x4, waiting for transfers between devices, swap(): lax.ppermute(value, 'aux', [(i, i ^ 1) for i in range(2 * SOLVE_BLOCKS)])  1.87 us
  transfers between devices with their start and end apart: 26, of which 18 were waited for; matrix products, arithmetic and copies ran while one was open for 0% of the time, Pallas kernels for 5%

profile of v3, /device:TPU:0, one launch (start us, length us, event | category | flops | bytes accessed | tf_op | source)
XLA Modules:
  0.0 85.1 jit_solution(11222137615956498614)
XLA Ops:
  0.0 0.5 collective-permute-start.5
  0.5 2.8 %copy-done = bf16[384,8192]{1,0:T(8,128)(2,1)S(1)} copy-done((bf16[384,8192]{1,0:T(8,128)(2,1)S(1)}, bf16[384,8192]{1,0:T(8,128)(2,1)}, u32[]{:S(2)}) %copy-start) | copy-done | bytes 6291480
  3.3 0.9 %copy-done.3 = bf16[16,8192]{1,0:T(8,128)(2,1)S(1)} copy-done((bf16[16,8192]{1,0:T(8,128)(2,1)S(1)}, bf16[16,8192]{1,0:T(8,128)(2,1)}, u32[]{:S(2)}) %copy-start.3) | copy-done | bytes 262168
  4.2 0.7 copy-done.4
  4.9 3.7 %fit.1 = (bf16[384,8192]{1,0:T(8,128)(2,1)S(1)}, f32[8,384]{1,0:T(8,128)S(1)}, f32[8,384]{1,0:T(8,128)S(1)}) custom-call(s32[3,64]{1,0:T(4,128)S(1)} %copy-done.4, bf16[16,8192]{1,0:T(8,128)(2,1)S(1)} %copy-done.3, bf16[384,8192]{1,0:T(8,128)(2,1)S(1)} %copy-done), custom_call_target="tpu_custom_call" | custom-call | tf_op jit(solution)/shard_map/fit/pallas_call | solution.py:28
  8.7 0.6 collective-permute-start
  9.2 0.8 collective-permute-done.mate
  10.1 4.9 %collective-permute-start.3 = (f32[8,768]{1,0:T(8,128)S(1)}, f32[8,768]{1,0:T(8,128)S(1)}, u32[]{:S(2)}, u32[]{:S(2)}) collective-permute-start(f32[8,768]{1,0:T(8,128)S(1)} %merge.1.f0), channel_id=1, source_target_pairs={{0,3},{4,7},{1,5},{5,1},{2,6},{6,2},{3,0},{7,4},{8,11},{12,15},{9,... | collective-permute-start | bytes 73736 | tf_op jit(solution)/shard_map/ppermute | solution.py:334
  15.4 1.4 %collective-permute-done.3.f3 = f32[8,768]{1,0:T(8,128)S(1)} collective-permute-done((f32[8,768]{1,0:T(8,128)S(1)}, f32[8,768]{1,0:T(8,128)S(1)}, u32[]{:S(2)}, u32[]{:S(2)}) %collective-permute-start.3) | collective-permute-done | bytes 24608 | tf_op jit(solution)/shard_map/ppermute | solution.py:334
  16.8 2.9 %collective-permute-done.2.f2 = f32[8,768]{1,0:T(8,128)S(1)} collective-permute-done((f32[8,768]{1,0:T(8,128)S(1)}, f32[8,768]{1,0:T(8,128)S(1)}, u32[]{:S(2)}, u32[]{:S(2)}) %collective-permute-start.2) | collective-permute-done | bytes 24608 | tf_op jit(solution)/shard_map/ppermute | solution.py:334
  20.1 2.0 %collective-permute-start.8 = (f32[8,768]{1,0:T(8,128)S(1)}, f32[8,768]{1,0:T(8,128)S(1)}, u32[]{:S(2)}, u32[]{:S(2)}) collective-permute-start(f32[8,768]{1,0:T(8,128)S(1)} %begin.1.e), channel_id=1, source_target_pairs={{0,24},{4,28},{1,5},{5,1},{2,6},{6,2},{3,7},{7,3},{8,12},{12,8},{9... | collective-permute-start | bytes 73736 | tf_op jit(solution)/shard_map/ppermute | solution.py:314
  22.2 4.5 %collective-permute-done.8.three = f32[8,768]{1,0:T(8,128)S(1)} collective-permute-done((f32[8,768]{1,0:T(8,128)S(1)}, f32[8,768]{1,0:T(8,128)S(1)}, u32[]{:S(2)}, u32[]{:S(2)}) %collective-permute-start.8) | collective-permute-done | bytes 24608 | tf_op jit(solution)/shard_map/ppermute | solution.py:314
  26.7 1.9 %collective-permute-done.7.two = f32[8,768]{1,0:T(8,128)S(1)} collective-permute-done((f32[8,768]{1,0:T(8,128)S(1)}, f32[8,768]{1,0:T(8,128)S(1)}, u32[]{:S(2)}, u32[]{:S(2)}) %collective-permute-start.7) | collective-permute-done | bytes 24608 | tf_op jit(solution)/shard_map/ppermute | solution.py:314
  28.9 0.4 after_zero.1.s
  29.3 7.4 %collective-permute-done.10.second.z2 = f32[8,768]{1,0:T(8,128)S(1)} collective-permute-done((f32[8,768]{1,0:T(8,128)S(1)}, f32[8,768]{1,0:T(8,128)S(1)}, u32[]{:S(2)}, u32[]{:S(2)}) %collective-permute-start.10) | collective-permute-done | bytes 24608 | tf_op jit(solution)/shard_map/ppermute | solution.py:314
  37.0 0.4 after_one.1.s
  37.5 1.1 %collective-permute-done.12.known = f32[8,768]{1,0:T(8,128)S(1)} collective-permute-done((f32[8,768]{1,0:T(8,128)S(1)}, f32[8,768]{1,0:T(8,128)S(1)}, u32[]{:S(2)}, u32[]{:S(2)}) %collective-permute-start.12) | collective-permute-done | bytes 24608 | tf_op jit(solution)/shard_map/ppermute | solution.py:314
  38.6 5.4 %collective-permute-done.11.behind.z3 = f32[8,768]{1,0:T(8,128)S(1)} collective-permute-done((f32[8,768]{1,0:T(8,128)S(1)}, f32[8,768]{1,0:T(8,128)S(1)}, u32[]{:S(2)}, u32[]{:S(2)}) %collective-permute-start.11) | collective-permute-done | bytes 24608 | tf_op jit(solution)/shard_map/ppermute | solution.py:314
  44.0 0.9 %turn.1 = (f32[8,768]{1,0:T(8,128)S(1)}, f32[8,768]{1,0:T(8,128)S(1)}) custom-call(f32[8,768]{1,0:T(8,128)S(1)} %collective-permute-done.12.known, f32[8,768]{1,0:T(8,128)S(1)} %collective-permute-done.11.behind.z3, f32[8,768]{1,0:T(8,128)S(1)} %begin.1.e, bf16[768,768]{1,0:T(8,128)(2,1)S(1)} %get-tuple-element.25.high.kt_high, ...), custom_call_target="tpu_custom_call" | custom-call | tf_op jit(solution)/shard_map/turn/pallas_call | solution.py:28
  44.9 0.5 collective-permute-start.15
  45.4 0.7 collective-permute-done.13.into
  47.6 0.7 collective-permute-done.16.into
  48.8 11.4 %collective-permute-start.21 = (f32[8,768]{1,0:T(8,128)S(1)}, f32[8,768]{1,0:T(8,128)S(1)}, u32[]{:S(2)}, u32[]{:S(2)}) collective-permute-start(f32[8,768]{1,0:T(8,128)S(1)} %get-tuple-element.34), channel_id=1, source_target_pairs={{0,19},{4,23},{1,5},{5,1},{2,6},{6,2},{3,11},{7,15},{8,3},{12,7},{... | collective-permute-start | bytes 73736 | tf_op jit(solution)/shard_map/ppermute | solution.py:314
  60.3 0.5 collective-permute-start.19
  60.8 2.8 %collective-permute-start.18 = (f32[8,768]{1,0:T(8,128)S(1)}, f32[8,768]{1,0:T(8,128)S(1)}, u32[]{:S(2)}, u32[]{:S(2)}) collective-permute-start(f32[8,768]{1,0:T(8,128)S(1)} %get-tuple-element.34), channel_id=1, source_target_pairs={{0,11},{4,15},{1,19},{5,23},{2,6},{6,2},{3,7},{7,3},{8,0},{12,4},{... | collective-permute-start | bytes 73736 | tf_op jit(solution)/shard_map/ppermute | solution.py:314
  63.6 0.5 collective-permute-start.23
  64.2 0.9 %collective-permute-done.18.i0 = f32[8,768]{1,0:T(8,128)S(1)} collective-permute-done((f32[8,768]{1,0:T(8,128)S(1)}, f32[8,768]{1,0:T(8,128)S(1)}, u32[]{:S(2)}, u32[]{:S(2)}) %collective-permute-start.18) | collective-permute-done | bytes 24608 | tf_op jit(solution)/shard_map/ppermute | solution.py:314
  65.6 1.0 %collective-permute-done.25.mate = f32[8,768]{1,0:T(8,128)S(1)} collective-permute-done((f32[8,768]{1,0:T(8,128)S(1)}, f32[8,768]{1,0:T(8,128)S(1)}, u32[]{:S(2)}, u32[]{:S(2)}) %collective-permute-start.25) | collective-permute-done | bytes 24608 | tf_op jit(solution)/shard_map/ppermute | solution.py:317
  66.6 0.4 finish.1.rounded
  67.1 1.8 %coulomb.1 = bf16[8,16,1024]{2,1,0:T(8,128)(2,1)S(1)} custom-call(s32[3,64]{1,0:T(4,128)S(1)} %copy-done.5, bf16[16,384]{1,0:T(8,128)(2,1)S(1)} %finish.1.rounded, bf16[384,8192]{1,0:T(8,128)(2,1)S(1)} %get-tuple-element.36.held), custom_call_target="tpu_custom_call" | custom-call | tf_op jit(solution)/shard_map/coulomb/pallas_call | solution.py:28
  68.9 15.5 %all_to_all.5 = bf16[8,16,1024]{2,1,0:T(8,128)(2,1)S(1)} all-to-all(bf16[8,16,1024]{2,1,0:T(8,128)(2,1)S(1)} %coulomb.1), channel_id=1, replica_groups=mesh['aux'=8,'pair'=4] {'aux'}, dimensions={0} | all-to-all | bytes 524288 | tf_op jit(solution)/shard_map/all_to_all | solution.py:145
  84.4 0.7 convert_reduce_fusion
  (46 shorter events, 4.1 us)
Async XLA Ops:
  0.0 15.0 %collective-permute-start.5 = (f32[384,768]{1,0:T(8,128)}, f32[384,768]{1,0:T(8,128)S(1)}, u32[]{:S(2)}, u32[]{:S(2)}) collective-permute-start(f32[384,768]{1,0:T(8,128)} %own_fac.1), channel_id=1, source_target_pairs={{0,4},{4,0},{8,12},{12,8},{16,20},{20,16},{24,28},{28,24},{1,5},{5... | collective-permute-start | bytes 3538952 | tf_op jit(solution)/shard_map/ppermute | solution.py:317
  0.5 14.5 %collective-permute-start.4 = (f32[384,768]{1,0:T(8,128)}, f32[384,768]{1,0:T(8,128)S(1)}, u32[]{:S(2)}, u32[]{:S(2)}) collective-permute-start(f32[384,768]{1,0:T(8,128)} %inv.1), channel_id=1, source_target_pairs={{0,4},{4,0},{8,12},{12,8},{16,20},{20,16},{24,28},{28,24},{1,5},{5... | collective-permute-start | bytes 3538952 | tf_op jit(solution)/shard_map/ppermute | solution.py:317
  0.5 2.8 %copy-start = (bf16[384,8192]{1,0:T(8,128)(2,1)S(1)}, bf16[384,8192]{1,0:T(8,128)(2,1)}, u32[]{:S(2)}) copy-start(bf16[384,8192]{1,0:T(8,128)(2,1)} %integrals.1) | copy-start | bytes 18874372
  3.3 0.9 %copy-start.3 = (bf16[16,8192]{1,0:T(8,128)(2,1)S(1)}, bf16[16,8192]{1,0:T(8,128)(2,1)}, u32[]{:S(2)}) copy-start(bf16[16,8192]{1,0:T(8,128)(2,1)} %densities_in.1) | copy-start | bytes 786436
  4.2 0.7 copy-start.4
  4.9 10.1 %copy-start.1 = (f32[384,768]{1,0:T(8,128)S(1)}, f32[384,768]{1,0:T(8,128)}, u32[]{:S(2)}) copy-start(f32[384,768]{1,0:T(8,128)} %inv.1) | copy-start | bytes 3538948
  4.9 10.1 %copy-start.2 = (f32[384,768]{1,0:T(8,128)S(1)}, f32[384,768]{1,0:T(8,128)}, u32[]{:S(2)}) copy-start(f32[384,768]{1,0:T(8,128)} %own_fac.1) | copy-start | bytes 3538948
  8.7 1.4 %collective-permute-start = (f32[8,384]{1,0:T(8,128)S(1)}, f32[8,384]{1,0:T(8,128)S(1)}, u32[]{:S(2)}, u32[]{:S(2)}) collective-permute-start(f32[8,384]{1,0:T(8,128)S(1)} %get-tuple-element.22), channel_id=1, source_target_pairs={{0,4},{4,0},{8,12},{12,8},{16,20},{20,16},{24,28},{28,24},{1,5},{5... | collective-permute-start | bytes 36872 | tf_op jit(solution)/shard_map/ppermute | solution.py:317
  10.1 6.7 %collective-permute-start.3 = (f32[8,768]{1,0:T(8,128)S(1)}, f32[8,768]{1,0:T(8,128)S(1)}, u32[]{:S(2)}, u32[]{:S(2)}) collective-permute-start(f32[8,768]{1,0:T(8,128)S(1)} %merge.1.f0), channel_id=1, source_target_pairs={{0,3},{4,7},{1,5},{5,1},{2,6},{6,2},{3,0},{7,4},{8,11},{12,15},{9,... | collective-permute-start | bytes 73736 | tf_op jit(solution)/shard_map/ppermute | solution.py:334
  15.0 4.7 %collective-permute-start.2 = (f32[8,768]{1,0:T(8,128)S(1)}, f32[8,768]{1,0:T(8,128)S(1)}, u32[]{:S(2)}, u32[]{:S(2)}) collective-permute-start(f32[8,768]{1,0:T(8,128)S(1)} %merge.1.f0), channel_id=1, source_target_pairs={{0,2},{4,6},{1,5},{5,1},{2,0},{6,4},{3,7},{7,3},{8,10},{12,14},{9,... | collective-permute-start | bytes 73736 | tf_op jit(solution)/shard_map/ppermute | solution.py:334
  15.0 4.7 %collective-permute-start.1 = (f32[8,768]{1,0:T(8,128)S(1)}, f32[8,768]{1,0:T(8,128)S(1)}, u32[]{:S(2)}, u32[]{:S(2)}) collective-permute-start(f32[8,768]{1,0:T(8,128)S(1)} %merge.1.f0), channel_id=1, source_target_pairs={{0,1},{4,5},{1,0},{5,4},{2,6},{6,2},{3,7},{7,3},{8,9},{12,13},{9,8... | collective-permute-start | bytes 73736 | tf_op jit(solution)/shard_map/ppermute | solution.py:334
  20.1 6.5 %collective-permute-start.8 = (f32[8,768]{1,0:T(8,128)S(1)}, f32[8,768]{1,0:T(8,128)S(1)}, u32[]{:S(2)}, u32[]{:S(2)}) collective-permute-start(f32[8,768]{1,0:T(8,128)S(1)} %begin.1.e), channel_id=1, source_target_pairs={{0,24},{4,28},{1,5},{5,1},{2,6},{6,2},{3,7},{7,3},{8,12},{12,8},{9... | collective-permute-start | bytes 73736 | tf_op jit(solution)/shard_map/ppermute | solution.py:314
  22.1 6.5 %collective-permute-start.7 = (f32[8,768]{1,0:T(8,128)S(1)}, f32[8,768]{1,0:T(8,128)S(1)}, u32[]{:S(2)}, u32[]{:S(2)}) collective-permute-start(f32[8,768]{1,0:T(8,128)S(1)} %begin.1.e), channel_id=1, source_target_pairs={{0,16},{4,20},{1,5},{5,1},{2,6},{6,2},{3,7},{7,3},{8,12},{12,8},{9... | collective-permute-start | bytes 73736 | tf_op jit(solution)/shard_map/ppermute | solution.py:314
  22.1 6.8 %collective-permute-start.6 = (f32[8,768]{1,0:T(8,128)S(1)}, f32[8,768]{1,0:T(8,128)S(1)}, u32[]{:S(2)}, u32[]{:S(2)}) collective-permute-start(f32[8,768]{1,0:T(8,128)S(1)} %begin.1.e), channel_id=1, source_target_pairs={{0,8},{4,12},{1,5},{5,1},{2,6},{6,2},{3,7},{7,3},{8,11},{12,15},{9... | collective-permute-start | bytes 73736 | tf_op jit(solution)/shard_map/ppermute | solution.py:314
  29.3 7.4 %collective-permute-start.10 = (f32[8,768]{1,0:T(8,128)S(1)}, f32[8,768]{1,0:T(8,128)S(1)}, u32[]{:S(2)}, u32[]{:S(2)}) collective-permute-start(f32[8,768]{1,0:T(8,128)S(1)} %after_zero.1.s), channel_id=1, source_target_pairs={{0,2},{4,6},{1,5},{5,1},{2,27},{6,31},{3,7},{7,3},{8,25},{12,29},{... | collective-permute-start | bytes 73736 | tf_op jit(solution)/shard_map/ppermute | solution.py:314
  29.3 7.7 %collective-permute-start.9 = (f32[8,768]{1,0:T(8,128)S(1)}, f32[8,768]{1,0:T(8,128)S(1)}, u32[]{:S(2)}, u32[]{:S(2)}) collective-permute-start(f32[8,768]{1,0:T(8,128)S(1)} %after_zero.1.s), channel_id=1, source_target_pairs={{0,1},{4,5},{1,27},{5,31},{2,6},{6,2},{3,7},{7,3},{8,17},{12,21},{... | collective-permute-start | bytes 73736 | tf_op jit(solution)/shard_map/ppermute | solution.py:314
  37.4 1.2 %collective-permute-start.12 = (f32[8,768]{1,0:T(8,128)S(1)}, f32[8,768]{1,0:T(8,128)S(1)}, u32[]{:S(2)}, u32[]{:S(2)}) collective-permute-start(f32[8,768]{1,0:T(8,128)S(1)} %after_one.1.s), channel_id=1, source_target_pairs={{0,4},{4,0},{1,5},{5,1},{2,6},{6,2},{3,7},{7,3},{8,12},{12,8},{9,1... | collective-permute-start | bytes 73736 | tf_op jit(solution)/shard_map/ppermute | solution.py:314
  37.4 6.6 %collective-permute-start.11 = (f32[8,768]{1,0:T(8,128)S(1)}, f32[8,768]{1,0:T(8,128)S(1)}, u32[]{:S(2)}, u32[]{:S(2)}) collective-permute-start(f32[8,768]{1,0:T(8,128)S(1)} %after_one.1.s), channel_id=1, source_target_pairs={{0,3},{4,7},{1,5},{5,1},{2,6},{6,2},{3,19},{7,23},{8,12},{12,8},{9... | collective-permute-start | bytes 73736 | tf_op jit(solution)/shard_map/ppermute | solution.py:314
  44.9 1.2 %collective-permute-start.13 = (f32[8,768]{1,0:T(8,128)S(1)}, f32[8,768]{1,0:T(8,128)S(1)}, u32[]{:S(2)}, u32[]{:S(2)}) collective-permute-start(f32[8,768]{1,0:T(8,128)S(1)} %get-tuple-element.29), channel_id=1, source_target_pairs={{0,4},{4,0},{1,5},{5,1},{2,6},{6,2},{3,7},{7,3},{8,12},{12,8},{9,1... | collective-permute-start | bytes 73736 | tf_op jit(solution)/shard_map/ppermute | solution.py:314
  44.9 1.4 %collective-permute-start.15 = (f32[8,768]{1,0:T(8,128)S(1)}, f32[8,768]{1,0:T(8,128)S(1)}, u32[]{:S(2)}, u32[]{:S(2)}) collective-permute-start(f32[8,768]{1,0:T(8,128)S(1)} %get-tuple-element.30.t), channel_id=1, source_target_pairs={{0,4},{4,0},{1,5},{5,1},{2,6},{6,2},{3,7},{7,3},{8,12},{12,8},{9,1... | collective-permute-start | bytes 73736 | tf_op jit(solution)/shard_map/ppermute | solution.py:314
  45.4 1.2 %collective-permute-start.14 = (f32[8,768]{1,0:T(8,128)S(1)}, f32[8,768]{1,0:T(8,128)S(1)}, u32[]{:S(2)}, u32[]{:S(2)}) collective-permute-start(f32[8,768]{1,0:T(8,128)S(1)} %get-tuple-element.30.t), channel_id=1, source_target_pairs={{0,4},{4,0},{1,5},{5,1},{2,6},{6,2},{3,7},{7,3},{8,12},{12,8},{9,1... | collective-permute-start | bytes 73736 | tf_op jit(solution)/shard_map/ppermute | solution.py:314
  47.0 1.2 %collective-permute-start.16 = (f32[8,768]{1,0:T(8,128)S(1)}, f32[8,768]{1,0:T(8,128)S(1)}, u32[]{:S(2)}, u32[]{:S(2)}) collective-permute-start(f32[8,768]{1,0:T(8,128)S(1)} %get-tuple-element.31), channel_id=1, source_target_pairs={{0,4},{4,0},{1,5},{5,1},{2,6},{6,2},{3,7},{7,3},{8,11},{12,15},{9,... | collective-permute-start | bytes 73736 | tf_op jit(solution)/shard_map/ppermute | solution.py:314
  47.2 1.2 %collective-permute-start.17 = (f32[8,768]{1,0:T(8,128)S(1)}, f32[8,768]{1,0:T(8,128)S(1)}, u32[]{:S(2)}, u32[]{:S(2)}) collective-permute-start(f32[8,768]{1,0:T(8,128)S(1)} %get-tuple-element.32), channel_id=1, source_target_pairs={{0,4},{4,0},{1,5},{5,1},{2,6},{6,2},{3,7},{7,3},{8,11},{12,15},{9,... | collective-permute-start | bytes 73736 | tf_op jit(solution)/shard_map/ppermute | solution.py:314
  48.8 18.2 %copy-start.5 = (s32[3,64]{1,0:T(4,128)S(1)}, s32[3,64]{1,0:T(4,128)}, u32[]{:S(2)}) copy-start(s32[3,64]{1,0:T(4,128)} %screen.1) | copy-start | bytes 2308
  48.8 14.8 %collective-permute-start.21 = (f32[8,768]{1,0:T(8,128)S(1)}, f32[8,768]{1,0:T(8,128)S(1)}, u32[]{:S(2)}, u32[]{:S(2)}) collective-permute-start(f32[8,768]{1,0:T(8,128)S(1)} %get-tuple-element.34), channel_id=1, source_target_pairs={{0,19},{4,23},{1,5},{5,1},{2,6},{6,2},{3,11},{7,15},{8,3},{12,7},{... | collective-permute-start | bytes 73736 | tf_op jit(solution)/shard_map/ppermute | solution.py:314
  60.3 3.8 %collective-permute-start.20 = (f32[8,768]{1,0:T(8,128)S(1)}, f32[8,768]{1,0:T(8,128)S(1)}, u32[]{:S(2)}, u32[]{:S(2)}) collective-permute-start(f32[8,768]{1,0:T(8,128)S(1)} %get-tuple-element.34), channel_id=1, source_target_pairs={{0,4},{4,0},{1,5},{5,1},{2,11},{6,15},{3,19},{7,23},{8,2},{12,6},{... | collective-permute-start | bytes 73736 | tf_op jit(solution)/shard_map/ppermute | solution.py:314
  60.3 3.9 %collective-permute-start.19 = (f32[8,768]{1,0:T(8,128)S(1)}, f32[8,768]{1,0:T(8,128)S(1)}, u32[]{:S(2)}, u32[]{:S(2)}) collective-permute-start(f32[8,768]{1,0:T(8,128)S(1)} %get-tuple-element.34), channel_id=1, source_target_pairs={{0,4},{4,0},{1,11},{5,15},{2,19},{6,23},{3,7},{7,3},{8,1},{12,5},{... | collective-permute-start | bytes 73736 | tf_op jit(solution)/shard_map/ppermute | solution.py:314
  60.8 4.3 %collective-permute-start.18 = (f32[8,768]{1,0:T(8,128)S(1)}, f32[8,768]{1,0:T(8,128)S(1)}, u32[]{:S(2)}, u32[]{:S(2)}) collective-permute-start(f32[8,768]{1,0:T(8,128)S(1)} %get-tuple-element.34), channel_id=1, source_target_pairs={{0,11},{4,15},{1,19},{5,23},{2,6},{6,2},{3,7},{7,3},{8,0},{12,4},{... | collective-permute-start | bytes 73736 | tf_op jit(solution)/shard_map/ppermute | solution.py:314
  63.6 1.5 %collective-permute-start.24 = (f32[8,768]{1,0:T(8,128)S(1)}, f32[8,768]{1,0:T(8,128)S(1)}, u32[]{:S(2)}, u32[]{:S(2)}) collective-permute-start(f32[8,768]{1,0:T(8,128)S(1)} %get-tuple-element.35.t), channel_id=1, source_target_pairs={{0,4},{4,0},{1,5},{5,1},{2,6},{6,2},{3,7},{7,3},{8,11},{12,15},{9,... | collective-permute-start | bytes 73736 | tf_op jit(solution)/shard_map/ppermute | solution.py:314
  63.6 1.5 %collective-permute-start.23 = (f32[8,768]{1,0:T(8,128)S(1)}, f32[8,768]{1,0:T(8,128)S(1)}, u32[]{:S(2)}, u32[]{:S(2)}) collective-permute-start(f32[8,768]{1,0:T(8,128)S(1)} %get-tuple-element.35.t), channel_id=1, source_target_pairs={{0,4},{4,0},{1,5},{5,1},{2,6},{6,2},{3,7},{7,3},{8,10},{12,14},{9,... | collective-permute-start | bytes 73736 | tf_op jit(solution)/shard_map/ppermute | solution.py:314
  64.1 1.2 %collective-permute-start.22 = (f32[8,768]{1,0:T(8,128)S(1)}, f32[8,768]{1,0:T(8,128)S(1)}, u32[]{:S(2)}, u32[]{:S(2)}) collective-permute-start(f32[8,768]{1,0:T(8,128)S(1)} %get-tuple-element.35.t), channel_id=1, source_target_pairs={{0,4},{4,0},{1,5},{5,1},{2,6},{6,2},{3,26},{7,30},{8,9},{12,13},{9... | collective-permute-start | bytes 73736 | tf_op jit(solution)/shard_map/ppermute | solution.py:314
  65.3 1.3 %collective-permute-start.25 = (f32[8,768]{1,0:T(8,128)S(1)}, f32[8,768]{1,0:T(8,128)S(1)}, u32[]{:S(2)}, u32[]{:S(2)}) collective-permute-start(f32[8,768]{1,0:T(8,128)S(1)} %collect.1.own), channel_id=1, source_target_pairs={{0,4},{4,0},{8,12},{12,8},{16,20},{20,16},{24,28},{28,24},{1,5},{5... | collective-permute-start | bytes 73736 | tf_op jit(solution)/shard_map/ppermute | solution.py:317

commit v4 on v3

--- a/solution.py
+++ b/solution.py
@@ -32,7 +32,6 @@
         out_specs=jax.tree.map(lambda _: VMEM, outs),
         scratch_shapes=scratch,
         compiler_params=pltpu.CompilerParams(vmem_limit_bytes=limit * MIB),
-        name=kernel.__name__,
     )(*operands)
 
 
@@ -44,7 +43,9 @@
     return lax.div(lax.axis_index("aux"), 2)
 
 
-def fit(screen_in, densities_in, integrals, held, kept, given, screen, densities, total, arrived):
+def fit(
+    screen_in, densities_in, integrals, left, right, kept, given, screen, densities, total, arrived
+):
     height, width = integrals.shape
     pieces = arrived.shape[0] - 2
     chunk = width // pieces
@@ -53,14 +54,17 @@
         pltpu.make_async_copy(screen_in, screen, arrived.at[pieces]),
         pltpu.make_async_copy(densities_in, densities, arrived.at[pieces + 1]),
     ]
-    copies = [
-        pltpu.make_async_copy(
-            integrals.at[:, j * chunk : (j + 1) * chunk],
-            held.at[:, j * chunk : (j + 1) * chunk],
-            arrived.at[j],
+    copies = []
+    held = []
+    for j in range(pieces):
+        ref = left if 2 * j < pieces else right
+        start = j * chunk if ref is left else j * chunk - width // 2
+        held.append(ref.at[:, start : start + chunk])
+        copies.append(
+            pltpu.make_async_copy(
+                integrals.at[:, j * chunk : (j + 1) * chunk], held[j], arrived.at[j]
+            )
         )
-        for j in range(pieces)
-    ]
     for copy in small + copies:
         copy.start()
     total[...] = jnp.zeros_like(total)
@@ -68,7 +72,6 @@
         copy.wait()
     for j in range(pieces):
         copies[j].wait()
-        columns = slice(j * chunk, (j + 1) * chunk)
         for i in range(height // TILE):
             rows = slice(i * TILE, (i + 1) * TILE)
             masked = jnp.concatenate(
@@ -83,7 +86,7 @@
                 axis=1,
             )
             total[rows, :] += lax.dot_general(
-                held[rows, columns], masked, NT, preferred_element_type=F32
+                held[j][rows, :], masked, NT, preferred_element_type=F32
             )
     done = total[...].T
     even = side_of() == 0
@@ -98,10 +101,8 @@
     half = struct((count // 2, height))
     return call(
         fit,
-        [struct(integrals.shape, BF16), half, half],
-        screen,
-        densities,
-        integrals,
+        [struct((height, width // 2), BF16)] * 2 + [half, half],
+        *(pltpu.with_memory_space_constraint(x, pltpu.HBM) for x in (screen, densities, integrals)),
         specs=[HBM] * 3,
         scratch=[
             pltpu.SMEM(screen.shape, jnp.int32),
@@ -112,9 +113,9 @@
     )
 
 
-def coulomb(screen, rounded, held, out):
+def coulomb(screen, rounded, left, right, out):
     members, _, chunk = out.shape
-    height = held.shape[0]
+    height, width = left.shape
     for m in range(members):
         for t in range(m * chunk // TILE, (m + 1) * chunk // TILE):
             masked = jnp.concatenate(
@@ -128,17 +129,19 @@
                 ],
                 axis=1,
             )
+            held = left if t * TILE < width else right
+            start = t * TILE if held is left else t * TILE - width
             part = jnp.dot(
-                masked, held[:, t * TILE : (t + 1) * TILE], preferred_element_type=F32
+                masked, held[:, start : start + TILE], preferred_element_type=F32
             )
             first = t * TILE - m * chunk
             out[m, :, first : first + TILE] = part.astype(out.dtype)
 
 
-def coulomb_partial(rounded, held, screen):
+def coulomb_partial(rounded, left, right, screen):
     members = lax.axis_size("aux")
-    out = struct((members, rounded.shape[0], held.shape[1] // members), BF16)
-    return call(coulomb, out, screen, rounded, held, specs=[SMEM, VMEM, VMEM])
+    out = struct((members, rounded.shape[0], 2 * left.shape[1] // members), BF16)
+    return call(coulomb, out, screen, rounded, left, right, specs=[SMEM, VMEM, VMEM, VMEM])
 
 
 def scatter_sum(slabs):
@@ -280,19 +283,13 @@
     return lax.dot_general(a, b, NT, precision=HIGHEST, preferred_element_type=F32)
 
 
-def complete(moves, idle):
+def complete(moves):
+    to = {}
+    for source, target, *via in moves:
+        chain = [source, target, *via]
+        to.update(zip(chain, chain[1:] + chain[:1]))
     chips = [(k, plane) for k in range(SOLVE_BLOCKS) for plane in range(SOLVE_BLOCKS)]
-    used = {chip for move in moves for chip in move}
-    spare = [chip for chip in idle if chip not in used] + [
-        chip for chip in reversed(chips) if chip not in used and chip not in idle
-    ]
-    to = {}
-    for (source, target), via in zip(moves, spare):
-        to.update({source: target, target: via, via: source})
     return [(chip, to.get(chip, chip)) for chip in chips]
-
-
-IDLE = [(1, 3), (2, 3), (3, 3), (0, 3), (1, 2), (2, 2), (0, 2), (1, 1), (0, 1)]
 
 
 def chip_solve(kept, given, factor, diag_inv):
@@ -311,7 +308,7 @@
         return pairs
 
     def send(value, *moves):
-        return lax.ppermute(value, AXES, pairs_of(complete(moves, IDLE)))
+        return lax.ppermute(value, AXES, pairs_of(complete(moves)))
 
     def swap(value):
         return lax.ppermute(value, "aux", [(i, i ^ 1) for i in range(2 * SOLVE_BLOCKS)])
@@ -323,33 +320,32 @@
     )
     part = call(merge, panel, kept, swap(given))
     home = [max(k - 1, 0) for k in range(SOLVE_BLOCKS)]
-    gathered = []
-    for step in range(1, planes):
-        routes = []
-        for k in range(SOLVE_BLOCKS):
-            far = (home[k] + step) % planes
-            for plane in range(planes):
-                to = {home[k]: far, far: home[k]}.get(plane, plane)
-                routes.append(((k, plane), (k, to)))
-        gathered.append(lax.ppermute(part, AXES, pairs_of(routes)))
+    gathered = [
+        send(
+            part,
+            *(((k, (home[k] + step) % planes), (k, home[k])) for k in range(SOLVE_BLOCKS)),
+        )
+        for step in range(1, planes)
+    ]
     e = call(begin, panel, part, *gathered, inv_high, inv_low)
     reach = [send(e, ((0, 0), (k, 0))) for k in range(1, SOLVE_BLOCKS)]
     one = call(after_zero, panel, *reach, e, kt_high, kt_low)
-    first = send(one, ((1, 0), (2, 1)), ((3, 0), (3, 1)), ((0, 0), (0, 1)))
+    first = send(one, ((1, 0), (2, 1), (1, 3)), ((3, 0), (3, 1), (3, 3)), ((0, 0), (0, 1)))
     second = send(one, ((1, 0), (3, 1)), ((2, 0), (2, 1)), ((0, 0), (0, 2)))
     two = call(after_one, panel, first, second, e, kt_high, kt_low)
-    behind = send(two, ((3, 1), (3, 2)), ((0, 0), (0, 3)))
+    behind = send(two, ((3, 1), (3, 2), (2, 3)), ((0, 0), (0, 3)))
     known = send(two, ((2, 1), (3, 2)))
     t, back = call(turn, [panel] * 2, known, behind, e, kt_high, kt_low, k_high, k_low)
     into = send(back, ((3, 2), (2, 1)))
     near = send(t, ((3, 2), (3, 1)))
     far = send(t, ((3, 2), (3, 0)))
     t, back, mixed = call(back_two, [panel] * 3, into, near, far, t, two, k_high, k_low)
-    into = send(back, ((2, 1), (1, 0)), ((3, 0), (2, 0)))
+    into = send(back, ((2, 1), (1, 0), (2, 3)), ((3, 0), (2, 0), (3, 3)))
     other = send(mixed, ((3, 1), (1, 0)), ((2, 1), (2, 0)))
     t, back = call(back_one, [panel] * 2, into, other, t, one, k_high, k_low)
+    vias = [(2, 2), (2, 3), (3, 3), (3, 1)]
     into = [
-        send(back, ((1, 0), (0, plane)), ((2, 0), (0, (plane + 1) % planes)))
+        send(back, ((1, 0), (0, plane)), ((2, 0), (0, (plane + 1) % planes), vias[plane]))
         for plane in range(planes)
     ]
     spread = []
@@ -433,9 +429,9 @@
         and lax.axis_size("pair") == SOLVE_BLOCKS
     )
     solve = chip_solve if chip_blocks else chain_solve
-    held, kept, given = fit_partial(densities, integrals, screen)
+    left, right, kept, given = fit_partial(densities, integrals, screen)
     rounded = solve(kept, given, factor, diag_inv)
-    return scatter_sum(coulomb_partial(rounded, held, screen))
+    return scatter_sum(coulomb_partial(rounded, left, right, screen))
 
 
 def solution(mesh):

time: 85.3 us -> 69.3 us (0.81)
  starting transfers between devices: 24.8 us -> 18.8 us
  waiting for transfers between devices: 30.2 us -> 25.7 us
  local copies, waits for them, and re-layouts: 4.43 us -> 0.01 us
  blocking collectives: 15.5 us -> 13.9 us
    ppermute x22, starting transfers between devices: 23.5 us -> 17.6 us  [send(): return lax.ppermute(value, AXES, pairs_of(complete(moves)))]
    ppermute x22, waiting for transfers between devices: 28.3 us -> 23.6 us  [send(): return lax.ppermute(value, AXES, pairs_of(complete(moves)))]
    unnamed x12 -> x6, local copies, waits for them, and re-layouts: 4.43 us -> 0.01 us
    all_to_all x1, blocking collectives: 15.5 us -> 13.9 us  [scatter_sum(): arrived = lax.all_to_all(slabs, 'aux', 0, 0, tiled=True)]
  transfers between devices with their start and end apart: 26 -> 26, of which waited for: 18 -> 16; matrix products, arithmetic and copies ran while one was open for 0% -> 0% of each run, Pallas kernels for 5% -> 7%
where the time goes in v4:
time: 69.3 us; the launch traced here: 69.1 us
  waiting for transfers between devices  25.7 us (37%)
  starting transfers between devices  18.8 us (27%)
  blocking collectives  13.9 us (20%)
  Pallas kernels  9.93 us (14%)
    ppermute x22, waiting for transfers between devices, send(): return lax.ppermute(value, AXES, pairs_of(complete(moves)))  23.6 us
    ppermute x22, starting transfers between devices, send(): return lax.ppermute(value, AXES, pairs_of(complete(moves)))  17.6 us
    all_to_all x1, blocking collectives, scatter_sum(): arrived = lax.all_to_all(slabs, 'aux', 0, 0, tiled=True)  13.9 us
    pallas_call x12, Pallas kernels, call(): pl.pallas_call(kernel, out_shape=outs, in_specs=specs or [VMEM] * len(ope...  9.93 us
    ppermute x4, waiting for transfers between devices, swap(): lax.ppermute(value, 'aux', [(i, i ^ 1) for i in range(2 * SOLVE_BLOCKS)])  2.02 us
  transfers between devices with their start and end apart: 26, of which 16 were waited for; matrix products, arithmetic and copies ran while one was open for 0% of the time, Pallas kernels for 7%

profile of v4, /device:TPU:0, one launch (start us, length us, event | category | flops | bytes accessed | tf_op | source)
XLA Modules:
  0.0 69.1 jit_solution(11657879571260093092)
XLA Ops:
  0.0 0.5 collective-permute-start.5
  0.6 4.3 %shard_map.55 = (bf16[384,4096]{1,0:T(8,128)(2,1)S(1)}, bf16[384,4096]{1,0:T(8,128)(2,1)S(1)}, f32[8,384]{1,0:T(8,128)S(1)}, f32[8,384]{1,0:T(8,128)S(1)}) custom-call(s32[3,64]{1,0:T(4,128)} %screen.1, bf16[16,8192]{1,0:T(8,128)(2,1)} %densities_in.1, bf16[384,8192]{1,0:T(8,128)(2,1)} %integrals.1), custom_call_target="tpu_custom_call" | custom-call | tf_op jit(solution)/shard_map/pallas_call | solution.py:28
  4.9 0.6 collective-permute-start
  5.4 0.8 %collective-permute-done.mate = f32[8,384]{1,0:T(8,128)S(1)} collective-permute-done((f32[8,384]{1,0:T(8,128)S(1)}, f32[8,384]{1,0:T(8,128)S(1)}, u32[]{:S(2)}, u32[]{:S(2)}) %collective-permute-start) | collective-permute-done | bytes 12320 | tf_op jit(solution)/shard_map/ppermute | solution.py:314
  6.3 4.9 %collective-permute-start.3 = (f32[8,768]{1,0:T(8,128)S(1)}, f32[8,768]{1,0:T(8,128)S(1)}, u32[]{:S(2)}, u32[]{:S(2)}) collective-permute-start(f32[8,768]{1,0:T(8,128)S(1)} %shard_map.56.f0), channel_id=1, source_target_pairs={{0,3},{4,7},{1,5},{5,1},{2,6},{6,2},{3,0},{7,4},{8,11},{12,15},{9,... | collective-permute-start | bytes 73736 | tf_op jit(solution)/shard_map/ppermute | solution.py:311
  11.6 1.4 %collective-permute-done.3.f3 = f32[8,768]{1,0:T(8,128)S(1)} collective-permute-done((f32[8,768]{1,0:T(8,128)S(1)}, f32[8,768]{1,0:T(8,128)S(1)}, u32[]{:S(2)}, u32[]{:S(2)}) %collective-permute-start.3) | collective-permute-done | bytes 24608 | tf_op jit(solution)/shard_map/ppermute | solution.py:311
  13.0 2.9 %collective-permute-done.2.f2 = f32[8,768]{1,0:T(8,128)S(1)} collective-permute-done((f32[8,768]{1,0:T(8,128)S(1)}, f32[8,768]{1,0:T(8,128)S(1)}, u32[]{:S(2)}, u32[]{:S(2)}) %collective-permute-start.2) | collective-permute-done | bytes 24608 | tf_op jit(solution)/shard_map/ppermute | solution.py:311
  15.9 0.4 shard_map.58.e
  16.3 2.0 %collective-permute-start.8 = (f32[8,768]{1,0:T(8,128)S(1)}, f32[8,768]{1,0:T(8,128)S(1)}, u32[]{:S(2)}, u32[]{:S(2)}) collective-permute-start(f32[8,768]{1,0:T(8,128)S(1)} %shard_map.58.e), channel_id=1, source_target_pairs={{0,24},{4,28},{1,5},{5,1},{2,6},{6,2},{3,7},{7,3},{8,12},{12,8},{9... | collective-permute-start | bytes 73736 | tf_op jit(solution)/shard_map/ppermute | solution.py:311
  18.4 2.7 %collective-permute-done.8.three = f32[8,768]{1,0:T(8,128)S(1)} collective-permute-done((f32[8,768]{1,0:T(8,128)S(1)}, f32[8,768]{1,0:T(8,128)S(1)}, u32[]{:S(2)}, u32[]{:S(2)}) %collective-permute-start.8) | collective-permute-done | bytes 24608 | tf_op jit(solution)/shard_map/ppermute | solution.py:311
  21.1 1.0 %collective-permute-done.7.two = f32[8,768]{1,0:T(8,128)S(1)} collective-permute-done((f32[8,768]{1,0:T(8,128)S(1)}, f32[8,768]{1,0:T(8,128)S(1)}, u32[]{:S(2)}, u32[]{:S(2)}) %collective-permute-start.7) | collective-permute-done | bytes 24608 | tf_op jit(solution)/shard_map/ppermute | solution.py:311
  22.1 0.4 shard_map.59.s
  22.6 4.7 %collective-permute-done.10.second.z2 = f32[8,768]{1,0:T(8,128)S(1)} collective-permute-done((f32[8,768]{1,0:T(8,128)S(1)}, f32[8,768]{1,0:T(8,128)S(1)}, u32[]{:S(2)}, u32[]{:S(2)}) %collective-permute-start.10) | collective-permute-done | bytes 24608 | tf_op jit(solution)/shard_map/ppermute | solution.py:311
  27.3 0.4 shard_map.60.s
  27.8 1.1 %collective-permute-done.12.known = f32[8,768]{1,0:T(8,128)S(1)} collective-permute-done((f32[8,768]{1,0:T(8,128)S(1)}, f32[8,768]{1,0:T(8,128)S(1)}, u32[]{:S(2)}, u32[]{:S(2)}) %collective-permute-start.12) | collective-permute-done | bytes 24608 | tf_op jit(solution)/shard_map/ppermute | solution.py:311
  28.9 4.5 %collective-permute-done.11.behind.z3 = f32[8,768]{1,0:T(8,128)S(1)} collective-permute-done((f32[8,768]{1,0:T(8,128)S(1)}, f32[8,768]{1,0:T(8,128)S(1)}, u32[]{:S(2)}, u32[]{:S(2)}) %collective-permute-start.11) | collective-permute-done | bytes 24608 | tf_op jit(solution)/shard_map/ppermute | solution.py:311
  33.4 0.9 %shard_map.61 = (f32[8,768]{1,0:T(8,128)S(1)}, f32[8,768]{1,0:T(8,128)S(1)}) custom-call(f32[8,768]{1,0:T(8,128)S(1)} %collective-permute-done.12.known, f32[8,768]{1,0:T(8,128)S(1)} %collective-permute-done.11.behind.z3, f32[8,768]{1,0:T(8,128)S(1)} %shard_map.58.e, bf16[768,768]{1,0:T(8,128)(2,1)S(1)} %get-tuple-element.26.high.kt_high, ...), custom_call_target="tpu_custom_call" | custom-call | tf_op jit(solution)/shard_map/pallas_call | solution.py:28
  34.3 0.5 collective-permute-start.15
  34.9 0.6 collective-permute-done.13.into
  36.0 0.4 shard_map.62
  37.0 0.7 collective-permute-done.16.into
  37.8 0.4 shard_map.63
  38.2 8.4 %collective-permute-start.21 = (f32[8,768]{1,0:T(8,128)S(1)}, f32[8,768]{1,0:T(8,128)S(1)}, u32[]{:S(2)}, u32[]{:S(2)}) collective-permute-start(f32[8,768]{1,0:T(8,128)S(1)} %get-tuple-element.35), channel_id=1, source_target_pairs={{0,25},{4,29},{1,5},{5,1},{2,6},{6,2},{3,8},{7,12},{8,3},{12,7},{9... | collective-permute-start | bytes 73736 | tf_op jit(solution)/shard_map/ppermute | solution.py:311
  46.6 0.5 collective-permute-start.19
  47.1 1.0 %collective-permute-done.21.i3 = f32[8,768]{1,0:T(8,128)S(1)} collective-permute-done((f32[8,768]{1,0:T(8,128)S(1)}, f32[8,768]{1,0:T(8,128)S(1)}, u32[]{:S(2)}, u32[]{:S(2)}) %collective-permute-start.21) | collective-permute-done | bytes 24608 | tf_op jit(solution)/shard_map/ppermute | solution.py:311
  48.2 0.5 collective-permute-start.22
  48.7 2.3 %collective-permute-done.18.i0 = f32[8,768]{1,0:T(8,128)S(1)} collective-permute-done((f32[8,768]{1,0:T(8,128)S(1)}, f32[8,768]{1,0:T(8,128)S(1)}, u32[]{:S(2)}, u32[]{:S(2)}) %collective-permute-start.18) | collective-permute-done | bytes 24608 | tf_op jit(solution)/shard_map/ppermute | solution.py:311
  51.1 1.2 %collective-permute-done.25.mate = f32[8,768]{1,0:T(8,128)S(1)} collective-permute-done((f32[8,768]{1,0:T(8,128)S(1)}, f32[8,768]{1,0:T(8,128)S(1)}, u32[]{:S(2)}, u32[]{:S(2)}) %collective-permute-start.25) | collective-permute-done | bytes 24608 | tf_op jit(solution)/shard_map/ppermute | solution.py:314
  52.3 0.5 shard_map.65.rounded
  52.7 1.8 %shard_map.66 = bf16[8,16,1024]{2,1,0:T(8,128)(2,1)S(1)} custom-call(s32[3,64]{1,0:T(4,128)S(1)} %copy-done.2, bf16[16,384]{1,0:T(8,128)(2,1)S(1)} %shard_map.65.rounded, bf16[384,4096]{1,0:T(8,128)(2,1)S(1)} %get-tuple-element.37.left, bf16[384,4096]{1,0:T(8,128)(2,1)S(1)} %get-tuple-element.38.right), custom_call_target="tpu_custom_call" | custom-call | tf_op jit(solution)/shard_map/pallas_call | solution.py:28
  54.6 13.9 %all_to_all.5 = bf16[8,16,1024]{2,1,0:T(8,128)(2,1)S(1)} all-to-all(bf16[8,16,1024]{2,1,0:T(8,128)(2,1)S(1)} %shard_map.66), channel_id=1, replica_groups=mesh['aux'=8,'pair'=4] {'aux'}, dimensions={0} | all-to-all | bytes 524288 | tf_op jit(solution)/shard_map/all_to_all | solution.py:148
  68.5 0.7 convert_reduce_fusion
  (40 shorter events, 2.1 us)
Async XLA Ops:
  0.0 11.2 %copy-start.1 = (f32[384,768]{1,0:T(8,128)S(1)}, f32[384,768]{1,0:T(8,128)}, u32[]{:S(2)}) copy-start(f32[384,768]{1,0:T(8,128)} %own_fac.1) | copy-start | bytes 3538948
  0.0 11.2 %copy-start = (f32[384,768]{1,0:T(8,128)S(1)}, f32[384,768]{1,0:T(8,128)}, u32[]{:S(2)}) copy-start(f32[384,768]{1,0:T(8,128)} %inv.1) | copy-start | bytes 3538948
  0.0 11.2 %collective-permute-start.5 = (f32[384,768]{1,0:T(8,128)}, f32[384,768]{1,0:T(8,128)S(1)}, u32[]{:S(2)}, u32[]{:S(2)}) collective-permute-start(f32[384,768]{1,0:T(8,128)} %own_fac.1), channel_id=1, source_target_pairs={{0,4},{4,0},{8,12},{12,8},{16,20},{20,16},{24,28},{28,24},{1,5},{5... | collective-permute-start | bytes 3538952 | tf_op jit(solution)/shard_map/ppermute | solution.py:314
  0.5 10.7 %collective-permute-start.4 = (f32[384,768]{1,0:T(8,128)}, f32[384,768]{1,0:T(8,128)S(1)}, u32[]{:S(2)}, u32[]{:S(2)}) collective-permute-start(f32[384,768]{1,0:T(8,128)} %inv.1), channel_id=1, source_target_pairs={{0,4},{4,0},{8,12},{12,8},{16,20},{20,16},{24,28},{28,24},{1,5},{5... | collective-permute-start | bytes 3538952 | tf_op jit(solution)/shard_map/ppermute | solution.py:314
  4.9 1.4 %collective-permute-start = (f32[8,384]{1,0:T(8,128)S(1)}, f32[8,384]{1,0:T(8,128)S(1)}, u32[]{:S(2)}, u32[]{:S(2)}) collective-permute-start(f32[8,384]{1,0:T(8,128)S(1)} %get-tuple-element.23), channel_id=1, source_target_pairs={{0,4},{4,0},{8,12},{12,8},{16,20},{20,16},{24,28},{28,24},{1,5},{5... | collective-permute-start | bytes 36872 | tf_op jit(solution)/shard_map/ppermute | solution.py:314
  6.3 6.7 %collective-permute-start.3 = (f32[8,768]{1,0:T(8,128)S(1)}, f32[8,768]{1,0:T(8,128)S(1)}, u32[]{:S(2)}, u32[]{:S(2)}) collective-permute-start(f32[8,768]{1,0:T(8,128)S(1)} %shard_map.56.f0), channel_id=1, source_target_pairs={{0,3},{4,7},{1,5},{5,1},{2,6},{6,2},{3,0},{7,4},{8,11},{12,15},{9,... | collective-permute-start | bytes 73736 | tf_op jit(solution)/shard_map/ppermute | solution.py:311
  11.2 4.7 %collective-permute-start.2 = (f32[8,768]{1,0:T(8,128)S(1)}, f32[8,768]{1,0:T(8,128)S(1)}, u32[]{:S(2)}, u32[]{:S(2)}) collective-permute-start(f32[8,768]{1,0:T(8,128)S(1)} %shard_map.56.f0), channel_id=1, source_target_pairs={{0,2},{4,6},{1,5},{5,1},{2,0},{6,4},{3,7},{7,3},{8,10},{12,14},{9,... | collective-permute-start | bytes 73736 | tf_op jit(solution)/shard_map/ppermute | solution.py:311
  11.2 4.7 %collective-permute-start.1 = (f32[8,768]{1,0:T(8,128)S(1)}, f32[8,768]{1,0:T(8,128)S(1)}, u32[]{:S(2)}, u32[]{:S(2)}) collective-permute-start(f32[8,768]{1,0:T(8,128)S(1)} %shard_map.56.f0), channel_id=1, source_target_pairs={{0,1},{4,5},{1,0},{5,4},{2,6},{6,2},{3,7},{7,3},{8,9},{12,13},{9,8... | collective-permute-start | bytes 73736 | tf_op jit(solution)/shard_map/ppermute | solution.py:311
  16.3 4.7 %collective-permute-start.8 = (f32[8,768]{1,0:T(8,128)S(1)}, f32[8,768]{1,0:T(8,128)S(1)}, u32[]{:S(2)}, u32[]{:S(2)}) collective-permute-start(f32[8,768]{1,0:T(8,128)S(1)} %shard_map.58.e), channel_id=1, source_target_pairs={{0,24},{4,28},{1,5},{5,1},{2,6},{6,2},{3,7},{7,3},{8,12},{12,8},{9... | collective-permute-start | bytes 73736 | tf_op jit(solution)/shard_map/ppermute | solution.py:311
  18.3 3.8 %collective-permute-start.7 = (f32[8,768]{1,0:T(8,128)S(1)}, f32[8,768]{1,0:T(8,128)S(1)}, u32[]{:S(2)}, u32[]{:S(2)}) collective-permute-start(f32[8,768]{1,0:T(8,128)S(1)} %shard_map.58.e), channel_id=1, source_target_pairs={{0,16},{4,20},{1,5},{5,1},{2,6},{6,2},{3,7},{7,3},{8,12},{12,8},{9... | collective-permute-start | bytes 73736 | tf_op jit(solution)/shard_map/ppermute | solution.py:311
  18.3 3.8 %collective-permute-start.6 = (f32[8,768]{1,0:T(8,128)S(1)}, f32[8,768]{1,0:T(8,128)S(1)}, u32[]{:S(2)}, u32[]{:S(2)}) collective-permute-start(f32[8,768]{1,0:T(8,128)S(1)} %shard_map.58.e), channel_id=1, source_target_pairs={{0,8},{4,12},{1,5},{5,1},{2,6},{6,2},{3,7},{7,3},{8,0},{12,4},{9,1... | collective-permute-start | bytes 73736 | tf_op jit(solution)/shard_map/ppermute | solution.py:311
  22.5 4.7 %collective-permute-start.10 = (f32[8,768]{1,0:T(8,128)S(1)}, f32[8,768]{1,0:T(8,128)S(1)}, u32[]{:S(2)}, u32[]{:S(2)}) collective-permute-start(f32[8,768]{1,0:T(8,128)S(1)} %shard_map.59.s), channel_id=1, source_target_pairs={{0,2},{4,6},{1,5},{5,1},{2,0},{6,4},{3,7},{7,3},{8,25},{12,29},{9,... | collective-permute-start | bytes 73736 | tf_op jit(solution)/shard_map/ppermute | solution.py:311
  22.5 4.7 %collective-permute-start.9 = (f32[8,768]{1,0:T(8,128)S(1)}, f32[8,768]{1,0:T(8,128)S(1)}, u32[]{:S(2)}, u32[]{:S(2)}) collective-permute-start(f32[8,768]{1,0:T(8,128)S(1)} %shard_map.59.s), channel_id=1, source_target_pairs={{0,1},{4,5},{1,0},{5,4},{2,6},{6,2},{3,7},{7,3},{8,17},{12,21},{9,... | collective-permute-start | bytes 73736 | tf_op jit(solution)/shard_map/ppermute | solution.py:311
  27.7 1.2 %collective-permute-start.12 = (f32[8,768]{1,0:T(8,128)S(1)}, f32[8,768]{1,0:T(8,128)S(1)}, u32[]{:S(2)}, u32[]{:S(2)}) collective-permute-start(f32[8,768]{1,0:T(8,128)S(1)} %shard_map.60.s), channel_id=1, source_target_pairs={{0,4},{4,0},{1,5},{5,1},{2,6},{6,2},{3,7},{7,3},{8,12},{12,8},{9,1... | collective-permute-start | bytes 73736 | tf_op jit(solution)/shard_map/ppermute | solution.py:311
  27.7 5.7 %collective-permute-start.11 = (f32[8,768]{1,0:T(8,128)S(1)}, f32[8,768]{1,0:T(8,128)S(1)}, u32[]{:S(2)}, u32[]{:S(2)}) collective-permute-start(f32[8,768]{1,0:T(8,128)S(1)} %shard_map.60.s), channel_id=1, source_target_pairs={{0,3},{4,7},{1,5},{5,1},{2,6},{6,2},{3,0},{7,4},{8,12},{12,8},{9,1... | collective-permute-start | bytes 73736 | tf_op jit(solution)/shard_map/ppermute | solution.py:311
  34.3 1.2 %collective-permute-start.13 = (f32[8,768]{1,0:T(8,128)S(1)}, f32[8,768]{1,0:T(8,128)S(1)}, u32[]{:S(2)}, u32[]{:S(2)}) collective-permute-start(f32[8,768]{1,0:T(8,128)S(1)} %get-tuple-element.30), channel_id=1, source_target_pairs={{0,4},{4,0},{1,5},{5,1},{2,6},{6,2},{3,7},{7,3},{8,12},{12,8},{9,1... | collective-permute-start | bytes 73736 | tf_op jit(solution)/shard_map/ppermute | solution.py:311
  34.3 1.4 %collective-permute-start.15 = (f32[8,768]{1,0:T(8,128)S(1)}, f32[8,768]{1,0:T(8,128)S(1)}, u32[]{:S(2)}, u32[]{:S(2)}) collective-permute-start(f32[8,768]{1,0:T(8,128)S(1)} %get-tuple-element.31.t), channel_id=1, source_target_pairs={{0,4},{4,0},{1,5},{5,1},{2,6},{6,2},{3,7},{7,3},{8,12},{12,8},{9,1... | collective-permute-start | bytes 73736 | tf_op jit(solution)/shard_map/ppermute | solution.py:311
  34.8 1.2 %collective-permute-start.14 = (f32[8,768]{1,0:T(8,128)S(1)}, f32[8,768]{1,0:T(8,128)S(1)}, u32[]{:S(2)}, u32[]{:S(2)}) collective-permute-start(f32[8,768]{1,0:T(8,128)S(1)} %get-tuple-element.31.t), channel_id=1, source_target_pairs={{0,4},{4,0},{1,5},{5,1},{2,6},{6,2},{3,7},{7,3},{8,12},{12,8},{9,1... | collective-permute-start | bytes 73736 | tf_op jit(solution)/shard_map/ppermute | solution.py:311
  36.5 1.2 %collective-permute-start.16 = (f32[8,768]{1,0:T(8,128)S(1)}, f32[8,768]{1,0:T(8,128)S(1)}, u32[]{:S(2)}, u32[]{:S(2)}) collective-permute-start(f32[8,768]{1,0:T(8,128)S(1)} %get-tuple-element.32), channel_id=1, source_target_pairs={{0,4},{4,0},{1,5},{5,1},{2,6},{6,2},{3,7},{7,3},{8,19},{12,23},{9,... | collective-permute-start | bytes 73736 | tf_op jit(solution)/shard_map/ppermute | solution.py:311
  36.6 1.2 %collective-permute-start.17 = (f32[8,768]{1,0:T(8,128)S(1)}, f32[8,768]{1,0:T(8,128)S(1)}, u32[]{:S(2)}, u32[]{:S(2)}) collective-permute-start(f32[8,768]{1,0:T(8,128)S(1)} %get-tuple-element.33), channel_id=1, source_target_pairs={{0,4},{4,0},{1,5},{5,1},{2,6},{6,2},{3,7},{7,3},{8,25},{12,29},{9,... | collective-permute-start | bytes 73736 | tf_op jit(solution)/shard_map/ppermute | solution.py:311
  38.2 14.5 %copy-start.2 = (s32[3,64]{1,0:T(4,128)S(1)}, s32[3,64]{1,0:T(4,128)}, u32[]{:S(2)}) copy-start(s32[3,64]{1,0:T(4,128)} %screen.1) | copy-start | bytes 2308
  38.2 9.9 %collective-permute-start.21 = (f32[8,768]{1,0:T(8,128)S(1)}, f32[8,768]{1,0:T(8,128)S(1)}, u32[]{:S(2)}, u32[]{:S(2)}) collective-permute-start(f32[8,768]{1,0:T(8,128)S(1)} %get-tuple-element.35), channel_id=1, source_target_pairs={{0,25},{4,29},{1,5},{5,1},{2,6},{6,2},{3,8},{7,12},{8,3},{12,7},{9... | collective-permute-start | bytes 73736 | tf_op jit(solution)/shard_map/ppermute | solution.py:311
  46.6 1.5 %collective-permute-start.20 = (f32[8,768]{1,0:T(8,128)S(1)}, f32[8,768]{1,0:T(8,128)S(1)}, u32[]{:S(2)}, u32[]{:S(2)}) collective-permute-start(f32[8,768]{1,0:T(8,128)S(1)} %get-tuple-element.35), channel_id=1, source_target_pairs={{0,4},{4,0},{1,5},{5,1},{2,8},{6,12},{3,27},{7,31},{8,2},{12,6},{9... | collective-permute-start | bytes 73736 | tf_op jit(solution)/shard_map/ppermute | solution.py:311
  46.6 2.0 %collective-permute-start.19 = (f32[8,768]{1,0:T(8,128)S(1)}, f32[8,768]{1,0:T(8,128)S(1)}, u32[]{:S(2)}, u32[]{:S(2)}) collective-permute-start(f32[8,768]{1,0:T(8,128)S(1)} %get-tuple-element.35), channel_id=1, source_target_pairs={{0,4},{4,0},{1,8},{5,12},{2,19},{6,23},{3,7},{7,3},{8,1},{12,5},{9... | collective-permute-start | bytes 73736 | tf_op jit(solution)/shard_map/ppermute | solution.py:311
  47.1 3.8 %collective-permute-start.18 = (f32[8,768]{1,0:T(8,128)S(1)}, f32[8,768]{1,0:T(8,128)S(1)}, u32[]{:S(2)}, u32[]{:S(2)}) collective-permute-start(f32[8,768]{1,0:T(8,128)S(1)} %get-tuple-element.35), channel_id=1, source_target_pairs={{0,8},{4,12},{1,18},{5,22},{2,6},{6,2},{3,7},{7,3},{8,0},{12,4},{9... | collective-permute-start | bytes 73736 | tf_op jit(solution)/shard_map/ppermute | solution.py:311
  47.1 3.8 %collective-permute-start.24 = (f32[8,768]{1,0:T(8,128)S(1)}, f32[8,768]{1,0:T(8,128)S(1)}, u32[]{:S(2)}, u32[]{:S(2)}) collective-permute-start(f32[8,768]{1,0:T(8,128)S(1)} %get-tuple-element.36.t), channel_id=1, source_target_pairs={{0,4},{4,0},{1,5},{5,1},{2,6},{6,2},{3,7},{7,3},{8,11},{12,15},{9,... | collective-permute-start | bytes 73736 | tf_op jit(solution)/shard_map/ppermute | solution.py:311
  48.1 2.8 %collective-permute-start.23 = (f32[8,768]{1,0:T(8,128)S(1)}, f32[8,768]{1,0:T(8,128)S(1)}, u32[]{:S(2)}, u32[]{:S(2)}) collective-permute-start(f32[8,768]{1,0:T(8,128)S(1)} %get-tuple-element.36.t), channel_id=1, source_target_pairs={{0,4},{4,0},{1,5},{5,1},{2,6},{6,2},{3,7},{7,3},{8,10},{12,14},{9,... | collective-permute-start | bytes 73736 | tf_op jit(solution)/shard_map/ppermute | solution.py:311
  48.2 2.8 %collective-permute-start.22 = (f32[8,768]{1,0:T(8,128)S(1)}, f32[8,768]{1,0:T(8,128)S(1)}, u32[]{:S(2)}, u32[]{:S(2)}) collective-permute-start(f32[8,768]{1,0:T(8,128)S(1)} %get-tuple-element.36.t), channel_id=1, source_target_pairs={{0,4},{4,0},{1,5},{5,1},{2,6},{6,2},{3,7},{7,3},{8,9},{12,13},{9,8... | collective-permute-start | bytes 73736 | tf_op jit(solution)/shard_map/ppermute | solution.py:311
  51.0 1.3 %collective-permute-start.25 = (f32[8,768]{1,0:T(8,128)S(1)}, f32[8,768]{1,0:T(8,128)S(1)}, u32[]{:S(2)}, u32[]{:S(2)}) collective-permute-start(f32[8,768]{1,0:T(8,128)S(1)} %shard_map.64.own), channel_id=1, source_target_pairs={{0,4},{4,0},{8,12},{12,8},{16,20},{20,16},{24,28},{28,24},{1,5},{5... | collective-permute-start | bytes 73736 | tf_op jit(solution)/shard_map/ppermute | solution.py:314

commit v5 on v4

--- a/solution.py
+++ b/solution.py
@@ -44,12 +44,11 @@
 
 
 def fit(
-    screen_in, densities_in, integrals, left, right, kept, given, screen, densities, total, arrived
+    screen_in, densities_in, integrals, left, right, out, screen, densities, total, arrived
 ):
     height, width = integrals.shape
     pieces = arrived.shape[0] - 2
     chunk = width // pieces
-    half = kept.shape[0]
     small = [
         pltpu.make_async_copy(screen_in, screen, arrived.at[pieces]),
         pltpu.make_async_copy(densities_in, densities, arrived.at[pieces + 1]),
@@ -88,20 +87,16 @@
             total[rows, :] += lax.dot_general(
                 held[j][rows, :], masked, NT, preferred_element_type=F32
             )
-    done = total[...].T
-    even = side_of() == 0
-    kept[...] = jnp.where(even, done[:half], done[half:])
-    given[...] = jnp.where(even, done[half:], done[:half])
+    out[...] = total[...].T
 
 
 def fit_partial(densities, integrals, screen):
     count = densities.shape[0]
     height, width = integrals.shape
     pieces = 8 if width % (8 * TILE) == 0 else width // TILE
-    half = struct((count // 2, height))
     return call(
         fit,
-        [struct((height, width // 2), BF16)] * 2 + [half, half],
+        [struct((height, width // 2), BF16)] * 2 + [struct((count, height))],
         *(pltpu.with_memory_space_constraint(x, pltpu.HBM) for x in (screen, densities, integrals)),
         specs=[HBM] * 3,
         scratch=[
@@ -163,17 +158,8 @@
     return both[:rows] + both[rows:]
 
 
-def prepare(own_inv, mate_inv, own_fac, mate_fac, inv_high, inv_low, k_high, k_low, kt_high, kt_low):
-    height = own_inv.shape[0]
-    side = side_of()
-    here = pl.ds(pl.multiple_of(side * height, height), height)
-    there = pl.ds(pl.multiple_of((1 - side) * height, height), height)
-    for ref, rows in ((own_inv, here), (mate_inv, there)):
-        high, low = high_low(ref[...])
-        inv_high[rows, :] = high
-        inv_low[rows, :] = low
-
-    @pl.when(block_of() > 0)
+def prepare(own_inv, mate_inv, own_fac, mate_fac, k_high, k_low, kt_high, kt_low):
+    @pl.when((block_of() > 0) & (side_of() == 0))
     def _():
         total = jnp.zeros(k_high.shape, F32)
         for inv, fac in ((own_inv, own_fac), (mate_inv, mate_fac)):
@@ -190,15 +176,13 @@
         kt_low[...] = low
 
 
-def merge(kept, mate, out):
-    even = side_of() == 0
-    height = kept.shape[1]
-    out[:, :height] = jnp.where(even, kept[...], mate[...])
-    out[:, height:] = jnp.where(even, mate[...], kept[...])
-
-
-def begin(f0, f1, f2, f3, high, low, out):
-    out[...] = times(f0[...] + f1[...] + f2[...] + f3[...], high[...], low[...])
+def begin(f0, f1, f2, f3, inv, after, out):
+    high, low = high_low(inv[...])
+    out[...] = times(f0[...] + f1[...] + f2[...] + f3[...], high, low)
+
+
+def both(own, mate, out):
+    out[...] = own[...] + mate[...]
 
 
 def after_zero(one, two, three, e, high, low, out):
@@ -267,10 +251,7 @@
 
 
 def finish(own, mate, inv, out):
-    even = side_of() == 0
-    value = jnp.concatenate(
-        [jnp.where(even, own[...], mate[...]), jnp.where(even, mate[...], own[...])], axis=0
-    )
+    value = jnp.where(side_of() == 0, own[...], mate[...])
     high, low = high_low(inv[...])
     out[...] = times(value, high, low, NT).astype(out.dtype)
 
@@ -283,69 +264,65 @@
     return lax.dot_general(a, b, NT, precision=HIGHEST, preferred_element_type=F32)
 
 
-def complete(moves):
-    to = {}
-    for source, target, *via in moves:
-        chain = [source, target, *via]
-        to.update(zip(chain, chain[1:] + chain[:1]))
-    chips = [(k, plane) for k in range(SOLVE_BLOCKS) for plane in range(SOLVE_BLOCKS)]
-    return [(chip, to.get(chip, chip)) for chip in chips]
-
-
-def chip_solve(kept, given, factor, diag_inv):
-    half, height = kept.shape
+def chip_solve(partial_fit, factor, diag_inv):
+    count, height = partial_fit.shape
     size = 2 * height
     planes = lax.axis_size("pair")
-
-    def pairs_of(routes):
-        pairs = []
-        for (k_from, z_from), (k_to, z_to) in routes:
+    chips = [(k, plane) for k in range(SOLVE_BLOCKS) for plane in range(planes)]
+
+    def device(chip, c):
+        return (2 * chip[0] + c) * planes + chip[1]
+
+    def permute(value, to):
+        for chip in chips:
             for c in range(2):
-                d = 1 - c if (k_from, z_from) == (k_to, z_to) else c
-                pairs.append(
-                    ((2 * k_from + c) * planes + z_from, (2 * k_to + d) * planes + z_to)
-                )
-        return pairs
+                to.setdefault(device(chip, c), device(chip, 1 - c))
+        return lax.ppermute(value, AXES, sorted(to.items()))
 
     def send(value, *moves):
-        return lax.ppermute(value, AXES, pairs_of(complete(moves)))
+        to = {}
+        for source, target in moves:
+            loop = [device(source, 0), device(target, 0), device(target, 1), device(source, 1)]
+            to.update(zip(loop, loop[1:] + loop[:1]))
+        return permute(value, to)
 
     def swap(value):
         return lax.ppermute(value, "aux", [(i, i ^ 1) for i in range(2 * SOLVE_BLOCKS)])
 
-    panel = struct((half, size))
+    panel = struct((count, size))
     square = struct((size, size), BF16)
-    inv_high, inv_low, k_high, k_low, kt_high, kt_low = call(
-        prepare, [square] * 6, diag_inv, swap(diag_inv), factor, swap(factor), limit=32
-    )
-    part = call(merge, panel, kept, swap(given))
+    k_high, k_low, kt_high, kt_low = call(
+        prepare, [square] * 4, diag_inv, swap(diag_inv), factor, swap(factor), limit=32
+    )
     home = [max(k - 1, 0) for k in range(SOLVE_BLOCKS)]
-    gathered = [
-        send(
-            part,
-            *(((k, (home[k] + step) % planes), (k, home[k])) for k in range(SOLVE_BLOCKS)),
-        )
-        for step in range(1, planes)
-    ]
-    e = call(begin, panel, part, *gathered, inv_high, inv_low)
+    gathered = []
+    for step in range(1, planes):
+        to = {}
+        for k in range(SOLVE_BLOCKS):
+            for c in range(2):
+                near = device((k, home[k]), c)
+                far = device((k, (home[k] + step) % planes), c)
+                to.update({near: far, far: near})
+        gathered.append(permute(partial_fit, to))
+    e = call(begin, panel, partial_fit, *gathered, diag_inv, k_high)
+    e = call(both, panel, e, swap(e))
     reach = [send(e, ((0, 0), (k, 0))) for k in range(1, SOLVE_BLOCKS)]
     one = call(after_zero, panel, *reach, e, kt_high, kt_low)
-    first = send(one, ((1, 0), (2, 1), (1, 3)), ((3, 0), (3, 1), (3, 3)), ((0, 0), (0, 1)))
+    first = send(one, ((1, 0), (2, 1)), ((3, 0), (3, 1)), ((0, 0), (0, 1)))
     second = send(one, ((1, 0), (3, 1)), ((2, 0), (2, 1)), ((0, 0), (0, 2)))
     two = call(after_one, panel, first, second, e, kt_high, kt_low)
-    behind = send(two, ((3, 1), (3, 2), (2, 3)), ((0, 0), (0, 3)))
+    behind = send(two, ((3, 1), (3, 2)), ((0, 0), (0, 3)))
     known = send(two, ((2, 1), (3, 2)))
     t, back = call(turn, [panel] * 2, known, behind, e, kt_high, kt_low, k_high, k_low)
     into = send(back, ((3, 2), (2, 1)))
     near = send(t, ((3, 2), (3, 1)))
     far = send(t, ((3, 2), (3, 0)))
     t, back, mixed = call(back_two, [panel] * 3, into, near, far, t, two, k_high, k_low)
-    into = send(back, ((2, 1), (1, 0), (2, 3)), ((3, 0), (2, 0), (3, 3)))
+    into = send(back, ((2, 1), (1, 0)), ((3, 0), (2, 0)))
     other = send(mixed, ((3, 1), (1, 0)), ((2, 1), (2, 0)))
     t, back = call(back_one, [panel] * 2, into, other, t, one, k_high, k_low)
-    vias = [(2, 2), (2, 3), (3, 3), (3, 1)]
     into = [
-        send(back, ((1, 0), (0, plane)), ((2, 0), (0, (plane + 1) % planes), vias[plane]))
+        send(back, ((1, 0), (0, plane)), ((2, 0), (0, (plane + 1) % planes)))
         for plane in range(planes)
     ]
     spread = []
@@ -357,14 +334,10 @@
             moves.append(((3, 2), (3, 2 + step)))
         spread.append(send(t, *moves))
     t = call(collect, panel, e, first, second, behind, *into, t, *spread)
-    return call(finish, struct((2 * half, height), BF16), t, swap(t), diag_inv)
-
-
-def chain_solve(kept, given, factor, diag_inv):
-    even = lax.rem(lax.axis_index("aux"), 2) == 0
-    partial_fit = jnp.concatenate(
-        [jnp.where(even, kept, given), jnp.where(even, given, kept)], axis=0
-    )
+    return call(finish, struct((count, height), BF16), t, swap(t), diag_inv)
+
+
+def chain_solve(partial_fit, factor, diag_inv):
     count, height = partial_fit.shape
     breadth = factor.shape[1]
     block_size = diag_inv.shape[1]
@@ -429,8 +402,8 @@
         and lax.axis_size("pair") == SOLVE_BLOCKS
     )
     solve = chip_solve if chip_blocks else chain_solve
-    left, right, kept, given = fit_partial(densities, integrals, screen)
-    rounded = solve(kept, given, factor, diag_inv)
+    left, right, partial_fit = fit_partial(densities, integrals, screen)
+    rounded = solve(partial_fit, factor, diag_inv)
     return scatter_sum(coulomb_partial(rounded, left, right, screen))
 
 

time: 69.3 us -> 62.9 us (0.908)
  waiting for transfers between devices: 25.7 us -> 16.1 us
  starting transfers between devices: 18.8 us -> 21.8 us
    ppermute x22, waiting for transfers between devices: 23.6 us -> 14 us  [permute(): return lax.ppermute(value, AXES, sorted(to.items()))]
    ppermute x22, starting transfers between devices: 17.6 us -> 20.8 us  [permute(): return lax.ppermute(value, AXES, sorted(to.items()))]
  transfers between devices with their start and end apart: 26 -> 26, of which waited for: 16 -> 19; matrix products, arithmetic and copies ran while one was open for 0% -> 0% of each run, Pallas kernels for 7% -> 7%
where the time goes in v5:
time: 62.9 us; the launch traced here: 62.7 us
  starting transfers between devices  21.8 us (35%)
  waiting for transfers between devices  16.1 us (26%)
  blocking collectives  14.1 us (22%)
  Pallas kernels  9.87 us (16%)
  other arithmetic  0.67 us (1%)
    ppermute x22, starting transfers between devices, permute(): return lax.ppermute(value, AXES, sorted(to.items()))  20.8 us
    all_to_all x1, blocking collectives, scatter_sum(): arrived = lax.all_to_all(slabs, 'aux', 0, 0, tiled=True)  14.1 us
    ppermute x22, waiting for transfers between devices, permute(): return lax.ppermute(value, AXES, sorted(to.items()))  14 us
    pallas_call x12, Pallas kernels, call(): pl.pallas_call(kernel, out_shape=outs, in_specs=specs or [VMEM] * len(ope...  9.87 us
    ppermute x4, waiting for transfers between devices, swap(): lax.ppermute(value, 'aux', [(i, i ^ 1) for i in range(2 * SOLVE_BLOCKS)])  2.14 us
  transfers between devices with their start and end apart: 26, of which 19 were waited for; matrix products, arithmetic and copies ran while one was open for 0% of the time, Pallas kernels for 7%

profile of v5, /device:TPU:0, one launch (start us, length us, event | category | flops | bytes accessed | tf_op | source)
XLA Modules:
  0.0 62.7 jit_solution(9777028506614925248)
XLA Ops:
  0.0 0.5 collective-permute-start.4
  0.6 4.3 %shard_map.55 = (bf16[384,4096]{1,0:T(8,128)(2,1)S(1)}, bf16[384,4096]{1,0:T(8,128)(2,1)S(1)}, f32[16,384]{1,0:T(8,128)S(1)}) custom-call(s32[3,64]{1,0:T(4,128)} %screen.1, bf16[16,8192]{1,0:T(8,128)(2,1)} %densities_in.1, bf16[384,8192]{1,0:T(8,128)(2,1)} %integrals.1), custom_call_target="tpu_custom_call" | custom-call | tf_op jit(solution)/shard_map/pallas_call | solution.py:28
  4.9 5.1 %collective-permute-start.2 = (f32[16,384]{1,0:T(8,128)S(1)}, f32[16,384]{1,0:T(8,128)S(1)}, u32[]{:S(2)}, u32[]{:S(2)}) collective-permute-start(f32[16,384]{1,0:T(8,128)S(1)} %get-tuple-element.19.f0), channel_id=1, source_target_pairs={{0,3},{1,5},{2,6},{3,0},{4,7},{5,1},{6,2},{7,4},{8,11},{9,13},{10,... | collective-permute-start | bytes 73736 | tf_op jit(solution)/shard_map/ppermute | solution.py:280
  10.1 1.7 %collective-permute-done.2.f3 = f32[16,384]{1,0:T(8,128)S(1)} collective-permute-done((f32[16,384]{1,0:T(8,128)S(1)}, f32[16,384]{1,0:T(8,128)S(1)}, u32[]{:S(2)}, u32[]{:S(2)}) %collective-permute-start.2) | collective-permute-done | bytes 24608 | tf_op jit(solution)/shard_map/ppermute | solution.py:280
  11.8 2.9 %collective-permute-done.1.f2 = f32[16,384]{1,0:T(8,128)S(1)} collective-permute-done((f32[16,384]{1,0:T(8,128)S(1)}, f32[16,384]{1,0:T(8,128)S(1)}, u32[]{:S(2)}, u32[]{:S(2)}) %collective-permute-start.1) | collective-permute-done | bytes 24608 | tf_op jit(solution)/shard_map/ppermute | solution.py:280
  15.1 1.3 %collective-permute-done.5.mate = f32[16,768]{1,0:T(8,128)S(1)} collective-permute-done((f32[16,768]{1,0:T(8,128)S(1)}, f32[16,768]{1,0:T(8,128)S(1)}, u32[]{:S(2)}, u32[]{:S(2)}) %collective-permute-start.5) | collective-permute-done | bytes 49184 | tf_op jit(solution)/shard_map/ppermute | solution.py:290
  16.3 1.7 %collective-permute-start.8 = (f32[16,768]{1,0:T(8,128)S(1)}, f32[16,768]{1,0:T(8,128)S(1)}, u32[]{:S(2)}, u32[]{:S(2)}) collective-permute-start(f32[16,768]{1,0:T(8,128)S(1)} %shard_map.58.e), channel_id=1, source_target_pairs={{0,24},{1,5},{2,6},{3,7},{4,0},{5,1},{6,2},{7,3},{8,12},{9,13},{10... | collective-permute-start | bytes 147464 | tf_op jit(solution)/shard_map/ppermute | solution.py:280
  18.4 1.4 %collective-permute-done.8.three = f32[16,768]{1,0:T(8,128)S(1)} collective-permute-done((f32[16,768]{1,0:T(8,128)S(1)}, f32[16,768]{1,0:T(8,128)S(1)}, u32[]{:S(2)}, u32[]{:S(2)}) %collective-permute-start.8) | collective-permute-done | bytes 49184 | tf_op jit(solution)/shard_map/ppermute | solution.py:280
  19.8 0.5 collective-permute-done.6.one
  20.2 0.5 shard_map.59.s
  20.8 1.9 %collective-permute-done.10.second.z2 = f32[16,768]{1,0:T(8,128)S(1)} collective-permute-done((f32[16,768]{1,0:T(8,128)S(1)}, f32[16,768]{1,0:T(8,128)S(1)}, u32[]{:S(2)}, u32[]{:S(2)}) %collective-permute-start.10) | collective-permute-done | bytes 49184 | tf_op jit(solution)/shard_map/ppermute | solution.py:280
  22.9 0.5 shard_map.60.s
  23.4 2.9 %collective-permute-start.12 = (f32[16,768]{1,0:T(8,128)S(1)}, f32[16,768]{1,0:T(8,128)S(1)}, u32[]{:S(2)}, u32[]{:S(2)}) collective-permute-start(f32[16,768]{1,0:T(8,128)S(1)} %shard_map.60.s), channel_id=1, source_target_pairs={{0,4},{1,5},{2,6},{3,7},{4,0},{5,1},{6,2},{7,3},{8,12},{9,13},{10,... | collective-permute-start | bytes 147464 | tf_op jit(solution)/shard_map/ppermute | solution.py:280
  26.3 0.9 %collective-permute-done.12.known = f32[16,768]{1,0:T(8,128)S(1)} collective-permute-done((f32[16,768]{1,0:T(8,128)S(1)}, f32[16,768]{1,0:T(8,128)S(1)}, u32[]{:S(2)}, u32[]{:S(2)}) %collective-permute-start.12) | collective-permute-done | bytes 49184 | tf_op jit(solution)/shard_map/ppermute | solution.py:280
  27.2 0.9 %collective-permute-done.11.behind.z3 = f32[16,768]{1,0:T(8,128)S(1)} collective-permute-done((f32[16,768]{1,0:T(8,128)S(1)}, f32[16,768]{1,0:T(8,128)S(1)}, u32[]{:S(2)}, u32[]{:S(2)}) %collective-permute-start.11) | collective-permute-done | bytes 49184 | tf_op jit(solution)/shard_map/ppermute | solution.py:280
  28.0 1.0 %shard_map.61 = (f32[16,768]{1,0:T(8,128)S(1)}, f32[16,768]{1,0:T(8,128)S(1)}) custom-call(f32[16,768]{1,0:T(8,128)S(1)} %collective-permute-done.12.known, f32[16,768]{1,0:T(8,128)S(1)} %collective-permute-done.11.behind.z3, f32[16,768]{1,0:T(8,128)S(1)} %shard_map.58.e, bf16[768,768]{1,0:T(8,128)(2,1)S(1)} %get-tuple-element.21.high.kt_high, ...), custom_call_target="tpu_custom_call" | custom-call | tf_op jit(solution)/shard_map/pallas_call | solution.py:28
  29.1 3.1 %collective-permute-start.13 = (f32[16,768]{1,0:T(8,128)S(1)}, f32[16,768]{1,0:T(8,128)S(1)}, u32[]{:S(2)}, u32[]{:S(2)}) collective-permute-start(f32[16,768]{1,0:T(8,128)S(1)} %get-tuple-element.24), channel_id=1, source_target_pairs={{0,4},{1,5},{2,6},{3,7},{4,0},{5,1},{6,2},{7,3},{8,12},{9,13},{10,... | collective-permute-start | bytes 147464 | tf_op jit(solution)/shard_map/ppermute | solution.py:280
  32.1 0.5 collective-permute-start.14
  33.5 0.5 shard_map.62
  34.5 0.7 %collective-permute-done.16.into = f32[16,768]{1,0:T(8,128)S(1)} collective-permute-done((f32[16,768]{1,0:T(8,128)S(1)}, f32[16,768]{1,0:T(8,128)S(1)}, u32[]{:S(2)}, u32[]{:S(2)}) %collective-permute-start.16) | collective-permute-done | bytes 49184 | tf_op jit(solution)/shard_map/ppermute | solution.py:280
  35.6 0.5 shard_map.63
  36.2 3.1 %collective-permute-start.20 = (f32[16,768]{1,0:T(8,128)S(1)}, f32[16,768]{1,0:T(8,128)S(1)}, u32[]{:S(2)}, u32[]{:S(2)}) collective-permute-start(f32[16,768]{1,0:T(8,128)S(1)} %get-tuple-element.29), channel_id=1, source_target_pairs={{0,4},{1,5},{2,6},{3,7},{4,0},{5,1},{6,12},{7,20},{8,2},{9,13},{10... | collective-permute-start | bytes 147464 | tf_op jit(solution)/shard_map/ppermute | solution.py:280
  39.4 0.5 collective-permute-start.18
  39.9 2.2 %collective-permute-start.24 = (f32[16,768]{1,0:T(8,128)S(1)}, f32[16,768]{1,0:T(8,128)S(1)}, u32[]{:S(2)}, u32[]{:S(2)}) collective-permute-start(f32[16,768]{1,0:T(8,128)S(1)} %get-tuple-element.30.t), channel_id=1, source_target_pairs={{0,4},{1,5},{2,6},{3,7},{4,0},{5,1},{6,2},{7,3},{8,11},{9,13},{10,... | collective-permute-start | bytes 147464 | tf_op jit(solution)/shard_map/ppermute | solution.py:280
  42.1 0.8 %collective-permute-done.21.i3 = f32[16,768]{1,0:T(8,128)S(1)} collective-permute-done((f32[16,768]{1,0:T(8,128)S(1)}, f32[16,768]{1,0:T(8,128)S(1)}, u32[]{:S(2)}, u32[]{:S(2)}) %collective-permute-start.21) | collective-permute-done | bytes 49184 | tf_op jit(solution)/shard_map/ppermute | solution.py:280
  42.9 0.5 collective-permute-start.22
  43.4 0.6 collective-permute-done.18.i0
  44.8 0.9 %collective-permute-done.25.mate = f32[16,768]{1,0:T(8,128)S(1)} collective-permute-done((f32[16,768]{1,0:T(8,128)S(1)}, f32[16,768]{1,0:T(8,128)S(1)}, u32[]{:S(2)}, u32[]{:S(2)}) %collective-permute-start.25) | collective-permute-done | bytes 49184 | tf_op jit(solution)/shard_map/ppermute | solution.py:290
  45.6 0.4 shard_map.65.rounded
  46.1 1.8 %shard_map.66 = bf16[8,16,1024]{2,1,0:T(8,128)(2,1)S(1)} custom-call(s32[3,64]{1,0:T(4,128)S(1)} %copy-done.2, bf16[16,384]{1,0:T(8,128)(2,1)S(1)} %shard_map.65.rounded, bf16[384,4096]{1,0:T(8,128)(2,1)S(1)} %get-tuple-element.31.left, bf16[384,4096]{1,0:T(8,128)(2,1)S(1)} %get-tuple-element.32.right), custom_call_target="tpu_custom_call" | custom-call | tf_op jit(solution)/shard_map/pallas_call | solution.py:28
  47.9 14.1 %all_to_all.5 = bf16[8,16,1024]{2,1,0:T(8,128)(2,1)S(1)} all-to-all(bf16[8,16,1024]{2,1,0:T(8,128)(2,1)S(1)} %shard_map.66), channel_id=1, replica_groups=mesh['aux'=8,'pair'=4] {'aux'}, dimensions={0} | all-to-all | bytes 524288 | tf_op jit(solution)/shard_map/all_to_all | solution.py:143
  62.0 0.7 %convert_reduce_fusion = f32[16,1024]{1,0:T(8,128)} fusion(bf16[8,16,1024]{2,1,0:T(8,128)(2,1)S(1)} %all_to_all.5), kind=kLoop, calls=%fused_computation | loop fusion | flops 245760 | bytes 327680 | tf_op jit(solution)/shard_map/reduce_sum | solution.py:144
  (40 shorter events, 3.9 us)
Async XLA Ops:
  0.0 10.0 %copy-start.1 = (f32[384,768]{1,0:T(8,128)S(1)}, f32[384,768]{1,0:T(8,128)}, u32[]{:S(2)}) copy-start(f32[384,768]{1,0:T(8,128)} %own_fac.1) | copy-start | bytes 3538948
  0.0 10.1 %copy-start = (f32[384,768]{1,0:T(8,128)S(1)}, f32[384,768]{1,0:T(8,128)}, u32[]{:S(2)}) copy-start(f32[384,768]{1,0:T(8,128)} %inv.3) | copy-start | bytes 3538948
  0.0 10.0 %collective-permute-start.4 = (f32[384,768]{1,0:T(8,128)}, f32[384,768]{1,0:T(8,128)S(1)}, u32[]{:S(2)}, u32[]{:S(2)}) collective-permute-start(f32[384,768]{1,0:T(8,128)} %own_fac.1), channel_id=1, source_target_pairs={{0,4},{4,0},{8,12},{12,8},{16,20},{20,16},{24,28},{28,24},{1,5},{5... | collective-permute-start | bytes 3538952 | tf_op jit(solution)/shard_map/ppermute | solution.py:290
  0.5 9.5 %collective-permute-start.3 = (f32[384,768]{1,0:T(8,128)}, f32[384,768]{1,0:T(8,128)S(1)}, u32[]{:S(2)}, u32[]{:S(2)}) collective-permute-start(f32[384,768]{1,0:T(8,128)} %inv.3), channel_id=1, source_target_pairs={{0,4},{4,0},{8,12},{12,8},{16,20},{20,16},{24,28},{28,24},{1,5},{5... | collective-permute-start | bytes 3538952 | tf_op jit(solution)/shard_map/ppermute | solution.py:290
  4.9 6.9 %collective-permute-start.2 = (f32[16,384]{1,0:T(8,128)S(1)}, f32[16,384]{1,0:T(8,128)S(1)}, u32[]{:S(2)}, u32[]{:S(2)}) collective-permute-start(f32[16,384]{1,0:T(8,128)S(1)} %get-tuple-element.19.f0), channel_id=1, source_target_pairs={{0,3},{1,5},{2,6},{3,0},{4,7},{5,1},{6,2},{7,4},{8,11},{9,13},{10,... | collective-permute-start | bytes 73736 | tf_op jit(solution)/shard_map/ppermute | solution.py:280
  10.0 4.7 %collective-permute-start.1 = (f32[16,384]{1,0:T(8,128)S(1)}, f32[16,384]{1,0:T(8,128)S(1)}, u32[]{:S(2)}, u32[]{:S(2)}) collective-permute-start(f32[16,384]{1,0:T(8,128)S(1)} %get-tuple-element.19.f0), channel_id=1, source_target_pairs={{0,2},{1,5},{2,0},{3,7},{4,6},{5,1},{6,4},{7,3},{8,10},{9,13},{10,... | collective-permute-start | bytes 73736 | tf_op jit(solution)/shard_map/ppermute | solution.py:280
  10.0 4.7 %collective-permute-start = (f32[16,384]{1,0:T(8,128)S(1)}, f32[16,384]{1,0:T(8,128)S(1)}, u32[]{:S(2)}, u32[]{:S(2)}) collective-permute-start(f32[16,384]{1,0:T(8,128)S(1)} %get-tuple-element.19.f0), channel_id=1, source_target_pairs={{0,1},{1,0},{2,6},{3,7},{4,5},{5,4},{6,2},{7,3},{8,9},{9,8},{10,14... | collective-permute-start | bytes 73736 | tf_op jit(solution)/shard_map/ppermute | solution.py:280
  15.1 1.3 %collective-permute-start.5 = (f32[16,768]{1,0:T(8,128)S(1)}, f32[16,768]{1,0:T(8,128)S(1)}, u32[]{:S(2)}, u32[]{:S(2)}) collective-permute-start(f32[16,768]{1,0:T(8,128)S(1)} %shard_map.57.own), channel_id=1, source_target_pairs={{0,4},{4,0},{8,12},{12,8},{16,20},{20,16},{24,28},{28,24},{1,5},{5... | collective-permute-start | bytes 147464 | tf_op jit(solution)/shard_map/ppermute | solution.py:290
  16.3 3.4 %collective-permute-start.8 = (f32[16,768]{1,0:T(8,128)S(1)}, f32[16,768]{1,0:T(8,128)S(1)}, u32[]{:S(2)}, u32[]{:S(2)}) collective-permute-start(f32[16,768]{1,0:T(8,128)S(1)} %shard_map.58.e), channel_id=1, source_target_pairs={{0,24},{1,5},{2,6},{3,7},{4,0},{5,1},{6,2},{7,3},{8,12},{9,13},{10... | collective-permute-start | bytes 147464 | tf_op jit(solution)/shard_map/ppermute | solution.py:280
  18.0 1.8 %collective-permute-start.7 = (f32[16,768]{1,0:T(8,128)S(1)}, f32[16,768]{1,0:T(8,128)S(1)}, u32[]{:S(2)}, u32[]{:S(2)}) collective-permute-start(f32[16,768]{1,0:T(8,128)S(1)} %shard_map.58.e), channel_id=1, source_target_pairs={{0,16},{1,5},{2,6},{3,7},{4,0},{5,1},{6,2},{7,3},{8,12},{9,13},{10... | collective-permute-start | bytes 147464 | tf_op jit(solution)/shard_map/ppermute | solution.py:280
  18.0 2.2 %collective-permute-start.6 = (f32[16,768]{1,0:T(8,128)S(1)}, f32[16,768]{1,0:T(8,128)S(1)}, u32[]{:S(2)}, u32[]{:S(2)}) collective-permute-start(f32[16,768]{1,0:T(8,128)S(1)} %shard_map.58.e), channel_id=1, source_target_pairs={{0,8},{1,5},{2,6},{3,7},{4,0},{5,1},{6,2},{7,3},{8,12},{9,13},{10,... | collective-permute-start | bytes 147464 | tf_op jit(solution)/shard_map/ppermute | solution.py:280
  20.7 2.0 %collective-permute-start.10 = (f32[16,768]{1,0:T(8,128)S(1)}, f32[16,768]{1,0:T(8,128)S(1)}, u32[]{:S(2)}, u32[]{:S(2)}) collective-permute-start(f32[16,768]{1,0:T(8,128)S(1)} %shard_map.59.s), channel_id=1, source_target_pairs={{0,2},{1,5},{2,6},{3,7},{4,0},{5,1},{6,4},{7,3},{8,25},{9,13},{10,... | collective-permute-start | bytes 147464 | tf_op jit(solution)/shard_map/ppermute | solution.py:280
  20.7 2.2 %collective-permute-start.9 = (f32[16,768]{1,0:T(8,128)S(1)}, f32[16,768]{1,0:T(8,128)S(1)}, u32[]{:S(2)}, u32[]{:S(2)}) collective-permute-start(f32[16,768]{1,0:T(8,128)S(1)} %shard_map.59.s), channel_id=1, source_target_pairs={{0,1},{1,5},{2,6},{3,7},{4,0},{5,4},{6,2},{7,3},{8,17},{9,13},{10,... | collective-permute-start | bytes 147464 | tf_op jit(solution)/shard_map/ppermute | solution.py:280
  23.4 3.8 %collective-permute-start.12 = (f32[16,768]{1,0:T(8,128)S(1)}, f32[16,768]{1,0:T(8,128)S(1)}, u32[]{:S(2)}, u32[]{:S(2)}) collective-permute-start(f32[16,768]{1,0:T(8,128)S(1)} %shard_map.60.s), channel_id=1, source_target_pairs={{0,4},{1,5},{2,6},{3,7},{4,0},{5,1},{6,2},{7,3},{8,12},{9,13},{10,... | collective-permute-start | bytes 147464 | tf_op jit(solution)/shard_map/ppermute | solution.py:280
  26.3 1.8 %collective-permute-start.11 = (f32[16,768]{1,0:T(8,128)S(1)}, f32[16,768]{1,0:T(8,128)S(1)}, u32[]{:S(2)}, u32[]{:S(2)}) collective-permute-start(f32[16,768]{1,0:T(8,128)S(1)} %shard_map.60.s), channel_id=1, source_target_pairs={{0,3},{1,5},{2,6},{3,7},{4,0},{5,1},{6,2},{7,4},{8,12},{9,13},{10,... | collective-permute-start | bytes 147464 | tf_op jit(solution)/shard_map/ppermute | solution.py:280
  29.1 3.9 %collective-permute-start.13 = (f32[16,768]{1,0:T(8,128)S(1)}, f32[16,768]{1,0:T(8,128)S(1)}, u32[]{:S(2)}, u32[]{:S(2)}) collective-permute-start(f32[16,768]{1,0:T(8,128)S(1)} %get-tuple-element.24), channel_id=1, source_target_pairs={{0,4},{1,5},{2,6},{3,7},{4,0},{5,1},{6,2},{7,3},{8,12},{9,13},{10,... | collective-permute-start | bytes 147464 | tf_op jit(solution)/shard_map/ppermute | solution.py:280
  32.1 1.2 %collective-permute-start.15 = (f32[16,768]{1,0:T(8,128)S(1)}, f32[16,768]{1,0:T(8,128)S(1)}, u32[]{:S(2)}, u32[]{:S(2)}) collective-permute-start(f32[16,768]{1,0:T(8,128)S(1)} %get-tuple-element.25.t), channel_id=1, source_target_pairs={{0,4},{1,5},{2,6},{3,7},{4,0},{5,1},{6,2},{7,3},{8,12},{9,13},{10,... | collective-permute-start | bytes 147464 | tf_op jit(solution)/shard_map/ppermute | solution.py:280
  32.1 1.4 %collective-permute-start.14 = (f32[16,768]{1,0:T(8,128)S(1)}, f32[16,768]{1,0:T(8,128)S(1)}, u32[]{:S(2)}, u32[]{:S(2)}) collective-permute-start(f32[16,768]{1,0:T(8,128)S(1)} %get-tuple-element.25.t), channel_id=1, source_target_pairs={{0,4},{1,5},{2,6},{3,7},{4,0},{5,1},{6,2},{7,3},{8,12},{9,13},{10,... | collective-permute-start | bytes 147464 | tf_op jit(solution)/shard_map/ppermute | solution.py:280
  34.0 1.2 %collective-permute-start.16 = (f32[16,768]{1,0:T(8,128)S(1)}, f32[16,768]{1,0:T(8,128)S(1)}, u32[]{:S(2)}, u32[]{:S(2)}) collective-permute-start(f32[16,768]{1,0:T(8,128)S(1)} %get-tuple-element.26), channel_id=1, source_target_pairs={{0,4},{1,5},{2,6},{3,7},{4,0},{5,1},{6,2},{7,3},{8,12},{9,13},{10,... | collective-permute-start | bytes 147464 | tf_op jit(solution)/shard_map/ppermute | solution.py:280
  34.4 1.2 %collective-permute-start.17 = (f32[16,768]{1,0:T(8,128)S(1)}, f32[16,768]{1,0:T(8,128)S(1)}, u32[]{:S(2)}, u32[]{:S(2)}) collective-permute-start(f32[16,768]{1,0:T(8,128)S(1)} %get-tuple-element.27), channel_id=1, source_target_pairs={{0,4},{1,5},{2,6},{3,7},{4,0},{5,1},{6,2},{7,3},{8,12},{9,13},{10,... | collective-permute-start | bytes 147464 | tf_op jit(solution)/shard_map/ppermute | solution.py:280
  36.1 10.0 %copy-start.2 = (s32[3,64]{1,0:T(4,128)S(1)}, s32[3,64]{1,0:T(4,128)}, u32[]{:S(2)}) copy-start(s32[3,64]{1,0:T(4,128)} %screen.1) | copy-start | bytes 2308
  36.1 6.8 %collective-permute-start.21 = (f32[16,768]{1,0:T(8,128)S(1)}, f32[16,768]{1,0:T(8,128)S(1)}, u32[]{:S(2)}, u32[]{:S(2)}) collective-permute-start(f32[16,768]{1,0:T(8,128)S(1)} %get-tuple-element.29), channel_id=1, source_target_pairs={{0,4},{1,5},{2,6},{3,7},{4,20},{5,1},{6,2},{7,12},{8,3},{9,13},{10... | collective-permute-start | bytes 147464 | tf_op jit(solution)/shard_map/ppermute | solution.py:280
  36.2 6.7 %collective-permute-start.20 = (f32[16,768]{1,0:T(8,128)S(1)}, f32[16,768]{1,0:T(8,128)S(1)}, u32[]{:S(2)}, u32[]{:S(2)}) collective-permute-start(f32[16,768]{1,0:T(8,128)S(1)} %get-tuple-element.29), channel_id=1, source_target_pairs={{0,4},{1,5},{2,6},{3,7},{4,0},{5,1},{6,12},{7,20},{8,2},{9,13},{10... | collective-permute-start | bytes 147464 | tf_op jit(solution)/shard_map/ppermute | solution.py:280
  39.4 4.1 %collective-permute-start.19 = (f32[16,768]{1,0:T(8,128)S(1)}, f32[16,768]{1,0:T(8,128)S(1)}, u32[]{:S(2)}, u32[]{:S(2)}) collective-permute-start(f32[16,768]{1,0:T(8,128)S(1)} %get-tuple-element.29), channel_id=1, source_target_pairs={{0,4},{1,5},{2,6},{3,7},{4,0},{5,12},{6,20},{7,3},{8,1},{9,13},{10... | collective-permute-start | bytes 147464 | tf_op jit(solution)/shard_map/ppermute | solution.py:280
  39.4 4.7 %collective-permute-start.18 = (f32[16,768]{1,0:T(8,128)S(1)}, f32[16,768]{1,0:T(8,128)S(1)}, u32[]{:S(2)}, u32[]{:S(2)}) collective-permute-start(f32[16,768]{1,0:T(8,128)S(1)} %get-tuple-element.29), channel_id=1, source_target_pairs={{0,4},{1,5},{2,6},{3,7},{4,12},{5,20},{6,2},{7,3},{8,0},{9,13},{10... | collective-permute-start | bytes 147464 | tf_op jit(solution)/shard_map/ppermute | solution.py:280
  39.9 4.1 %collective-permute-start.24 = (f32[16,768]{1,0:T(8,128)S(1)}, f32[16,768]{1,0:T(8,128)S(1)}, u32[]{:S(2)}, u32[]{:S(2)}) collective-permute-start(f32[16,768]{1,0:T(8,128)S(1)} %get-tuple-element.30.t), channel_id=1, source_target_pairs={{0,4},{1,5},{2,6},{3,7},{4,0},{5,1},{6,2},{7,3},{8,11},{9,13},{10,... | collective-permute-start | bytes 147464 | tf_op jit(solution)/shard_map/ppermute | solution.py:280
  42.9 1.2 %collective-permute-start.23 = (f32[16,768]{1,0:T(8,128)S(1)}, f32[16,768]{1,0:T(8,128)S(1)}, u32[]{:S(2)}, u32[]{:S(2)}) collective-permute-start(f32[16,768]{1,0:T(8,128)S(1)} %get-tuple-element.30.t), channel_id=1, source_target_pairs={{0,4},{1,5},{2,6},{3,7},{4,0},{5,1},{6,2},{7,3},{8,10},{9,13},{10,... | collective-permute-start | bytes 147464 | tf_op jit(solution)/shard_map/ppermute | solution.py:280
  42.9 1.4 %collective-permute-start.22 = (f32[16,768]{1,0:T(8,128)S(1)}, f32[16,768]{1,0:T(8,128)S(1)}, u32[]{:S(2)}, u32[]{:S(2)}) collective-permute-start(f32[16,768]{1,0:T(8,128)S(1)} %get-tuple-element.30.t), channel_id=1, source_target_pairs={{0,4},{1,5},{2,6},{3,7},{4,0},{5,1},{6,2},{7,3},{8,9},{9,13},{10,1... | collective-permute-start | bytes 147464 | tf_op jit(solution)/shard_map/ppermute | solution.py:280
  44.3 1.3 %collective-permute-start.25 = (f32[16,768]{1,0:T(8,128)S(1)}, f32[16,768]{1,0:T(8,128)S(1)}, u32[]{:S(2)}, u32[]{:S(2)}) collective-permute-start(f32[16,768]{1,0:T(8,128)S(1)} %shard_map.64.own), channel_id=1, source_target_pairs={{0,4},{4,0},{8,12},{12,8},{16,20},{20,16},{24,28},{28,24},{1,5},{5... | collective-permute-start | bytes 147464 | tf_op jit(solution)/shard_map/ppermute | solution.py:290

commit v6 on v5

--- a/solution.py
+++ b/solution.py
@@ -41,6 +41,17 @@
 
 def block_of():
     return lax.div(lax.axis_index("aux"), 2)
+
+
+def masked_row(screen, densities, i, tiles):
+    zero = jnp.zeros((), densities.dtype)
+    return jnp.concatenate(
+        [
+            jnp.where(screen[i, t] != 0, densities[:, t * TILE : (t + 1) * TILE], zero)
+            for t in tiles
+        ],
+        axis=1,
+    )
 
 
 def fit(
@@ -69,25 +80,18 @@
     total[...] = jnp.zeros_like(total)
     for copy in small:
         copy.wait()
+    count = densities.shape[0]
+    strips = height // TILE
     for j in range(pieces):
+        tiles = range(j * chunk // TILE, (j + 1) * chunk // TILE)
+        stacked = jnp.concatenate([masked_row(screen, densities, i, tiles) for i in range(strips)])
         copies[j].wait()
-        for i in range(height // TILE):
-            rows = slice(i * TILE, (i + 1) * TILE)
-            masked = jnp.concatenate(
-                [
-                    jnp.where(
-                        screen[i, t] != 0,
-                        densities[:, t * TILE : (t + 1) * TILE],
-                        jnp.zeros((), BF16),
-                    )
-                    for t in range(j * chunk // TILE, (j + 1) * chunk // TILE)
-                ],
-                axis=1,
-            )
-            total[rows, :] += lax.dot_general(
-                held[j][rows, :], masked, NT, preferred_element_type=F32
-            )
-    out[...] = total[...].T
+        total[...] += lax.dot_general(held[j][...], stacked, NT, preferred_element_type=F32)
+    done = total[...].T
+    for i in range(strips):
+        out[:, i * TILE : (i + 1) * TILE] = done[
+            i * count : (i + 1) * count, i * TILE : (i + 1) * TILE
+        ]
 
 
 def fit_partial(densities, integrals, screen):
@@ -102,35 +106,32 @@
         scratch=[
             pltpu.SMEM(screen.shape, jnp.int32),
             pltpu.VMEM(densities.shape, BF16),
-            pltpu.VMEM((height, count), F32),
+            pltpu.VMEM((height, height // TILE * count), F32),
             pltpu.SemaphoreType.DMA((pieces + 2,)),
         ],
     )
 
 
 def coulomb(screen, rounded, left, right, out):
-    members, _, chunk = out.shape
+    members, count, chunk = out.shape
     height, width = left.shape
+    strips = height // TILE
+    value = rounded[...]
+    strip_of = lax.broadcasted_iota(jnp.int32, value.shape, 1) // TILE
+    stacked = jnp.concatenate(
+        [jnp.where(strip_of == i, value, jnp.zeros((), BF16)) for i in range(strips)]
+    )
     for m in range(members):
-        for t in range(m * chunk // TILE, (m + 1) * chunk // TILE):
-            masked = jnp.concatenate(
-                [
-                    jnp.where(
-                        screen[i, t] != 0,
-                        rounded[:, i * TILE : (i + 1) * TILE],
-                        jnp.zeros((), BF16),
-                    )
-                    for i in range(height // TILE)
-                ],
-                axis=1,
-            )
-            held = left if t * TILE < width else right
-            start = t * TILE if held is left else t * TILE - width
-            part = jnp.dot(
-                masked, held[:, start : start + TILE], preferred_element_type=F32
-            )
-            first = t * TILE - m * chunk
-            out[m, :, first : first + TILE] = part.astype(out.dtype)
+        held = left if m * chunk < width else right
+        start = m * chunk if held is left else m * chunk - width
+        parts = jnp.dot(stacked, held[:, start : start + chunk], preferred_element_type=F32)
+        for t in range(chunk // TILE):
+            lanes = slice(t * TILE, (t + 1) * TILE)
+            total = jnp.zeros((count, TILE), F32)
+            for i in range(strips):
+                part = parts[i * count : (i + 1) * count, lanes]
+                total += jnp.where(screen[i, m * chunk // TILE + t] != 0, part, 0.0)
+            out[m, :, lanes] = total.astype(out.dtype)
 
 
 def coulomb_partial(rounded, left, right, screen):
@@ -158,25 +159,29 @@
     return both[:rows] + both[rows:]
 
 
-def prepare(own_inv, mate_inv, own_fac, mate_fac, k_high, k_low, kt_high, kt_low):
+def prepare(inv0, inv1, fac0, fac1, k_high, k_low, kt_high, kt_low, lhs, rhs):
+    height = inv0.shape[0]
+
     @pl.when((block_of() > 0) & (side_of() == 0))
     def _():
-        total = jnp.zeros(k_high.shape, F32)
-        for inv, fac in ((own_inv, own_fac), (mate_inv, mate_fac)):
-            ih, il = high_low(inv[...])
-            fh, fl = high_low(fac[...])
-            total += lax.dot_general(ih, fh, TN, preferred_element_type=F32)
-            total += lax.dot_general(ih, fl, TN, preferred_element_type=F32)
-            total += lax.dot_general(il, fh, TN, preferred_element_type=F32)
-        high, low = high_low(total)
-        k_high[...] = high
-        k_low[...] = low
-        high, low = high_low(total.T)
-        kt_high[...] = high
-        kt_low[...] = low
-
-
-def begin(f0, f1, f2, f3, inv, after, out):
+        for n, (inv, fac) in enumerate(((inv0, fac0), (inv1, fac1))):
+            rows = [slice((3 * n + r) * height, (3 * n + r + 1) * height) for r in range(3)]
+            high, low = high_low(inv[...])
+            lhs[rows[0], :], lhs[rows[1], :], lhs[rows[2], :] = high, low, high
+            high, low = high_low(fac[...])
+            rhs[rows[0], :], rhs[rows[1], :], rhs[rows[2], :] = high, high, low
+        depth = 3 * height
+        halves = (
+            (slice(0, height), slice(0, depth)),
+            (slice(height, 2 * height), slice(0, 2 * depth)),
+        )
+        for part, used in halves:
+            product = lax.dot_general(lhs[used, part], rhs[used, :], TN, preferred_element_type=F32)
+            k_high[part, :], k_low[part, :] = high_low(product)
+            kt_high[:, part], kt_low[:, part] = high_low(product.T)
+
+
+def begin(f0, f1, f2, f3, inv, out):
     high, low = high_low(inv[...])
     out[...] = times(f0[...] + f1[...] + f2[...] + f3[...], high, low)
 
@@ -231,7 +236,7 @@
     back[...] = jnp.where(block == 2, product + into[...], product)
 
 
-def collect(e, z1, z2, z3, i0, i1, i2, i3, t, p1, p2, p3, out):
+def collect(z0, z1, z2, z3, i0, i1, i2, i3, t, p1, p2, p3, out):
     plane = lax.axis_index("pair")
     block = block_of()
 
@@ -240,7 +245,7 @@
             plane == 0, a[...], jnp.where(plane == 1, b[...], jnp.where(plane == 2, c[...], d[...]))
         )
 
-    start = by_plane(e, z1, z2, z3)
+    start = by_plane(z0, z1, z2, z3)
     zero = start - by_plane(i0, i1, i2, i3) - by_plane(i3, i0, i1, i2)
     one = by_plane(t, p1, p2, p3)
     two = by_plane(t, t, p1, p2)
@@ -281,8 +286,11 @@
 
     def send(value, *moves):
         to = {}
-        for source, target in moves:
-            loop = [device(source, 0), device(target, 0), device(target, 1), device(source, 1)]
+        for source, target, *via in moves:
+            loop = [device(source, 0), device(target, 0), device(target, 1)]
+            for chip in via:
+                loop += [device(chip, 0), device(chip, 1)]
+            loop.append(device(source, 1))
             to.update(zip(loop, loop[1:] + loop[:1]))
         return permute(value, to)
 
@@ -292,11 +300,18 @@
     panel = struct((count, size))
     square = struct((size, size), BF16)
     k_high, k_low, kt_high, kt_low = call(
-        prepare, [square] * 4, diag_inv, swap(diag_inv), factor, swap(factor), limit=32
-    )
-    home = [max(k - 1, 0) for k in range(SOLVE_BLOCKS)]
+        prepare,
+        [square] * 4,
+        diag_inv,
+        swap(diag_inv),
+        factor,
+        swap(factor),
+        limit=32,
+        scratch=[pltpu.VMEM((3 * size, size), BF16)] * 2,
+    )
+    home = [1] + list(range(SOLVE_BLOCKS - 1))
     gathered = []
-    for step in range(1, planes):
+    for step in reversed(range(1, planes)):
         to = {}
         for k in range(SOLVE_BLOCKS):
             for c in range(2):
@@ -304,14 +319,14 @@
                 far = device((k, (home[k] + step) % planes), c)
                 to.update({near: far, far: near})
         gathered.append(permute(partial_fit, to))
-    e = call(begin, panel, partial_fit, *gathered, diag_inv, k_high)
+    e = call(begin, panel, partial_fit, *gathered, diag_inv)
     e = call(both, panel, e, swap(e))
-    reach = [send(e, ((0, 0), (k, 0))) for k in range(1, SOLVE_BLOCKS)]
+    reach = [send(e, ((0, 1), (k, 0))) for k in range(1, SOLVE_BLOCKS)]
     one = call(after_zero, panel, *reach, e, kt_high, kt_low)
-    first = send(one, ((1, 0), (2, 1)), ((3, 0), (3, 1)), ((0, 0), (0, 1)))
-    second = send(one, ((1, 0), (3, 1)), ((2, 0), (2, 1)), ((0, 0), (0, 2)))
+    first = send(one, ((1, 0), (2, 1)), ((3, 0), (3, 1)), ((0, 1), (0, 0)))
+    second = send(one, ((1, 0), (3, 1)), ((2, 0), (2, 1)), ((0, 1), (0, 2)))
     two = call(after_one, panel, first, second, e, kt_high, kt_low)
-    behind = send(two, ((3, 1), (3, 2)), ((0, 0), (0, 3)))
+    behind = send(two, ((3, 1), (3, 2)), ((0, 1), (0, 3)))
     known = send(two, ((2, 1), (3, 2)))
     t, back = call(turn, [panel] * 2, known, behind, e, kt_high, kt_low, k_high, k_low)
     into = send(back, ((3, 2), (2, 1)))
@@ -321,19 +336,27 @@
     into = send(back, ((2, 1), (1, 0)), ((3, 0), (2, 0)))
     other = send(mixed, ((3, 1), (1, 0)), ((2, 1), (2, 0)))
     t, back = call(back_one, [panel] * 2, into, other, t, one, k_high, k_low)
-    into = [
-        send(back, ((1, 0), (0, plane)), ((2, 0), (0, (plane + 1) % planes)))
-        for plane in range(planes)
-    ]
-    spread = []
-    for step in range(1, planes):
+    near = {
+        ((1, 0), (0, 3)): (3, 0),
+        ((1, 0), (0, 2)): (1, 1),
+        ((2, 0), (0, 3)): (2, 1),
+        ((2, 0), (0, 2)): (3, 1),
+    }
+    into = [None] * planes
+    spread = [None] * planes
+    for plane in reversed(range(planes)):
+        moves = [((1, 0), (0, plane)), ((2, 0), (0, (plane + 1) % planes))]
+        into[plane] = send(
+            back, *((*move, near[move]) if move in near else move for move in moves)
+        )
+    for step in reversed(range(1, planes)):
         moves = [((1, 0), (1, step))]
         if 1 + step < planes:
             moves.append(((2, 1), (2, 1 + step)))
         if 2 + step < planes:
             moves.append(((3, 2), (3, 2 + step)))
-        spread.append(send(t, *moves))
-    t = call(collect, panel, e, first, second, behind, *into, t, *spread)
+        spread[step] = send(t, *moves)
+    t = call(collect, panel, first, e, second, behind, *into, t, *spread[1:])
     return call(finish, struct((count, height), BF16), t, swap(t), diag_inv)
 
 

time: 62.9 us -> 61.5 us (0.978)
  blocking collectives: 14.1 us -> 12.2 us
  waiting for transfers between devices: 16.1 us -> 16.9 us
    all_to_all x1, blocking collectives: 14.1 us -> 12.2 us  [scatter_sum(): arrived = lax.all_to_all(slabs, 'aux', 0, 0, tiled=True)]
    ppermute x22, waiting for transfers between devices: 14 us -> 14.8 us  [permute(): return lax.ppermute(value, AXES, sorted(to.items()))]
where the time goes in v6:
time: 61.5 us; the launch traced here: 61.3 us
  starting transfers between devices  21.7 us (35%)
  waiting for transfers between devices  16.9 us (27%)
  blocking collectives  12.2 us (20%)
  Pallas kernels  9.78 us (16%)
  other arithmetic  0.67 us (1%)
    ppermute x22, starting transfers between devices, permute(): return lax.ppermute(value, AXES, sorted(to.items()))  20.7 us
    ppermute x22, waiting for transfers between devices, permute(): return lax.ppermute(value, AXES, sorted(to.items()))  14.8 us
    all_to_all x1, blocking collectives, scatter_sum(): arrived = lax.all_to_all(slabs, 'aux', 0, 0, tiled=True)  12.2 us
    pallas_call x12, Pallas kernels, call(): pl.pallas_call(kernel, out_shape=outs, in_specs=specs or [VMEM] * len(ope...  9.78 us
    ppermute x4, waiting for transfers between devices, swap(): lax.ppermute(value, 'aux', [(i, i ^ 1) for i in range(2 * SOLVE_BLOCKS)])  2.14 us
  transfers between devices with their start and end apart: 26, of which 19 were waited for; matrix products, arithmetic and copies ran while one was open for 0% of the time, Pallas kernels for 7%

profile of v6, /device:TPU:0, one launch (start us, length us, event | category | flops | bytes accessed | tf_op | source)
XLA Modules:
  0.0 61.3 jit_solution(17866260866509109913)
XLA Ops:
  0.0 0.5 collective-permute-start.8
  0.6 4.2 %shard_map.55 = (bf16[384,4096]{1,0:T(8,128)(2,1)S(1)}, bf16[384,4096]{1,0:T(8,128)(2,1)S(1)}, f32[16,384]{1,0:T(8,128)S(1)}) custom-call(s32[3,64]{1,0:T(4,128)} %screen.1, bf16[16,8192]{1,0:T(8,128)(2,1)} %densities_in.1, bf16[384,8192]{1,0:T(8,128)(2,1)} %integrals.1), custom_call_target="tpu_custom_call" | custom-call | tf_op jit(solution)/shard_map/pallas_call | solution.py:28
  4.8 0.5 collective-permute-start.2
  5.4 5.1 %collective-permute-start = (f32[16,384]{1,0:T(8,128)S(1)}, f32[16,384]{1,0:T(8,128)S(1)}, u32[]{:S(2)}, u32[]{:S(2)}) collective-permute-start(f32[16,384]{1,0:T(8,128)S(1)} %get-tuple-element.19.f0), channel_id=1, source_target_pairs={{0,1},{1,0},{2,6},{3,7},{4,5},{5,4},{6,2},{7,3},{8,11},{9,13},{10,... | collective-permute-start | bytes 73736 | tf_op jit(solution)/shard_map/ppermute | solution.py:285
  10.5 1.8 %collective-permute-done.f1 = f32[16,384]{1,0:T(8,128)S(1)} collective-permute-done((f32[16,384]{1,0:T(8,128)S(1)}, f32[16,384]{1,0:T(8,128)S(1)}, u32[]{:S(2)}, u32[]{:S(2)}) %collective-permute-start) | collective-permute-done | bytes 24608 | tf_op jit(solution)/shard_map/ppermute | solution.py:285
  12.6 1.2 %collective-permute-done.3.mate = f32[16,768]{1,0:T(8,128)S(1)} collective-permute-done((f32[16,768]{1,0:T(8,128)S(1)}, f32[16,768]{1,0:T(8,128)S(1)}, u32[]{:S(2)}, u32[]{:S(2)}) %collective-permute-start.3) | collective-permute-done | bytes 49184 | tf_op jit(solution)/shard_map/ppermute | solution.py:298
  14.0 0.4 collective-permute-start.5
  14.6 0.6 collective-permute-done.6.three
  15.7 0.5 shard_map.59.s
  16.7 0.7 %collective-permute-done.10.second.z2 = f32[16,768]{1,0:T(8,128)S(1)} collective-permute-done((f32[16,768]{1,0:T(8,128)S(1)}, f32[16,768]{1,0:T(8,128)S(1)}, u32[]{:S(2)}, u32[]{:S(2)}) %collective-permute-start.10) | collective-permute-done | bytes 49184 | tf_op jit(solution)/shard_map/ppermute | solution.py:285
  17.4 6.6 %collective-permute-done.9.first.z0 = f32[16,768]{1,0:T(8,128)S(1)} collective-permute-done((f32[16,768]{1,0:T(8,128)S(1)}, f32[16,768]{1,0:T(8,128)S(1)}, u32[]{:S(2)}, u32[]{:S(2)}) %collective-permute-start.9) | collective-permute-done | bytes 49184 | tf_op jit(solution)/shard_map/ppermute | solution.py:285
  24.1 0.5 shard_map.60.s
  24.6 0.5 collective-permute-start.11
  25.1 0.7 %collective-permute-done.12.known = f32[16,768]{1,0:T(8,128)S(1)} collective-permute-done((f32[16,768]{1,0:T(8,128)S(1)}, f32[16,768]{1,0:T(8,128)S(1)}, u32[]{:S(2)}, u32[]{:S(2)}) %collective-permute-start.12) | collective-permute-done | bytes 49184 | tf_op jit(solution)/shard_map/ppermute | solution.py:285
  26.0 1.0 %shard_map.61 = (f32[16,768]{1,0:T(8,128)S(1)}, f32[16,768]{1,0:T(8,128)S(1)}) custom-call(f32[16,768]{1,0:T(8,128)S(1)} %collective-permute-done.12.known, f32[16,768]{1,0:T(8,128)S(1)} %collective-permute-done.11.behind.z3, f32[16,768]{1,0:T(8,128)S(1)} %shard_map.57.e.z1, bf16[768,768]{1,0:T(8,128)(2,1)S(1)} %get-tuple-element.20.high.kt_high, ...), custom_call_target="tpu_custom_call" | custom-call | tf_op jit(solution)/shard_map/pallas_call | solution.py:28
  27.0 0.4 collective-permute-start.13
  27.9 0.4 collective-permute-done.13.into
  28.8 0.5 shard_map.62
  29.8 0.7 %collective-permute-done.16.into = f32[16,768]{1,0:T(8,128)S(1)} collective-permute-done((f32[16,768]{1,0:T(8,128)S(1)}, f32[16,768]{1,0:T(8,128)S(1)}, u32[]{:S(2)}, u32[]{:S(2)}) %collective-permute-start.16) | collective-permute-done | bytes 49184 | tf_op jit(solution)/shard_map/ppermute | solution.py:285
  30.8 0.5 shard_map.63
  31.5 8.5 %collective-permute-start.20 = (f32[16,768]{1,0:T(8,128)S(1)}, f32[16,768]{1,0:T(8,128)S(1)}, u32[]{:S(2)}, u32[]{:S(2)}) collective-permute-start(f32[16,768]{1,0:T(8,128)S(1)} %get-tuple-element.29), channel_id=1, source_target_pairs={{0,4},{1,5},{2,6},{3,7},{4,0},{5,1},{6,9},{7,17},{8,2},{9,13},{10,... | collective-permute-start | bytes 147464 | tf_op jit(solution)/shard_map/ppermute | solution.py:285
  39.9 0.5 collective-permute-start.18
  40.5 2.2 %collective-permute-start.24 = (f32[16,768]{1,0:T(8,128)S(1)}, f32[16,768]{1,0:T(8,128)S(1)}, u32[]{:S(2)}, u32[]{:S(2)}) collective-permute-start(f32[16,768]{1,0:T(8,128)S(1)} %get-tuple-element.30.t), channel_id=1, source_target_pairs={{0,4},{1,5},{2,6},{3,7},{4,0},{5,1},{6,2},{7,3},{8,11},{9,13},{10,... | collective-permute-start | bytes 147464 | tf_op jit(solution)/shard_map/ppermute | solution.py:285
  42.7 0.8 %collective-permute-done.21.i3 = f32[16,768]{1,0:T(8,128)S(1)} collective-permute-done((f32[16,768]{1,0:T(8,128)S(1)}, f32[16,768]{1,0:T(8,128)S(1)}, u32[]{:S(2)}, u32[]{:S(2)}) %collective-permute-start.21) | collective-permute-done | bytes 49184 | tf_op jit(solution)/shard_map/ppermute | solution.py:285
  43.5 0.5 collective-permute-start.22
  44.0 0.6 collective-permute-done.18.i0
  44.9 0.4 collective-permute-start.25
  45.3 0.9 %collective-permute-done.25.mate = f32[16,768]{1,0:T(8,128)S(1)} collective-permute-done((f32[16,768]{1,0:T(8,128)S(1)}, f32[16,768]{1,0:T(8,128)S(1)}, u32[]{:S(2)}, u32[]{:S(2)}) %collective-permute-start.25) | collective-permute-done | bytes 49184 | tf_op jit(solution)/shard_map/ppermute | solution.py:298
  46.2 0.5 shard_map.65.rounded
  46.7 1.8 %shard_map.66 = bf16[8,16,1024]{2,1,0:T(8,128)(2,1)S(1)} custom-call(s32[3,64]{1,0:T(4,128)S(1)} %copy-done.2, bf16[16,384]{1,0:T(8,128)(2,1)S(1)} %shard_map.65.rounded, bf16[384,4096]{1,0:T(8,128)(2,1)S(1)} %get-tuple-element.31.left, bf16[384,4096]{1,0:T(8,128)(2,1)S(1)} %get-tuple-element.32.right), custom_call_target="tpu_custom_call" | custom-call | tf_op jit(solution)/shard_map/pallas_call | solution.py:28
  48.5 12.2 %all_to_all.5 = bf16[8,16,1024]{2,1,0:T(8,128)(2,1)S(1)} all-to-all(bf16[8,16,1024]{2,1,0:T(8,128)(2,1)S(1)} %shard_map.66), channel_id=1, replica_groups=mesh['aux'=8,'pair'=4] {'aux'}, dimensions={0} | all-to-all | bytes 524288 | tf_op jit(solution)/shard_map/all_to_all | solution.py:144
  60.7 0.7 %convert_reduce_fusion = f32[16,1024]{1,0:T(8,128)} fusion(bf16[8,16,1024]{2,1,0:T(8,128)(2,1)S(1)} %all_to_all.5), kind=kLoop, calls=%fused_computation | loop fusion | flops 245760 | bytes 327680 | tf_op jit(solution)/shard_map/reduce_sum | solution.py:145
  (40 shorter events, 4.4 us)
Async XLA Ops:
  0.0 12.3 %copy-start = (f32[384,768]{1,0:T(8,128)S(1)}, f32[384,768]{1,0:T(8,128)}, u32[]{:S(2)}) copy-start(f32[384,768]{1,0:T(8,128)} %inv.3) | copy-start | bytes 3538948
  0.0 14.6 %collective-permute-start.8 = (f32[384,768]{1,0:T(8,128)}, f32[384,768]{1,0:T(8,128)S(1)}, u32[]{:S(2)}, u32[]{:S(2)}) collective-permute-start(f32[384,768]{1,0:T(8,128)} %fac0.1), channel_id=1, source_target_pairs={{0,4},{4,0},{8,12},{12,8},{16,20},{20,16},{24,28},{28,24},{1,5},{5... | collective-permute-start | bytes 3538952 | tf_op jit(solution)/shard_map/ppermute | solution.py:298
  0.5 14.1 %collective-permute-start.7 = (f32[384,768]{1,0:T(8,128)}, f32[384,768]{1,0:T(8,128)S(1)}, u32[]{:S(2)}, u32[]{:S(2)}) collective-permute-start(f32[384,768]{1,0:T(8,128)} %inv.3), channel_id=1, source_target_pairs={{0,4},{4,0},{8,12},{12,8},{16,20},{20,16},{24,28},{28,24},{1,5},{5... | collective-permute-start | bytes 3538952 | tf_op jit(solution)/shard_map/ppermute | solution.py:298
  4.8 9.8 %copy-start.1 = (f32[384,768]{1,0:T(8,128)S(1)}, f32[384,768]{1,0:T(8,128)}, u32[]{:S(2)}) copy-start(f32[384,768]{1,0:T(8,128)} %fac0.1) | copy-start | bytes 3538948
  4.8 5.7 %collective-permute-start.2 = (f32[16,384]{1,0:T(8,128)S(1)}, f32[16,384]{1,0:T(8,128)S(1)}, u32[]{:S(2)}, u32[]{:S(2)}) collective-permute-start(f32[16,384]{1,0:T(8,128)S(1)} %get-tuple-element.19.f0), channel_id=1, source_target_pairs={{0,4},{1,2},{2,1},{3,7},{4,0},{5,6},{6,5},{7,3},{8,9},{9,8},{10,14... | collective-permute-start | bytes 73736 | tf_op jit(solution)/shard_map/ppermute | solution.py:285
  5.3 5.2 %collective-permute-start.1 = (f32[16,384]{1,0:T(8,128)S(1)}, f32[16,384]{1,0:T(8,128)S(1)}, u32[]{:S(2)}, u32[]{:S(2)}) collective-permute-start(f32[16,384]{1,0:T(8,128)S(1)} %get-tuple-element.19.f0), channel_id=1, source_target_pairs={{0,4},{1,3},{2,6},{3,1},{4,0},{5,7},{6,2},{7,5},{8,10},{9,13},{10,... | collective-permute-start | bytes 73736 | tf_op jit(solution)/shard_map/ppermute | solution.py:285
  5.4 7.0 %collective-permute-start = (f32[16,384]{1,0:T(8,128)S(1)}, f32[16,384]{1,0:T(8,128)S(1)}, u32[]{:S(2)}, u32[]{:S(2)}) collective-permute-start(f32[16,384]{1,0:T(8,128)S(1)} %get-tuple-element.19.f0), channel_id=1, source_target_pairs={{0,1},{1,0},{2,6},{3,7},{4,5},{5,4},{6,2},{7,3},{8,11},{9,13},{10,... | collective-permute-start | bytes 73736 | tf_op jit(solution)/shard_map/ppermute | solution.py:285
  12.6 1.3 %collective-permute-start.3 = (f32[16,768]{1,0:T(8,128)S(1)}, f32[16,768]{1,0:T(8,128)S(1)}, u32[]{:S(2)}, u32[]{:S(2)}) collective-permute-start(f32[16,768]{1,0:T(8,128)S(1)} %shard_map.56.own), channel_id=1, source_target_pairs={{0,4},{4,0},{8,12},{12,8},{16,20},{20,16},{24,28},{28,24},{1,5},{5... | collective-permute-start | bytes 147464 | tf_op jit(solution)/shard_map/ppermute | solution.py:298
  13.9 1.3 %collective-permute-start.6 = (f32[16,768]{1,0:T(8,128)S(1)}, f32[16,768]{1,0:T(8,128)S(1)}, u32[]{:S(2)}, u32[]{:S(2)}) collective-permute-start(f32[16,768]{1,0:T(8,128)S(1)} %shard_map.57.e.z1), channel_id=1, source_target_pairs={{0,4},{1,24},{2,6},{3,7},{4,0},{5,1},{6,2},{7,3},{8,12},{9,13},{10... | collective-permute-start | bytes 147464 | tf_op jit(solution)/shard_map/ppermute | solution.py:285
  14.0 1.3 %collective-permute-start.5 = (f32[16,768]{1,0:T(8,128)S(1)}, f32[16,768]{1,0:T(8,128)S(1)}, u32[]{:S(2)}, u32[]{:S(2)}) collective-permute-start(f32[16,768]{1,0:T(8,128)S(1)} %shard_map.57.e.z1), channel_id=1, source_target_pairs={{0,4},{1,16},{2,6},{3,7},{4,0},{5,1},{6,2},{7,3},{8,12},{9,13},{10... | collective-permute-start | bytes 147464 | tf_op jit(solution)/shard_map/ppermute | solution.py:285
  14.5 1.2 %collective-permute-start.4 = (f32[16,768]{1,0:T(8,128)S(1)}, f32[16,768]{1,0:T(8,128)S(1)}, u32[]{:S(2)}, u32[]{:S(2)}) collective-permute-start(f32[16,768]{1,0:T(8,128)S(1)} %shard_map.57.e.z1), channel_id=1, source_target_pairs={{0,4},{1,8},{2,6},{3,7},{4,0},{5,1},{6,2},{7,3},{8,12},{9,13},{10,... | collective-permute-start | bytes 147464 | tf_op jit(solution)/shard_map/ppermute | solution.py:285
  16.2 1.2 %collective-permute-start.10 = (f32[16,768]{1,0:T(8,128)S(1)}, f32[16,768]{1,0:T(8,128)S(1)}, u32[]{:S(2)}, u32[]{:S(2)}) collective-permute-start(f32[16,768]{1,0:T(8,128)S(1)} %shard_map.59.s), channel_id=1, source_target_pairs={{0,4},{1,2},{2,6},{3,7},{4,0},{5,1},{6,5},{7,3},{8,25},{9,13},{10,... | collective-permute-start | bytes 147464 | tf_op jit(solution)/shard_map/ppermute | solution.py:285
  16.4 7.7 %collective-permute-start.9 = (f32[16,768]{1,0:T(8,128)S(1)}, f32[16,768]{1,0:T(8,128)S(1)}, u32[]{:S(2)}, u32[]{:S(2)}) collective-permute-start(f32[16,768]{1,0:T(8,128)S(1)} %shard_map.59.s), channel_id=1, source_target_pairs={{0,4},{1,0},{2,6},{3,7},{4,5},{5,1},{6,2},{7,3},{8,17},{9,13},{10,... | collective-permute-start | bytes 147464 | tf_op jit(solution)/shard_map/ppermute | solution.py:285
  24.6 1.2 %collective-permute-start.12 = (f32[16,768]{1,0:T(8,128)S(1)}, f32[16,768]{1,0:T(8,128)S(1)}, u32[]{:S(2)}, u32[]{:S(2)}) collective-permute-start(f32[16,768]{1,0:T(8,128)S(1)} %shard_map.60.s), channel_id=1, source_target_pairs={{0,4},{1,5},{2,6},{3,7},{4,0},{5,1},{6,2},{7,3},{8,12},{9,13},{10,... | collective-permute-start | bytes 147464 | tf_op jit(solution)/shard_map/ppermute | solution.py:285
  24.6 1.4 %collective-permute-start.11 = (f32[16,768]{1,0:T(8,128)S(1)}, f32[16,768]{1,0:T(8,128)S(1)}, u32[]{:S(2)}, u32[]{:S(2)}) collective-permute-start(f32[16,768]{1,0:T(8,128)S(1)} %shard_map.60.s), channel_id=1, source_target_pairs={{0,4},{1,3},{2,6},{3,7},{4,0},{5,1},{6,2},{7,5},{8,12},{9,13},{10,... | collective-permute-start | bytes 147464 | tf_op jit(solution)/shard_map/ppermute | solution.py:285
  27.0 1.3 %collective-permute-start.13 = (f32[16,768]{1,0:T(8,128)S(1)}, f32[16,768]{1,0:T(8,128)S(1)}, u32[]{:S(2)}, u32[]{:S(2)}) collective-permute-start(f32[16,768]{1,0:T(8,128)S(1)} %get-tuple-element.24), channel_id=1, source_target_pairs={{0,4},{1,5},{2,6},{3,7},{4,0},{5,1},{6,2},{7,3},{8,12},{9,13},{10,... | collective-permute-start | bytes 147464 | tf_op jit(solution)/shard_map/ppermute | solution.py:285
  27.4 1.2 %collective-permute-start.15 = (f32[16,768]{1,0:T(8,128)S(1)}, f32[16,768]{1,0:T(8,128)S(1)}, u32[]{:S(2)}, u32[]{:S(2)}) collective-permute-start(f32[16,768]{1,0:T(8,128)S(1)} %get-tuple-element.25.t), channel_id=1, source_target_pairs={{0,4},{1,5},{2,6},{3,7},{4,0},{5,1},{6,2},{7,3},{8,12},{9,13},{10,... | collective-permute-start | bytes 147464 | tf_op jit(solution)/shard_map/ppermute | solution.py:285
  27.5 1.2 %collective-permute-start.14 = (f32[16,768]{1,0:T(8,128)S(1)}, f32[16,768]{1,0:T(8,128)S(1)}, u32[]{:S(2)}, u32[]{:S(2)}) collective-permute-start(f32[16,768]{1,0:T(8,128)S(1)} %get-tuple-element.25.t), channel_id=1, source_target_pairs={{0,4},{1,5},{2,6},{3,7},{4,0},{5,1},{6,2},{7,3},{8,12},{9,13},{10,... | collective-permute-start | bytes 147464 | tf_op jit(solution)/shard_map/ppermute | solution.py:285
  29.2 1.2 %collective-permute-start.16 = (f32[16,768]{1,0:T(8,128)S(1)}, f32[16,768]{1,0:T(8,128)S(1)}, u32[]{:S(2)}, u32[]{:S(2)}) collective-permute-start(f32[16,768]{1,0:T(8,128)S(1)} %get-tuple-element.26), channel_id=1, source_target_pairs={{0,4},{1,5},{2,6},{3,7},{4,0},{5,1},{6,2},{7,3},{8,12},{9,13},{10,... | collective-permute-start | bytes 147464 | tf_op jit(solution)/shard_map/ppermute | solution.py:285
  29.6 1.2 %collective-permute-start.17 = (f32[16,768]{1,0:T(8,128)S(1)}, f32[16,768]{1,0:T(8,128)S(1)}, u32[]{:S(2)}, u32[]{:S(2)}) collective-permute-start(f32[16,768]{1,0:T(8,128)S(1)} %get-tuple-element.27), channel_id=1, source_target_pairs={{0,4},{1,5},{2,6},{3,7},{4,0},{5,1},{6,2},{7,3},{8,12},{9,13},{10,... | collective-permute-start | bytes 147464 | tf_op jit(solution)/shard_map/ppermute | solution.py:285
  31.3 15.4 %copy-start.2 = (s32[3,64]{1,0:T(4,128)S(1)}, s32[3,64]{1,0:T(4,128)}, u32[]{:S(2)}) copy-start(s32[3,64]{1,0:T(4,128)} %screen.1) | copy-start | bytes 2308
  31.3 12.2 %collective-permute-start.21 = (f32[16,768]{1,0:T(8,128)S(1)}, f32[16,768]{1,0:T(8,128)S(1)}, u32[]{:S(2)}, u32[]{:S(2)}) collective-permute-start(f32[16,768]{1,0:T(8,128)S(1)} %get-tuple-element.29), channel_id=1, source_target_pairs={{0,4},{1,5},{2,6},{3,7},{4,20},{5,1},{6,2},{7,24},{8,3},{9,13},{10... | collective-permute-start | bytes 147464 | tf_op jit(solution)/shard_map/ppermute | solution.py:285
  31.5 12.0 %collective-permute-start.20 = (f32[16,768]{1,0:T(8,128)S(1)}, f32[16,768]{1,0:T(8,128)S(1)}, u32[]{:S(2)}, u32[]{:S(2)}) collective-permute-start(f32[16,768]{1,0:T(8,128)S(1)} %get-tuple-element.29), channel_id=1, source_target_pairs={{0,4},{1,5},{2,6},{3,7},{4,0},{5,1},{6,9},{7,17},{8,2},{9,13},{10,... | collective-permute-start | bytes 147464 | tf_op jit(solution)/shard_map/ppermute | solution.py:285
  39.9 4.0 %collective-permute-start.19 = (f32[16,768]{1,0:T(8,128)S(1)}, f32[16,768]{1,0:T(8,128)S(1)}, u32[]{:S(2)}, u32[]{:S(2)}) collective-permute-start(f32[16,768]{1,0:T(8,128)S(1)} %get-tuple-element.29), channel_id=1, source_target_pairs={{0,4},{1,5},{2,6},{3,7},{4,0},{5,12},{6,25},{7,3},{8,1},{9,13},{10... | collective-permute-start | bytes 147464 | tf_op jit(solution)/shard_map/ppermute | solution.py:285
  39.9 4.7 %collective-permute-start.18 = (f32[16,768]{1,0:T(8,128)S(1)}, f32[16,768]{1,0:T(8,128)S(1)}, u32[]{:S(2)}, u32[]{:S(2)}) collective-permute-start(f32[16,768]{1,0:T(8,128)S(1)} %get-tuple-element.29), channel_id=1, source_target_pairs={{0,4},{1,5},{2,6},{3,7},{4,12},{5,20},{6,2},{7,3},{8,0},{9,13},{10... | collective-permute-start | bytes 147464 | tf_op jit(solution)/shard_map/ppermute | solution.py:285
  40.5 4.2 %collective-permute-start.24 = (f32[16,768]{1,0:T(8,128)S(1)}, f32[16,768]{1,0:T(8,128)S(1)}, u32[]{:S(2)}, u32[]{:S(2)}) collective-permute-start(f32[16,768]{1,0:T(8,128)S(1)} %get-tuple-element.30.t), channel_id=1, source_target_pairs={{0,4},{1,5},{2,6},{3,7},{4,0},{5,1},{6,2},{7,3},{8,11},{9,13},{10,... | collective-permute-start | bytes 147464 | tf_op jit(solution)/shard_map/ppermute | solution.py:285
  43.5 1.2 %collective-permute-start.23 = (f32[16,768]{1,0:T(8,128)S(1)}, f32[16,768]{1,0:T(8,128)S(1)}, u32[]{:S(2)}, u32[]{:S(2)}) collective-permute-start(f32[16,768]{1,0:T(8,128)S(1)} %get-tuple-element.30.t), channel_id=1, source_target_pairs={{0,4},{1,5},{2,6},{3,7},{4,0},{5,1},{6,2},{7,3},{8,10},{9,13},{10,... | collective-permute-start | bytes 147464 | tf_op jit(solution)/shard_map/ppermute | solution.py:285
  43.5 1.4 %collective-permute-start.22 = (f32[16,768]{1,0:T(8,128)S(1)}, f32[16,768]{1,0:T(8,128)S(1)}, u32[]{:S(2)}, u32[]{:S(2)}) collective-permute-start(f32[16,768]{1,0:T(8,128)S(1)} %get-tuple-element.30.t), channel_id=1, source_target_pairs={{0,4},{1,5},{2,6},{3,7},{4,0},{5,1},{6,2},{7,3},{8,9},{9,13},{10,1... | collective-permute-start | bytes 147464 | tf_op jit(solution)/shard_map/ppermute | solution.py:285
  44.9 1.3 %collective-permute-start.25 = (f32[16,768]{1,0:T(8,128)S(1)}, f32[16,768]{1,0:T(8,128)S(1)}, u32[]{:S(2)}, u32[]{:S(2)}) collective-permute-start(f32[16,768]{1,0:T(8,128)S(1)} %shard_map.64.own), channel_id=1, source_target_pairs={{0,4},{4,0},{8,12},{12,8},{16,20},{20,16},{24,28},{28,24},{1,5},{5... | collective-permute-start | bytes 147464 | tf_op jit(solution)/shard_map/ppermute | solution.py:298

commit v7 on v6

--- a/solution.py
+++ b/solution.py
@@ -186,8 +186,16 @@
     out[...] = times(f0[...] + f1[...] + f2[...] + f3[...], high, low)
 
 
+def begin_late(f0, f1, f2, f3, inv, after, out):
+    begin(f0, f1, f2, f3, inv, out)
+
+
 def both(own, mate, out):
     out[...] = own[...] + mate[...]
+
+
+def both_late(zero, own, mate, out):
+    out[...] = jnp.where(block_of() == 0, zero[...], own[...] + mate[...])
 
 
 def after_zero(one, two, three, e, high, low, out):
@@ -297,31 +305,41 @@
     def swap(value):
         return lax.ppermute(value, "aux", [(i, i ^ 1) for i in range(2 * SOLVE_BLOCKS)])
 
+    def gather(blocks):
+        gathered = []
+        for step in reversed(range(1, planes)):
+            to = {}
+            for k in blocks:
+                for c in range(2):
+                    near = device((k, home[k]), c)
+                    far = device((k, (home[k] + step) % planes), c)
+                    to.update({near: far, far: near})
+            gathered.append(permute(partial_fit, to))
+        return gathered
+
     panel = struct((count, size))
     square = struct((size, size), BF16)
+    diag_late, factor_late, partial_fit = lax.optimization_barrier((diag_inv, factor, partial_fit))
+    inv_other = permute(diag_late, {})
+    fac_other = permute(factor_late, {})
+    home = [1] + list(range(SOLVE_BLOCKS - 1))
+    gathered = gather([0])
+    gathered_late = gather(range(1, SOLVE_BLOCKS))
+    e = call(begin, panel, partial_fit, *gathered, diag_inv)
+    e = call(both, panel, e, swap(e))
+    reach = [send(e, ((0, 1), (k, 0))) for k in range(1, SOLVE_BLOCKS)]
     k_high, k_low, kt_high, kt_low = call(
         prepare,
         [square] * 4,
         diag_inv,
-        swap(diag_inv),
+        inv_other,
         factor,
-        swap(factor),
+        fac_other,
         limit=32,
         scratch=[pltpu.VMEM((3 * size, size), BF16)] * 2,
     )
-    home = [1] + list(range(SOLVE_BLOCKS - 1))
-    gathered = []
-    for step in reversed(range(1, planes)):
-        to = {}
-        for k in range(SOLVE_BLOCKS):
-            for c in range(2):
-                near = device((k, home[k]), c)
-                far = device((k, (home[k] + step) % planes), c)
-                to.update({near: far, far: near})
-        gathered.append(permute(partial_fit, to))
-    e = call(begin, panel, partial_fit, *gathered, diag_inv)
-    e = call(both, panel, e, swap(e))
-    reach = [send(e, ((0, 1), (k, 0))) for k in range(1, SOLVE_BLOCKS)]
+    e_late = call(begin_late, panel, partial_fit, *gathered_late, diag_inv, k_high)
+    e = call(both_late, panel, e, e_late, swap(e_late))
     one = call(after_zero, panel, *reach, e, kt_high, kt_low)
     first = send(one, ((1, 0), (2, 1)), ((3, 0), (3, 1)), ((0, 1), (0, 0)))
     second = send(one, ((1, 0), (3, 1)), ((2, 0), (2, 1)), ((0, 1), (0, 2)))

time: 61.5 us -> 65.9 us (1.072)
  starting transfers between devices: 21.7 us -> 30.8 us
  waiting for transfers between devices: 16.9 us -> 10.6 us
  blocking collectives: 12.2 us -> 13.2 us
    ppermute x22 -> x27, starting transfers between devices: 20.7 us -> 30 us  [permute(): return lax.ppermute(value, AXES, sorted(to.items()))]
    ppermute x22 -> x27, waiting for transfers between devices: 14.8 us -> 9.64 us  [permute(): return lax.ppermute(value, AXES, sorted(to.items()))]
    ppermute x4 -> x3, waiting for transfers between devices: 2.14 us -> 1 us  [swap(): lax.ppermute(value, 'aux', [(i, i ^ 1) for i in range(2 * SOLVE_BLOCKS)])]
    all_to_all x1, blocking collectives: 12.2 us -> 13.2 us  [scatter_sum(): arrived = lax.all_to_all(slabs, 'aux', 0, 0, tiled=True)]
    pallas_call x12 -> x14, Pallas kernels: 9.78 us -> 10.2 us  [call(): pl.pallas_call(kernel, out_shape=outs, in_specs=specs or [VMEM] * len(ope...]
  transfers between devices with their start and end apart: 26 -> 30, of which waited for: 19 -> 20; matrix products, arithmetic and copies ran while one was open for 0% -> 0% of each run, Pallas kernels for 7% -> 1%
where the time goes in v7:
time: 65.9 us; the launch traced here: 65.7 us
  starting transfers between devices  30.8 us (47%)
  blocking collectives  13.2 us (20%)
  waiting for transfers between devices  10.6 us (16%)
  Pallas kernels  10.2 us (15%)
  other arithmetic  0.67 us (1%)
    ppermute x27, starting transfers between devices, permute(): return lax.ppermute(value, AXES, sorted(to.items()))  30 us
    all_to_all x1, blocking collectives, scatter_sum(): arrived = lax.all_to_all(slabs, 'aux', 0, 0, tiled=True)  13.2 us
    pallas_call x14, Pallas kernels, call(): pl.pallas_call(kernel, out_shape=outs, in_specs=specs or [VMEM] * len(ope...  10.2 us
    ppermute x27, waiting for transfers between devices, permute(): return lax.ppermute(value, AXES, sorted(to.items()))  9.64 us
  transfers between devices with their start and end apart: 30, of which 20 were waited for; matrix products, arithmetic and copies ran while one was open for 0% of the time, Pallas kernels for 1%

profile of v7, /device:TPU:0, one launch (start us, length us, event | category | flops | bytes accessed | tf_op | source)
XLA Modules:
  0.0 65.7 jit_solution(16751998413359779168)
XLA Ops:
  0.0 4.3 %shard_map.55 = (bf16[384,4096]{1,0:T(8,128)(2,1)S(1)}, bf16[384,4096]{1,0:T(8,128)(2,1)S(1)}, f32[16,384]{1,0:T(8,128)S(1)}) custom-call(s32[3,64]{1,0:T(4,128)} %screen.1, bf16[16,8192]{1,0:T(8,128)(2,1)} %densities_in.1, bf16[384,8192]{1,0:T(8,128)(2,1)} %integrals.1), custom_call_target="tpu_custom_call" | custom-call | tf_op jit(solution)/shard_map/pallas_call | solution.py:28
  4.4 0.6 collective-permute-start.10
  5.0 3.0 %collective-permute-start = (f32[16,384]{1,0:T(8,128)S(1)}, f32[16,384]{1,0:T(8,128)S(1)}, u32[]{:S(2)}, u32[]{:S(2)}) collective-permute-start(f32[16,384]{1,0:T(8,128)S(1)} %get-tuple-element.23.f0), channel_id=1, source_target_pairs={{0,1},{1,0},{2,6},{3,7},{4,5},{5,4},{6,2},{7,3},{8,12},{9,13},{10,... | collective-permute-start | bytes 73736 | tf_op jit(solution)/shard_map/ppermute | solution.py:293
  8.0 0.5 collective-permute-start.2
  8.5 1.3 %collective-permute-done.f1 = f32[16,384]{1,0:T(8,128)S(1)} collective-permute-done((f32[16,384]{1,0:T(8,128)S(1)}, f32[16,384]{1,0:T(8,128)S(1)}, u32[]{:S(2)}, u32[]{:S(2)}) %collective-permute-start) | collective-permute-done | bytes 24608 | tf_op jit(solution)/shard_map/ppermute | solution.py:293
  10.1 0.5 collective-permute-start.7
  10.7 0.5 collective-permute-start.9
  12.3 0.4 collective-permute-start.12
  13.6 0.4 collective-permute-done.4.one
  14.5 0.5 shard_map.61.s
  15.2 13.0 %collective-permute-start.14 = (f32[16,768]{1,0:T(8,128)S(1)}, f32[16,768]{1,0:T(8,128)S(1)}, u32[]{:S(2)}, u32[]{:S(2)}) collective-permute-start(f32[16,768]{1,0:T(8,128)S(1)} %shard_map.61.s), channel_id=1, source_target_pairs={{0,4},{1,2},{2,6},{3,7},{4,0},{5,1},{6,5},{7,3},{8,25},{9,13},{10,... | collective-permute-start | bytes 147464 | tf_op jit(solution)/shard_map/ppermute | solution.py:293
  28.2 0.9 %collective-permute-done.14.second.z2 = f32[16,768]{1,0:T(8,128)S(1)} collective-permute-done((f32[16,768]{1,0:T(8,128)S(1)}, f32[16,768]{1,0:T(8,128)S(1)}, u32[]{:S(2)}, u32[]{:S(2)}) %collective-permute-start.14) | collective-permute-done | bytes 49184 | tf_op jit(solution)/shard_map/ppermute | solution.py:293
  29.1 0.5 shard_map.62.s
  29.5 0.4 collective-permute-start.15
  30.1 0.7 %collective-permute-done.15.behind.z3 = f32[16,768]{1,0:T(8,128)S(1)} collective-permute-done((f32[16,768]{1,0:T(8,128)S(1)}, f32[16,768]{1,0:T(8,128)S(1)}, u32[]{:S(2)}, u32[]{:S(2)}) %collective-permute-start.15) | collective-permute-done | bytes 49184 | tf_op jit(solution)/shard_map/ppermute | solution.py:293
  31.1 1.0 %shard_map.63 = (f32[16,768]{1,0:T(8,128)S(1)}, f32[16,768]{1,0:T(8,128)S(1)}) custom-call(f32[16,768]{1,0:T(8,128)S(1)} %collective-permute-done.16.known, f32[16,768]{1,0:T(8,128)S(1)} %collective-permute-done.15.behind.z3, f32[16,768]{1,0:T(8,128)S(1)} %shard_map.60.e.z1, bf16[768,768]{1,0:T(8,128)(2,1)S(1)} %get-tuple-element.27.high.kt_high, ...), custom_call_target="tpu_custom_call" | custom-call | tf_op jit(solution)/shard_map/pallas_call | solution.py:28
  32.9 0.6 collective-permute-done.17.into
  33.9 0.5 shard_map.64
  34.9 0.7 %collective-permute-done.20.into = f32[16,768]{1,0:T(8,128)S(1)} collective-permute-done((f32[16,768]{1,0:T(8,128)S(1)}, f32[16,768]{1,0:T(8,128)S(1)}, u32[]{:S(2)}, u32[]{:S(2)}) %collective-permute-start.20) | collective-permute-done | bytes 49184 | tf_op jit(solution)/shard_map/ppermute | solution.py:293
  35.8 0.5 shard_map.65
  36.7 6.5 %collective-permute-start.23 = (f32[16,768]{1,0:T(8,128)S(1)}, f32[16,768]{1,0:T(8,128)S(1)}, u32[]{:S(2)}, u32[]{:S(2)}) collective-permute-start(f32[16,768]{1,0:T(8,128)S(1)} %get-tuple-element.35), channel_id=1, source_target_pairs={{0,4},{1,5},{2,6},{3,7},{4,0},{5,12},{6,25},{7,3},{8,1},{9,13},{10... | collective-permute-start | bytes 147464 | tf_op jit(solution)/shard_map/ppermute | solution.py:293
  43.1 0.5 collective-permute-start.25
  43.7 1.3 %collective-permute-start.26 = (f32[16,768]{1,0:T(8,128)S(1)}, f32[16,768]{1,0:T(8,128)S(1)}, u32[]{:S(2)}, u32[]{:S(2)}) collective-permute-start(f32[16,768]{1,0:T(8,128)S(1)} %get-tuple-element.36.t), channel_id=1, source_target_pairs={{0,4},{1,5},{2,6},{3,7},{4,0},{5,1},{6,2},{7,3},{8,9},{9,13},{10,1... | collective-permute-start | bytes 147464 | tf_op jit(solution)/shard_map/ppermute | solution.py:293
  45.0 1.8 %collective-permute-done.22.i0 = f32[16,768]{1,0:T(8,128)S(1)} collective-permute-done((f32[16,768]{1,0:T(8,128)S(1)}, f32[16,768]{1,0:T(8,128)S(1)}, u32[]{:S(2)}, u32[]{:S(2)}) %collective-permute-start.22) | collective-permute-done | bytes 49184 | tf_op jit(solution)/shard_map/ppermute | solution.py:293
  46.8 0.5 collective-permute-start.28
  47.3 0.7 %collective-permute-done.27.p2 = f32[16,768]{1,0:T(8,128)S(1)} collective-permute-done((f32[16,768]{1,0:T(8,128)S(1)}, f32[16,768]{1,0:T(8,128)S(1)}, u32[]{:S(2)}, u32[]{:S(2)}) %collective-permute-start.27) | collective-permute-done | bytes 49184 | tf_op jit(solution)/shard_map/ppermute | solution.py:293
  48.2 0.4 collective-permute-start.29
  48.6 0.9 %collective-permute-done.29.mate = f32[16,768]{1,0:T(8,128)S(1)} collective-permute-done((f32[16,768]{1,0:T(8,128)S(1)}, f32[16,768]{1,0:T(8,128)S(1)}, u32[]{:S(2)}, u32[]{:S(2)}) %collective-permute-start.29) | collective-permute-done | bytes 49184 | tf_op jit(solution)/shard_map/ppermute | solution.py:306
  49.5 0.4 shard_map.67.rounded
  49.9 1.8 %shard_map.68 = bf16[8,16,1024]{2,1,0:T(8,128)(2,1)S(1)} custom-call(s32[3,64]{1,0:T(4,128)S(1)} %copy-done.2, bf16[16,384]{1,0:T(8,128)(2,1)S(1)} %shard_map.67.rounded, bf16[384,4096]{1,0:T(8,128)(2,1)S(1)} %get-tuple-element.37.left, bf16[384,4096]{1,0:T(8,128)(2,1)S(1)} %get-tuple-element.38.right), custom_call_target="tpu_custom_call" | custom-call | tf_op jit(solution)/shard_map/pallas_call | solution.py:28
  51.8 13.2 %all_to_all.5 = bf16[8,16,1024]{2,1,0:T(8,128)(2,1)S(1)} all-to-all(bf16[8,16,1024]{2,1,0:T(8,128)(2,1)S(1)} %shard_map.68), channel_id=1, replica_groups=mesh['aux'=8,'pair'=4] {'aux'}, dimensions={0} | all-to-all | bytes 524288 | tf_op jit(solution)/shard_map/all_to_all | solution.py:144
  65.0 0.7 %convert_reduce_fusion = f32[16,1024]{1,0:T(8,128)} fusion(bf16[8,16,1024]{2,1,0:T(8,128)(2,1)S(1)} %all_to_all.5), kind=kLoop, calls=%fused_computation | loop fusion | flops 245760 | bytes 327680 | tf_op jit(solution)/shard_map/reduce_sum | solution.py:145
  (50 shorter events, 6.2 us)
Async XLA Ops:
  0.0 4.9 %copy-start.1 = (f32[384,768]{1,0:T(8,128)S(1)}, f32[384,768]{1,0:T(8,128)}, u32[]{:S(2)}) copy-start(f32[384,768]{1,0:T(8,128)} %fac0.1) | copy-start | bytes 3538948
  4.4 6.3 %collective-permute-start.10 = (f32[384,768]{1,0:T(8,128)S(1)}, f32[384,768]{1,0:T(8,128)S(1)}, u32[]{:S(2)}, u32[]{:S(2)}) collective-permute-start(f32[384,768]{1,0:T(8,128)S(1)} %copy-done), channel_id=1, source_target_pairs={{0,4},{1,5},{2,6},{3,7},{4,0},{5,1},{6,2},{7,3},{8,12},{9,13},{10,... | collective-permute-start | bytes 3538952 | tf_op jit(solution)/shard_map/ppermute | solution.py:293
  4.9 6.2 %collective-permute-start.11 = (f32[384,768]{1,0:T(8,128)S(1)}, f32[384,768]{1,0:T(8,128)S(1)}, u32[]{:S(2)}, u32[]{:S(2)}) collective-permute-start(f32[384,768]{1,0:T(8,128)S(1)} %copy-done.1), channel_id=1, source_target_pairs={{0,4},{1,5},{2,6},{3,7},{4,0},{5,1},{6,2},{7,3},{8,12},{9,13},{10,... | collective-permute-start | bytes 3538952 | tf_op jit(solution)/shard_map/ppermute | solution.py:293
  5.0 4.8 %collective-permute-start = (f32[16,384]{1,0:T(8,128)S(1)}, f32[16,384]{1,0:T(8,128)S(1)}, u32[]{:S(2)}, u32[]{:S(2)}) collective-permute-start(f32[16,384]{1,0:T(8,128)S(1)} %get-tuple-element.23.f0), channel_id=1, source_target_pairs={{0,1},{1,0},{2,6},{3,7},{4,5},{5,4},{6,2},{7,3},{8,12},{9,13},{10,... | collective-permute-start | bytes 73736 | tf_op jit(solution)/shard_map/ppermute | solution.py:293
  8.0 1.8 %collective-permute-start.1 = (f32[16,384]{1,0:T(8,128)S(1)}, f32[16,384]{1,0:T(8,128)S(1)}, u32[]{:S(2)}, u32[]{:S(2)}) collective-permute-start(f32[16,384]{1,0:T(8,128)S(1)} %get-tuple-element.23.f0), channel_id=1, source_target_pairs={{0,4},{1,3},{2,6},{3,1},{4,0},{5,7},{6,2},{7,5},{8,12},{9,13},{10,... | collective-permute-start | bytes 73736 | tf_op jit(solution)/shard_map/ppermute | solution.py:293
  8.0 1.8 %collective-permute-start.2 = (f32[16,384]{1,0:T(8,128)S(1)}, f32[16,384]{1,0:T(8,128)S(1)}, u32[]{:S(2)}, u32[]{:S(2)}) collective-permute-start(f32[16,384]{1,0:T(8,128)S(1)} %get-tuple-element.23.f0), channel_id=1, source_target_pairs={{0,4},{1,2},{2,1},{3,7},{4,0},{5,6},{6,5},{7,3},{8,12},{9,13},{10,... | collective-permute-start | bytes 73736 | tf_op jit(solution)/shard_map/ppermute | solution.py:293
  10.1 2.6 %collective-permute-start.3 = (f32[16,768]{1,0:T(8,128)S(1)}, f32[16,768]{1,0:T(8,128)S(1)}, u32[]{:S(2)}, u32[]{:S(2)}) collective-permute-start(f32[16,768]{1,0:T(8,128)S(1)} %shard_map.56.own), channel_id=1, source_target_pairs={{0,4},{4,0},{8,12},{12,8},{16,20},{20,16},{24,28},{28,24},{1,5},{5... | collective-permute-start | bytes 147464 | tf_op jit(solution)/shard_map/ppermute | solution.py:306
  10.1 1.4 %collective-permute-start.7 = (f32[16,384]{1,0:T(8,128)S(1)}, f32[16,384]{1,0:T(8,128)S(1)}, u32[]{:S(2)}, u32[]{:S(2)}) collective-permute-start(f32[16,384]{1,0:T(8,128)S(1)} %get-tuple-element.23.f0), channel_id=1, source_target_pairs={{0,4},{1,5},{2,6},{3,7},{4,0},{5,1},{6,2},{7,3},{8,11},{9,13},{10,... | collective-permute-start | bytes 73736 | tf_op jit(solution)/shard_map/ppermute | solution.py:293
  10.6 1.2 %collective-permute-start.8 = (f32[16,384]{1,0:T(8,128)S(1)}, f32[16,384]{1,0:T(8,128)S(1)}, u32[]{:S(2)}, u32[]{:S(2)}) collective-permute-start(f32[16,384]{1,0:T(8,128)S(1)} %get-tuple-element.23.f0), channel_id=1, source_target_pairs={{0,4},{1,5},{2,6},{3,7},{4,0},{5,1},{6,2},{7,3},{8,10},{9,13},{10,... | collective-permute-start | bytes 73736 | tf_op jit(solution)/shard_map/ppermute | solution.py:293
  10.7 1.3 %collective-permute-start.9 = (f32[16,384]{1,0:T(8,128)S(1)}, f32[16,384]{1,0:T(8,128)S(1)}, u32[]{:S(2)}, u32[]{:S(2)}) collective-permute-start(f32[16,384]{1,0:T(8,128)S(1)} %get-tuple-element.23.f0), channel_id=1, source_target_pairs={{0,4},{1,5},{2,6},{3,7},{4,0},{5,1},{6,2},{7,3},{8,9},{9,8},{10,14... | collective-permute-start | bytes 73736 | tf_op jit(solution)/shard_map/ppermute | solution.py:293
  12.3 1.3 %collective-permute-start.12 = (f32[16,768]{1,0:T(8,128)S(1)}, f32[16,768]{1,0:T(8,128)S(1)}, u32[]{:S(2)}, u32[]{:S(2)}) collective-permute-start(f32[16,768]{1,0:T(8,128)S(1)} %shard_map.59.own), channel_id=1, source_target_pairs={{0,4},{4,0},{8,12},{12,8},{16,20},{20,16},{24,28},{28,24},{1,5},{5... | collective-permute-start | bytes 147464 | tf_op jit(solution)/shard_map/ppermute | solution.py:306
  12.7 1.3 %collective-permute-start.4 = (f32[16,768]{1,0:T(8,128)S(1)}, f32[16,768]{1,0:T(8,128)S(1)}, u32[]{:S(2)}, u32[]{:S(2)}) collective-permute-start(f32[16,768]{1,0:T(8,128)S(1)} %shard_map.57.zero), channel_id=1, source_target_pairs={{0,4},{1,8},{2,6},{3,7},{4,0},{5,1},{6,2},{7,3},{8,12},{9,13},{10,... | collective-permute-start | bytes 147464 | tf_op jit(solution)/shard_map/ppermute | solution.py:293
  12.9 1.2 %collective-permute-start.5 = (f32[16,768]{1,0:T(8,128)S(1)}, f32[16,768]{1,0:T(8,128)S(1)}, u32[]{:S(2)}, u32[]{:S(2)}) collective-permute-start(f32[16,768]{1,0:T(8,128)S(1)} %shard_map.57.zero), channel_id=1, source_target_pairs={{0,4},{1,16},{2,6},{3,7},{4,0},{5,1},{6,2},{7,3},{8,12},{9,13},{10... | collective-permute-start | bytes 147464 | tf_op jit(solution)/shard_map/ppermute | solution.py:293
  13.3 1.2 %collective-permute-start.6 = (f32[16,768]{1,0:T(8,128)S(1)}, f32[16,768]{1,0:T(8,128)S(1)}, u32[]{:S(2)}, u32[]{:S(2)}) collective-permute-start(f32[16,768]{1,0:T(8,128)S(1)} %shard_map.57.zero), channel_id=1, source_target_pairs={{0,4},{1,24},{2,6},{3,7},{4,0},{5,1},{6,2},{7,3},{8,12},{9,13},{10... | collective-permute-start | bytes 147464 | tf_op jit(solution)/shard_map/ppermute | solution.py:293
  15.0 13.2 %collective-permute-start.13 = (f32[16,768]{1,0:T(8,128)S(1)}, f32[16,768]{1,0:T(8,128)S(1)}, u32[]{:S(2)}, u32[]{:S(2)}) collective-permute-start(f32[16,768]{1,0:T(8,128)S(1)} %shard_map.61.s), channel_id=1, source_target_pairs={{0,4},{1,0},{2,6},{3,7},{4,5},{5,1},{6,2},{7,3},{8,17},{9,13},{10,... | collective-permute-start | bytes 147464 | tf_op jit(solution)/shard_map/ppermute | solution.py:293
  15.2 13.9 %collective-permute-start.14 = (f32[16,768]{1,0:T(8,128)S(1)}, f32[16,768]{1,0:T(8,128)S(1)}, u32[]{:S(2)}, u32[]{:S(2)}) collective-permute-start(f32[16,768]{1,0:T(8,128)S(1)} %shard_map.61.s), channel_id=1, source_target_pairs={{0,4},{1,2},{2,6},{3,7},{4,0},{5,1},{6,5},{7,3},{8,25},{9,13},{10,... | collective-permute-start | bytes 147464 | tf_op jit(solution)/shard_map/ppermute | solution.py:293
  29.5 1.2 %collective-permute-start.15 = (f32[16,768]{1,0:T(8,128)S(1)}, f32[16,768]{1,0:T(8,128)S(1)}, u32[]{:S(2)}, u32[]{:S(2)}) collective-permute-start(f32[16,768]{1,0:T(8,128)S(1)} %shard_map.62.s), channel_id=1, source_target_pairs={{0,4},{1,3},{2,6},{3,7},{4,0},{5,1},{6,2},{7,5},{8,12},{9,13},{10,... | collective-permute-start | bytes 147464 | tf_op jit(solution)/shard_map/ppermute | solution.py:293
  29.9 1.2 %collective-permute-start.16 = (f32[16,768]{1,0:T(8,128)S(1)}, f32[16,768]{1,0:T(8,128)S(1)}, u32[]{:S(2)}, u32[]{:S(2)}) collective-permute-start(f32[16,768]{1,0:T(8,128)S(1)} %shard_map.62.s), channel_id=1, source_target_pairs={{0,4},{1,5},{2,6},{3,7},{4,0},{5,1},{6,2},{7,3},{8,12},{9,13},{10,... | collective-permute-start | bytes 147464 | tf_op jit(solution)/shard_map/ppermute | solution.py:293
  32.2 1.2 %collective-permute-start.17 = (f32[16,768]{1,0:T(8,128)S(1)}, f32[16,768]{1,0:T(8,128)S(1)}, u32[]{:S(2)}, u32[]{:S(2)}) collective-permute-start(f32[16,768]{1,0:T(8,128)S(1)} %get-tuple-element.30), channel_id=1, source_target_pairs={{0,4},{1,5},{2,6},{3,7},{4,0},{5,1},{6,2},{7,3},{8,12},{9,13},{10,... | collective-permute-start | bytes 147464 | tf_op jit(solution)/shard_map/ppermute | solution.py:293
  32.3 1.2 %collective-permute-start.18 = (f32[16,768]{1,0:T(8,128)S(1)}, f32[16,768]{1,0:T(8,128)S(1)}, u32[]{:S(2)}, u32[]{:S(2)}) collective-permute-start(f32[16,768]{1,0:T(8,128)S(1)} %get-tuple-element.31.t), channel_id=1, source_target_pairs={{0,4},{1,5},{2,6},{3,7},{4,0},{5,1},{6,2},{7,3},{8,12},{9,13},{10,... | collective-permute-start | bytes 147464 | tf_op jit(solution)/shard_map/ppermute | solution.py:293
  32.7 1.2 %collective-permute-start.19 = (f32[16,768]{1,0:T(8,128)S(1)}, f32[16,768]{1,0:T(8,128)S(1)}, u32[]{:S(2)}, u32[]{:S(2)}) collective-permute-start(f32[16,768]{1,0:T(8,128)S(1)} %get-tuple-element.31.t), channel_id=1, source_target_pairs={{0,4},{1,5},{2,6},{3,7},{4,0},{5,1},{6,2},{7,3},{8,12},{9,13},{10,... | collective-permute-start | bytes 147464 | tf_op jit(solution)/shard_map/ppermute | solution.py:293
  34.4 1.2 %collective-permute-start.20 = (f32[16,768]{1,0:T(8,128)S(1)}, f32[16,768]{1,0:T(8,128)S(1)}, u32[]{:S(2)}, u32[]{:S(2)}) collective-permute-start(f32[16,768]{1,0:T(8,128)S(1)} %get-tuple-element.32), channel_id=1, source_target_pairs={{0,4},{1,5},{2,6},{3,7},{4,0},{5,1},{6,2},{7,3},{8,12},{9,13},{10,... | collective-permute-start | bytes 147464 | tf_op jit(solution)/shard_map/ppermute | solution.py:293
  34.6 1.2 %collective-permute-start.21 = (f32[16,768]{1,0:T(8,128)S(1)}, f32[16,768]{1,0:T(8,128)S(1)}, u32[]{:S(2)}, u32[]{:S(2)}) collective-permute-start(f32[16,768]{1,0:T(8,128)S(1)} %get-tuple-element.33), channel_id=1, source_target_pairs={{0,4},{1,5},{2,6},{3,7},{4,0},{5,1},{6,2},{7,3},{8,12},{9,13},{10,... | collective-permute-start | bytes 147464 | tf_op jit(solution)/shard_map/ppermute | solution.py:293
  36.3 13.7 %copy-start.2 = (s32[3,64]{1,0:T(4,128)S(1)}, s32[3,64]{1,0:T(4,128)}, u32[]{:S(2)}) copy-start(s32[3,64]{1,0:T(4,128)} %screen.1) | copy-start | bytes 2308
  36.3 10.5 %collective-permute-start.22 = (f32[16,768]{1,0:T(8,128)S(1)}, f32[16,768]{1,0:T(8,128)S(1)}, u32[]{:S(2)}, u32[]{:S(2)}) collective-permute-start(f32[16,768]{1,0:T(8,128)S(1)} %get-tuple-element.35), channel_id=1, source_target_pairs={{0,4},{1,5},{2,6},{3,7},{4,12},{5,20},{6,2},{7,3},{8,0},{9,13},{10... | collective-permute-start | bytes 147464 | tf_op jit(solution)/shard_map/ppermute | solution.py:293
  36.7 10.1 %collective-permute-start.23 = (f32[16,768]{1,0:T(8,128)S(1)}, f32[16,768]{1,0:T(8,128)S(1)}, u32[]{:S(2)}, u32[]{:S(2)}) collective-permute-start(f32[16,768]{1,0:T(8,128)S(1)} %get-tuple-element.35), channel_id=1, source_target_pairs={{0,4},{1,5},{2,6},{3,7},{4,0},{5,12},{6,25},{7,3},{8,1},{9,13},{10... | collective-permute-start | bytes 147464 | tf_op jit(solution)/shard_map/ppermute | solution.py:293
  43.1 4.1 %collective-permute-start.24 = (f32[16,768]{1,0:T(8,128)S(1)}, f32[16,768]{1,0:T(8,128)S(1)}, u32[]{:S(2)}, u32[]{:S(2)}) collective-permute-start(f32[16,768]{1,0:T(8,128)S(1)} %get-tuple-element.35), channel_id=1, source_target_pairs={{0,4},{1,5},{2,6},{3,7},{4,0},{5,1},{6,9},{7,17},{8,2},{9,13},{10,... | collective-permute-start | bytes 147464 | tf_op jit(solution)/shard_map/ppermute | solution.py:293
  43.1 4.1 %collective-permute-start.25 = (f32[16,768]{1,0:T(8,128)S(1)}, f32[16,768]{1,0:T(8,128)S(1)}, u32[]{:S(2)}, u32[]{:S(2)}) collective-permute-start(f32[16,768]{1,0:T(8,128)S(1)} %get-tuple-element.35), channel_id=1, source_target_pairs={{0,4},{1,5},{2,6},{3,7},{4,20},{5,1},{6,2},{7,24},{8,3},{9,13},{10... | collective-permute-start | bytes 147464 | tf_op jit(solution)/shard_map/ppermute | solution.py:293
  43.7 3.6 %collective-permute-start.26 = (f32[16,768]{1,0:T(8,128)S(1)}, f32[16,768]{1,0:T(8,128)S(1)}, u32[]{:S(2)}, u32[]{:S(2)}) collective-permute-start(f32[16,768]{1,0:T(8,128)S(1)} %get-tuple-element.36.t), channel_id=1, source_target_pairs={{0,4},{1,5},{2,6},{3,7},{4,0},{5,1},{6,2},{7,3},{8,9},{9,13},{10,1... | collective-permute-start | bytes 147464 | tf_op jit(solution)/shard_map/ppermute | solution.py:293
  46.7 1.2 %collective-permute-start.27 = (f32[16,768]{1,0:T(8,128)S(1)}, f32[16,768]{1,0:T(8,128)S(1)}, u32[]{:S(2)}, u32[]{:S(2)}) collective-permute-start(f32[16,768]{1,0:T(8,128)S(1)} %get-tuple-element.36.t), channel_id=1, source_target_pairs={{0,4},{1,5},{2,6},{3,7},{4,0},{5,1},{6,2},{7,3},{8,10},{9,13},{10,... | collective-permute-start | bytes 147464 | tf_op jit(solution)/shard_map/ppermute | solution.py:293
  46.8 1.4 %collective-permute-start.28 = (f32[16,768]{1,0:T(8,128)S(1)}, f32[16,768]{1,0:T(8,128)S(1)}, u32[]{:S(2)}, u32[]{:S(2)}) collective-permute-start(f32[16,768]{1,0:T(8,128)S(1)} %get-tuple-element.36.t), channel_id=1, source_target_pairs={{0,4},{1,5},{2,6},{3,7},{4,0},{5,1},{6,2},{7,3},{8,11},{9,13},{10,... | collective-permute-start | bytes 147464 | tf_op jit(solution)/shard_map/ppermute | solution.py:293
  48.2 1.3 %collective-permute-start.29 = (f32[16,768]{1,0:T(8,128)S(1)}, f32[16,768]{1,0:T(8,128)S(1)}, u32[]{:S(2)}, u32[]{:S(2)}) collective-permute-start(f32[16,768]{1,0:T(8,128)S(1)} %shard_map.66.own), channel_id=1, source_target_pairs={{0,4},{4,0},{8,12},{12,8},{16,20},{20,16},{24,28},{28,24},{1,5},{5... | collective-permute-start | bytes 147464 | tf_op jit(solution)/shard_map/ppermute | solution.py:306
  (1 other events, 4.4 us)

commit v8 on v7

--- a/solution.py
+++ b/solution.py
@@ -7,6 +7,7 @@
 
 TILE = 128
 SOLVE_BLOCKS = 4
+LEAD = 1
 AXES = ("aux", "pair")
 HIGHEST = lax.Precision.HIGHEST
 F32 = jnp.float32
@@ -159,35 +160,38 @@
     return both[:rows] + both[rows:]
 
 
-def prepare(inv0, inv1, fac0, fac1, k_high, k_low, kt_high, kt_low, lhs, rhs):
-    height = inv0.shape[0]
-
-    @pl.when((block_of() > 0) & (side_of() == 0))
+def prepare(inv_own, inv_mate, fac_own, fac_mate, k_high, k_low, kt_high, kt_low, lhs, rhs):
+    height = inv_own.shape[0]
+    halves = [(inv_own, fac_own), (inv_mate, fac_mate)]
+    if LEAD == 1:
+        halves.reverse()
+
+    @pl.when((block_of() > 0) & (side_of() == LEAD))
     def _():
-        for n, (inv, fac) in enumerate(((inv0, fac0), (inv1, fac1))):
+        for n, (inv, fac) in enumerate(halves):
             rows = [slice((3 * n + r) * height, (3 * n + r + 1) * height) for r in range(3)]
             high, low = high_low(inv[...])
             lhs[rows[0], :], lhs[rows[1], :], lhs[rows[2], :] = high, low, high
             high, low = high_low(fac[...])
             rhs[rows[0], :], rhs[rows[1], :], rhs[rows[2], :] = high, high, low
         depth = 3 * height
-        halves = (
+        parts = (
             (slice(0, height), slice(0, depth)),
             (slice(height, 2 * height), slice(0, 2 * depth)),
         )
-        for part, used in halves:
+        for part, used in parts:
             product = lax.dot_general(lhs[used, part], rhs[used, :], TN, preferred_element_type=F32)
             k_high[part, :], k_low[part, :] = high_low(product)
             kt_high[:, part], kt_low[:, part] = high_low(product.T)
 
 
-def begin(f0, f1, f2, f3, inv, out):
+def begin(f0, f1, f2, f3, inv, after, out):
+    begin_late(f0, f1, f2, f3, inv, out)
+
+
+def begin_late(f0, f1, f2, f3, inv, out):
     high, low = high_low(inv[...])
     out[...] = times(f0[...] + f1[...] + f2[...] + f3[...], high, low)
-
-
-def begin_late(f0, f1, f2, f3, inv, after, out):
-    begin(f0, f1, f2, f3, inv, out)
 
 
 def both(own, mate, out):
@@ -264,7 +268,7 @@
 
 
 def finish(own, mate, inv, out):
-    value = jnp.where(side_of() == 0, own[...], mate[...])
+    value = jnp.where(side_of() == LEAD, own[...], mate[...])
     high, low = high_low(inv[...])
     out[...] = times(value, high, low, NT).astype(out.dtype)
 
@@ -295,39 +299,36 @@
     def send(value, *moves):
         to = {}
         for source, target, *via in moves:
-            loop = [device(source, 0), device(target, 0), device(target, 1)]
+            loop = [device(source, LEAD), device(target, LEAD), device(target, 1 - LEAD)]
             for chip in via:
-                loop += [device(chip, 0), device(chip, 1)]
-            loop.append(device(source, 1))
+                loop += [device(chip, LEAD), device(chip, 1 - LEAD)]
+            loop.append(device(source, 1 - LEAD))
             to.update(zip(loop, loop[1:] + loop[:1]))
         return permute(value, to)
 
     def swap(value):
         return lax.ppermute(value, "aux", [(i, i ^ 1) for i in range(2 * SOLVE_BLOCKS)])
 
-    def gather(blocks):
+    def gather(blocks, near):
         gathered = []
-        for step in reversed(range(1, planes)):
+        for index, step in enumerate(reversed(range(1, planes))):
             to = {}
             for k in blocks:
                 for c in range(2):
-                    near = device((k, home[k]), c)
-                    far = device((k, (home[k] + step) % planes), c)
-                    to.update({near: far, far: near})
+                    loop = [device((k, (home[k] + step) % planes), c), device((k, home[k]), c)]
+                    if k in near:
+                        loop.append(device(near[k][index], c))
+                    to.update(zip(loop, loop[1:] + loop[:1]))
             gathered.append(permute(partial_fit, to))
         return gathered
 
     panel = struct((count, size))
     square = struct((size, size), BF16)
-    diag_late, factor_late, partial_fit = lax.optimization_barrier((diag_inv, factor, partial_fit))
-    inv_other = permute(diag_late, {})
-    fac_other = permute(factor_late, {})
+    inv_other = swap(diag_inv)
+    fac_other = swap(factor)
     home = [1] + list(range(SOLVE_BLOCKS - 1))
-    gathered = gather([0])
-    gathered_late = gather(range(1, SOLVE_BLOCKS))
-    e = call(begin, panel, partial_fit, *gathered, diag_inv)
-    e = call(both, panel, e, swap(e))
-    reach = [send(e, ((0, 1), (k, 0))) for k in range(1, SOLVE_BLOCKS)]
+    gathered = gather([0], {0: [(1, 1), (2, 1), (3, 1)]})
+    gathered_late = gather(range(1, SOLVE_BLOCKS), {1: [(0, 0), (0, 2), (0, 3)]})
     k_high, k_low, kt_high, kt_low = call(
         prepare,
         [square] * 4,
@@ -338,7 +339,10 @@
         limit=32,
         scratch=[pltpu.VMEM((3 * size, size), BF16)] * 2,
     )
-    e_late = call(begin_late, panel, partial_fit, *gathered_late, diag_inv, k_high)
+    e = call(begin, panel, partial_fit, *gathered, diag_inv, k_high)
+    e = call(both, panel, e, swap(e))
+    reach = [send(e, ((0, 1), (k, 0))) for k in range(1, SOLVE_BLOCKS)]
+    e_late = call(begin_late, panel, partial_fit, *gathered_late, diag_inv)
     e = call(both_late, panel, e, e_late, swap(e_late))
     one = call(after_zero, panel, *reach, e, kt_high, kt_low)
     first = send(one, ((1, 0), (2, 1)), ((3, 0), (3, 1)), ((0, 1), (0, 0)))

time: 65.9 us -> 68.4 us (1.038)
  waiting for transfers between devices: 10.6 us -> 13 us
  blocking collectives: 13.2 us -> 15.1 us
  starting transfers between devices: 30.8 us -> 29.1 us
    ppermute x27 -> x25, waiting for transfers between devices: 9.64 us -> 11.8 us  [permute(): return lax.ppermute(value, AXES, sorted(to.items()))]
    all_to_all x1, blocking collectives: 13.2 us -> 15.1 us  [scatter_sum(): arrived = lax.all_to_all(slabs, 'aux', 0, 0, tiled=True)]
    ppermute x27 -> x25, starting transfers between devices: 30 us -> 28.3 us  [permute(): return lax.ppermute(value, AXES, sorted(to.items()))]
  transfers between devices with their start and end apart: 30 -> 30, of which waited for: 20 -> 16; matrix products, arithmetic and copies ran while one was open for 0% -> 0% of each run, Pallas kernels for 1% -> 7%
where the time goes in v8:
time: 68.4 us; the launch traced here: 68.2 us
  starting transfers between devices  29.1 us (43%)
  blocking collectives  15.1 us (22%)
  waiting for transfers between devices  13 us (19%)
  Pallas kernels  10.3 us (15%)
    ppermute x25, starting transfers between devices, permute(): return lax.ppermute(value, AXES, sorted(to.items()))  28.3 us
    all_to_all x1, blocking collectives, scatter_sum(): arrived = lax.all_to_all(slabs, 'aux', 0, 0, tiled=True)  15.1 us
    ppermute x25, waiting for transfers between devices, permute(): return lax.ppermute(value, AXES, sorted(to.items()))  11.8 us
    pallas_call x14, Pallas kernels, call(): pl.pallas_call(kernel, out_shape=outs, in_specs=specs or [VMEM] * len(ope...  10.3 us
  transfers between devices with their start and end apart: 30, of which 16 were waited for; matrix products, arithmetic and copies ran while one was open for 0% of the time, Pallas kernels for 7%

profile of v8, /device:TPU:0, one launch (start us, length us, event | category | flops | bytes accessed | tf_op | source)
XLA Modules:
  0.0 68.2 jit_solution(6640575821319331595)
XLA Ops:
  0.0 0.5 collective-permute-start.4
  0.6 4.3 %shard_map.55 = (bf16[384,4096]{1,0:T(8,128)(2,1)S(1)}, bf16[384,4096]{1,0:T(8,128)(2,1)S(1)}, f32[16,384]{1,0:T(8,128)S(1)}) custom-call(s32[3,64]{1,0:T(4,128)} %screen.1, bf16[16,8192]{1,0:T(8,128)(2,1)} %densities_in.1, bf16[384,8192]{1,0:T(8,128)(2,1)} %integrals.1), custom_call_target="tpu_custom_call" | custom-call | tf_op jit(solution)/shard_map/pallas_call | solution.py:29
  4.9 0.5 collective-permute-start.2
  5.5 4.9 %collective-permute-start = (f32[16,384]{1,0:T(8,128)S(1)}, f32[16,384]{1,0:T(8,128)S(1)}, u32[]{:S(2)}, u32[]{:S(2)}) collective-permute-start(f32[16,384]{1,0:T(8,128)S(1)} %get-tuple-element.19.f0), channel_id=1, source_target_pairs={{0,1},{1,9},{2,6},{3,7},{4,5},{5,13},{6,2},{7,3},{8,12},{9,0},{10,... | collective-permute-start | bytes 73736 | tf_op jit(solution)/shard_map/ppermute | solution.py:297
  10.5 1.4 %collective-permute-done.f1 = f32[16,384]{1,0:T(8,128)S(1)} collective-permute-done((f32[16,384]{1,0:T(8,128)S(1)}, f32[16,384]{1,0:T(8,128)S(1)}, u32[]{:S(2)}, u32[]{:S(2)}) %collective-permute-start) | collective-permute-done | bytes 24608 | tf_op jit(solution)/shard_map/ppermute | solution.py:297
  12.3 0.5 collective-permute-start.11
  12.8 2.7 %collective-permute-start.9 = (f32[16,384]{1,0:T(8,128)S(1)}, f32[16,384]{1,0:T(8,128)S(1)}, u32[]{:S(2)}, u32[]{:S(2)}) collective-permute-start(f32[16,384]{1,0:T(8,128)S(1)} %get-tuple-element.19.f0), channel_id=1, source_target_pairs={{0,11},{1,5},{2,6},{3,7},{4,15},{5,1},{6,2},{7,3},{8,0},{9,13},{10... | collective-permute-start | bytes 73736 | tf_op jit(solution)/shard_map/ppermute | solution.py:297
  15.5 3.8 %collective-permute-done.9.f1 = f32[16,384]{1,0:T(8,128)S(1)} collective-permute-done((f32[16,384]{1,0:T(8,128)S(1)}, f32[16,384]{1,0:T(8,128)S(1)}, u32[]{:S(2)}, u32[]{:S(2)}) %collective-permute-start.9) | collective-permute-done | bytes 24608 | tf_op jit(solution)/shard_map/ppermute | solution.py:297
  19.7 0.6 collective-permute-start.8
  20.4 0.4 collective-permute-start.6
  21.7 0.5 shard_map.61.s
  22.5 5.8 %collective-permute-start.13 = (f32[16,768]{1,0:T(8,128)S(1)}, f32[16,768]{1,0:T(8,128)S(1)}, u32[]{:S(2)}, u32[]{:S(2)}) collective-permute-start(f32[16,768]{1,0:T(8,128)S(1)} %shard_map.61.s), channel_id=1, source_target_pairs={{0,1},{1,5},{2,6},{3,7},{4,0},{5,4},{6,2},{7,3},{8,12},{9,13},{10,... | collective-permute-start | bytes 147464 | tf_op jit(solution)/shard_map/ppermute | solution.py:297
  28.3 1.7 %collective-permute-done.13.first.z0 = f32[16,768]{1,0:T(8,128)S(1)} collective-permute-done((f32[16,768]{1,0:T(8,128)S(1)}, f32[16,768]{1,0:T(8,128)S(1)}, u32[]{:S(2)}, u32[]{:S(2)}) %collective-permute-start.13) | collective-permute-done | bytes 49184 | tf_op jit(solution)/shard_map/ppermute | solution.py:297
  30.0 0.5 shard_map.62.s
  30.5 0.5 collective-permute-start.15
  31.0 0.7 %collective-permute-done.16.known = f32[16,768]{1,0:T(8,128)S(1)} collective-permute-done((f32[16,768]{1,0:T(8,128)S(1)}, f32[16,768]{1,0:T(8,128)S(1)}, u32[]{:S(2)}, u32[]{:S(2)}) %collective-permute-start.16) | collective-permute-done | bytes 49184 | tf_op jit(solution)/shard_map/ppermute | solution.py:297
  31.9 1.0 %shard_map.63 = (f32[16,768]{1,0:T(8,128)S(1)}, f32[16,768]{1,0:T(8,128)S(1)}) custom-call(f32[16,768]{1,0:T(8,128)S(1)} %collective-permute-done.16.known, f32[16,768]{1,0:T(8,128)S(1)} %collective-permute-done.15.behind.z3, f32[16,768]{1,0:T(8,128)S(1)} %shard_map.60.e.z1, bf16[768,768]{1,0:T(8,128)(2,1)S(1)} %get-tuple-element.21.high.kt_high, ...), custom_call_target="tpu_custom_call" | custom-call | tf_op jit(solution)/shard_map/pallas_call | solution.py:29
  33.0 0.4 collective-permute-start.17
  33.8 0.4 collective-permute-done.17.into
  34.7 0.5 shard_map.64
  35.7 0.7 %collective-permute-done.20.into = f32[16,768]{1,0:T(8,128)S(1)} collective-permute-done((f32[16,768]{1,0:T(8,128)S(1)}, f32[16,768]{1,0:T(8,128)S(1)}, u32[]{:S(2)}, u32[]{:S(2)}) %collective-permute-start.20) | collective-permute-done | bytes 49184 | tf_op jit(solution)/shard_map/ppermute | solution.py:297
  36.8 0.5 shard_map.65
  37.3 7.6 %collective-permute-start.25 = (f32[16,768]{1,0:T(8,128)S(1)}, f32[16,768]{1,0:T(8,128)S(1)}, u32[]{:S(2)}, u32[]{:S(2)}) collective-permute-start(f32[16,768]{1,0:T(8,128)S(1)} %get-tuple-element.29), channel_id=1, source_target_pairs={{0,16},{1,5},{2,6},{3,28},{4,0},{5,1},{6,2},{7,3},{8,12},{9,13},{1... | collective-permute-start | bytes 147464 | tf_op jit(solution)/shard_map/ppermute | solution.py:297
  44.9 0.5 collective-permute-start.23
  45.4 1.7 %collective-permute-start.22 = (f32[16,768]{1,0:T(8,128)S(1)}, f32[16,768]{1,0:T(8,128)S(1)}, u32[]{:S(2)}, u32[]{:S(2)}) collective-permute-start(f32[16,768]{1,0:T(8,128)S(1)} %get-tuple-element.29), channel_id=1, source_target_pairs={{0,8},{1,16},{2,6},{3,7},{4,0},{5,1},{6,2},{7,3},{8,12},{9,13},{10... | collective-permute-start | bytes 147464 | tf_op jit(solution)/shard_map/ppermute | solution.py:297
  47.1 0.5 collective-permute-start.27
  47.7 1.2 %collective-permute-done.22.i0 = f32[16,768]{1,0:T(8,128)S(1)} collective-permute-done((f32[16,768]{1,0:T(8,128)S(1)}, f32[16,768]{1,0:T(8,128)S(1)}, u32[]{:S(2)}, u32[]{:S(2)}) %collective-permute-start.22) | collective-permute-done | bytes 49184 | tf_op jit(solution)/shard_map/ppermute | solution.py:297
  49.1 1.1 %collective-permute-done.29.mate = f32[16,768]{1,0:T(8,128)S(1)} collective-permute-done((f32[16,768]{1,0:T(8,128)S(1)}, f32[16,768]{1,0:T(8,128)S(1)}, u32[]{:S(2)}, u32[]{:S(2)}) %collective-permute-start.29) | collective-permute-done | bytes 49184 | tf_op jit(solution)/shard_map/ppermute | solution.py:310
  50.2 0.5 shard_map.67.rounded
  50.7 1.8 %shard_map.68 = bf16[8,16,1024]{2,1,0:T(8,128)(2,1)S(1)} custom-call(s32[3,64]{1,0:T(4,128)S(1)} %copy-done.2, bf16[16,384]{1,0:T(8,128)(2,1)S(1)} %shard_map.67.rounded, bf16[384,4096]{1,0:T(8,128)(2,1)S(1)} %get-tuple-element.31.left, bf16[384,4096]{1,0:T(8,128)(2,1)S(1)} %get-tuple-element.32.right), custom_call_target="tpu_custom_call" | custom-call | tf_op jit(solution)/shard_map/pallas_call | solution.py:29
  52.5 15.1 %all_to_all.5 = bf16[8,16,1024]{2,1,0:T(8,128)(2,1)S(1)} all-to-all(bf16[8,16,1024]{2,1,0:T(8,128)(2,1)S(1)} %shard_map.68), channel_id=1, replica_groups=mesh['aux'=8,'pair'=4] {'aux'}, dimensions={0} | all-to-all | bytes 524288 | tf_op jit(solution)/shard_map/all_to_all | solution.py:145
  67.5 0.7 convert_reduce_fusion
  (50 shorter events, 4.6 us)
Async XLA Ops:
  0.0 10.5 %copy-start = (f32[384,768]{1,0:T(8,128)S(1)}, f32[384,768]{1,0:T(8,128)}, u32[]{:S(2)}) copy-start(f32[384,768]{1,0:T(8,128)} %inv.5) | copy-start | bytes 3538948
  0.0 10.5 %collective-permute-start.4 = (f32[384,768]{1,0:T(8,128)}, f32[384,768]{1,0:T(8,128)S(1)}, u32[]{:S(2)}, u32[]{:S(2)}) collective-permute-start(f32[384,768]{1,0:T(8,128)} %fac_own.1), channel_id=1, source_target_pairs={{0,4},{4,0},{8,12},{12,8},{16,20},{20,16},{24,28},{28,24},{1,5},{5... | collective-permute-start | bytes 3538952 | tf_op jit(solution)/shard_map/ppermute | solution.py:310
  0.5 10.0 %collective-permute-start.3 = (f32[384,768]{1,0:T(8,128)}, f32[384,768]{1,0:T(8,128)S(1)}, u32[]{:S(2)}, u32[]{:S(2)}) collective-permute-start(f32[384,768]{1,0:T(8,128)} %inv.5), channel_id=1, source_target_pairs={{0,4},{4,0},{8,12},{12,8},{16,20},{20,16},{24,28},{28,24},{1,5},{5... | collective-permute-start | bytes 3538952 | tf_op jit(solution)/shard_map/ppermute | solution.py:310
  4.9 5.6 %collective-permute-start.2 = (f32[16,384]{1,0:T(8,128)S(1)}, f32[16,384]{1,0:T(8,128)S(1)}, u32[]{:S(2)}, u32[]{:S(2)}) collective-permute-start(f32[16,384]{1,0:T(8,128)S(1)} %get-tuple-element.19.f0), channel_id=1, source_target_pairs={{0,4},{1,25},{2,1},{3,7},{4,0},{5,29},{6,5},{7,3},{8,12},{9,13},{1... | collective-permute-start | bytes 73736 | tf_op jit(solution)/shard_map/ppermute | solution.py:297
  5.5 5.1 %collective-permute-start.1 = (f32[16,384]{1,0:T(8,128)S(1)}, f32[16,384]{1,0:T(8,128)S(1)}, u32[]{:S(2)}, u32[]{:S(2)}) collective-permute-start(f32[16,384]{1,0:T(8,128)S(1)} %get-tuple-element.19.f0), channel_id=1, source_target_pairs={{0,4},{1,17},{2,6},{3,1},{4,0},{5,21},{6,2},{7,5},{8,12},{9,13},{1... | collective-permute-start | bytes 73736 | tf_op jit(solution)/shard_map/ppermute | solution.py:297
  5.5 6.5 %collective-permute-start = (f32[16,384]{1,0:T(8,128)S(1)}, f32[16,384]{1,0:T(8,128)S(1)}, u32[]{:S(2)}, u32[]{:S(2)}) collective-permute-start(f32[16,384]{1,0:T(8,128)S(1)} %get-tuple-element.19.f0), channel_id=1, source_target_pairs={{0,1},{1,9},{2,6},{3,7},{4,5},{5,13},{6,2},{7,3},{8,12},{9,0},{10,... | collective-permute-start | bytes 73736 | tf_op jit(solution)/shard_map/ppermute | solution.py:297
  12.3 7.4 %collective-permute-start.5 = (f32[16,768]{1,0:T(8,128)S(1)}, f32[16,768]{1,0:T(8,128)S(1)}, u32[]{:S(2)}, u32[]{:S(2)}) collective-permute-start(f32[16,768]{1,0:T(8,128)S(1)} %shard_map.57.own), channel_id=1, source_target_pairs={{0,4},{4,0},{8,12},{12,8},{16,20},{20,16},{24,28},{28,24},{1,5},{5... | collective-permute-start | bytes 147464 | tf_op jit(solution)/shard_map/ppermute | solution.py:310
  12.3 3.2 %collective-permute-start.11 = (f32[16,384]{1,0:T(8,128)S(1)}, f32[16,384]{1,0:T(8,128)S(1)}, u32[]{:S(2)}, u32[]{:S(2)}) collective-permute-start(f32[16,384]{1,0:T(8,128)S(1)} %get-tuple-element.19.f0), channel_id=1, source_target_pairs={{0,4},{1,5},{2,6},{3,9},{4,0},{5,1},{6,2},{7,13},{8,3},{9,8},{10,1... | collective-permute-start | bytes 73736 | tf_op jit(solution)/shard_map/ppermute | solution.py:297
  12.8 2.7 %collective-permute-start.10 = (f32[16,384]{1,0:T(8,128)S(1)}, f32[16,384]{1,0:T(8,128)S(1)}, u32[]{:S(2)}, u32[]{:S(2)}) collective-permute-start(f32[16,384]{1,0:T(8,128)S(1)} %get-tuple-element.19.f0), channel_id=1, source_target_pairs={{0,4},{1,5},{2,10},{3,7},{4,0},{5,1},{6,14},{7,3},{8,2},{9,13},{10... | collective-permute-start | bytes 73736 | tf_op jit(solution)/shard_map/ppermute | solution.py:297
  12.8 6.5 %collective-permute-start.9 = (f32[16,384]{1,0:T(8,128)S(1)}, f32[16,384]{1,0:T(8,128)S(1)}, u32[]{:S(2)}, u32[]{:S(2)}) collective-permute-start(f32[16,384]{1,0:T(8,128)S(1)} %get-tuple-element.19.f0), channel_id=1, source_target_pairs={{0,11},{1,5},{2,6},{3,7},{4,15},{5,1},{6,2},{7,3},{8,0},{9,13},{10... | collective-permute-start | bytes 73736 | tf_op jit(solution)/shard_map/ppermute | solution.py:297
  19.6 1.3 %collective-permute-start.12 = (f32[16,768]{1,0:T(8,128)S(1)}, f32[16,768]{1,0:T(8,128)S(1)}, u32[]{:S(2)}, u32[]{:S(2)}) collective-permute-start(f32[16,768]{1,0:T(8,128)S(1)} %shard_map.59.own), channel_id=1, source_target_pairs={{0,4},{4,0},{8,12},{12,8},{16,20},{20,16},{24,28},{28,24},{1,5},{5... | collective-permute-start | bytes 147464 | tf_op jit(solution)/shard_map/ppermute | solution.py:310
  19.7 1.5 %collective-permute-start.8 = (f32[16,768]{1,0:T(8,128)S(1)}, f32[16,768]{1,0:T(8,128)S(1)}, u32[]{:S(2)}, u32[]{:S(2)}) collective-permute-start(f32[16,768]{1,0:T(8,128)S(1)} %shard_map.58.zero), channel_id=1, source_target_pairs={{0,4},{1,5},{2,6},{3,7},{4,0},{5,28},{6,2},{7,3},{8,12},{9,13},{10... | collective-permute-start | bytes 147464 | tf_op jit(solution)/shard_map/ppermute | solution.py:297
  20.3 1.2 %collective-permute-start.7 = (f32[16,768]{1,0:T(8,128)S(1)}, f32[16,768]{1,0:T(8,128)S(1)}, u32[]{:S(2)}, u32[]{:S(2)}) collective-permute-start(f32[16,768]{1,0:T(8,128)S(1)} %shard_map.58.zero), channel_id=1, source_target_pairs={{0,4},{1,5},{2,6},{3,7},{4,0},{5,20},{6,2},{7,3},{8,12},{9,13},{10... | collective-permute-start | bytes 147464 | tf_op jit(solution)/shard_map/ppermute | solution.py:297
  20.4 1.3 %collective-permute-start.6 = (f32[16,768]{1,0:T(8,128)S(1)}, f32[16,768]{1,0:T(8,128)S(1)}, u32[]{:S(2)}, u32[]{:S(2)}) collective-permute-start(f32[16,768]{1,0:T(8,128)S(1)} %shard_map.58.zero), channel_id=1, source_target_pairs={{0,4},{1,5},{2,6},{3,7},{4,0},{5,12},{6,2},{7,3},{8,1},{9,13},{10,... | collective-permute-start | bytes 147464 | tf_op jit(solution)/shard_map/ppermute | solution.py:297
  22.1 6.2 %collective-permute-start.14 = (f32[16,768]{1,0:T(8,128)S(1)}, f32[16,768]{1,0:T(8,128)S(1)}, u32[]{:S(2)}, u32[]{:S(2)}) collective-permute-start(f32[16,768]{1,0:T(8,128)S(1)} %shard_map.61.s), channel_id=1, source_target_pairs={{0,4},{1,5},{2,1},{3,7},{4,0},{5,6},{6,2},{7,3},{8,12},{9,13},{10,... | collective-permute-start | bytes 147464 | tf_op jit(solution)/shard_map/ppermute | solution.py:297
  22.5 7.5 %collective-permute-start.13 = (f32[16,768]{1,0:T(8,128)S(1)}, f32[16,768]{1,0:T(8,128)S(1)}, u32[]{:S(2)}, u32[]{:S(2)}) collective-permute-start(f32[16,768]{1,0:T(8,128)S(1)} %shard_map.61.s), channel_id=1, source_target_pairs={{0,1},{1,5},{2,6},{3,7},{4,0},{5,4},{6,2},{7,3},{8,12},{9,13},{10,... | collective-permute-start | bytes 147464 | tf_op jit(solution)/shard_map/ppermute | solution.py:297
  30.5 1.2 %collective-permute-start.16 = (f32[16,768]{1,0:T(8,128)S(1)}, f32[16,768]{1,0:T(8,128)S(1)}, u32[]{:S(2)}, u32[]{:S(2)}) collective-permute-start(f32[16,768]{1,0:T(8,128)S(1)} %shard_map.62.s), channel_id=1, source_target_pairs={{0,4},{1,5},{2,6},{3,7},{4,0},{5,1},{6,2},{7,3},{8,12},{9,13},{10,... | collective-permute-start | bytes 147464 | tf_op jit(solution)/shard_map/ppermute | solution.py:297
  30.5 1.4 %collective-permute-start.15 = (f32[16,768]{1,0:T(8,128)S(1)}, f32[16,768]{1,0:T(8,128)S(1)}, u32[]{:S(2)}, u32[]{:S(2)}) collective-permute-start(f32[16,768]{1,0:T(8,128)S(1)} %shard_map.62.s), channel_id=1, source_target_pairs={{0,4},{1,5},{2,6},{3,1},{4,0},{5,7},{6,2},{7,3},{8,12},{9,13},{10,... | collective-permute-start | bytes 147464 | tf_op jit(solution)/shard_map/ppermute | solution.py:297
  33.0 1.3 %collective-permute-start.17 = (f32[16,768]{1,0:T(8,128)S(1)}, f32[16,768]{1,0:T(8,128)S(1)}, u32[]{:S(2)}, u32[]{:S(2)}) collective-permute-start(f32[16,768]{1,0:T(8,128)S(1)} %get-tuple-element.24), channel_id=1, source_target_pairs={{0,4},{1,5},{2,6},{3,7},{4,0},{5,1},{6,2},{7,3},{8,12},{9,13},{10,... | collective-permute-start | bytes 147464 | tf_op jit(solution)/shard_map/ppermute | solution.py:297
  33.3 1.2 %collective-permute-start.19 = (f32[16,768]{1,0:T(8,128)S(1)}, f32[16,768]{1,0:T(8,128)S(1)}, u32[]{:S(2)}, u32[]{:S(2)}) collective-permute-start(f32[16,768]{1,0:T(8,128)S(1)} %get-tuple-element.25.t), channel_id=1, source_target_pairs={{0,4},{1,5},{2,6},{3,7},{4,0},{5,1},{6,2},{7,3},{8,12},{9,13},{10,... | collective-permute-start | bytes 147464 | tf_op jit(solution)/shard_map/ppermute | solution.py:297
  33.5 1.2 %collective-permute-start.18 = (f32[16,768]{1,0:T(8,128)S(1)}, f32[16,768]{1,0:T(8,128)S(1)}, u32[]{:S(2)}, u32[]{:S(2)}) collective-permute-start(f32[16,768]{1,0:T(8,128)S(1)} %get-tuple-element.25.t), channel_id=1, source_target_pairs={{0,4},{1,5},{2,6},{3,7},{4,0},{5,1},{6,2},{7,3},{8,12},{9,13},{10,... | collective-permute-start | bytes 147464 | tf_op jit(solution)/shard_map/ppermute | solution.py:297
  35.2 1.2 %collective-permute-start.20 = (f32[16,768]{1,0:T(8,128)S(1)}, f32[16,768]{1,0:T(8,128)S(1)}, u32[]{:S(2)}, u32[]{:S(2)}) collective-permute-start(f32[16,768]{1,0:T(8,128)S(1)} %get-tuple-element.26), channel_id=1, source_target_pairs={{0,4},{1,5},{2,6},{3,7},{4,0},{5,1},{6,2},{7,3},{8,17},{9,13},{10,... | collective-permute-start | bytes 147464 | tf_op jit(solution)/shard_map/ppermute | solution.py:297
  35.6 1.2 %collective-permute-start.21 = (f32[16,768]{1,0:T(8,128)S(1)}, f32[16,768]{1,0:T(8,128)S(1)}, u32[]{:S(2)}, u32[]{:S(2)}) collective-permute-start(f32[16,768]{1,0:T(8,128)S(1)} %get-tuple-element.27), channel_id=1, source_target_pairs={{0,4},{1,5},{2,6},{3,7},{4,0},{5,1},{6,2},{7,3},{8,25},{9,13},{10,... | collective-permute-start | bytes 147464 | tf_op jit(solution)/shard_map/ppermute | solution.py:297
  37.3 13.4 %copy-start.2 = (s32[3,64]{1,0:T(4,128)S(1)}, s32[3,64]{1,0:T(4,128)}, u32[]{:S(2)}) copy-start(s32[3,64]{1,0:T(4,128)} %screen.1) | copy-start | bytes 2308
  37.3 9.8 %collective-permute-start.25 = (f32[16,768]{1,0:T(8,128)S(1)}, f32[16,768]{1,0:T(8,128)S(1)}, u32[]{:S(2)}, u32[]{:S(2)}) collective-permute-start(f32[16,768]{1,0:T(8,128)S(1)} %get-tuple-element.29), channel_id=1, source_target_pairs={{0,16},{1,5},{2,6},{3,28},{4,0},{5,1},{6,2},{7,3},{8,12},{9,13},{1... | collective-permute-start | bytes 147464 | tf_op jit(solution)/shard_map/ppermute | solution.py:297
  44.9 2.8 %collective-permute-start.24 = (f32[16,768]{1,0:T(8,128)S(1)}, f32[16,768]{1,0:T(8,128)S(1)}, u32[]{:S(2)}, u32[]{:S(2)}) collective-permute-start(f32[16,768]{1,0:T(8,128)S(1)} %get-tuple-element.29), channel_id=1, source_target_pairs={{0,4},{1,5},{2,13},{3,21},{4,0},{5,1},{6,2},{7,3},{8,12},{9,8},{10... | collective-permute-start | bytes 147464 | tf_op jit(solution)/shard_map/ppermute | solution.py:297
  44.9 2.8 %collective-permute-start.23 = (f32[16,768]{1,0:T(8,128)S(1)}, f32[16,768]{1,0:T(8,128)S(1)}, u32[]{:S(2)}, u32[]{:S(2)}) collective-permute-start(f32[16,768]{1,0:T(8,128)S(1)} %get-tuple-element.29), channel_id=1, source_target_pairs={{0,4},{1,8},{2,29},{3,7},{4,0},{5,1},{6,2},{7,3},{8,12},{9,13},{10... | collective-permute-start | bytes 147464 | tf_op jit(solution)/shard_map/ppermute | solution.py:297
  45.4 3.5 %collective-permute-start.22 = (f32[16,768]{1,0:T(8,128)S(1)}, f32[16,768]{1,0:T(8,128)S(1)}, u32[]{:S(2)}, u32[]{:S(2)}) collective-permute-start(f32[16,768]{1,0:T(8,128)S(1)} %get-tuple-element.29), channel_id=1, source_target_pairs={{0,8},{1,16},{2,6},{3,7},{4,0},{5,1},{6,2},{7,3},{8,12},{9,13},{10... | collective-permute-start | bytes 147464 | tf_op jit(solution)/shard_map/ppermute | solution.py:297
  47.1 1.8 %collective-permute-start.28 = (f32[16,768]{1,0:T(8,128)S(1)}, f32[16,768]{1,0:T(8,128)S(1)}, u32[]{:S(2)}, u32[]{:S(2)}) collective-permute-start(f32[16,768]{1,0:T(8,128)S(1)} %get-tuple-element.30.t), channel_id=1, source_target_pairs={{0,4},{1,5},{2,6},{3,7},{4,0},{5,1},{6,2},{7,3},{8,12},{9,13},{10,... | collective-permute-start | bytes 147464 | tf_op jit(solution)/shard_map/ppermute | solution.py:297
  47.1 1.8 %collective-permute-start.27 = (f32[16,768]{1,0:T(8,128)S(1)}, f32[16,768]{1,0:T(8,128)S(1)}, u32[]{:S(2)}, u32[]{:S(2)}) collective-permute-start(f32[16,768]{1,0:T(8,128)S(1)} %get-tuple-element.30.t), channel_id=1, source_target_pairs={{0,4},{1,5},{2,6},{3,7},{4,0},{5,1},{6,2},{7,3},{8,12},{9,13},{10,... | collective-permute-start | bytes 147464 | tf_op jit(solution)/shard_map/ppermute | solution.py:297
  47.6 1.2 %collective-permute-start.26 = (f32[16,768]{1,0:T(8,128)S(1)}, f32[16,768]{1,0:T(8,128)S(1)}, u32[]{:S(2)}, u32[]{:S(2)}) collective-permute-start(f32[16,768]{1,0:T(8,128)S(1)} %get-tuple-element.30.t), channel_id=1, source_target_pairs={{0,4},{1,5},{2,6},{3,7},{4,0},{5,1},{6,2},{7,3},{8,12},{9,8},{10,1... | collective-permute-start | bytes 147464 | tf_op jit(solution)/shard_map/ppermute | solution.py:297
  48.9 1.3 %collective-permute-start.29 = (f32[16,768]{1,0:T(8,128)S(1)}, f32[16,768]{1,0:T(8,128)S(1)}, u32[]{:S(2)}, u32[]{:S(2)}) collective-permute-start(f32[16,768]{1,0:T(8,128)S(1)} %shard_map.66.own), channel_id=1, source_target_pairs={{0,4},{4,0},{8,12},{12,8},{16,20},{20,16},{24,28},{28,24},{1,5},{5... | collective-permute-start | bytes 147464 | tf_op jit(solution)/shard_map/ppermute | solution.py:310
  (1 other events, 10.5 us)

commit v9 on v6

--- a/solution.py
+++ b/solution.py
@@ -181,7 +181,7 @@
             kt_high[:, part], kt_low[:, part] = high_low(product.T)
 
 
-def begin(f0, f1, f2, f3, inv, out):
+def begin(f0, f1, f2, f3, inv, after, out):
     high, low = high_low(inv[...])
     out[...] = times(f0[...] + f1[...] + f2[...] + f3[...], high, low)
 
@@ -194,7 +194,7 @@
     block = block_of()
     known = jnp.where(block == 1, one[...], jnp.where(block == 2, two[...], three[...]))
     term = times(known, high[...], low[...])
-    out[...] = jnp.where(block == 0, e[...], jnp.where(block == 1, e[...] - term, term))
+    out[...] = jnp.where(block == 0, e[...], jnp.where(block == 1, two[...] - term, term))
 
 
 def after_one(first, second, e, high, low, out):
@@ -309,25 +309,31 @@
         limit=32,
         scratch=[pltpu.VMEM((3 * size, size), BF16)] * 2,
     )
-    home = [1] + list(range(SOLVE_BLOCKS - 1))
+    home = [1, 1, 1, 2]
     gathered = []
-    for step in reversed(range(1, planes)):
+    for route in ("far", "middle", "other"):
         to = {}
         for k in range(SOLVE_BLOCKS):
+            turn_to = 1 if home[k] < 2 else -1
+            middle, far, other = home[k] + turn_to, home[k] + 2 * turn_to, home[k] - turn_to
+            ring = {"far": (far, home[k], middle), "middle": (middle, home[k]), "other": (other, home[k])}
             for c in range(2):
-                near = device((k, home[k]), c)
-                far = device((k, (home[k] + step) % planes), c)
-                to.update({near: far, far: near})
+                loop = [device((k, plane), c) for plane in ring[route]]
+                to.update(zip(loop, loop[1:] + loop[:1]))
         gathered.append(permute(partial_fit, to))
-    e = call(begin, panel, partial_fit, *gathered, diag_inv)
+    e = call(begin, panel, partial_fit, *gathered, diag_inv, k_high)
     e = call(both, panel, e, swap(e))
-    reach = [send(e, ((0, 1), (k, 0))) for k in range(1, SOLVE_BLOCKS)]
+    reach = [
+        send(e, ((0, 1), (1, 0))),
+        send(e, ((0, 1), (2, 0)), ((1, 1), (1, 0))),
+        send(e, ((0, 1), (3, 0))),
+    ]
     one = call(after_zero, panel, *reach, e, kt_high, kt_low)
     first = send(one, ((1, 0), (2, 1)), ((3, 0), (3, 1)), ((0, 1), (0, 0)))
     second = send(one, ((1, 0), (3, 1)), ((2, 0), (2, 1)), ((0, 1), (0, 2)))
     two = call(after_one, panel, first, second, e, kt_high, kt_low)
     behind = send(two, ((3, 1), (3, 2)), ((0, 1), (0, 3)))
-    known = send(two, ((2, 1), (3, 2)))
+    known = send(two, ((2, 1), (3, 2), (2, 2)))
     t, back = call(turn, [panel] * 2, known, behind, e, kt_high, kt_low, k_high, k_low)
     into = send(back, ((3, 2), (2, 1)))
     near = send(t, ((3, 2), (3, 1)))

time: 61.5 us -> 61.8 us (level)
  waiting for transfers between devices: 16.9 us -> 19.3 us
  starting transfers between devices: 21.7 us -> 19.5 us
    ppermute x22, waiting for transfers between devices: 14.8 us -> 17.1 us  [permute(): return lax.ppermute(value, AXES, sorted(to.items()))]
    ppermute x22, starting transfers between devices: 20.7 us -> 18.5 us  [permute(): return lax.ppermute(value, AXES, sorted(to.items()))]
where the time goes in v9:
time: 61.8 us; the launch traced here: 61.6 us
  starting transfers between devices  19.5 us (32%)
  waiting for transfers between devices  19.3 us (31%)
  blocking collectives  12.2 us (20%)
  Pallas kernels  9.92 us (16%)
  other arithmetic  0.67 us (1%)
    ppermute x22, starting transfers between devices, permute(): return lax.ppermute(value, AXES, sorted(to.items()))  18.5 us
    ppermute x22, waiting for transfers between devices, permute(): return lax.ppermute(value, AXES, sorted(to.items()))  17.1 us
    all_to_all x1, blocking collectives, scatter_sum(): arrived = lax.all_to_all(slabs, 'aux', 0, 0, tiled=True)  12.2 us
    pallas_call x12, Pallas kernels, call(): pl.pallas_call(kernel, out_shape=outs, in_specs=specs or [VMEM] * len(ope...  9.92 us
    ppermute x4, waiting for transfers between devices, swap(): lax.ppermute(value, 'aux', [(i, i ^ 1) for i in range(2 * SOLVE_BLOCKS)])  2.14 us
  transfers between devices with their start and end apart: 26, of which 19 were waited for; matrix products, arithmetic and copies ran while one was open for 0% of the time, Pallas kernels for 7%

profile of v9, /device:TPU:0, one launch (start us, length us, event | category | flops | bytes accessed | tf_op | source)
XLA Modules:
  0.0 61.6 jit_solution(8583473279815949001)
XLA Ops:
  0.0 0.5 collective-permute-start.4
  0.6 4.3 %shard_map.55 = (bf16[384,4096]{1,0:T(8,128)(2,1)S(1)}, bf16[384,4096]{1,0:T(8,128)(2,1)S(1)}, f32[16,384]{1,0:T(8,128)S(1)}) custom-call(s32[3,64]{1,0:T(4,128)} %screen.1, bf16[16,8192]{1,0:T(8,128)(2,1)} %densities_in.1, bf16[384,8192]{1,0:T(8,128)(2,1)} %integrals.1), custom_call_target="tpu_custom_call" | custom-call | tf_op jit(solution)/shard_map/pallas_call | solution.py:28
  4.9 3.1 %collective-permute-start.2 = (f32[16,384]{1,0:T(8,128)S(1)}, f32[16,384]{1,0:T(8,128)S(1)}, u32[]{:S(2)}, u32[]{:S(2)}) collective-permute-start(f32[16,384]{1,0:T(8,128)S(1)} %get-tuple-element.19.f0), channel_id=1, source_target_pairs={{0,1},{1,0},{2,6},{3,7},{4,5},{5,4},{6,2},{7,3},{8,9},{9,8},{10,14... | collective-permute-start | bytes 73736 | tf_op jit(solution)/shard_map/ppermute | solution.py:285
  8.0 0.5 collective-permute-start
  8.6 1.2 %collective-permute-done.2.f3 = f32[16,384]{1,0:T(8,128)S(1)} collective-permute-done((f32[16,384]{1,0:T(8,128)S(1)}, f32[16,384]{1,0:T(8,128)S(1)}, u32[]{:S(2)}, u32[]{:S(2)}) %collective-permute-start.2) | collective-permute-done | bytes 24608 | tf_op jit(solution)/shard_map/ppermute | solution.py:285
  10.2 1.2 %collective-permute-done.5.mate = f32[16,768]{1,0:T(8,128)S(1)} collective-permute-done((f32[16,768]{1,0:T(8,128)S(1)}, f32[16,768]{1,0:T(8,128)S(1)}, u32[]{:S(2)}, u32[]{:S(2)}) %collective-permute-start.5) | collective-permute-done | bytes 49184 | tf_op jit(solution)/shard_map/ppermute | solution.py:298
  11.6 0.4 collective-permute-start.7
  12.1 0.6 %collective-permute-done.8.three = f32[16,768]{1,0:T(8,128)S(1)} collective-permute-done((f32[16,768]{1,0:T(8,128)S(1)}, f32[16,768]{1,0:T(8,128)S(1)}, u32[]{:S(2)}, u32[]{:S(2)}) %collective-permute-start.8) | collective-permute-done | bytes 49184 | tf_op jit(solution)/shard_map/ppermute | solution.py:285
  13.2 0.5 shard_map.59.s
  14.2 0.7 %collective-permute-done.10.second.z2 = f32[16,768]{1,0:T(8,128)S(1)} collective-permute-done((f32[16,768]{1,0:T(8,128)S(1)}, f32[16,768]{1,0:T(8,128)S(1)}, u32[]{:S(2)}, u32[]{:S(2)}) %collective-permute-start.10) | collective-permute-done | bytes 49184 | tf_op jit(solution)/shard_map/ppermute | solution.py:285
  15.0 9.2 %collective-permute-done.9.first.z0 = f32[16,768]{1,0:T(8,128)S(1)} collective-permute-done((f32[16,768]{1,0:T(8,128)S(1)}, f32[16,768]{1,0:T(8,128)S(1)}, u32[]{:S(2)}, u32[]{:S(2)}) %collective-permute-start.9) | collective-permute-done | bytes 49184 | tf_op jit(solution)/shard_map/ppermute | solution.py:285
  24.2 0.5 shard_map.60.s
  24.6 0.5 collective-permute-start.12
  25.2 0.8 %collective-permute-done.12.known = f32[16,768]{1,0:T(8,128)S(1)} collective-permute-done((f32[16,768]{1,0:T(8,128)S(1)}, f32[16,768]{1,0:T(8,128)S(1)}, u32[]{:S(2)}, u32[]{:S(2)}) %collective-permute-start.12) | collective-permute-done | bytes 49184 | tf_op jit(solution)/shard_map/ppermute | solution.py:285
  26.4 1.0 %shard_map.61 = (f32[16,768]{1,0:T(8,128)S(1)}, f32[16,768]{1,0:T(8,128)S(1)}) custom-call(f32[16,768]{1,0:T(8,128)S(1)} %collective-permute-done.12.known, f32[16,768]{1,0:T(8,128)S(1)} %collective-permute-done.11.behind.z3, f32[16,768]{1,0:T(8,128)S(1)} %shard_map.58.e.z1, bf16[768,768]{1,0:T(8,128)(2,1)S(1)} %get-tuple-element.21.high.kt_high, ...), custom_call_target="tpu_custom_call" | custom-call | tf_op jit(solution)/shard_map/pallas_call | solution.py:28
  28.1 0.6 collective-permute-done.13.into
  29.2 0.5 shard_map.62
  30.2 0.7 %collective-permute-done.16.into = f32[16,768]{1,0:T(8,128)S(1)} collective-permute-done((f32[16,768]{1,0:T(8,128)S(1)}, f32[16,768]{1,0:T(8,128)S(1)}, u32[]{:S(2)}, u32[]{:S(2)}) %collective-permute-start.16) | collective-permute-done | bytes 49184 | tf_op jit(solution)/shard_map/ppermute | solution.py:285
  31.1 0.5 shard_map.63
  31.6 0.4 collective-permute-start.21
  31.9 8.3 %collective-permute-start.20 = (f32[16,768]{1,0:T(8,128)S(1)}, f32[16,768]{1,0:T(8,128)S(1)}, u32[]{:S(2)}, u32[]{:S(2)}) collective-permute-start(f32[16,768]{1,0:T(8,128)S(1)} %get-tuple-element.29), channel_id=1, source_target_pairs={{0,4},{1,5},{2,6},{3,7},{4,0},{5,1},{6,9},{7,17},{8,2},{9,13},{10,... | collective-permute-start | bytes 147464 | tf_op jit(solution)/shard_map/ppermute | solution.py:285
  40.2 0.5 collective-permute-start.18
  40.7 2.2 %collective-permute-start.24 = (f32[16,768]{1,0:T(8,128)S(1)}, f32[16,768]{1,0:T(8,128)S(1)}, u32[]{:S(2)}, u32[]{:S(2)}) collective-permute-start(f32[16,768]{1,0:T(8,128)S(1)} %get-tuple-element.30.t), channel_id=1, source_target_pairs={{0,4},{1,5},{2,6},{3,7},{4,0},{5,1},{6,2},{7,3},{8,11},{9,13},{10,... | collective-permute-start | bytes 147464 | tf_op jit(solution)/shard_map/ppermute | solution.py:285
  42.9 0.8 %collective-permute-done.21.i3 = f32[16,768]{1,0:T(8,128)S(1)} collective-permute-done((f32[16,768]{1,0:T(8,128)S(1)}, f32[16,768]{1,0:T(8,128)S(1)}, u32[]{:S(2)}, u32[]{:S(2)}) %collective-permute-start.21) | collective-permute-done | bytes 49184 | tf_op jit(solution)/shard_map/ppermute | solution.py:285
  43.7 0.5 collective-permute-start.22
  44.2 0.6 collective-permute-done.18.i0
  45.2 0.4 collective-permute-start.25
  45.6 0.9 %collective-permute-done.25.mate = f32[16,768]{1,0:T(8,128)S(1)} collective-permute-done((f32[16,768]{1,0:T(8,128)S(1)}, f32[16,768]{1,0:T(8,128)S(1)}, u32[]{:S(2)}, u32[]{:S(2)}) %collective-permute-start.25) | collective-permute-done | bytes 49184 | tf_op jit(solution)/shard_map/ppermute | solution.py:298
  46.5 0.5 shard_map.65.rounded
  46.9 1.8 %shard_map.66 = bf16[8,16,1024]{2,1,0:T(8,128)(2,1)S(1)} custom-call(s32[3,64]{1,0:T(4,128)S(1)} %copy-done.2, bf16[16,384]{1,0:T(8,128)(2,1)S(1)} %shard_map.65.rounded, bf16[384,4096]{1,0:T(8,128)(2,1)S(1)} %get-tuple-element.31.left, bf16[384,4096]{1,0:T(8,128)(2,1)S(1)} %get-tuple-element.32.right), custom_call_target="tpu_custom_call" | custom-call | tf_op jit(solution)/shard_map/pallas_call | solution.py:28
  48.7 12.2 %all_to_all.5 = bf16[8,16,1024]{2,1,0:T(8,128)(2,1)S(1)} all-to-all(bf16[8,16,1024]{2,1,0:T(8,128)(2,1)S(1)} %shard_map.66), channel_id=1, replica_groups=mesh['aux'=8,'pair'=4] {'aux'}, dimensions={0} | all-to-all | bytes 524288 | tf_op jit(solution)/shard_map/all_to_all | solution.py:144
  60.9 0.7 %convert_reduce_fusion = f32[16,1024]{1,0:T(8,128)} fusion(bf16[8,16,1024]{2,1,0:T(8,128)(2,1)S(1)} %all_to_all.5), kind=kLoop, calls=%fused_computation | loop fusion | flops 245760 | bytes 327680 | tf_op jit(solution)/shard_map/reduce_sum | solution.py:145
  (40 shorter events, 4.3 us)
Async XLA Ops:
  0.0 8.6 %copy-start.1 = (f32[384,768]{1,0:T(8,128)S(1)}, f32[384,768]{1,0:T(8,128)}, u32[]{:S(2)}) copy-start(f32[384,768]{1,0:T(8,128)} %fac0.1) | copy-start | bytes 3538948
  0.0 8.6 %copy-start = (f32[384,768]{1,0:T(8,128)S(1)}, f32[384,768]{1,0:T(8,128)}, u32[]{:S(2)}) copy-start(f32[384,768]{1,0:T(8,128)} %inv.3) | copy-start | bytes 3538948
  0.0 8.5 %collective-permute-start.4 = (f32[384,768]{1,0:T(8,128)}, f32[384,768]{1,0:T(8,128)S(1)}, u32[]{:S(2)}, u32[]{:S(2)}) collective-permute-start(f32[384,768]{1,0:T(8,128)} %fac0.1), channel_id=1, source_target_pairs={{0,4},{4,0},{8,12},{12,8},{16,20},{20,16},{24,28},{28,24},{1,5},{5... | collective-permute-start | bytes 3538952 | tf_op jit(solution)/shard_map/ppermute | solution.py:298
  0.5 8.1 %collective-permute-start.3 = (f32[384,768]{1,0:T(8,128)}, f32[384,768]{1,0:T(8,128)S(1)}, u32[]{:S(2)}, u32[]{:S(2)}) collective-permute-start(f32[384,768]{1,0:T(8,128)} %inv.3), channel_id=1, source_target_pairs={{0,4},{4,0},{8,12},{12,8},{16,20},{20,16},{24,28},{28,24},{1,5},{5... | collective-permute-start | bytes 3538952 | tf_op jit(solution)/shard_map/ppermute | solution.py:298
  4.9 4.9 %collective-permute-start.2 = (f32[16,384]{1,0:T(8,128)S(1)}, f32[16,384]{1,0:T(8,128)S(1)}, u32[]{:S(2)}, u32[]{:S(2)}) collective-permute-start(f32[16,384]{1,0:T(8,128)S(1)} %get-tuple-element.19.f0), channel_id=1, source_target_pairs={{0,1},{1,0},{2,6},{3,7},{4,5},{5,4},{6,2},{7,3},{8,9},{9,8},{10,14... | collective-permute-start | bytes 73736 | tf_op jit(solution)/shard_map/ppermute | solution.py:285
  8.0 1.8 %collective-permute-start.1 = (f32[16,384]{1,0:T(8,128)S(1)}, f32[16,384]{1,0:T(8,128)S(1)}, u32[]{:S(2)}, u32[]{:S(2)}) collective-permute-start(f32[16,384]{1,0:T(8,128)S(1)} %get-tuple-element.19.f0), channel_id=1, source_target_pairs={{0,4},{1,2},{2,1},{3,7},{4,0},{5,6},{6,5},{7,3},{8,12},{9,10},{10,... | collective-permute-start | bytes 73736 | tf_op jit(solution)/shard_map/ppermute | solution.py:285
  8.0 1.8 %collective-permute-start = (f32[16,384]{1,0:T(8,128)S(1)}, f32[16,384]{1,0:T(8,128)S(1)}, u32[]{:S(2)}, u32[]{:S(2)}) collective-permute-start(f32[16,384]{1,0:T(8,128)S(1)} %get-tuple-element.19.f0), channel_id=1, source_target_pairs={{0,4},{1,2},{2,3},{3,1},{4,0},{5,6},{6,7},{7,5},{8,12},{9,10},{10,... | collective-permute-start | bytes 73736 | tf_op jit(solution)/shard_map/ppermute | solution.py:285
  10.2 1.3 %collective-permute-start.5 = (f32[16,768]{1,0:T(8,128)S(1)}, f32[16,768]{1,0:T(8,128)S(1)}, u32[]{:S(2)}, u32[]{:S(2)}) collective-permute-start(f32[16,768]{1,0:T(8,128)S(1)} %shard_map.57.own), channel_id=1, source_target_pairs={{0,4},{4,0},{8,12},{12,8},{16,20},{20,16},{24,28},{28,24},{1,5},{5... | collective-permute-start | bytes 147464 | tf_op jit(solution)/shard_map/ppermute | solution.py:298
  11.4 1.3 %collective-permute-start.8 = (f32[16,768]{1,0:T(8,128)S(1)}, f32[16,768]{1,0:T(8,128)S(1)}, u32[]{:S(2)}, u32[]{:S(2)}) collective-permute-start(f32[16,768]{1,0:T(8,128)S(1)} %shard_map.58.e.z1), channel_id=1, source_target_pairs={{0,4},{1,24},{2,6},{3,7},{4,0},{5,1},{6,2},{7,3},{8,12},{9,13},{10... | collective-permute-start | bytes 147464 | tf_op jit(solution)/shard_map/ppermute | solution.py:285
  11.6 1.3 %collective-permute-start.7 = (f32[16,768]{1,0:T(8,128)S(1)}, f32[16,768]{1,0:T(8,128)S(1)}, u32[]{:S(2)}, u32[]{:S(2)}) collective-permute-start(f32[16,768]{1,0:T(8,128)S(1)} %shard_map.58.e.z1), channel_id=1, source_target_pairs={{0,4},{1,16},{2,6},{3,7},{4,0},{5,1},{6,2},{7,3},{8,12},{9,8},{10,... | collective-permute-start | bytes 147464 | tf_op jit(solution)/shard_map/ppermute | solution.py:285
  12.0 1.2 %collective-permute-start.6 = (f32[16,768]{1,0:T(8,128)S(1)}, f32[16,768]{1,0:T(8,128)S(1)}, u32[]{:S(2)}, u32[]{:S(2)}) collective-permute-start(f32[16,768]{1,0:T(8,128)S(1)} %shard_map.58.e.z1), channel_id=1, source_target_pairs={{0,4},{1,8},{2,6},{3,7},{4,0},{5,1},{6,2},{7,3},{8,12},{9,13},{10,... | collective-permute-start | bytes 147464 | tf_op jit(solution)/shard_map/ppermute | solution.py:285
  13.7 1.2 %collective-permute-start.10 = (f32[16,768]{1,0:T(8,128)S(1)}, f32[16,768]{1,0:T(8,128)S(1)}, u32[]{:S(2)}, u32[]{:S(2)}) collective-permute-start(f32[16,768]{1,0:T(8,128)S(1)} %shard_map.59.s), channel_id=1, source_target_pairs={{0,4},{1,2},{2,6},{3,7},{4,0},{5,1},{6,5},{7,3},{8,25},{9,13},{10,... | collective-permute-start | bytes 147464 | tf_op jit(solution)/shard_map/ppermute | solution.py:285
  13.9 10.3 %collective-permute-start.9 = (f32[16,768]{1,0:T(8,128)S(1)}, f32[16,768]{1,0:T(8,128)S(1)}, u32[]{:S(2)}, u32[]{:S(2)}) collective-permute-start(f32[16,768]{1,0:T(8,128)S(1)} %shard_map.59.s), channel_id=1, source_target_pairs={{0,4},{1,0},{2,6},{3,7},{4,5},{5,1},{6,2},{7,3},{8,17},{9,13},{10,... | collective-permute-start | bytes 147464 | tf_op jit(solution)/shard_map/ppermute | solution.py:285
  24.6 1.4 %collective-permute-start.12 = (f32[16,768]{1,0:T(8,128)S(1)}, f32[16,768]{1,0:T(8,128)S(1)}, u32[]{:S(2)}, u32[]{:S(2)}) collective-permute-start(f32[16,768]{1,0:T(8,128)S(1)} %shard_map.60.s), channel_id=1, source_target_pairs={{0,4},{1,5},{2,6},{3,7},{4,0},{5,1},{6,2},{7,3},{8,12},{9,13},{10,... | collective-permute-start | bytes 147464 | tf_op jit(solution)/shard_map/ppermute | solution.py:285
  25.2 1.2 %collective-permute-start.11 = (f32[16,768]{1,0:T(8,128)S(1)}, f32[16,768]{1,0:T(8,128)S(1)}, u32[]{:S(2)}, u32[]{:S(2)}) collective-permute-start(f32[16,768]{1,0:T(8,128)S(1)} %shard_map.60.s), channel_id=1, source_target_pairs={{0,4},{1,3},{2,6},{3,7},{4,0},{5,1},{6,2},{7,5},{8,12},{9,13},{10,... | collective-permute-start | bytes 147464 | tf_op jit(solution)/shard_map/ppermute | solution.py:285
  27.4 1.2 %collective-permute-start.13 = (f32[16,768]{1,0:T(8,128)S(1)}, f32[16,768]{1,0:T(8,128)S(1)}, u32[]{:S(2)}, u32[]{:S(2)}) collective-permute-start(f32[16,768]{1,0:T(8,128)S(1)} %get-tuple-element.24), channel_id=1, source_target_pairs={{0,4},{1,5},{2,6},{3,7},{4,0},{5,1},{6,2},{7,3},{8,12},{9,13},{10,... | collective-permute-start | bytes 147464 | tf_op jit(solution)/shard_map/ppermute | solution.py:285
  27.6 1.2 %collective-permute-start.15 = (f32[16,768]{1,0:T(8,128)S(1)}, f32[16,768]{1,0:T(8,128)S(1)}, u32[]{:S(2)}, u32[]{:S(2)}) collective-permute-start(f32[16,768]{1,0:T(8,128)S(1)} %get-tuple-element.25.t), channel_id=1, source_target_pairs={{0,4},{1,5},{2,6},{3,7},{4,0},{5,1},{6,2},{7,3},{8,12},{9,13},{10,... | collective-permute-start | bytes 147464 | tf_op jit(solution)/shard_map/ppermute | solution.py:285
  28.0 1.2 %collective-permute-start.14 = (f32[16,768]{1,0:T(8,128)S(1)}, f32[16,768]{1,0:T(8,128)S(1)}, u32[]{:S(2)}, u32[]{:S(2)}) collective-permute-start(f32[16,768]{1,0:T(8,128)S(1)} %get-tuple-element.25.t), channel_id=1, source_target_pairs={{0,4},{1,5},{2,6},{3,7},{4,0},{5,1},{6,2},{7,3},{8,12},{9,13},{10,... | collective-permute-start | bytes 147464 | tf_op jit(solution)/shard_map/ppermute | solution.py:285
  29.7 1.2 %collective-permute-start.16 = (f32[16,768]{1,0:T(8,128)S(1)}, f32[16,768]{1,0:T(8,128)S(1)}, u32[]{:S(2)}, u32[]{:S(2)}) collective-permute-start(f32[16,768]{1,0:T(8,128)S(1)} %get-tuple-element.26), channel_id=1, source_target_pairs={{0,4},{1,5},{2,6},{3,7},{4,0},{5,1},{6,2},{7,3},{8,12},{9,13},{10,... | collective-permute-start | bytes 147464 | tf_op jit(solution)/shard_map/ppermute | solution.py:285
  29.8 1.2 %collective-permute-start.17 = (f32[16,768]{1,0:T(8,128)S(1)}, f32[16,768]{1,0:T(8,128)S(1)}, u32[]{:S(2)}, u32[]{:S(2)}) collective-permute-start(f32[16,768]{1,0:T(8,128)S(1)} %get-tuple-element.27), channel_id=1, source_target_pairs={{0,4},{1,5},{2,6},{3,7},{4,0},{5,1},{6,2},{7,3},{8,12},{9,13},{10,... | collective-permute-start | bytes 147464 | tf_op jit(solution)/shard_map/ppermute | solution.py:285
  31.5 15.4 %copy-start.2 = (s32[3,64]{1,0:T(4,128)S(1)}, s32[3,64]{1,0:T(4,128)}, u32[]{:S(2)}) copy-start(s32[3,64]{1,0:T(4,128)} %screen.1) | copy-start | bytes 2308
  31.6 12.2 %collective-permute-start.21 = (f32[16,768]{1,0:T(8,128)S(1)}, f32[16,768]{1,0:T(8,128)S(1)}, u32[]{:S(2)}, u32[]{:S(2)}) collective-permute-start(f32[16,768]{1,0:T(8,128)S(1)} %get-tuple-element.29), channel_id=1, source_target_pairs={{0,4},{1,5},{2,6},{3,7},{4,20},{5,1},{6,2},{7,24},{8,3},{9,13},{10... | collective-permute-start | bytes 147464 | tf_op jit(solution)/shard_map/ppermute | solution.py:285
  31.9 11.8 %collective-permute-start.20 = (f32[16,768]{1,0:T(8,128)S(1)}, f32[16,768]{1,0:T(8,128)S(1)}, u32[]{:S(2)}, u32[]{:S(2)}) collective-permute-start(f32[16,768]{1,0:T(8,128)S(1)} %get-tuple-element.29), channel_id=1, source_target_pairs={{0,4},{1,5},{2,6},{3,7},{4,0},{5,1},{6,9},{7,17},{8,2},{9,13},{10,... | collective-permute-start | bytes 147464 | tf_op jit(solution)/shard_map/ppermute | solution.py:285
  40.2 4.0 %collective-permute-start.19 = (f32[16,768]{1,0:T(8,128)S(1)}, f32[16,768]{1,0:T(8,128)S(1)}, u32[]{:S(2)}, u32[]{:S(2)}) collective-permute-start(f32[16,768]{1,0:T(8,128)S(1)} %get-tuple-element.29), channel_id=1, source_target_pairs={{0,4},{1,5},{2,6},{3,7},{4,0},{5,12},{6,25},{7,3},{8,1},{9,13},{10... | collective-permute-start | bytes 147464 | tf_op jit(solution)/shard_map/ppermute | solution.py:285
  40.2 4.7 %collective-permute-start.18 = (f32[16,768]{1,0:T(8,128)S(1)}, f32[16,768]{1,0:T(8,128)S(1)}, u32[]{:S(2)}, u32[]{:S(2)}) collective-permute-start(f32[16,768]{1,0:T(8,128)S(1)} %get-tuple-element.29), channel_id=1, source_target_pairs={{0,4},{1,5},{2,6},{3,7},{4,12},{5,20},{6,2},{7,3},{8,0},{9,13},{10... | collective-permute-start | bytes 147464 | tf_op jit(solution)/shard_map/ppermute | solution.py:285
  40.7 4.2 %collective-permute-start.24 = (f32[16,768]{1,0:T(8,128)S(1)}, f32[16,768]{1,0:T(8,128)S(1)}, u32[]{:S(2)}, u32[]{:S(2)}) collective-permute-start(f32[16,768]{1,0:T(8,128)S(1)} %get-tuple-element.30.t), channel_id=1, source_target_pairs={{0,4},{1,5},{2,6},{3,7},{4,0},{5,1},{6,2},{7,3},{8,11},{9,13},{10,... | collective-permute-start | bytes 147464 | tf_op jit(solution)/shard_map/ppermute | solution.py:285
  43.7 1.2 %collective-permute-start.23 = (f32[16,768]{1,0:T(8,128)S(1)}, f32[16,768]{1,0:T(8,128)S(1)}, u32[]{:S(2)}, u32[]{:S(2)}) collective-permute-start(f32[16,768]{1,0:T(8,128)S(1)} %get-tuple-element.30.t), channel_id=1, source_target_pairs={{0,4},{1,5},{2,6},{3,7},{4,0},{5,1},{6,2},{7,3},{8,10},{9,13},{10,... | collective-permute-start | bytes 147464 | tf_op jit(solution)/shard_map/ppermute | solution.py:285
  43.7 1.4 %collective-permute-start.22 = (f32[16,768]{1,0:T(8,128)S(1)}, f32[16,768]{1,0:T(8,128)S(1)}, u32[]{:S(2)}, u32[]{:S(2)}) collective-permute-start(f32[16,768]{1,0:T(8,128)S(1)} %get-tuple-element.30.t), channel_id=1, source_target_pairs={{0,4},{1,5},{2,6},{3,7},{4,0},{5,1},{6,2},{7,3},{8,9},{9,13},{10,1... | collective-permute-start | bytes 147464 | tf_op jit(solution)/shard_map/ppermute | solution.py:285
  45.2 1.3 %collective-permute-start.25 = (f32[16,768]{1,0:T(8,128)S(1)}, f32[16,768]{1,0:T(8,128)S(1)}, u32[]{:S(2)}, u32[]{:S(2)}) collective-permute-start(f32[16,768]{1,0:T(8,128)S(1)} %shard_map.64.own), channel_id=1, source_target_pairs={{0,4},{4,0},{8,12},{12,8},{16,20},{20,16},{24,28},{28,24},{1,5},{5... | collective-permute-start | bytes 147464 | tf_op jit(solution)/shard_map/ppermute | solution.py:298

commit v10 on v9

--- a/solution.py
+++ b/solution.py
@@ -1,3 +1,5 @@
+import functools
+
 import jax
 import jax.numpy as jnp
 from jax import lax
@@ -181,7 +183,7 @@
             kt_high[:, part], kt_low[:, part] = high_low(product.T)
 
 
-def begin(f0, f1, f2, f3, inv, after, out):
+def begin(f0, f1, f2, f3, inv, out):
     high, low = high_low(inv[...])
     out[...] = times(f0[...] + f1[...] + f2[...] + f3[...], high, low)
 
@@ -190,6 +192,15 @@
     out[...] = own[...] + mate[...]
 
 
+def lead_only(kernel):
+    @functools.wraps(kernel)
+    def guarded(*refs):
+        pl.when(side_of() == 0)(lambda: kernel(*refs))
+
+    return guarded
+
+
+@lead_only
 def after_zero(one, two, three, e, high, low, out):
     block = block_of()
     known = jnp.where(block == 1, one[...], jnp.where(block == 2, two[...], three[...]))
@@ -197,6 +208,7 @@
     out[...] = jnp.where(block == 0, e[...], jnp.where(block == 1, two[...] - term, term))
 
 
+@lead_only
 def after_one(first, second, e, high, low, out):
     block = block_of()
     known = jnp.where(block == 3, second[...], first[...])
@@ -205,12 +217,14 @@
     out[...] = jnp.where(block == 0, e[...], jnp.where(block == 3, total, e[...] - total))
 
 
+@lead_only
 def turn(known, behind, e, kt_high, kt_low, high, low, settled, back):
     value = e[...] - behind[...] - times(known[...], kt_high[...], kt_low[...])
     settled[...] = value
     back[...] = times(value, high[...], low[...])
 
 
+@lead_only
 def back_two(into, near, far, t, s, high, low, settled, back, mixed):
     plane = lax.axis_index("pair")
     last = block_of() == 3
@@ -222,6 +236,7 @@
     mixed[...] = jnp.where(last, product, value)
 
 
+@lead_only
 def back_one(into, other, t, s, high, low, settled, back):
     plane = lax.axis_index("pair")
     block = block_of()
@@ -321,7 +336,7 @@
                 loop = [device((k, plane), c) for plane in ring[route]]
                 to.update(zip(loop, loop[1:] + loop[:1]))
         gathered.append(permute(partial_fit, to))
-    e = call(begin, panel, partial_fit, *gathered, diag_inv, k_high)
+    e = call(begin, panel, partial_fit, *gathered, diag_inv)
     e = call(both, panel, e, swap(e))
     reach = [
         send(e, ((0, 1), (1, 0))),

time: 61.8 us -> 61.3 us (level)
  no operation moved by 1% of the time
where the time goes in v10:
time: 61.3 us; the launch traced here: 61.1 us
  starting transfers between devices  19.5 us (32%)
  waiting for transfers between devices  18.8 us (31%)
  blocking collectives  12.2 us (20%)
  Pallas kernels  9.78 us (16%)
  other arithmetic  0.67 us (1%)
    ppermute x22, starting transfers between devices, permute(): return lax.ppermute(value, AXES, sorted(to.items()))  18.5 us
    ppermute x22, waiting for transfers between devices, permute(): return lax.ppermute(value, AXES, sorted(to.items()))  16.7 us
    all_to_all x1, blocking collectives, scatter_sum(): arrived = lax.all_to_all(slabs, 'aux', 0, 0, tiled=True)  12.2 us
    pallas_call x12, Pallas kernels, call(): pl.pallas_call(kernel, out_shape=outs, in_specs=specs or [VMEM] * len(ope...  9.78 us
    ppermute x4, waiting for transfers between devices, swap(): lax.ppermute(value, 'aux', [(i, i ^ 1) for i in range(2 * SOLVE_BLOCKS)])  2.14 us
  transfers between devices with their start and end apart: 26, of which 19 were waited for; matrix products, arithmetic and copies ran while one was open for 0% of the time, Pallas kernels for 7%

profile of v10, /device:TPU:0, one launch (start us, length us, event | category | flops | bytes accessed | tf_op | source)
XLA Modules:
  0.0 61.1 jit_solution(8332797498019450627)
XLA Ops:
  0.0 0.5 collective-permute-start.8
  0.6 4.2 %shard_map.55 = (bf16[384,4096]{1,0:T(8,128)(2,1)S(1)}, bf16[384,4096]{1,0:T(8,128)(2,1)S(1)}, f32[16,384]{1,0:T(8,128)S(1)}) custom-call(s32[3,64]{1,0:T(4,128)} %screen.1, bf16[16,8192]{1,0:T(8,128)(2,1)} %densities_in.1, bf16[384,8192]{1,0:T(8,128)(2,1)} %integrals.1), custom_call_target="tpu_custom_call" | custom-call | tf_op jit(solution)/shard_map/pallas_call | solution.py:30
  4.8 3.1 %collective-permute-start.2 = (f32[16,384]{1,0:T(8,128)S(1)}, f32[16,384]{1,0:T(8,128)S(1)}, u32[]{:S(2)}, u32[]{:S(2)}) collective-permute-start(f32[16,384]{1,0:T(8,128)S(1)} %get-tuple-element.19.f0), channel_id=1, source_target_pairs={{0,1},{1,0},{2,6},{3,7},{4,5},{5,4},{6,2},{7,3},{8,9},{9,8},{10,14... | collective-permute-start | bytes 73736 | tf_op jit(solution)/shard_map/ppermute | solution.py:300
  7.8 0.5 collective-permute-start
  8.4 1.3 %collective-permute-done.2.f3 = f32[16,384]{1,0:T(8,128)S(1)} collective-permute-done((f32[16,384]{1,0:T(8,128)S(1)}, f32[16,384]{1,0:T(8,128)S(1)}, u32[]{:S(2)}, u32[]{:S(2)}) %collective-permute-start.2) | collective-permute-done | bytes 24608 | tf_op jit(solution)/shard_map/ppermute | solution.py:300
  10.0 1.2 %collective-permute-done.3.mate = f32[16,768]{1,0:T(8,128)S(1)} collective-permute-done((f32[16,768]{1,0:T(8,128)S(1)}, f32[16,768]{1,0:T(8,128)S(1)}, u32[]{:S(2)}, u32[]{:S(2)}) %collective-permute-start.3) | collective-permute-done | bytes 49184 | tf_op jit(solution)/shard_map/ppermute | solution.py:313
  12.0 0.6 collective-permute-done.6.three
  13.0 0.5 shard_map.59.s
  13.5 0.5 collective-permute-start.9
  14.1 0.7 %collective-permute-done.10.second.z2 = f32[16,768]{1,0:T(8,128)S(1)} collective-permute-done((f32[16,768]{1,0:T(8,128)S(1)}, f32[16,768]{1,0:T(8,128)S(1)}, u32[]{:S(2)}, u32[]{:S(2)}) %collective-permute-start.10) | collective-permute-done | bytes 49184 | tf_op jit(solution)/shard_map/ppermute | solution.py:300
  14.8 8.9 %collective-permute-done.9.first.z0 = f32[16,768]{1,0:T(8,128)S(1)} collective-permute-done((f32[16,768]{1,0:T(8,128)S(1)}, f32[16,768]{1,0:T(8,128)S(1)}, u32[]{:S(2)}, u32[]{:S(2)}) %collective-permute-start.9) | collective-permute-done | bytes 49184 | tf_op jit(solution)/shard_map/ppermute | solution.py:300
  23.7 0.5 shard_map.60.s
  24.2 0.5 collective-permute-start.11
  24.7 0.7 %collective-permute-done.12.known = f32[16,768]{1,0:T(8,128)S(1)} collective-permute-done((f32[16,768]{1,0:T(8,128)S(1)}, f32[16,768]{1,0:T(8,128)S(1)}, u32[]{:S(2)}, u32[]{:S(2)}) %collective-permute-start.12) | collective-permute-done | bytes 49184 | tf_op jit(solution)/shard_map/ppermute | solution.py:300
  25.6 1.0 %shard_map.61 = (f32[16,768]{1,0:T(8,128)S(1)}, f32[16,768]{1,0:T(8,128)S(1)}) custom-call(f32[16,768]{1,0:T(8,128)S(1)} %collective-permute-done.12.known, f32[16,768]{1,0:T(8,128)S(1)} %collective-permute-done.11.behind.z3, f32[16,768]{1,0:T(8,128)S(1)} %shard_map.57.e.z1, bf16[768,768]{1,0:T(8,128)(2,1)S(1)} %get-tuple-element.20.high.kt_high, ...), custom_call_target="tpu_custom_call" | custom-call | tf_op jit(solution)/shard_map/pallas_call | solution.py:30
  26.6 0.5 collective-permute-start.15
  27.1 0.7 %collective-permute-done.13.into = f32[16,768]{1,0:T(8,128)S(1)} collective-permute-done((f32[16,768]{1,0:T(8,128)S(1)}, f32[16,768]{1,0:T(8,128)S(1)}, u32[]{:S(2)}, u32[]{:S(2)}) %collective-permute-start.13) | collective-permute-done | bytes 49184 | tf_op jit(solution)/shard_map/ppermute | solution.py:300
  28.4 0.5 shard_map.62
  28.8 0.5 collective-permute-start.17
  29.4 0.7 %collective-permute-done.16.into = f32[16,768]{1,0:T(8,128)S(1)} collective-permute-done((f32[16,768]{1,0:T(8,128)S(1)}, f32[16,768]{1,0:T(8,128)S(1)}, u32[]{:S(2)}, u32[]{:S(2)}) %collective-permute-start.16) | collective-permute-done | bytes 49184 | tf_op jit(solution)/shard_map/ppermute | solution.py:300
  30.2 0.5 shard_map.63
  30.7 8.5 %collective-permute-start.20 = (f32[16,768]{1,0:T(8,128)S(1)}, f32[16,768]{1,0:T(8,128)S(1)}, u32[]{:S(2)}, u32[]{:S(2)}) collective-permute-start(f32[16,768]{1,0:T(8,128)S(1)} %get-tuple-element.29), channel_id=1, source_target_pairs={{0,4},{1,5},{2,6},{3,7},{4,0},{5,1},{6,9},{7,17},{8,2},{9,13},{10,... | collective-permute-start | bytes 147464 | tf_op jit(solution)/shard_map/ppermute | solution.py:300
  39.2 0.5 collective-permute-start.18
  39.7 2.7 %collective-permute-start.24 = (f32[16,768]{1,0:T(8,128)S(1)}, f32[16,768]{1,0:T(8,128)S(1)}, u32[]{:S(2)}, u32[]{:S(2)}) collective-permute-start(f32[16,768]{1,0:T(8,128)S(1)} %get-tuple-element.30.t), channel_id=1, source_target_pairs={{0,4},{1,5},{2,6},{3,7},{4,0},{5,1},{6,2},{7,3},{8,11},{9,13},{10,... | collective-permute-start | bytes 147464 | tf_op jit(solution)/shard_map/ppermute | solution.py:300
  42.4 0.8 %collective-permute-done.21.i3 = f32[16,768]{1,0:T(8,128)S(1)} collective-permute-done((f32[16,768]{1,0:T(8,128)S(1)}, f32[16,768]{1,0:T(8,128)S(1)}, u32[]{:S(2)}, u32[]{:S(2)}) %collective-permute-start.21) | collective-permute-done | bytes 49184 | tf_op jit(solution)/shard_map/ppermute | solution.py:300
  43.2 0.5 collective-permute-start.22
  43.7 0.6 %collective-permute-done.18.i0 = f32[16,768]{1,0:T(8,128)S(1)} collective-permute-done((f32[16,768]{1,0:T(8,128)S(1)}, f32[16,768]{1,0:T(8,128)S(1)}, u32[]{:S(2)}, u32[]{:S(2)}) %collective-permute-start.18) | collective-permute-done | bytes 49184 | tf_op jit(solution)/shard_map/ppermute | solution.py:300
  45.1 0.9 %collective-permute-done.25.mate = f32[16,768]{1,0:T(8,128)S(1)} collective-permute-done((f32[16,768]{1,0:T(8,128)S(1)}, f32[16,768]{1,0:T(8,128)S(1)}, u32[]{:S(2)}, u32[]{:S(2)}) %collective-permute-start.25) | collective-permute-done | bytes 49184 | tf_op jit(solution)/shard_map/ppermute | solution.py:313
  46.0 0.4 shard_map.65.rounded
  46.4 1.8 %shard_map.66 = bf16[8,16,1024]{2,1,0:T(8,128)(2,1)S(1)} custom-call(s32[3,64]{1,0:T(4,128)S(1)} %copy-done.2, bf16[16,384]{1,0:T(8,128)(2,1)S(1)} %shard_map.65.rounded, bf16[384,4096]{1,0:T(8,128)(2,1)S(1)} %get-tuple-element.31.left, bf16[384,4096]{1,0:T(8,128)(2,1)S(1)} %get-tuple-element.32.right), custom_call_target="tpu_custom_call" | custom-call | tf_op jit(solution)/shard_map/pallas_call | solution.py:30
  48.2 12.2 %all_to_all.5 = bf16[8,16,1024]{2,1,0:T(8,128)(2,1)S(1)} all-to-all(bf16[8,16,1024]{2,1,0:T(8,128)(2,1)S(1)} %shard_map.66), channel_id=1, replica_groups=mesh['aux'=8,'pair'=4] {'aux'}, dimensions={0} | all-to-all | bytes 524288 | tf_op jit(solution)/shard_map/all_to_all | solution.py:146
  60.4 0.7 %convert_reduce_fusion = f32[16,1024]{1,0:T(8,128)} fusion(bf16[8,16,1024]{2,1,0:T(8,128)(2,1)S(1)} %all_to_all.5), kind=kLoop, calls=%fused_computation | loop fusion | flops 245760 | bytes 327680 | tf_op jit(solution)/shard_map/reduce_sum | solution.py:147
  (40 shorter events, 3.2 us)
Async XLA Ops:
  0.0 9.7 %copy-start = (f32[384,768]{1,0:T(8,128)S(1)}, f32[384,768]{1,0:T(8,128)}, u32[]{:S(2)}) copy-start(f32[384,768]{1,0:T(8,128)} %inv.3) | copy-start | bytes 3538948
  0.0 11.9 %collective-permute-start.8 = (f32[384,768]{1,0:T(8,128)}, f32[384,768]{1,0:T(8,128)S(1)}, u32[]{:S(2)}, u32[]{:S(2)}) collective-permute-start(f32[384,768]{1,0:T(8,128)} %fac0.1), channel_id=1, source_target_pairs={{0,4},{4,0},{8,12},{12,8},{16,20},{20,16},{24,28},{28,24},{1,5},{5... | collective-permute-start | bytes 3538952 | tf_op jit(solution)/shard_map/ppermute | solution.py:313
  0.5 11.4 %collective-permute-start.7 = (f32[384,768]{1,0:T(8,128)}, f32[384,768]{1,0:T(8,128)S(1)}, u32[]{:S(2)}, u32[]{:S(2)}) collective-permute-start(f32[384,768]{1,0:T(8,128)} %inv.3), channel_id=1, source_target_pairs={{0,4},{4,0},{8,12},{12,8},{16,20},{20,16},{24,28},{28,24},{1,5},{5... | collective-permute-start | bytes 3538952 | tf_op jit(solution)/shard_map/ppermute | solution.py:313
  4.8 7.2 %copy-start.1 = (f32[384,768]{1,0:T(8,128)S(1)}, f32[384,768]{1,0:T(8,128)}, u32[]{:S(2)}) copy-start(f32[384,768]{1,0:T(8,128)} %fac0.1) | copy-start | bytes 3538948
  4.8 4.9 %collective-permute-start.2 = (f32[16,384]{1,0:T(8,128)S(1)}, f32[16,384]{1,0:T(8,128)S(1)}, u32[]{:S(2)}, u32[]{:S(2)}) collective-permute-start(f32[16,384]{1,0:T(8,128)S(1)} %get-tuple-element.19.f0), channel_id=1, source_target_pairs={{0,1},{1,0},{2,6},{3,7},{4,5},{5,4},{6,2},{7,3},{8,9},{9,8},{10,14... | collective-permute-start | bytes 73736 | tf_op jit(solution)/shard_map/ppermute | solution.py:300
  7.8 1.8 %collective-permute-start.1 = (f32[16,384]{1,0:T(8,128)S(1)}, f32[16,384]{1,0:T(8,128)S(1)}, u32[]{:S(2)}, u32[]{:S(2)}) collective-permute-start(f32[16,384]{1,0:T(8,128)S(1)} %get-tuple-element.19.f0), channel_id=1, source_target_pairs={{0,4},{1,2},{2,1},{3,7},{4,0},{5,6},{6,5},{7,3},{8,12},{9,10},{10,... | collective-permute-start | bytes 73736 | tf_op jit(solution)/shard_map/ppermute | solution.py:300
  7.8 1.8 %collective-permute-start = (f32[16,384]{1,0:T(8,128)S(1)}, f32[16,384]{1,0:T(8,128)S(1)}, u32[]{:S(2)}, u32[]{:S(2)}) collective-permute-start(f32[16,384]{1,0:T(8,128)S(1)} %get-tuple-element.19.f0), channel_id=1, source_target_pairs={{0,4},{1,2},{2,3},{3,1},{4,0},{5,6},{6,7},{7,5},{8,12},{9,10},{10,... | collective-permute-start | bytes 73736 | tf_op jit(solution)/shard_map/ppermute | solution.py:300
  10.0 1.3 %collective-permute-start.3 = (f32[16,768]{1,0:T(8,128)S(1)}, f32[16,768]{1,0:T(8,128)S(1)}, u32[]{:S(2)}, u32[]{:S(2)}) collective-permute-start(f32[16,768]{1,0:T(8,128)S(1)} %shard_map.56.own), channel_id=1, source_target_pairs={{0,4},{4,0},{8,12},{12,8},{16,20},{20,16},{24,28},{28,24},{1,5},{5... | collective-permute-start | bytes 147464 | tf_op jit(solution)/shard_map/ppermute | solution.py:313
  11.2 1.3 %collective-permute-start.6 = (f32[16,768]{1,0:T(8,128)S(1)}, f32[16,768]{1,0:T(8,128)S(1)}, u32[]{:S(2)}, u32[]{:S(2)}) collective-permute-start(f32[16,768]{1,0:T(8,128)S(1)} %shard_map.57.e.z1), channel_id=1, source_target_pairs={{0,4},{1,24},{2,6},{3,7},{4,0},{5,1},{6,2},{7,3},{8,12},{9,13},{10... | collective-permute-start | bytes 147464 | tf_op jit(solution)/shard_map/ppermute | solution.py:300
  11.4 1.3 %collective-permute-start.5 = (f32[16,768]{1,0:T(8,128)S(1)}, f32[16,768]{1,0:T(8,128)S(1)}, u32[]{:S(2)}, u32[]{:S(2)}) collective-permute-start(f32[16,768]{1,0:T(8,128)S(1)} %shard_map.57.e.z1), channel_id=1, source_target_pairs={{0,4},{1,16},{2,6},{3,7},{4,0},{5,1},{6,2},{7,3},{8,12},{9,8},{10,... | collective-permute-start | bytes 147464 | tf_op jit(solution)/shard_map/ppermute | solution.py:300
  11.8 1.2 %collective-permute-start.4 = (f32[16,768]{1,0:T(8,128)S(1)}, f32[16,768]{1,0:T(8,128)S(1)}, u32[]{:S(2)}, u32[]{:S(2)}) collective-permute-start(f32[16,768]{1,0:T(8,128)S(1)} %shard_map.57.e.z1), channel_id=1, source_target_pairs={{0,4},{1,8},{2,6},{3,7},{4,0},{5,1},{6,2},{7,3},{8,12},{9,13},{10,... | collective-permute-start | bytes 147464 | tf_op jit(solution)/shard_map/ppermute | solution.py:300
  13.5 1.2 %collective-permute-start.10 = (f32[16,768]{1,0:T(8,128)S(1)}, f32[16,768]{1,0:T(8,128)S(1)}, u32[]{:S(2)}, u32[]{:S(2)}) collective-permute-start(f32[16,768]{1,0:T(8,128)S(1)} %shard_map.59.s), channel_id=1, source_target_pairs={{0,4},{1,2},{2,6},{3,7},{4,0},{5,1},{6,5},{7,3},{8,25},{9,13},{10,... | collective-permute-start | bytes 147464 | tf_op jit(solution)/shard_map/ppermute | solution.py:300
  13.5 10.1 %collective-permute-start.9 = (f32[16,768]{1,0:T(8,128)S(1)}, f32[16,768]{1,0:T(8,128)S(1)}, u32[]{:S(2)}, u32[]{:S(2)}) collective-permute-start(f32[16,768]{1,0:T(8,128)S(1)} %shard_map.59.s), channel_id=1, source_target_pairs={{0,4},{1,0},{2,6},{3,7},{4,5},{5,1},{6,2},{7,3},{8,17},{9,13},{10,... | collective-permute-start | bytes 147464 | tf_op jit(solution)/shard_map/ppermute | solution.py:300
  24.2 1.2 %collective-permute-start.12 = (f32[16,768]{1,0:T(8,128)S(1)}, f32[16,768]{1,0:T(8,128)S(1)}, u32[]{:S(2)}, u32[]{:S(2)}) collective-permute-start(f32[16,768]{1,0:T(8,128)S(1)} %shard_map.60.s), channel_id=1, source_target_pairs={{0,4},{1,5},{2,6},{3,7},{4,0},{5,1},{6,2},{7,3},{8,12},{9,13},{10,... | collective-permute-start | bytes 147464 | tf_op jit(solution)/shard_map/ppermute | solution.py:300
  24.2 1.4 %collective-permute-start.11 = (f32[16,768]{1,0:T(8,128)S(1)}, f32[16,768]{1,0:T(8,128)S(1)}, u32[]{:S(2)}, u32[]{:S(2)}) collective-permute-start(f32[16,768]{1,0:T(8,128)S(1)} %shard_map.60.s), channel_id=1, source_target_pairs={{0,4},{1,3},{2,6},{3,7},{4,0},{5,1},{6,2},{7,5},{8,12},{9,13},{10,... | collective-permute-start | bytes 147464 | tf_op jit(solution)/shard_map/ppermute | solution.py:300
  26.6 1.2 %collective-permute-start.13 = (f32[16,768]{1,0:T(8,128)S(1)}, f32[16,768]{1,0:T(8,128)S(1)}, u32[]{:S(2)}, u32[]{:S(2)}) collective-permute-start(f32[16,768]{1,0:T(8,128)S(1)} %get-tuple-element.24), channel_id=1, source_target_pairs={{0,4},{1,5},{2,6},{3,7},{4,0},{5,1},{6,2},{7,3},{8,12},{9,13},{10,... | collective-permute-start | bytes 147464 | tf_op jit(solution)/shard_map/ppermute | solution.py:300
  26.6 1.4 %collective-permute-start.15 = (f32[16,768]{1,0:T(8,128)S(1)}, f32[16,768]{1,0:T(8,128)S(1)}, u32[]{:S(2)}, u32[]{:S(2)}) collective-permute-start(f32[16,768]{1,0:T(8,128)S(1)} %get-tuple-element.25.t), channel_id=1, source_target_pairs={{0,4},{1,5},{2,6},{3,7},{4,0},{5,1},{6,2},{7,3},{8,12},{9,13},{10,... | collective-permute-start | bytes 147464 | tf_op jit(solution)/shard_map/ppermute | solution.py:300
  27.1 1.2 %collective-permute-start.14 = (f32[16,768]{1,0:T(8,128)S(1)}, f32[16,768]{1,0:T(8,128)S(1)}, u32[]{:S(2)}, u32[]{:S(2)}) collective-permute-start(f32[16,768]{1,0:T(8,128)S(1)} %get-tuple-element.25.t), channel_id=1, source_target_pairs={{0,4},{1,5},{2,6},{3,7},{4,0},{5,1},{6,2},{7,3},{8,12},{9,13},{10,... | collective-permute-start | bytes 147464 | tf_op jit(solution)/shard_map/ppermute | solution.py:300
  28.8 1.2 %collective-permute-start.16 = (f32[16,768]{1,0:T(8,128)S(1)}, f32[16,768]{1,0:T(8,128)S(1)}, u32[]{:S(2)}, u32[]{:S(2)}) collective-permute-start(f32[16,768]{1,0:T(8,128)S(1)} %get-tuple-element.26), channel_id=1, source_target_pairs={{0,4},{1,5},{2,6},{3,7},{4,0},{5,1},{6,2},{7,3},{8,12},{9,13},{10,... | collective-permute-start | bytes 147464 | tf_op jit(solution)/shard_map/ppermute | solution.py:300
  28.8 1.4 %collective-permute-start.17 = (f32[16,768]{1,0:T(8,128)S(1)}, f32[16,768]{1,0:T(8,128)S(1)}, u32[]{:S(2)}, u32[]{:S(2)}) collective-permute-start(f32[16,768]{1,0:T(8,128)S(1)} %get-tuple-element.27), channel_id=1, source_target_pairs={{0,4},{1,5},{2,6},{3,7},{4,0},{5,1},{6,2},{7,3},{8,12},{9,13},{10,... | collective-permute-start | bytes 147464 | tf_op jit(solution)/shard_map/ppermute | solution.py:300
  30.7 15.7 %copy-start.2 = (s32[3,64]{1,0:T(4,128)S(1)}, s32[3,64]{1,0:T(4,128)}, u32[]{:S(2)}) copy-start(s32[3,64]{1,0:T(4,128)} %screen.1) | copy-start | bytes 2308
  30.7 12.5 %collective-permute-start.21 = (f32[16,768]{1,0:T(8,128)S(1)}, f32[16,768]{1,0:T(8,128)S(1)}, u32[]{:S(2)}, u32[]{:S(2)}) collective-permute-start(f32[16,768]{1,0:T(8,128)S(1)} %get-tuple-element.29), channel_id=1, source_target_pairs={{0,4},{1,5},{2,6},{3,7},{4,20},{5,1},{6,2},{7,24},{8,3},{9,13},{10... | collective-permute-start | bytes 147464 | tf_op jit(solution)/shard_map/ppermute | solution.py:300
  30.7 12.5 %collective-permute-start.20 = (f32[16,768]{1,0:T(8,128)S(1)}, f32[16,768]{1,0:T(8,128)S(1)}, u32[]{:S(2)}, u32[]{:S(2)}) collective-permute-start(f32[16,768]{1,0:T(8,128)S(1)} %get-tuple-element.29), channel_id=1, source_target_pairs={{0,4},{1,5},{2,6},{3,7},{4,0},{5,1},{6,9},{7,17},{8,2},{9,13},{10,... | collective-permute-start | bytes 147464 | tf_op jit(solution)/shard_map/ppermute | solution.py:300
  39.2 4.5 %collective-permute-start.19 = (f32[16,768]{1,0:T(8,128)S(1)}, f32[16,768]{1,0:T(8,128)S(1)}, u32[]{:S(2)}, u32[]{:S(2)}) collective-permute-start(f32[16,768]{1,0:T(8,128)S(1)} %get-tuple-element.29), channel_id=1, source_target_pairs={{0,4},{1,5},{2,6},{3,7},{4,0},{5,12},{6,25},{7,3},{8,1},{9,13},{10... | collective-permute-start | bytes 147464 | tf_op jit(solution)/shard_map/ppermute | solution.py:300
  39.2 5.1 %collective-permute-start.18 = (f32[16,768]{1,0:T(8,128)S(1)}, f32[16,768]{1,0:T(8,128)S(1)}, u32[]{:S(2)}, u32[]{:S(2)}) collective-permute-start(f32[16,768]{1,0:T(8,128)S(1)} %get-tuple-element.29), channel_id=1, source_target_pairs={{0,4},{1,5},{2,6},{3,7},{4,12},{5,20},{6,2},{7,3},{8,0},{9,13},{10... | collective-permute-start | bytes 147464 | tf_op jit(solution)/shard_map/ppermute | solution.py:300
  39.7 4.6 %collective-permute-start.24 = (f32[16,768]{1,0:T(8,128)S(1)}, f32[16,768]{1,0:T(8,128)S(1)}, u32[]{:S(2)}, u32[]{:S(2)}) collective-permute-start(f32[16,768]{1,0:T(8,128)S(1)} %get-tuple-element.30.t), channel_id=1, source_target_pairs={{0,4},{1,5},{2,6},{3,7},{4,0},{5,1},{6,2},{7,3},{8,11},{9,13},{10,... | collective-permute-start | bytes 147464 | tf_op jit(solution)/shard_map/ppermute | solution.py:300
  43.2 1.2 %collective-permute-start.23 = (f32[16,768]{1,0:T(8,128)S(1)}, f32[16,768]{1,0:T(8,128)S(1)}, u32[]{:S(2)}, u32[]{:S(2)}) collective-permute-start(f32[16,768]{1,0:T(8,128)S(1)} %get-tuple-element.30.t), channel_id=1, source_target_pairs={{0,4},{1,5},{2,6},{3,7},{4,0},{5,1},{6,2},{7,3},{8,10},{9,13},{10,... | collective-permute-start | bytes 147464 | tf_op jit(solution)/shard_map/ppermute | solution.py:300
  43.2 1.4 %collective-permute-start.22 = (f32[16,768]{1,0:T(8,128)S(1)}, f32[16,768]{1,0:T(8,128)S(1)}, u32[]{:S(2)}, u32[]{:S(2)}) collective-permute-start(f32[16,768]{1,0:T(8,128)S(1)} %get-tuple-element.30.t), channel_id=1, source_target_pairs={{0,4},{1,5},{2,6},{3,7},{4,0},{5,1},{6,2},{7,3},{8,9},{9,13},{10,1... | collective-permute-start | bytes 147464 | tf_op jit(solution)/shard_map/ppermute | solution.py:300
  44.7 1.3 %collective-permute-start.25 = (f32[16,768]{1,0:T(8,128)S(1)}, f32[16,768]{1,0:T(8,128)S(1)}, u32[]{:S(2)}, u32[]{:S(2)}) collective-permute-start(f32[16,768]{1,0:T(8,128)S(1)} %shard_map.64.own), channel_id=1, source_target_pairs={{0,4},{4,0},{8,12},{12,8},{16,20},{20,16},{24,28},{28,24},{1,5},{5... | collective-permute-start | bytes 147464 | tf_op jit(solution)/shard_map/ppermute | solution.py:313

commit v11 on v10

--- a/solution.py
+++ b/solution.py
@@ -114,32 +114,92 @@
     )
 
 
+def slab(screen, stacked, left, right, member, index):
+    strips = left.shape[0] // TILE
+    count = stacked.shape[0] // strips
+    members, base = index
+    chunk = 2 * left.shape[1] // members
+    held = left if 2 * base < members else right
+    offset = 0 if held is left else members // 2
+    columns = pl.ds(pl.multiple_of((member - offset) * chunk, TILE), chunk)
+    parts = jnp.dot(stacked, held[:, columns], preferred_element_type=F32)
+    tiles = []
+    for t in range(chunk // TILE):
+        total = jnp.zeros((count, TILE), F32)
+        for i in range(strips):
+            part = parts[i * count : (i + 1) * count, t * TILE : (t + 1) * TILE]
+            total += jnp.where(screen[i, member * (chunk // TILE) + t] != 0, part, 0.0)
+        tiles.append(total)
+    return jnp.concatenate(tiles, axis=1)
+
+
+def by_strip(value, strips):
+    strip_of = lax.broadcasted_iota(jnp.int32, value.shape, 1) // TILE
+    return jnp.concatenate(
+        [jnp.where(strip_of == i, value, jnp.zeros((), BF16)) for i in range(strips)]
+    )
+
+
 def coulomb(screen, rounded, left, right, out):
-    members, count, chunk = out.shape
-    height, width = left.shape
-    strips = height // TILE
-    value = rounded[...]
-    strip_of = lax.broadcasted_iota(jnp.int32, value.shape, 1) // TILE
-    stacked = jnp.concatenate(
-        [jnp.where(strip_of == i, value, jnp.zeros((), BF16)) for i in range(strips)]
-    )
+    members = out.shape[0]
+    stacked = by_strip(rounded[...], left.shape[0] // TILE)
     for m in range(members):
-        held = left if m * chunk < width else right
-        start = m * chunk if held is left else m * chunk - width
-        parts = jnp.dot(stacked, held[:, start : start + chunk], preferred_element_type=F32)
-        for t in range(chunk // TILE):
-            lanes = slice(t * TILE, (t + 1) * TILE)
-            total = jnp.zeros((count, TILE), F32)
-            for i in range(strips):
-                part = parts[i * count : (i + 1) * count, lanes]
-                total += jnp.where(screen[i, m * chunk // TILE + t] != 0, part, 0.0)
-            out[m, :, lanes] = total.astype(out.dtype)
+        out[m] = slab(screen, stacked, left, right, m, (members, m)).astype(out.dtype)
+
+
+def coulomb_side(side, screen, rounded, left, right, out):
+    chips = out.shape[0]
+    stacked = by_strip(rounded[...], left.shape[0] // TILE)
+    for k in range(chips):
+        part = slab(screen, stacked, left, right, 2 * k + side, (2 * chips, 2 * k))
+        out[k] = part.astype(out.dtype)
+
+
+def coulomb_mate(*refs):
+    coulomb_side(1 - side_of(), *refs)
+
+
+def coulomb_own(*refs):
+    coulomb_side(side_of(), *refs)
+
+
+def share(own, got, keep, one, two, three):
+    block = block_of()
+    keep[...] = own[block] + got[block].astype(F32)
+    for distance, out in ((1, one), (2, two), (3, three)):
+        chip = lax.bitwise_xor(block, distance)
+        out[...] = (own[chip] + got[chip].astype(F32)).astype(out.dtype)
+
+
+def gather_up(keep, one, two, three, out):
+    out[...] = keep[...] + one[...].astype(F32) + two[...].astype(F32) + three[...].astype(F32)
 
 
 def coulomb_partial(rounded, left, right, screen):
     members = lax.axis_size("aux")
     out = struct((members, rounded.shape[0], 2 * left.shape[1] // members), BF16)
     return call(coulomb, out, screen, rounded, left, right, specs=[SMEM, VMEM, VMEM, VMEM])
+
+
+def chip_coulomb(rounded, left, right, screen):
+    members = 2 * SOLVE_BLOCKS
+    count = rounded.shape[0]
+    chunk = 2 * left.shape[1] // members
+    specs = [SMEM, VMEM, VMEM, VMEM]
+    operands = (screen, rounded, left, right)
+    given = call(coulomb_mate, struct((SOLVE_BLOCKS, count, chunk), BF16), *operands, specs=specs)
+
+    def move(value, to):
+        return lax.ppermute(value, "aux", [(i, to(i)) for i in range(members)])
+
+    got = move(given, lambda i: i ^ 1)
+    own = call(coulomb_own, struct((SOLVE_BLOCKS, count, chunk)), *operands, specs=specs)
+    piece = struct((count, chunk), BF16)
+    keep, one, two, three = call(share, [struct((count, chunk))] + [piece] * 3, own, got)
+    three = move(three, lambda i: i ^ 6)
+    one = move(one, lambda i: i ^ 2)
+    two = move(two, lambda i: i ^ 4)
+    return call(gather_up, struct((count, chunk)), keep, one, two, three)
 
 
 def scatter_sum(slabs):
@@ -161,10 +221,19 @@
     return both[:rows] + both[rows:]
 
 
-def prepare(inv0, inv1, fac0, fac1, k_high, k_low, kt_high, kt_low, lhs, rhs):
+def prepare_first(*refs):
+    here = (block_of() == 0) | (lax.axis_index("pair") > 0)
+    prepare(here, *refs)
+
+
+def prepare_later(*refs):
+    prepare(lax.axis_index("pair") == 0, *refs)
+
+
+def prepare(here, inv0, inv1, fac0, fac1, k_high, k_low, kt_high, kt_low, lhs, rhs):
     height = inv0.shape[0]
 
-    @pl.when((block_of() > 0) & (side_of() == 0))
+    @pl.when(here & (block_of() > 0) & (side_of() == 0))
     def _():
         for n, (inv, fac) in enumerate(((inv0, fac0), (inv1, fac1))):
             rows = [slice((3 * n + r) * height, (3 * n + r + 1) * height) for r in range(3)]
@@ -183,7 +252,7 @@
             kt_high[:, part], kt_low[:, part] = high_low(product.T)
 
 
-def begin(f0, f1, f2, f3, inv, out):
+def begin(f0, f1, f2, f3, inv, after, out):
     high, low = high_low(inv[...])
     out[...] = times(f0[...] + f1[...] + f2[...] + f3[...], high, low)
 
@@ -225,15 +294,20 @@
 
 
 @lead_only
-def back_two(into, near, far, t, s, high, low, settled, back, mixed):
+def back_two(into, near, far, t, s, high, low, high0, low0, settled, back, mixed):
     plane = lax.axis_index("pair")
     last = block_of() == 3
     passed = jnp.where(plane == 0, far[...], jnp.where(plane == 1, near[...], t[...]))
     value = jnp.where(last, passed, s[...] - into[...])
-    product = times(value, high[...], low[...])
     settled[...] = value
-    back[...] = product
-    mixed[...] = jnp.where(last, product, value)
+
+    def multiply(high, low):
+        product = times(value, high[...], low[...])
+        back[...] = product
+        mixed[...] = jnp.where(last, product, value)
+
+    pl.when(plane == 0)(lambda: multiply(high0, low0))
+    pl.when(plane > 0)(lambda: multiply(high, low))
 
 
 @lead_only
@@ -314,16 +388,14 @@
 
     panel = struct((count, size))
     square = struct((size, size), BF16)
-    k_high, k_low, kt_high, kt_low = call(
-        prepare,
-        [square] * 4,
-        diag_inv,
-        swap(diag_inv),
-        factor,
-        swap(factor),
-        limit=32,
-        scratch=[pltpu.VMEM((3 * size, size), BF16)] * 2,
-    )
+    halves = (diag_inv, swap(diag_inv), factor, swap(factor))
+
+    def prepared(kernel):
+        scratch = [pltpu.VMEM((3 * size, size), BF16)] * 2
+        return call(kernel, [square] * 4, *halves, limit=32, scratch=scratch)
+
+    k_high, k_low, kt_high, kt_low = prepared(prepare_first)
+    at_zero = prepared(prepare_later)
     home = [1, 1, 1, 2]
     gathered = []
     for route in ("far", "middle", "other"):
@@ -336,14 +408,14 @@
                 loop = [device((k, plane), c) for plane in ring[route]]
                 to.update(zip(loop, loop[1:] + loop[:1]))
         gathered.append(permute(partial_fit, to))
-    e = call(begin, panel, partial_fit, *gathered, diag_inv)
+    e = call(begin, panel, partial_fit, *gathered, diag_inv, k_high)
     e = call(both, panel, e, swap(e))
     reach = [
         send(e, ((0, 1), (1, 0))),
         send(e, ((0, 1), (2, 0)), ((1, 1), (1, 0))),
         send(e, ((0, 1), (3, 0))),
     ]
-    one = call(after_zero, panel, *reach, e, kt_high, kt_low)
+    one = call(after_zero, panel, *reach, e, *at_zero[2:])
     first = send(one, ((1, 0), (2, 1)), ((3, 0), (3, 1)), ((0, 1), (0, 0)))
     second = send(one, ((1, 0), (3, 1)), ((2, 0), (2, 1)), ((0, 1), (0, 2)))
     two = call(after_one, panel, first, second, e, kt_high, kt_low)
@@ -353,10 +425,10 @@
     into = send(back, ((3, 2), (2, 1)))
     near = send(t, ((3, 2), (3, 1)))
     far = send(t, ((3, 2), (3, 0)))
-    t, back, mixed = call(back_two, [panel] * 3, into, near, far, t, two, k_high, k_low)
+    t, back, mixed = call(back_two, [panel] * 3, into, near, far, t, two, k_high, k_low, *at_zero[:2])
     into = send(back, ((2, 1), (1, 0)), ((3, 0), (2, 0)))
     other = send(mixed, ((3, 1), (1, 0)), ((2, 1), (2, 0)))
-    t, back = call(back_one, [panel] * 2, into, other, t, one, k_high, k_low)
+    t, back = call(back_one, [panel] * 2, into, other, t, one, *at_zero[:2])
     near = {
         ((1, 0), (0, 3)): (3, 0),
         ((1, 0), (0, 2)): (1, 1),
@@ -448,6 +520,8 @@
     solve = chip_solve if chip_blocks else chain_solve
     left, right, partial_fit = fit_partial(densities, integrals, screen)
     rounded = solve(partial_fit, factor, diag_inv)
+    if chip_blocks:
+        return chip_coulomb(rounded, left, right, screen)
     return scatter_sum(coulomb_partial(rounded, left, right, screen))
 
 

time: 61.3 us -> 60.1 us (0.980)
  blocking collectives: 12.2 us -> 0 us
  starting transfers between devices: 19.5 us -> 25.1 us
  waiting for transfers between devices: 18.8 us -> 23.4 us
  Pallas kernels: 9.78 us -> 11.4 us
  other arithmetic: 0.67 us -> 0 us
    all_to_all x1 -> x0, blocking collectives: 12.2 us -> none  [scatter_sum(): arrived = lax.all_to_all(slabs, 'aux', 0, 0, tiled=True)]
    ppermute x0 -> x4, starting transfers between devices: none -> 5.5 us  [move(): return lax.ppermute(value, 'aux', [(i, to(i)) for i in range(members)])]
    ppermute x0 -> x4, waiting for transfers between devices: none -> 4.57 us  [move(): return lax.ppermute(value, 'aux', [(i, to(i)) for i in range(members)])]
    pallas_call x12 -> x16, Pallas kernels: 9.78 us -> 11.4 us  [call(): pl.pallas_call(kernel, out_shape=outs, in_specs=specs or [VMEM] * len(ope...]
    reduce_sum x1 -> x0, other arithmetic: 0.67 us -> none  [scatter_sum(): return jnp.sum(arrived.astype(F32), axis=0)]
  transfers between devices with their start and end apart: 26 -> 30, of which waited for: 19 -> 22; matrix products, arithmetic and copies ran while one was open for 0% -> 0% of each run, Pallas kernels for 7% -> 9%
where the time goes in v11:
time: 60.1 us; the launch traced here: 59.9 us
  starting transfers between devices  25.1 us (42%)
  waiting for transfers between devices  23.4 us (39%)
  Pallas kernels  11.4 us (19%)
    ppermute x22, starting transfers between devices, permute(): return lax.ppermute(value, AXES, sorted(to.items()))  18.6 us
    ppermute x22, waiting for transfers between devices, permute(): return lax.ppermute(value, AXES, sorted(to.items()))  16.7 us
    pallas_call x16, Pallas kernels, call(): pl.pallas_call(kernel, out_shape=outs, in_specs=specs or [VMEM] * len(ope...  11.4 us
    ppermute x4, starting transfers between devices, move(): return lax.ppermute(value, 'aux', [(i, to(i)) for i in range(members)])  5.5 us
    ppermute x4, waiting for transfers between devices, move(): return lax.ppermute(value, 'aux', [(i, to(i)) for i in range(members)])  4.57 us
    ppermute x4, waiting for transfers between devices, swap(): lax.ppermute(value, 'aux', [(i, i ^ 1) for i in range(2 * SOLVE_BLOCKS)])  2.14 us
  transfers between devices with their start and end apart: 30, of which 22 were waited for; matrix products, arithmetic and copies ran while one was open for 0% of the time, Pallas kernels for 9%

profile of v11, /device:TPU:0, one launch (start us, length us, event | category | flops | bytes accessed | tf_op | source)
XLA Modules:
  0.0 59.9 jit_solution(2724921213280814091)
XLA Ops:
  0.0 0.5 collective-permute-start.4
  0.6 4.3 %shard_map.55 = (bf16[384,4096]{1,0:T(8,128)(2,1)S(1)}, bf16[384,4096]{1,0:T(8,128)(2,1)S(1)}, f32[16,384]{1,0:T(8,128)S(1)}) custom-call(s32[3,64]{1,0:T(4,128)} %refs_0_.7, bf16[16,8192]{1,0:T(8,128)(2,1)} %densities_in.1, bf16[384,8192]{1,0:T(8,128)(2,1)} %integrals.1), custom_call_target="tpu_custom_call" | custom-call | tf_op jit(solution)/shard_map/pallas_call | solution.py:30
  4.9 3.1 %collective-permute-start.2 = (f32[16,384]{1,0:T(8,128)S(1)}, f32[16,384]{1,0:T(8,128)S(1)}, u32[]{:S(2)}, u32[]{:S(2)}) collective-permute-start(f32[16,384]{1,0:T(8,128)S(1)} %get-tuple-element.27.f0), channel_id=1, source_target_pairs={{0,1},{1,0},{2,6},{3,7},{4,5},{5,4},{6,2},{7,3},{8,9},{9,8},{10,14... | collective-permute-start | bytes 73736 | tf_op jit(solution)/shard_map/ppermute | solution.py:374
  8.0 0.5 collective-permute-start
  8.6 1.2 %collective-permute-done.2.f3 = f32[16,384]{1,0:T(8,128)S(1)} collective-permute-done((f32[16,384]{1,0:T(8,128)S(1)}, f32[16,384]{1,0:T(8,128)S(1)}, u32[]{:S(2)}, u32[]{:S(2)}) %collective-permute-start.2) | collective-permute-done | bytes 24608 | tf_op jit(solution)/shard_map/ppermute | solution.py:374
  10.2 1.2 %collective-permute-done.5.mate = f32[16,768]{1,0:T(8,128)S(1)} collective-permute-done((f32[16,768]{1,0:T(8,128)S(1)}, f32[16,768]{1,0:T(8,128)S(1)}, u32[]{:S(2)}, u32[]{:S(2)}) %collective-permute-start.5) | collective-permute-done | bytes 49184 | tf_op jit(solution)/shard_map/ppermute | solution.py:387
  12.1 0.6 %collective-permute-done.8.three = f32[16,768]{1,0:T(8,128)S(1)} collective-permute-done((f32[16,768]{1,0:T(8,128)S(1)}, f32[16,768]{1,0:T(8,128)S(1)}, u32[]{:S(2)}, u32[]{:S(2)}) %collective-permute-start.8) | collective-permute-done | bytes 49184 | tf_op jit(solution)/shard_map/ppermute | solution.py:374
  13.7 0.5 collective-permute-start.9
  14.2 0.7 %collective-permute-done.10.second.z2 = f32[16,768]{1,0:T(8,128)S(1)} collective-permute-done((f32[16,768]{1,0:T(8,128)S(1)}, f32[16,768]{1,0:T(8,128)S(1)}, u32[]{:S(2)}, u32[]{:S(2)}) %collective-permute-start.10) | collective-permute-done | bytes 49184 | tf_op jit(solution)/shard_map/ppermute | solution.py:374
  15.0 8.9 %collective-permute-done.9.first.z0 = f32[16,768]{1,0:T(8,128)S(1)} collective-permute-done((f32[16,768]{1,0:T(8,128)S(1)}, f32[16,768]{1,0:T(8,128)S(1)}, u32[]{:S(2)}, u32[]{:S(2)}) %collective-permute-start.9) | collective-permute-done | bytes 49184 | tf_op jit(solution)/shard_map/ppermute | solution.py:374
  24.4 0.5 collective-permute-start.11
  24.9 0.7 %collective-permute-done.12.known = f32[16,768]{1,0:T(8,128)S(1)} collective-permute-done((f32[16,768]{1,0:T(8,128)S(1)}, f32[16,768]{1,0:T(8,128)S(1)}, u32[]{:S(2)}, u32[]{:S(2)}) %collective-permute-start.12) | collective-permute-done | bytes 49184 | tf_op jit(solution)/shard_map/ppermute | solution.py:374
  25.7 1.0 %shard_map.62 = (f32[16,768]{1,0:T(8,128)S(1)}, f32[16,768]{1,0:T(8,128)S(1)}) custom-call(f32[16,768]{1,0:T(8,128)S(1)} %collective-permute-done.12.known, f32[16,768]{1,0:T(8,128)S(1)} %collective-permute-done.11.behind.z3, f32[16,768]{1,0:T(8,128)S(1)} %shard_map.58.e.z1, bf16[768,768]{1,0:T(8,128)(2,1)S(1)} %get-tuple-element.31.high.kt_high, ...), custom_call_target="tpu_custom_call" | custom-call | tf_op jit(solution)/shard_map/pallas_call | solution.py:30
  26.8 0.5 collective-permute-start.15
  27.3 0.7 %collective-permute-done.13.into = f32[16,768]{1,0:T(8,128)S(1)} collective-permute-done((f32[16,768]{1,0:T(8,128)S(1)}, f32[16,768]{1,0:T(8,128)S(1)}, u32[]{:S(2)}, u32[]{:S(2)}) %collective-permute-start.13) | collective-permute-done | bytes 49184 | tf_op jit(solution)/shard_map/ppermute | solution.py:374
  28.5 0.5 shard_map.63
  29.0 0.5 collective-permute-start.17
  29.5 0.7 %collective-permute-done.16.into = f32[16,768]{1,0:T(8,128)S(1)} collective-permute-done((f32[16,768]{1,0:T(8,128)S(1)}, f32[16,768]{1,0:T(8,128)S(1)}, u32[]{:S(2)}, u32[]{:S(2)}) %collective-permute-start.16) | collective-permute-done | bytes 49184 | tf_op jit(solution)/shard_map/ppermute | solution.py:374
  30.9 8.5 %collective-permute-start.20 = (f32[16,768]{1,0:T(8,128)S(1)}, f32[16,768]{1,0:T(8,128)S(1)}, u32[]{:S(2)}, u32[]{:S(2)}) collective-permute-start(f32[16,768]{1,0:T(8,128)S(1)} %get-tuple-element.41), channel_id=1, source_target_pairs={{0,4},{1,5},{2,6},{3,7},{4,0},{5,1},{6,9},{7,17},{8,2},{9,13},{10,... | collective-permute-start | bytes 147464 | tf_op jit(solution)/shard_map/ppermute | solution.py:374
  39.4 0.5 collective-permute-start.18
  39.9 2.7 %collective-permute-start.24 = (f32[16,768]{1,0:T(8,128)S(1)}, f32[16,768]{1,0:T(8,128)S(1)}, u32[]{:S(2)}, u32[]{:S(2)}) collective-permute-start(f32[16,768]{1,0:T(8,128)S(1)} %get-tuple-element.42.t), channel_id=1, source_target_pairs={{0,4},{1,5},{2,6},{3,7},{4,0},{5,1},{6,2},{7,3},{8,11},{9,13},{10,... | collective-permute-start | bytes 147464 | tf_op jit(solution)/shard_map/ppermute | solution.py:374
  42.6 0.8 %collective-permute-done.21.i3 = f32[16,768]{1,0:T(8,128)S(1)} collective-permute-done((f32[16,768]{1,0:T(8,128)S(1)}, f32[16,768]{1,0:T(8,128)S(1)}, u32[]{:S(2)}, u32[]{:S(2)}) %collective-permute-start.21) | collective-permute-done | bytes 49184 | tf_op jit(solution)/shard_map/ppermute | solution.py:374
  43.4 0.5 collective-permute-start.22
  43.9 0.6 %collective-permute-done.18.i0 = f32[16,768]{1,0:T(8,128)S(1)} collective-permute-done((f32[16,768]{1,0:T(8,128)S(1)}, f32[16,768]{1,0:T(8,128)S(1)}, u32[]{:S(2)}, u32[]{:S(2)}) %collective-permute-start.18) | collective-permute-done | bytes 49184 | tf_op jit(solution)/shard_map/ppermute | solution.py:374
  45.3 0.9 %collective-permute-done.25.mate = f32[16,768]{1,0:T(8,128)S(1)} collective-permute-done((f32[16,768]{1,0:T(8,128)S(1)}, f32[16,768]{1,0:T(8,128)S(1)}, u32[]{:S(2)}, u32[]{:S(2)}) %collective-permute-start.25) | collective-permute-done | bytes 49184 | tf_op jit(solution)/shard_map/ppermute | solution.py:387
  46.6 1.3 %shard_map.68 = bf16[4,16,1024]{2,1,0:T(8,128)(2,1)S(1)} custom-call(s32[3,64]{1,0:T(4,128)S(1)} %copy-done.2, bf16[16,384]{1,0:T(8,128)(2,1)S(1)} %shard_map.66.refs_1_, bf16[384,4096]{1,0:T(8,128)(2,1)S(1)} %get-tuple-element.43.refs_2_, bf16[384,4096]{1,0:T(8,128)(2,1)S(1)} %get-tuple-element.44.refs_3_), custom_call_target="tpu_custom_call" | custom-call | tf_op jit(solution)/shard_map/pallas_call | solution.py:30
  48.3 1.3 %shard_map.67.own = f32[4,16,1024]{2,1,0:T(8,128)S(1)} custom-call(s32[3,64]{1,0:T(4,128)S(1)} %copy-done.2, bf16[16,384]{1,0:T(8,128)(2,1)S(1)} %shard_map.66.refs_1_, bf16[384,4096]{1,0:T(8,128)(2,1)S(1)} %get-tuple-element.43.refs_2_, bf16[384,4096]{1,0:T(8,128)(2,1)S(1)} %get-tuple-element.44.refs_3_), custom_call_target="tpu_custom_call" | custom-call | tf_op jit(solution)/shard_map/pallas_call | solution.py:30
  49.6 3.5 %collective-permute-start.27 = (bf16[16,1024]{1,0:T(8,128)(2,1)S(1)}, bf16[16,1024]{1,0:T(8,128)(2,1)S(1)}, u32[]{:S(2)}, u32[]{:S(2)}) collective-permute-start(bf16[16,1024]{1,0:T(8,128)(2,1)S(1)} %get-tuple-element.46), channel_id=1, source_target_pairs={{0,8},{4,12},{8,0},{12,4},{16,24},{20,28},{24,16},{28,20},{1,9},{5... | collective-permute-start | bytes 98312 | tf_op jit(solution)/shard_map/ppermute | solution.py:193
  53.2 1.3 %collective-permute-start.28 = (bf16[16,1024]{1,0:T(8,128)(2,1)S(1)}, bf16[16,1024]{1,0:T(8,128)(2,1)S(1)}, u32[]{:S(2)}, u32[]{:S(2)}) collective-permute-start(bf16[16,1024]{1,0:T(8,128)(2,1)S(1)} %get-tuple-element.47), channel_id=1, source_target_pairs={{0,16},{4,20},{8,24},{12,28},{16,0},{20,4},{24,8},{28,12},{1,17},{... | collective-permute-start | bytes 98312 | tf_op jit(solution)/shard_map/ppermute | solution.py:193
  55.1 2.0 %collective-permute-done.28.two = bf16[16,1024]{1,0:T(8,128)(2,1)S(1)} collective-permute-done((bf16[16,1024]{1,0:T(8,128)(2,1)S(1)}, bf16[16,1024]{1,0:T(8,128)(2,1)S(1)}, u32[]{:S(2)}, u32[]{:S(2)}) %collective-permute-start.28) | collective-permute-done | bytes 32800 | tf_op jit(solution)/shard_map/ppermute | solution.py:193
  57.1 2.2 %collective-permute-done.29.three = bf16[16,1024]{1,0:T(8,128)(2,1)S(1)} collective-permute-done((bf16[16,1024]{1,0:T(8,128)(2,1)S(1)}, bf16[16,1024]{1,0:T(8,128)(2,1)S(1)}, u32[]{:S(2)}, u32[]{:S(2)}) %collective-permute-start.29) | collective-permute-done | bytes 32800 | tf_op jit(solution)/shard_map/ppermute | solution.py:193
  59.3 0.6 %shard_map.70 = f32[16,1024]{1,0:T(8,128)} custom-call(f32[16,1024]{1,0:T(8,128)S(1)} %get-tuple-element.45.keep, bf16[16,1024]{1,0:T(8,128)(2,1)S(1)} %collective-permute-done.27.one, bf16[16,1024]{1,0:T(8,128)(2,1)S(1)} %collective-permute-done.28.two, bf16[16,1024]{1,0:T(8,128)(2,1)S(1)} %collective-permute-done.29.three), custom_call_target="tpu_custom_call" | custom-call | tf_op jit(solution)/shard_map/pallas_call | solution.py:30
  (50 shorter events, 6.2 us)
Async XLA Ops:
  0.0 8.6 %copy-start = (f32[384,768]{1,0:T(8,128)S(1)}, f32[384,768]{1,0:T(8,128)}, u32[]{:S(2)}) copy-start(f32[384,768]{1,0:T(8,128)} %inv.3) | copy-start | bytes 3538948
  0.0 8.5 %collective-permute-start.4 = (f32[384,768]{1,0:T(8,128)}, f32[384,768]{1,0:T(8,128)S(1)}, u32[]{:S(2)}, u32[]{:S(2)}) collective-permute-start(f32[384,768]{1,0:T(8,128)} %refs_2_.3), channel_id=1, source_target_pairs={{0,4},{4,0},{8,12},{12,8},{16,20},{20,16},{24,28},{28,24},{1,5},{5... | collective-permute-start | bytes 3538952 | tf_op jit(solution)/shard_map/ppermute | solution.py:387
  0.5 8.1 %collective-permute-start.3 = (f32[384,768]{1,0:T(8,128)}, f32[384,768]{1,0:T(8,128)S(1)}, u32[]{:S(2)}, u32[]{:S(2)}) collective-permute-start(f32[384,768]{1,0:T(8,128)} %inv.3), channel_id=1, source_target_pairs={{0,4},{4,0},{8,12},{12,8},{16,20},{20,16},{24,28},{28,24},{1,5},{5... | collective-permute-start | bytes 3538952 | tf_op jit(solution)/shard_map/ppermute | solution.py:387
  4.9 4.9 %collective-permute-start.2 = (f32[16,384]{1,0:T(8,128)S(1)}, f32[16,384]{1,0:T(8,128)S(1)}, u32[]{:S(2)}, u32[]{:S(2)}) collective-permute-start(f32[16,384]{1,0:T(8,128)S(1)} %get-tuple-element.27.f0), channel_id=1, source_target_pairs={{0,1},{1,0},{2,6},{3,7},{4,5},{5,4},{6,2},{7,3},{8,9},{9,8},{10,14... | collective-permute-start | bytes 73736 | tf_op jit(solution)/shard_map/ppermute | solution.py:374
  8.0 1.8 %collective-permute-start.1 = (f32[16,384]{1,0:T(8,128)S(1)}, f32[16,384]{1,0:T(8,128)S(1)}, u32[]{:S(2)}, u32[]{:S(2)}) collective-permute-start(f32[16,384]{1,0:T(8,128)S(1)} %get-tuple-element.27.f0), channel_id=1, source_target_pairs={{0,4},{1,2},{2,1},{3,7},{4,0},{5,6},{6,5},{7,3},{8,12},{9,10},{10,... | collective-permute-start | bytes 73736 | tf_op jit(solution)/shard_map/ppermute | solution.py:374
  8.0 1.8 %collective-permute-start = (f32[16,384]{1,0:T(8,128)S(1)}, f32[16,384]{1,0:T(8,128)S(1)}, u32[]{:S(2)}, u32[]{:S(2)}) collective-permute-start(f32[16,384]{1,0:T(8,128)S(1)} %get-tuple-element.27.f0), channel_id=1, source_target_pairs={{0,4},{1,2},{2,3},{3,1},{4,0},{5,6},{6,7},{7,5},{8,12},{9,10},{10,... | collective-permute-start | bytes 73736 | tf_op jit(solution)/shard_map/ppermute | solution.py:374
  10.2 1.3 %collective-permute-start.5 = (f32[16,768]{1,0:T(8,128)S(1)}, f32[16,768]{1,0:T(8,128)S(1)}, u32[]{:S(2)}, u32[]{:S(2)}) collective-permute-start(f32[16,768]{1,0:T(8,128)S(1)} %shard_map.57.own), channel_id=1, source_target_pairs={{0,4},{4,0},{8,12},{12,8},{16,20},{20,16},{24,28},{28,24},{1,5},{5... | collective-permute-start | bytes 147464 | tf_op jit(solution)/shard_map/ppermute | solution.py:387
  11.4 1.3 %collective-permute-start.8 = (f32[16,768]{1,0:T(8,128)S(1)}, f32[16,768]{1,0:T(8,128)S(1)}, u32[]{:S(2)}, u32[]{:S(2)}) collective-permute-start(f32[16,768]{1,0:T(8,128)S(1)} %shard_map.58.e.z1), channel_id=1, source_target_pairs={{0,4},{1,24},{2,6},{3,7},{4,0},{5,1},{6,2},{7,3},{8,12},{9,13},{10... | collective-permute-start | bytes 147464 | tf_op jit(solution)/shard_map/ppermute | solution.py:374
  11.6 1.3 %collective-permute-start.7 = (f32[16,768]{1,0:T(8,128)S(1)}, f32[16,768]{1,0:T(8,128)S(1)}, u32[]{:S(2)}, u32[]{:S(2)}) collective-permute-start(f32[16,768]{1,0:T(8,128)S(1)} %shard_map.58.e.z1), channel_id=1, source_target_pairs={{0,4},{1,16},{2,6},{3,7},{4,0},{5,1},{6,2},{7,3},{8,12},{9,8},{10,... | collective-permute-start | bytes 147464 | tf_op jit(solution)/shard_map/ppermute | solution.py:374
  12.0 1.2 %collective-permute-start.6 = (f32[16,768]{1,0:T(8,128)S(1)}, f32[16,768]{1,0:T(8,128)S(1)}, u32[]{:S(2)}, u32[]{:S(2)}) collective-permute-start(f32[16,768]{1,0:T(8,128)S(1)} %shard_map.58.e.z1), channel_id=1, source_target_pairs={{0,4},{1,8},{2,6},{3,7},{4,0},{5,1},{6,2},{7,3},{8,12},{9,13},{10,... | collective-permute-start | bytes 147464 | tf_op jit(solution)/shard_map/ppermute | solution.py:374
  13.7 1.2 %collective-permute-start.10 = (f32[16,768]{1,0:T(8,128)S(1)}, f32[16,768]{1,0:T(8,128)S(1)}, u32[]{:S(2)}, u32[]{:S(2)}) collective-permute-start(f32[16,768]{1,0:T(8,128)S(1)} %shard_map.60.s), channel_id=1, source_target_pairs={{0,4},{1,2},{2,6},{3,7},{4,0},{5,1},{6,5},{7,3},{8,25},{9,13},{10,... | collective-permute-start | bytes 147464 | tf_op jit(solution)/shard_map/ppermute | solution.py:374
  13.7 10.1 %collective-permute-start.9 = (f32[16,768]{1,0:T(8,128)S(1)}, f32[16,768]{1,0:T(8,128)S(1)}, u32[]{:S(2)}, u32[]{:S(2)}) collective-permute-start(f32[16,768]{1,0:T(8,128)S(1)} %shard_map.60.s), channel_id=1, source_target_pairs={{0,4},{1,0},{2,6},{3,7},{4,5},{5,1},{6,2},{7,3},{8,17},{9,13},{10,... | collective-permute-start | bytes 147464 | tf_op jit(solution)/shard_map/ppermute | solution.py:374
  24.3 1.2 %collective-permute-start.12 = (f32[16,768]{1,0:T(8,128)S(1)}, f32[16,768]{1,0:T(8,128)S(1)}, u32[]{:S(2)}, u32[]{:S(2)}) collective-permute-start(f32[16,768]{1,0:T(8,128)S(1)} %shard_map.61.s), channel_id=1, source_target_pairs={{0,4},{1,5},{2,6},{3,7},{4,0},{5,1},{6,2},{7,3},{8,12},{9,13},{10,... | collective-permute-start | bytes 147464 | tf_op jit(solution)/shard_map/ppermute | solution.py:374
  24.4 1.4 %collective-permute-start.11 = (f32[16,768]{1,0:T(8,128)S(1)}, f32[16,768]{1,0:T(8,128)S(1)}, u32[]{:S(2)}, u32[]{:S(2)}) collective-permute-start(f32[16,768]{1,0:T(8,128)S(1)} %shard_map.61.s), channel_id=1, source_target_pairs={{0,4},{1,3},{2,6},{3,7},{4,0},{5,1},{6,2},{7,5},{8,12},{9,13},{10,... | collective-permute-start | bytes 147464 | tf_op jit(solution)/shard_map/ppermute | solution.py:374
  26.8 1.2 %collective-permute-start.13 = (f32[16,768]{1,0:T(8,128)S(1)}, f32[16,768]{1,0:T(8,128)S(1)}, u32[]{:S(2)}, u32[]{:S(2)}) collective-permute-start(f32[16,768]{1,0:T(8,128)S(1)} %get-tuple-element.34), channel_id=1, source_target_pairs={{0,4},{1,5},{2,6},{3,7},{4,0},{5,1},{6,2},{7,3},{8,12},{9,13},{10,... | collective-permute-start | bytes 147464 | tf_op jit(solution)/shard_map/ppermute | solution.py:374
  26.8 1.4 %collective-permute-start.15 = (f32[16,768]{1,0:T(8,128)S(1)}, f32[16,768]{1,0:T(8,128)S(1)}, u32[]{:S(2)}, u32[]{:S(2)}) collective-permute-start(f32[16,768]{1,0:T(8,128)S(1)} %get-tuple-element.35.t), channel_id=1, source_target_pairs={{0,4},{1,5},{2,6},{3,7},{4,0},{5,1},{6,2},{7,3},{8,12},{9,13},{10,... | collective-permute-start | bytes 147464 | tf_op jit(solution)/shard_map/ppermute | solution.py:374
  27.3 1.2 %collective-permute-start.14 = (f32[16,768]{1,0:T(8,128)S(1)}, f32[16,768]{1,0:T(8,128)S(1)}, u32[]{:S(2)}, u32[]{:S(2)}) collective-permute-start(f32[16,768]{1,0:T(8,128)S(1)} %get-tuple-element.35.t), channel_id=1, source_target_pairs={{0,4},{1,5},{2,6},{3,7},{4,0},{5,1},{6,2},{7,3},{8,12},{9,13},{10,... | collective-permute-start | bytes 147464 | tf_op jit(solution)/shard_map/ppermute | solution.py:374
  29.0 1.2 %collective-permute-start.16 = (f32[16,768]{1,0:T(8,128)S(1)}, f32[16,768]{1,0:T(8,128)S(1)}, u32[]{:S(2)}, u32[]{:S(2)}) collective-permute-start(f32[16,768]{1,0:T(8,128)S(1)} %get-tuple-element.38), channel_id=1, source_target_pairs={{0,4},{1,5},{2,6},{3,7},{4,0},{5,1},{6,2},{7,3},{8,12},{9,13},{10,... | collective-permute-start | bytes 147464 | tf_op jit(solution)/shard_map/ppermute | solution.py:374
  29.0 1.4 %collective-permute-start.17 = (f32[16,768]{1,0:T(8,128)S(1)}, f32[16,768]{1,0:T(8,128)S(1)}, u32[]{:S(2)}, u32[]{:S(2)}) collective-permute-start(f32[16,768]{1,0:T(8,128)S(1)} %get-tuple-element.39), channel_id=1, source_target_pairs={{0,4},{1,5},{2,6},{3,7},{4,0},{5,1},{6,2},{7,3},{8,12},{9,13},{10,... | collective-permute-start | bytes 147464 | tf_op jit(solution)/shard_map/ppermute | solution.py:374
  30.9 15.7 %copy-start.2 = (s32[3,64]{1,0:T(4,128)S(1)}, s32[3,64]{1,0:T(4,128)}, u32[]{:S(2)}) copy-start(s32[3,64]{1,0:T(4,128)} %refs_0_.7) | copy-start | bytes 2308
  30.9 12.5 %collective-permute-start.21 = (f32[16,768]{1,0:T(8,128)S(1)}, f32[16,768]{1,0:T(8,128)S(1)}, u32[]{:S(2)}, u32[]{:S(2)}) collective-permute-start(f32[16,768]{1,0:T(8,128)S(1)} %get-tuple-element.41), channel_id=1, source_target_pairs={{0,4},{1,5},{2,6},{3,7},{4,20},{5,1},{6,2},{7,24},{8,3},{9,13},{10... | collective-permute-start | bytes 147464 | tf_op jit(solution)/shard_map/ppermute | solution.py:374
  30.9 12.5 %collective-permute-start.20 = (f32[16,768]{1,0:T(8,128)S(1)}, f32[16,768]{1,0:T(8,128)S(1)}, u32[]{:S(2)}, u32[]{:S(2)}) collective-permute-start(f32[16,768]{1,0:T(8,128)S(1)} %get-tuple-element.41), channel_id=1, source_target_pairs={{0,4},{1,5},{2,6},{3,7},{4,0},{5,1},{6,9},{7,17},{8,2},{9,13},{10,... | collective-permute-start | bytes 147464 | tf_op jit(solution)/shard_map/ppermute | solution.py:374
  39.4 4.5 %collective-permute-start.19 = (f32[16,768]{1,0:T(8,128)S(1)}, f32[16,768]{1,0:T(8,128)S(1)}, u32[]{:S(2)}, u32[]{:S(2)}) collective-permute-start(f32[16,768]{1,0:T(8,128)S(1)} %get-tuple-element.41), channel_id=1, source_target_pairs={{0,4},{1,5},{2,6},{3,7},{4,0},{5,12},{6,25},{7,3},{8,1},{9,13},{10... | collective-permute-start | bytes 147464 | tf_op jit(solution)/shard_map/ppermute | solution.py:374
  39.4 5.1 %collective-permute-start.18 = (f32[16,768]{1,0:T(8,128)S(1)}, f32[16,768]{1,0:T(8,128)S(1)}, u32[]{:S(2)}, u32[]{:S(2)}) collective-permute-start(f32[16,768]{1,0:T(8,128)S(1)} %get-tuple-element.41), channel_id=1, source_target_pairs={{0,4},{1,5},{2,6},{3,7},{4,12},{5,20},{6,2},{7,3},{8,0},{9,13},{10... | collective-permute-start | bytes 147464 | tf_op jit(solution)/shard_map/ppermute | solution.py:374
  39.9 4.6 %collective-permute-start.24 = (f32[16,768]{1,0:T(8,128)S(1)}, f32[16,768]{1,0:T(8,128)S(1)}, u32[]{:S(2)}, u32[]{:S(2)}) collective-permute-start(f32[16,768]{1,0:T(8,128)S(1)} %get-tuple-element.42.t), channel_id=1, source_target_pairs={{0,4},{1,5},{2,6},{3,7},{4,0},{5,1},{6,2},{7,3},{8,11},{9,13},{10,... | collective-permute-start | bytes 147464 | tf_op jit(solution)/shard_map/ppermute | solution.py:374
  43.4 1.2 %collective-permute-start.23 = (f32[16,768]{1,0:T(8,128)S(1)}, f32[16,768]{1,0:T(8,128)S(1)}, u32[]{:S(2)}, u32[]{:S(2)}) collective-permute-start(f32[16,768]{1,0:T(8,128)S(1)} %get-tuple-element.42.t), channel_id=1, source_target_pairs={{0,4},{1,5},{2,6},{3,7},{4,0},{5,1},{6,2},{7,3},{8,10},{9,13},{10,... | collective-permute-start | bytes 147464 | tf_op jit(solution)/shard_map/ppermute | solution.py:374
  43.4 1.4 %collective-permute-start.22 = (f32[16,768]{1,0:T(8,128)S(1)}, f32[16,768]{1,0:T(8,128)S(1)}, u32[]{:S(2)}, u32[]{:S(2)}) collective-permute-start(f32[16,768]{1,0:T(8,128)S(1)} %get-tuple-element.42.t), channel_id=1, source_target_pairs={{0,4},{1,5},{2,6},{3,7},{4,0},{5,1},{6,2},{7,3},{8,9},{9,13},{10,1... | collective-permute-start | bytes 147464 | tf_op jit(solution)/shard_map/ppermute | solution.py:374
  44.9 1.3 %collective-permute-start.25 = (f32[16,768]{1,0:T(8,128)S(1)}, f32[16,768]{1,0:T(8,128)S(1)}, u32[]{:S(2)}, u32[]{:S(2)}) collective-permute-start(f32[16,768]{1,0:T(8,128)S(1)} %shard_map.65.own), channel_id=1, source_target_pairs={{0,4},{4,0},{8,12},{12,8},{16,20},{20,16},{24,28},{28,24},{1,5},{5... | collective-permute-start | bytes 147464 | tf_op jit(solution)/shard_map/ppermute | solution.py:387
  47.9 1.7 %collective-permute-start.26 = (bf16[4,16,1024]{2,1,0:T(8,128)(2,1)S(1)}, bf16[4,16,1024]{2,1,0:T(8,128)(2,1)S(1)}, u32[]{:S(2)}, u32[]{:S(2)}) collective-permute-start(bf16[4,16,1024]{2,1,0:T(8,128)(2,1)S(1)} %shard_map.68), channel_id=1, source_target_pairs={{0,4},{4,0},{8,12},{12,8},{16,20},{20,16},{24,28},{28,24},{1,5},{5... | collective-permute-start | bytes 393224 | tf_op jit(solution)/shard_map/ppermute | solution.py:193
  49.6 5.4 %collective-permute-start.27 = (bf16[16,1024]{1,0:T(8,128)(2,1)S(1)}, bf16[16,1024]{1,0:T(8,128)(2,1)S(1)}, u32[]{:S(2)}, u32[]{:S(2)}) collective-permute-start(bf16[16,1024]{1,0:T(8,128)(2,1)S(1)} %get-tuple-element.46), channel_id=1, source_target_pairs={{0,8},{4,12},{8,0},{12,4},{16,24},{20,28},{24,16},{28,20},{1,9},{5... | collective-permute-start | bytes 98312 | tf_op jit(solution)/shard_map/ppermute | solution.py:193
  53.2 3.9 %collective-permute-start.28 = (bf16[16,1024]{1,0:T(8,128)(2,1)S(1)}, bf16[16,1024]{1,0:T(8,128)(2,1)S(1)}, u32[]{:S(2)}, u32[]{:S(2)}) collective-permute-start(bf16[16,1024]{1,0:T(8,128)(2,1)S(1)} %get-tuple-element.47), channel_id=1, source_target_pairs={{0,16},{4,20},{8,24},{12,28},{16,0},{20,4},{24,8},{28,12},{1,17},{... | collective-permute-start | bytes 98312 | tf_op jit(solution)/shard_map/ppermute | solution.py:193
  54.5 4.8 %collective-permute-start.29 = (bf16[16,1024]{1,0:T(8,128)(2,1)S(1)}, bf16[16,1024]{1,0:T(8,128)(2,1)S(1)}, u32[]{:S(2)}, u32[]{:S(2)}) collective-permute-start(bf16[16,1024]{1,0:T(8,128)(2,1)S(1)} %get-tuple-element.48), channel_id=1, source_target_pairs={{0,24},{4,28},{8,16},{12,20},{16,8},{20,12},{24,0},{28,4},{1,25},{... | collective-permute-start | bytes 98312 | tf_op jit(solution)/shard_map/ppermute | solution.py:193
  (1 other events, 8.6 us)
